TPU v7x, 256 devices: a whole 4x4x8 slice. The times are simulated.
256 devices in a mesh: batch: 8 (over x, z_hi), seq: 4 (over y), mp: 8 (over z_lo, core).
Axes of the slice: x: 4, y: 4, z: 8 (z_hi: 2, z_lo: 4; z = z_hi * 4 + z_lo), core: 2. Of those that a mesh axis runs over, the one named last changes fastest.
Arguments:
- context: bfloat16 [4096, 6144], P(('batch', 'seq'), 'mp'), may hold values from -0.1875 to 0.1875
- cotangent: bfloat16 [4096, 6144], P(('batch', 'seq'), 'mp'), may hold values from -6 to 6
- out_weight: bfloat16 [6144, 6144], P(None, 'mp'), may hold values from -0.078125 to 0.078125
Outputs:
- grad_weight: float32 [6144, 6144], P(('batch', 'seq'), 'mp')
- grad_context: bfloat16 [4096, 6144], P(('batch', 'seq'), 'mp')
All inputs are finite; a program needn't handle non-finite values.
Results may differ from a plain program's by a relative error of at most 0.001.
Values may be sent and summed in bfloat16 or wider, within the bound.
No kernel may reach another device: no remote copies, remote signals or barrier semaphores. Data moves between devices by JAX's collectives and lax.ppermute only.
A program may use at most 64 MiB of HBM per device.

v0:
```python
import jax
import jax.numpy as jnp
from jax import lax
from jax.sharding import PartitionSpec as P


def joined_along(blocks, dim):
    dims = list(blocks.shape[1:])
    dims[dim] *= blocks.shape[0]
    return jnp.moveaxis(blocks, 0, dim).reshape(dims)


def copy_for_each(array, axis):
    copies = jnp.broadcast_to(array, (lax.axis_size(axis), *array.shape))
    return lax.all_to_all(copies, axis, split_axis=0, concat_axis=0, tiled=True)


def gathered_copies(array, axis, dim):
    return joined_along(copy_for_each(array, axis), dim)


def shards(context, cotangent, out_weight):
    groups = lax.axis_size(("batch", "seq"))
    members = lax.axis_size("mp")
    split_rows = lax.all_to_all(context, "mp", split_axis=0, concat_axis=1, tiled=True)
    block_rows = lax.all_to_all(
        split_rows, ("batch", "seq"), split_axis=1, concat_axis=0, tiled=True
    )
    feature_block = gathered_copies(block_rows, "mp", 0)
    all_cotangent = lax.all_gather(cotangent, ("batch", "seq"), axis=0, tiled=True)
    share = split_rows.shape[0]
    shaped_context = feature_block.reshape(members, groups, share, feature_block.shape[1])
    shaped_cotangent = all_cotangent.reshape(groups, members, share, all_cotangent.shape[1])
    grad_weight = lax.dot_general(
        shaped_context,
        shaped_cotangent,
        (((0, 1, 2), (1, 0, 2)), ((), ())),
        preferred_element_type=jnp.float32,
    )
    partial_input = lax.dot_general(
        cotangent, out_weight, (((1,), (1,)), ((), ())), preferred_element_type=jnp.float32
    )
    grad_context = lax.psum_scatter(partial_input, "mp", scatter_dimension=1, tiled=True).astype(
        jnp.bfloat16
    )
    return (grad_weight, grad_context)


def solution(mesh):
    return jax.shard_map(
        shards,
        mesh=mesh,
        in_specs=(P(("batch", "seq"), "mp"), P(("batch", "seq"), "mp"), P(None, "mp")),
        out_specs=(P(("batch", "seq"), "mp"), P(("batch", "seq"), "mp")),
        check_vma=False,
    )
```

profile of v0, /device:TPU:1, one launch (start us, length us, event | category | flops | bytes accessed | tf_op | source)
XLA Modules:
  0.0 193.0 jit_solution(11909060434958061613)
XLA Ops:
  8.0 0.0 copy-start
  8.0 0.0 reduce-scatter.2.cloned.1.call-start
  8.1 8.6 %fusion.5 = f32[128,6144]{1,0:T(8,128)} fusion(bf16[128,768]{1,0:T(8,128)(2,1)} %param.4, bf16[6144,768]{1,0:T(8,128)(2,1)} %param.5), kind=kOutput, calls=%fused_computation.3 | convolution fusion | flops 1207959552 | bytes 12779520 | tf_op jit(solution)/shard_map/dot_general | solution.py:40
  16.7 0.0 reduce-scatter.2.cloned.1.call-update
  16.7 0.0 all-gather.2.cloned.1.call-start
  16.7 0.5 all-gather.2.cloned.1.call-update
  17.3 0.0 copy-done
  17.3 13.7 %all_to_all.40 = bf16[8,16,768]{2,1,0:T(8,128)(2,1)S(1)} all-to-all(bf16[8,16,768]{2,1,0:T(8,128)(2,1)S(1)} %bitcast.17), channel_id=1, replica_groups=mesh['batch'=8,'seq'=4,'mp'=8] {'mp'}, dimensions={0} | all-to-all | bytes 393216 | tf_op jit(solution)/shard_map/all_to_all | solution.py:25
  31.0 0.1 copy.9
  31.1 0.3 all_to_all.32
  31.3 0.2 copy.10
  31.5 28.9 %all_to_all.41 = bf16[16,32,192]{2,0,1:T(8,128)(2,1)S(1)} all-to-all(bf16[16,32,192]{2,0,1:T(8,128)(2,1)S(1)} %copy.10), channel_id=1, replica_groups=mesh['batch'=8,'seq'=4,'mp'=8] {'batch','seq'}, dimensions={1} | all-to-all | bytes 393216 | tf_op jit(solution)/shard_map/all_to_all | solution.py:26
  60.4 0.1 copy.11
  60.5 0.1 broadcast_in_dim.3
  60.6 57.5 %all_to_all.42 = bf16[8,512,192]{1,2,0:T(8,128)(2,1)S(1)} all-to-all(bf16[8,512,192]{1,2,0:T(8,128)(2,1)S(1)} %broadcast_in_dim.3), channel_id=1, replica_groups=mesh['batch'=8,'seq'=4,'mp'=8] {'mp'}, dimensions={0} | all-to-all | bytes 3145728 | tf_op jit(solution)/shard_map/all_to_all | solution.py:15
  118.2 2.4 %copy.12 = bf16[8,512,192]{2,1,0:T(8,128)(2,1)} copy(bf16[8,512,192]{1,2,0:T(8,128)(2,1)S(1)} %all_to_all.42) | data formatting | bytes 3145728 | tf_op jit(solution)/shard_map/all_to_all | solution.py:15
  120.6 0.0 reduce-scatter.2.cloned.1.call-done
  120.6 1.7 convert_element_type.3
  122.3 57.6 %all-gather.2.cloned.1.call-done = bf16[4096,768]{1,0:T(8,128)(2,1)} async-done(((bf16[128,768]{1,0:T(8,128)(2,1)}), bf16[4096,768]{1,0:T(8,128)(2,1)}) %all-gather.2.cloned.1.call-update) | async-done | bytes 6291472 | tf_op jit(solution)/shard_map/all_gather | solution.py:30
  179.9 5.7 %fusion.2 = f32[192,768]{1,0:T(8,128)} fusion(bf16[8,32,16,192]{3,2,1,0:T(8,128)(2,1)} %bitcast.14, bf16[32,8,16,768]{3,2,1,0:T(8,128)(2,1)} %bitcast.18), kind=kOutput, calls=%fused_computation.2 | convolution fusion | flops 1207959552 | bytes 8454144 | tf_op jit(solution)/shard_map/dot_general | solution.py:34
Async XLA Ops:
  8.0 9.3 %copy-start = (bf16[128,768]{1,0:T(8,128)(2,1)S(1)}, bf16[128,768]{1,0:T(8,128)(2,1)}, u32[]{:S(2)}) copy-start(bf16[128,768]{1,0:T(8,128)(2,1)} %param.3) | copy-start | bytes 589828
  8.0 112.6 %reduce-scatter.2.cloned.1.call-start = ((), (), s32[]{:S(2)}) async-start(), calls=%async_computation.5 | async-start | bytes 3538944 | tf_op jit(solution)/shard_map/reduce_scatter | solution.py:43
  16.7 163.2 %all-gather.2.cloned.1.call-start = ((), (), s32[]{:S(2)}) async-start(), calls=%async_computation.4 | async-start | bytes 6488064 | tf_op jit(solution)/shard_map/all_gather | solution.py:30
Sparse Core Ops, SparseCore 0:
  16.8 84.8 reduce-scatter.1
Sparse Core Ops, SparseCore 1:
  20.6 159.2 all-gather.1
where the time goes:
time: 193 us
  blocking collectives  100 us (52%)
  waiting for transfers between devices  58.1 us (30%)
  between operations  15.5 us (8%)
  matrix products  14.3 us (7%)
  local copies, waits for them, and re-layouts  3.13 us (2%)
    all_gather x1, waiting for transfers between devices, shards(): lax.all_gather(cotangent, ('batch', 'seq'), axis=0, tiled=True)  57.6 us
    all_to_all x1, blocking collectives, copy_for_each(): return lax.all_to_all(copies, axis, split_axis=0, concat_axis=0, tiled=True)  57.5 us
    all_to_all x1, blocking collectives, shards(): lax.all_to_all(split_rows, ('batch', 'seq'), split_axis=1, concat_axis=0,...  28.9 us
    all_to_all x1, blocking collectives, shards(): lax.all_to_all(context, 'mp', split_axis=0, concat_axis=1, tiled=True)  13.7 us
    dot_general x1, matrix products, shards(): lax.dot_general(cotangent, out_weight, (((1,), (1,)), ((), ())), preferre...  8.62 us
    dot_general x1, matrix products, shards(): lax.dot_general(shaped_context, shaped_cotangent, (((0, 1, 2), (1, 0, 2))...  5.66 us
  transfers between devices with their start and end apart: 2, of which 1 were waited for; matrix products, arithmetic and copies ran while one was open for 2% of the time, Pallas kernels for 0%

commit v1 on v0

v1 whole, which is shorter than its diff:
```python
import functools

import jax
import jax.numpy as jnp
from jax import lax
from jax.experimental import pallas as pl
from jax.experimental.pallas import tpu as pltpu
from jax.sharding import PartitionSpec as P


AXES = ("batch", "seq", "mp")
F32 = jnp.float32
BF16 = jnp.bfloat16
VMEM = pl.BlockSpec(memory_space=pltpu.VMEM)
SMEM = pl.BlockSpec(memory_space=pltpu.SMEM)

GIVEN, KEPT, PICK, LOW, MIXED, CORE = 0, 8, 16, 24, 25, 26


def place(x, h, y, l, c):
    return ((x * 2 + h) * 4 + y) * 8 + l * 2 + c


def pairs(route):
    return [
        (place(x, h, y, l, c), place(*route(x, h, y, l, c)))
        for x in range(4)
        for h in range(2)
        for y in range(4)
        for l in range(4)
        for c in range(2)
    ]


def ring(step):
    def route(x, h, y, l, c):
        z = (4 * h + l + step) % 8
        return x, z // 4, y, z % 4, c

    return route


def crosswise(k, first):
    def route(x, h, y, l, c):
        if (c == 0) == first:
            return x ^ k, h, y, l, c
        return x, h, y ^ k, l, c

    return route


def send(array, route):
    return lax.ppermute(array, AXES, pairs(route))


def at(stack, index):
    return lax.dynamic_index_in_dim(stack, index, 0, keepdims=False)


def product(weight, near, far, use_far):
    right = jnp.where(use_far, far[...], near[...])
    return lax.dot_general(
        weight[...], right, (((1,), (1,)), ((), ())), preferred_element_type=F32
    )


def given_kernel(table, weight, near, far, out):
    i = pl.program_id(0)
    out[0] = product(weight, near, far, table[PICK + i] == 1)


def kept_kernel(table, weight, near, far, taken, here, after, before, skip_up, skip_down):
    i = pl.program_id(0)
    total = product(weight, near, far, table[PICK + i] == 1) + taken[0]
    for j, out in enumerate((here, after, before)):

        @pl.when(i // 2 == j)
        def _(out=out):
            out[...] = total

    for j, out in ((6, skip_up), (7, skip_down)):

        @pl.when(i == j)
        def _(out=out):
            out[...] = total


def products(start, table, weight, near, far, taken=None):
    tokens, depth = near.shape
    rows = depth // 2
    whole = pl.BlockSpec((tokens, depth), lambda i, t: (0, 0))
    specs = [pl.BlockSpec((rows, depth), lambda i, t: (t[start + i], 0)), whole, whole]
    step = pl.BlockSpec((1, rows, tokens), lambda i, t: (i, 0, 0))
    args = [table, weight, near, far]
    if taken is None:
        kernel, shapes, outs = given_kernel, jax.ShapeDtypeStruct((8, rows, tokens), F32), step
    else:
        kernel = kept_kernel
        specs.append(step)
        args.append(taken)
        shapes = [jax.ShapeDtypeStruct((n * rows, tokens), F32) for n in (2, 2, 2, 1, 1)]
        outs = [
            pl.BlockSpec((rows, tokens), lambda i, t, j=j: (jnp.clip(i - 2 * j, 0, 1), 0))
            for j in range(3)
        ] + [pl.BlockSpec((rows, tokens), lambda i, t: (0, 0))] * 2
    return pl.pallas_call(
        kernel,
        out_shape=shapes,
        grid_spec=pltpu.PrefetchScalarGridSpec(
            num_scalar_prefetch=1, grid=(8,), in_specs=specs, out_specs=outs
        ),
        cost_estimate=pl.CostEstimate(
            flops=16 * rows * tokens * depth,
            bytes_accessed=8 * rows * depth * 2 + 8 * rows * tokens * 4,
            transcendentals=0,
        ),
    )(*args)


def finish_kernel(here, before, after, two_before, two_after, out):
    rows = two_before.shape[0]
    for i, skip in enumerate((two_before, two_after)):
        part = pl.ds(i * rows, rows)
        total = here[part, :] + before[part, :] + after[part, :] + skip[...]
        out[:, part] = total.T.astype(BF16)


def weight_kernel(far, table, own, other, *refs):
    cots, out = refs[:4], refs[-1]
    low, core = table[LOW], table[CORE]
    use_own = table[MIXED] == far
    total = refs[4][...] if far else jnp.zeros(out.shape, F32)
    for piece, cot in enumerate(cots):
        for half in range(2):
            lefts = []
            for m in (2 * half, 2 * half + 1):
                r = jnp.where(core == 0, m, piece)
                s = jnp.where(core == 0, piece, m)
                k = low ^ r
                lefts.append(jnp.where(use_own, own[k, s], other[k, s]))
            left = jnp.concatenate(lefts, axis=1)
            right = cot[pl.ds(256 * half, 256), :]
            total += jnp.dot(left, right, preferred_element_type=F32)
    out[...] = total


def weight_part(far, table, own, other, cots, total=()):
    rows, width = own.shape[2], cots[0].shape[1]
    return pl.pallas_call(
        functools.partial(weight_kernel, far),
        out_shape=jax.ShapeDtypeStruct((rows, width), F32),
        in_specs=[SMEM] + [VMEM] * (6 + len(total)),
        out_specs=VMEM,
        cost_estimate=pl.CostEstimate(
            flops=2 * rows * width * 512 * 4,
            bytes_accessed=4 * 512 * width * 2,
            transcendentals=0,
        ),
    )(table, own, other, *cots, *total)


def scalars(h, l, c):
    relative = jnp.array([0, 0, 1, 1, 3, 3, 2, 2], jnp.int32)
    step = jnp.array([0, 0, 1, 1, -1, -1, 2, -2], jnp.int32)
    half = jnp.array([0, 1] * 4, jnp.int32)
    block = (l + relative) % 4 * 4 + half
    pick = ((4 * h + l + step + 8) % 8 // 4 != h).astype(jnp.int32)
    rest = jnp.stack([l, c ^ h, c])
    return jnp.concatenate([block + 2 * (1 - c), block + 2 * c, pick, rest]).astype(jnp.int32)


def step(context, cotangent, out_weight):
    batch, y, mp = (lax.axis_index(a) for a in AXES)
    h = batch % 2
    l, c = mp // 2, mp % 2
    tokens, width = cotangent.shape
    quarter = width // 4
    table = scalars(h, l, c)

    def gather(array):
        first = [array] + [send(array, crosswise(k, True)) for k in (1, 2, 3)]
        row = jnp.concatenate(first)
        return [row] + [send(row, crosswise(k, False)) for k in (1, 2, 3)]

    near_cots = gather(cotangent)
    far_cot = send(cotangent, ring(4))
    far_cots = gather(far_cot)

    turned = context.T.reshape(4, quarter, tokens)
    mine = jnp.stack(
        [
            send(at(turned, y ^ s), lambda x, h, y, l, c, s=s: (l, c, y ^ s, l ^ x, h))
            for s in range(4)
        ]
    )
    own = jnp.stack(
        [mine]
        + [send(mine, lambda x, h, y, l, c, k=k: (x, h, y, l ^ k, c)) for k in (1, 2, 3)]
    )
    swap = lambda x, h, y, l, c: (x, h, y, l, 1 - c)
    other = send(own, swap)

    given = products(GIVEN, table, out_weight, cotangent, far_cot)
    taken = send(given, swap)
    here, after, before, skip_up, skip_down = products(
        KEPT, table, out_weight, cotangent, far_cot, taken
    )
    from_before = send(after, ring(1))
    from_after = send(before, ring(-1))
    from_two_before = send(skip_up, ring(2))
    from_two_after = send(skip_down, ring(-2))

    near_part = weight_part(0, table, own, other, near_cots)
    grad_weight = weight_part(1, table, own, other, far_cots, (near_part,))
    grad_context = pl.pallas_call(
        finish_kernel,
        out_shape=jax.ShapeDtypeStruct((tokens, width), BF16),
        in_specs=[VMEM] * 5,
        out_specs=VMEM,
        cost_estimate=pl.CostEstimate(
            flops=4 * tokens * width, bytes_accessed=18 * tokens * width, transcendentals=0
        ),
    )(here, from_before, from_after, from_two_before, from_two_after)
    return grad_weight, grad_context


def solution(mesh):
    return jax.shard_map(
        step,
        mesh=mesh,
        in_specs=(P(("batch", "seq"), "mp"), P(("batch", "seq"), "mp"), P(None, "mp")),
        out_specs=(P(("batch", "seq"), "mp"), P(("batch", "seq"), "mp")),
        check_vma=False,
    )
```

time: 193 us -> 125 us (0.65)
  blocking collectives: 100 us -> 0 us
  starting transfers between devices: 0.08 us -> 64.9 us
  waiting for transfers between devices: 58.1 us -> 21.4 us
  Pallas kernels: 0 us -> 26.8 us
  between operations: 15.5 us -> 0.82 us
  matrix products: 14.3 us -> 0 us
  local copies, waits for them, and re-layouts: 3.13 us -> 9.05 us
    all_to_all x3 -> x0, blocking collectives: 100 us -> none  [the longest x1 57.5 us: copy_for_each(): return lax.all_to_all(copies, axis, split_axis=0, concat_axis=0, tiled=True)]
    ppermute x0 -> x26, starting transfers between devices: none -> 64.9 us  [send(): return lax.ppermute(array, AXES, pairs(route))]
    all_gather x1 -> x0, waiting for transfers between devices: 57.6 us -> none  [shards(): lax.all_gather(cotangent, ('batch', 'seq'), axis=0, tiled=True)]
    pallas_call x0 -> x5, Pallas kernels: none -> 26.8 us  [the longest x2 16.6 us: products(): pl.pallas_call(kernel, out_shape=shapes, grid_spec=pltpu.PrefetchScalarGr...]
    ppermute x0 -> x26, waiting for transfers between devices: none -> 21.4 us  [send(): return lax.ppermute(array, AXES, pairs(route))]
    dot_general x2 -> x0, matrix products: 14.3 us -> none  [the longest x1 8.62 us: shards(): lax.dot_general(cotangent, out_weight, (((1,), (1,)), ((), ())), preferre...]
    unnamed x2 -> x31, local copies, waits for them, and re-layouts: 0.01 us -> 6.95 us
    all_to_all x5 -> x0, local copies, waits for them, and re-layouts: 3 us -> none  [the longest x1 2.41 us: copy_for_each(): return lax.all_to_all(copies, axis, split_axis=0, concat_axis=0, tiled=True)]
  transfers between devices with their start and end apart: 2 -> 26, of which waited for: 1 -> 9; matrix products, arithmetic and copies ran while one was open for 2% -> 7% of each run, Pallas kernels for 0% -> 13%
where the time goes in v1:
time: 125 us
  starting transfers between devices  64.9 us (52%)
  Pallas kernels  26.8 us (21%)
  waiting for transfers between devices  21.4 us (17%)
  local copies, waits for them, and re-layouts  9.05 us (7%)
  other arithmetic  1.51 us (1%)
    ppermute x26, starting transfers between devices, send(): return lax.ppermute(array, AXES, pairs(route))  64.9 us
    ppermute x26, waiting for transfers between devices, send(): return lax.ppermute(array, AXES, pairs(route))  21.4 us
    pallas_call x2, Pallas kernels, products(): pl.pallas_call(kernel, out_shape=shapes, grid_spec=pltpu.PrefetchScalarGr...  16.6 us
    pallas_call x2, Pallas kernels, weight_part(): pl.pallas_call(functools.partial(weight_kernel, far), out_shape=jax.Shape...  8.04 us
    unnamed x31, local copies, waits for them, and re-layouts  6.95 us
  transfers between devices with their start and end apart: 26, of which 9 were waited for; matrix products, arithmetic and copies ran while one was open for 7% of the time, Pallas kernels for 13%

profile of v1, /device:TPU:1, one launch (start us, length us, event | category | flops | bytes accessed | tf_op | source)
XLA Modules:
  0.0 124.6 jit_solution(5350396227268590194)
XLA Ops:
  0.6 7.8 %collective-permute-start.8 = (bf16[128,768]{1,0:T(8,128)(2,1)}, bf16[128,768]{1,0:T(8,128)(2,1)S(1)}, u32[]{:S(2)}, u32[]{:S(2)}) collective-permute-start(bf16[128,768]{1,0:T(8,128)(2,1)} %near.3), channel_id=1, source_target_pairs={{0,32},{1,33},{2,34},{3,35},{4,36},{5,37},{6,38},{7,39},{8,40},{9,... | collective-permute-start | bytes 589832 | tf_op jit(solution)/shard_map/ppermute | solution.py:53
  8.4 1.1 copy.12
  9.5 0.7 compare_convert_fusion
  10.2 0.7 broadcast_add_fusion
  10.9 0.7 concatenate.9.table
  11.6 1.2 collective-permute-done.8.far
  12.8 0.7 copy-done.3
  13.5 8.0 %shard_map.79 = f32[8,384,128]{2,1,0:T(8,128)} custom-call(s32[27]{0:T(128)} %concatenate.9.table, bf16[6144,768]{1,0:T(8,128)(2,1)} %weight.3, bf16[128,768]{1,0:T(8,128)(2,1)} %near.3, bf16[128,768]{1,0:T(8,128)(2,1)} %copy-done.3), custom_call_target="tpu_custom_call" | custom-call | flops 603979776 | bytes 6291456 | tf_op jit(solution)/shard_map/pallas_call | solution.py:106
  21.5 1.8 %collective-permute-start.21 = (f32[8,384,128]{2,1,0:T(8,128)}, f32[8,384,128]{2,1,0:T(8,128)S(1)}, u32[]{:S(2)}, u32[]{:S(2)}) collective-permute-start(f32[8,384,128]{2,1,0:T(8,128)} %shard_map.79), channel_id=1, source_target_pairs={{0,1},{1,0},{2,3},{3,2},{4,5},{5,4},{6,7},{7,6},{8,9},{9,8},{10,11... | collective-permute-start | bytes 4718600 | tf_op jit(solution)/shard_map/ppermute | solution.py:53
  23.3 11.4 %collective-permute-start.2 = (bf16[192,128]{1,0:T(8,128)(2,1)S(1)}, bf16[192,128]{1,0:T(8,128)(2,1)S(1)}, u32[]{:S(2)}, u32[]{:S(2)}) collective-permute-start(bf16[192,128]{1,0:T(8,128)(2,1)S(1)} %get-tuple-element.18), channel_id=1, source_target_pairs={{0,16},{1,48},{2,82},{3,114},{4,148},{5,180},{6,214},{7,246},{8,24... | collective-permute-start | bytes 147464 | tf_op jit(solution)/shard_map/ppermute | solution.py:53
  35.1 2.2 %collective-permute-start.3 = (bf16[192,128]{1,0:T(8,128)(2,1)S(1)}, bf16[192,128]{1,0:T(8,128)(2,1)S(1)}, u32[]{:S(2)}, u32[]{:S(2)}) collective-permute-start(bf16[192,128]{1,0:T(8,128)(2,1)S(1)} %get-tuple-element.17), channel_id=1, source_target_pairs={{0,24},{1,56},{2,90},{3,122},{4,156},{5,188},{6,222},{7,254},{8,16... | collective-permute-start | bytes 147464 | tf_op jit(solution)/shard_map/ppermute | solution.py:53
  37.3 5.4 %collective-permute-start = (bf16[192,128]{1,0:T(8,128)(2,1)S(1)}, bf16[192,128]{1,0:T(8,128)(2,1)S(1)}, u32[]{:S(2)}, u32[]{:S(2)}) collective-permute-start(bf16[192,128]{1,0:T(8,128)(2,1)S(1)} %get-tuple-element.16), channel_id=1, source_target_pairs={{0,0},{1,32},{2,66},{3,98},{4,132},{5,164},{6,198},{7,230},{8,8},{... | collective-permute-start | bytes 147464 | tf_op jit(solution)/shard_map/ppermute | solution.py:53
  42.8 0.9 collective-permute-start.1
  43.7 0.7 constant_dynamic-update-slice_fusion.7
  44.6 3.9 %collective-permute-start.16 = (bf16[128,768]{1,0:T(8,128)(2,1)S(1)}, bf16[128,768]{1,0:T(8,128)(2,1)S(1)}, u32[]{:S(2)}, u32[]{:S(2)}) collective-permute-start(bf16[128,768]{1,0:T(8,128)(2,1)S(1)} %copy-done.2), channel_id=1, source_target_pairs={{0,128},{1,17},{2,130},{3,19},{4,132},{5,21},{6,134},{7,23},{8,136... | collective-permute-start | bytes 589832 | tf_op jit(solution)/shard_map/ppermute | solution.py:53
  48.5 0.8 collective-permute-start.17
  49.3 2.0 %collective-permute-done.1 = bf16[192,128]{1,0:T(8,128)(2,1)S(1)} collective-permute-done((bf16[192,128]{1,0:T(8,128)(2,1)S(1)}, bf16[192,128]{1,0:T(8,128)(2,1)S(1)}, u32[]{:S(2)}, u32[]{:S(2)}) %collective-permute-start.1) | collective-permute-done | bytes 49184 | tf_op jit(solution)/shard_map/ppermute | solution.py:53
  51.3 1.5 %collective-permute-start.4 = (bf16[4,192,128]{2,1,0:T(8,128)(2,1)S(1)}, bf16[4,192,128]{2,1,0:T(8,128)(2,1)S(1)}, u32[]{:S(2)}, u32[]{:S(2)}) collective-permute-start(bf16[4,192,128]{2,1,0:T(8,128)(2,1)S(1)} %get-tuple-element.15), channel_id=1, source_target_pairs={{0,2},{1,3},{2,0},{3,1},{4,6},{5,7},{6,4},{7,5},{8,10},{9,11},{10,... | collective-permute-start | bytes 589832 | tf_op jit(solution)/shard_map/ppermute | solution.py:53
  52.8 1.7 %collective-permute-start.5 = (bf16[4,192,128]{2,1,0:T(8,128)(2,1)S(1)}, bf16[4,192,128]{2,1,0:T(8,128)(2,1)S(1)}, u32[]{:S(2)}, u32[]{:S(2)}) collective-permute-start(bf16[4,192,128]{2,1,0:T(8,128)(2,1)S(1)} %get-tuple-element.15), channel_id=1, source_target_pairs={{0,4},{1,5},{2,6},{3,7},{4,0},{5,1},{6,2},{7,3},{8,12},{9,13},{10,... | collective-permute-start | bytes 589832 | tf_op jit(solution)/shard_map/ppermute | solution.py:53
  54.6 0.7 constant_dynamic-update-slice_fusion.6
  55.2 0.7 constant_dynamic-update-slice_fusion.5
  55.9 0.7 constant_dynamic-update-slice_fusion.4.refs_0_
  56.6 4.4 %collective-permute-start.18 = (bf16[512,768]{1,0:T(8,128)(2,1)}, bf16[512,768]{1,0:T(8,128)(2,1)S(1)}, u32[]{:S(2)}, u32[]{:S(2)}) collective-permute-start(bf16[512,768]{1,0:T(8,128)(2,1)} %constant_dynamic-update-slice_fusion.4.refs_0_), channel_id=1, source_target_pairs={{0,8},{1,65},{2,10},{3,67},{4,12},{5,69},{6,14},{7,71},{8,0},{9,73... | collective-permute-start | bytes 2359304 | tf_op jit(solution)/shard_map/ppermute | solution.py:53
  61.0 1.1 collective-permute-start.19
  62.1 1.1 collective-permute-start.6
  63.2 1.0 collective-permute-start.9
  64.2 0.7 constant_dynamic-update-slice_fusion.3
  64.8 3.9 %collective-permute-done.6 = bf16[4,192,128]{2,1,0:T(8,128)(2,1)S(1)} collective-permute-done((bf16[4,192,128]{2,1,0:T(8,128)(2,1)S(1)}, bf16[4,192,128]{2,1,0:T(8,128)(2,1)S(1)}, u32[]{:S(2)}, u32[]{:S(2)}) %collective-permute-start.6) | collective-permute-done | bytes 196640 | tf_op jit(solution)/shard_map/ppermute | solution.py:53
  68.8 2.8 %collective-permute-start.10 = (bf16[128,768]{1,0:T(8,128)(2,1)S(1)}, bf16[128,768]{1,0:T(8,128)(2,1)S(1)}, u32[]{:S(2)}, u32[]{:S(2)}) collective-permute-start(bf16[128,768]{1,0:T(8,128)(2,1)S(1)} %copy-done.4), channel_id=1, source_target_pairs={{0,128},{1,17},{2,130},{3,19},{4,132},{5,21},{6,134},{7,23},{8,136... | collective-permute-start | bytes 589832 | tf_op jit(solution)/shard_map/ppermute | solution.py:53
  71.6 1.6 %collective-permute-start.11 = (bf16[128,768]{1,0:T(8,128)(2,1)S(1)}, bf16[128,768]{1,0:T(8,128)(2,1)S(1)}, u32[]{:S(2)}, u32[]{:S(2)}) collective-permute-start(bf16[128,768]{1,0:T(8,128)(2,1)S(1)} %copy-done.4), channel_id=1, source_target_pairs={{0,192},{1,25},{2,194},{3,27},{4,196},{5,29},{6,198},{7,31},{8,200... | collective-permute-start | bytes 589832 | tf_op jit(solution)/shard_map/ppermute | solution.py:53
  73.3 0.7 constant_dynamic-update-slice_fusion.2
  74.0 3.2 %collective-permute-done.10 = bf16[128,768]{1,0:T(8,128)(2,1)S(1)} collective-permute-done((bf16[128,768]{1,0:T(8,128)(2,1)S(1)}, bf16[128,768]{1,0:T(8,128)(2,1)S(1)}, u32[]{:S(2)}, u32[]{:S(2)}) %collective-permute-start.10) | collective-permute-done | bytes 196640 | tf_op jit(solution)/shard_map/ppermute | solution.py:53
  77.2 1.4 %collective-permute-start.20 = (bf16[512,768]{1,0:T(8,128)(2,1)}, bf16[512,768]{1,0:T(8,128)(2,1)}, u32[]{:S(2)}, u32[]{:S(2)}) collective-permute-start(bf16[512,768]{1,0:T(8,128)(2,1)} %constant_dynamic-update-slice_fusion.4.refs_0_), channel_id=1, source_target_pairs={{0,24},{1,193},{2,26},{3,195},{4,28},{5,197},{6,30},{7,199},{8,16}... | collective-permute-start | bytes 2359304 | tf_op jit(solution)/shard_map/ppermute | solution.py:53
  78.6 5.5 %collective-permute-done.11 = bf16[128,768]{1,0:T(8,128)(2,1)S(1)} collective-permute-done((bf16[128,768]{1,0:T(8,128)(2,1)S(1)}, bf16[128,768]{1,0:T(8,128)(2,1)S(1)}, u32[]{:S(2)}, u32[]{:S(2)}) %collective-permute-start.11) | collective-permute-done | bytes 196640 | tf_op jit(solution)/shard_map/ppermute | solution.py:53
  84.0 0.7 constant_dynamic-update-slice_fusion.1
  84.7 0.7 constant_dynamic-update-slice_fusion.refs_0_
  85.5 2.6 %collective-permute-start.13 = (bf16[512,768]{1,0:T(8,128)(2,1)}, bf16[512,768]{1,0:T(8,128)(2,1)}, u32[]{:S(2)}, u32[]{:S(2)}) collective-permute-start(bf16[512,768]{1,0:T(8,128)(2,1)} %constant_dynamic-update-slice_fusion.refs_0_), channel_id=1, source_target_pairs={{0,16},{1,129},{2,18},{3,131},{4,20},{5,133},{6,22},{7,135},{8,24}... | collective-permute-start | bytes 2359304 | tf_op jit(solution)/shard_map/ppermute | solution.py:53
  88.1 1.3 %collective-permute-start.14 = (bf16[512,768]{1,0:T(8,128)(2,1)}, bf16[512,768]{1,0:T(8,128)(2,1)}, u32[]{:S(2)}, u32[]{:S(2)}) collective-permute-start(bf16[512,768]{1,0:T(8,128)(2,1)} %constant_dynamic-update-slice_fusion.refs_0_), channel_id=1, source_target_pairs={{0,24},{1,193},{2,26},{3,195},{4,28},{5,197},{6,30},{7,199},{8,16}... | collective-permute-start | bytes 2359304 | tf_op jit(solution)/shard_map/ppermute | solution.py:53
  89.4 8.6 %shard_map.80 = (f32[768,128]{1,0:T(8,128)}, f32[768,128]{1,0:T(8,128)}, f32[768,128]{1,0:T(8,128)}, f32[384,128]{1,0:T(8,128)}, f32[384,128]{1,0:T(8,128)}) custom-call(s32[27]{0:T(128)} %concatenate.9.table, bf16[6144,768]{1,0:T(8,128)(2,1)} %weight.3, bf16[128,768]{1,0:T(8,128)(2,1)} %near.3, bf16[128,768]{1,0:T(8,128)(2,1)} %copy-done.3, ...), custom_call_target="tpu_custom_call" | custom-call | flops 603979776 | bytes 6291456 | tf_op jit(solution)/shard_map/pallas_call | solution.py:106
  98.0 4.6 %collective-permute-start.22 = (f32[768,128]{1,0:T(8,128)}, f32[768,128]{1,0:T(8,128)S(1)}, u32[]{:S(2)}, u32[]{:S(2)}) collective-permute-start(f32[768,128]{1,0:T(8,128)} %get-tuple-element.8), channel_id=1, source_target_pairs={{0,2},{1,3},{2,4},{3,5},{4,6},{5,7},{6,32},{7,33},{8,10},{9,11},{1... | collective-permute-start | bytes 1179656 | tf_op jit(solution)/shard_map/ppermute | solution.py:53
  102.7 1.9 %collective-permute-start.24 = (f32[384,128]{1,0:T(8,128)}, f32[384,128]{1,0:T(8,128)S(1)}, u32[]{:S(2)}, u32[]{:S(2)}) collective-permute-start(f32[384,128]{1,0:T(8,128)} %get-tuple-element.10), channel_id=1, source_target_pairs={{0,4},{1,5},{2,6},{3,7},{4,32},{5,33},{6,34},{7,35},{8,12},{9,13},... | collective-permute-start | bytes 589832 | tf_op jit(solution)/shard_map/ppermute | solution.py:53
  104.6 1.9 %collective-permute-done.13.refs_2_ = bf16[512,768]{1,0:T(8,128)(2,1)} collective-permute-done((bf16[512,768]{1,0:T(8,128)(2,1)}, bf16[512,768]{1,0:T(8,128)(2,1)}, u32[]{:S(2)}, u32[]{:S(2)}) %collective-permute-start.13) | collective-permute-done | bytes 786464 | tf_op jit(solution)/shard_map/ppermute | solution.py:53
  106.5 3.4 %collective-permute-start.25 = (f32[384,128]{1,0:T(8,128)}, f32[384,128]{1,0:T(8,128)S(1)}, u32[]{:S(2)}, u32[]{:S(2)}) collective-permute-start(f32[384,128]{1,0:T(8,128)} %get-tuple-element.11), channel_id=1, source_target_pairs={{0,36},{1,37},{2,38},{3,39},{4,0},{5,1},{6,2},{7,3},{8,44},{9,45},... | collective-permute-start | bytes 589832 | tf_op jit(solution)/shard_map/ppermute | solution.py:53
  109.9 4.0 %shard_map.77.refs_4_ = f32[192,768]{1,0:T(8,128)} custom-call(s32[27]{0:T(128)} %concatenate.9.table, bf16[4,4,192,128]{3,2,1,0:T(8,128)(2,1)} %copy-done, bf16[4,4,192,128]{3,2,1,0:T(8,128)(2,1)} %copy-done.1, bf16[512,768]{1,0:T(8,128)(2,1)} %constant_dynamic-update-slice_fusion.4.refs_0_, bf16[512,768]{1,0:T(8,128)(2,1)} %copy-done.6, ...), custom_call_target="tpu_custom_call" | custom-call | flops 603979776 | bytes 3145728 | tf_op jit(solution)/shard_map/pallas_call | solution.py:149
  113.8 4.1 %shard_map.78 = f32[192,768]{1,0:T(8,128)} custom-call(s32[27]{0:T(128)} %concatenate.9.table, bf16[4,4,192,128]{3,2,1,0:T(8,128)(2,1)} %copy-done, bf16[4,4,192,128]{3,2,1,0:T(8,128)(2,1)} %copy-done.1, bf16[512,768]{1,0:T(8,128)(2,1)} %constant_dynamic-update-slice_fusion.refs_0_, bf16[512,768]{1,0:T(8,128)(2,1)} %collective-permute-done.12.refs_1_, ...), custom_call_target="tpu_custom_call" | custom-call | flops 603979776 | bytes 3145728 | tf_op jit(solution)/shard_map/pallas_call | solution.py:149
  117.9 1.1 collective-permute-done.24.two_before
  119.0 2.4 %collective-permute-done.25.two_after = f32[384,128]{1,0:T(8,128)S(1)} collective-permute-done((f32[384,128]{1,0:T(8,128)}, f32[384,128]{1,0:T(8,128)S(1)}, u32[]{:S(2)}, u32[]{:S(2)}) %collective-permute-start.25) | collective-permute-done | bytes 196640 | tf_op jit(solution)/shard_map/ppermute | solution.py:53
  122.4 2.2 %shard_map.81 = bf16[128,768]{1,0:T(8,128)(2,1)} custom-call(f32[768,128]{1,0:T(8,128)} %get-tuple-element.7.here, f32[768,128]{1,0:T(8,128)} %copy-done.8, f32[768,128]{1,0:T(8,128)} %copy-done.9, f32[384,128]{1,0:T(8,128)} %copy-done.10, f32[384,128]{1,0:T(8,128)} %copy-done.11), custom_call_target="tpu_custom_call" | custom-call | flops 393216 | bytes 1769472 | tf_op jit(solution)/shard_map/pallas_call | solution.py:215
  (49 shorter events, 1.8 us)
Async XLA Ops:
  0.6 12.2 %collective-permute-start.8 = (bf16[128,768]{1,0:T(8,128)(2,1)}, bf16[128,768]{1,0:T(8,128)(2,1)S(1)}, u32[]{:S(2)}, u32[]{:S(2)}) collective-permute-start(bf16[128,768]{1,0:T(8,128)(2,1)} %near.3), channel_id=1, source_target_pairs={{0,32},{1,33},{2,34},{3,35},{4,36},{5,37},{6,38},{7,39},{8,40},{9,... | collective-permute-start | bytes 589832 | tf_op jit(solution)/shard_map/ppermute | solution.py:53
  11.6 23.1 %copy-start.2 = (bf16[128,768]{1,0:T(8,128)(2,1)S(1)}, bf16[128,768]{1,0:T(8,128)(2,1)}, u32[]{:S(2)}) copy-start(bf16[128,768]{1,0:T(8,128)(2,1)} %near.3) | copy-start | bytes 589828
  12.8 0.7 copy-start.3
  21.5 41.7 %copy-start.4 = (bf16[128,768]{1,0:T(8,128)(2,1)S(1)}, bf16[128,768]{1,0:T(8,128)(2,1)}, u32[]{:S(2)}) copy-start(bf16[128,768]{1,0:T(8,128)(2,1)} %copy-done.3) | copy-start | bytes 589828
  21.5 66.6 %collective-permute-start.21 = (f32[8,384,128]{2,1,0:T(8,128)}, f32[8,384,128]{2,1,0:T(8,128)S(1)}, u32[]{:S(2)}, u32[]{:S(2)}) collective-permute-start(f32[8,384,128]{2,1,0:T(8,128)} %shard_map.79), channel_id=1, source_target_pairs={{0,1},{1,0},{2,3},{3,2},{4,5},{5,4},{6,7},{7,6},{8,9},{9,8},{10,11... | collective-permute-start | bytes 4718600 | tf_op jit(solution)/shard_map/ppermute | solution.py:53
  23.3 19.4 %collective-permute-start.2 = (bf16[192,128]{1,0:T(8,128)(2,1)S(1)}, bf16[192,128]{1,0:T(8,128)(2,1)S(1)}, u32[]{:S(2)}, u32[]{:S(2)}) collective-permute-start(bf16[192,128]{1,0:T(8,128)(2,1)S(1)} %get-tuple-element.18), channel_id=1, source_target_pairs={{0,16},{1,48},{2,82},{3,114},{4,148},{5,180},{6,214},{7,246},{8,24... | collective-permute-start | bytes 147464 | tf_op jit(solution)/shard_map/ppermute | solution.py:53
  34.7 18.1 %collective-permute-start.15 = (bf16[128,768]{1,0:T(8,128)(2,1)S(1)}, bf16[128,768]{1,0:T(8,128)(2,1)S(1)}, u32[]{:S(2)}, u32[]{:S(2)}) collective-permute-start(bf16[128,768]{1,0:T(8,128)(2,1)S(1)} %copy-done.2), channel_id=1, source_target_pairs={{0,64},{1,9},{2,66},{3,11},{4,68},{5,13},{6,70},{7,15},{8,72},{9,1... | collective-permute-start | bytes 589832 | tf_op jit(solution)/shard_map/ppermute | solution.py:53
  35.1 9.5 %collective-permute-start.3 = (bf16[192,128]{1,0:T(8,128)(2,1)S(1)}, bf16[192,128]{1,0:T(8,128)(2,1)S(1)}, u32[]{:S(2)}, u32[]{:S(2)}) collective-permute-start(bf16[192,128]{1,0:T(8,128)(2,1)S(1)} %get-tuple-element.17), channel_id=1, source_target_pairs={{0,24},{1,56},{2,90},{3,122},{4,156},{5,188},{6,222},{7,254},{8,16... | collective-permute-start | bytes 147464 | tf_op jit(solution)/shard_map/ppermute | solution.py:53
  37.3 11.2 %collective-permute-start = (bf16[192,128]{1,0:T(8,128)(2,1)S(1)}, bf16[192,128]{1,0:T(8,128)(2,1)S(1)}, u32[]{:S(2)}, u32[]{:S(2)}) collective-permute-start(bf16[192,128]{1,0:T(8,128)(2,1)S(1)} %get-tuple-element.16), channel_id=1, source_target_pairs={{0,0},{1,32},{2,66},{3,98},{4,132},{5,164},{6,198},{7,230},{8,8},{... | collective-permute-start | bytes 147464 | tf_op jit(solution)/shard_map/ppermute | solution.py:53
  42.8 8.5 %collective-permute-start.1 = (bf16[192,128]{1,0:T(8,128)(2,1)S(1)}, bf16[192,128]{1,0:T(8,128)(2,1)S(1)}, u32[]{:S(2)}, u32[]{:S(2)}) collective-permute-start(bf16[192,128]{1,0:T(8,128)(2,1)S(1)} %get-tuple-element.19), channel_id=1, source_target_pairs={{0,8},{1,40},{2,74},{3,106},{4,140},{5,172},{6,206},{7,238},{8,0},... | collective-permute-start | bytes 147464 | tf_op jit(solution)/shard_map/ppermute | solution.py:53
  44.6 10.6 %collective-permute-start.16 = (bf16[128,768]{1,0:T(8,128)(2,1)S(1)}, bf16[128,768]{1,0:T(8,128)(2,1)S(1)}, u32[]{:S(2)}, u32[]{:S(2)}) collective-permute-start(bf16[128,768]{1,0:T(8,128)(2,1)S(1)} %copy-done.2), channel_id=1, source_target_pairs={{0,128},{1,17},{2,130},{3,19},{4,132},{5,21},{6,134},{7,23},{8,136... | collective-permute-start | bytes 589832 | tf_op jit(solution)/shard_map/ppermute | solution.py:53
  48.5 7.4 %collective-permute-start.17 = (bf16[128,768]{1,0:T(8,128)(2,1)S(1)}, bf16[128,768]{1,0:T(8,128)(2,1)S(1)}, u32[]{:S(2)}, u32[]{:S(2)}) collective-permute-start(bf16[128,768]{1,0:T(8,128)(2,1)S(1)} %copy-done.2), channel_id=1, source_target_pairs={{0,192},{1,25},{2,194},{3,27},{4,196},{5,29},{6,198},{7,31},{8,200... | collective-permute-start | bytes 589832 | tf_op jit(solution)/shard_map/ppermute | solution.py:53
  51.3 10.8 %collective-permute-start.4 = (bf16[4,192,128]{2,1,0:T(8,128)(2,1)S(1)}, bf16[4,192,128]{2,1,0:T(8,128)(2,1)S(1)}, u32[]{:S(2)}, u32[]{:S(2)}) collective-permute-start(bf16[4,192,128]{2,1,0:T(8,128)(2,1)S(1)} %get-tuple-element.15), channel_id=1, source_target_pairs={{0,2},{1,3},{2,0},{3,1},{4,6},{5,7},{6,4},{7,5},{8,10},{9,11},{10,... | collective-permute-start | bytes 589832 | tf_op jit(solution)/shard_map/ppermute | solution.py:53
  52.8 10.4 %collective-permute-start.5 = (bf16[4,192,128]{2,1,0:T(8,128)(2,1)S(1)}, bf16[4,192,128]{2,1,0:T(8,128)(2,1)S(1)}, u32[]{:S(2)}, u32[]{:S(2)}) collective-permute-start(bf16[4,192,128]{2,1,0:T(8,128)(2,1)S(1)} %get-tuple-element.15), channel_id=1, source_target_pairs={{0,4},{1,5},{2,6},{3,7},{4,0},{5,1},{6,2},{7,3},{8,12},{9,13},{10,... | collective-permute-start | bytes 589832 | tf_op jit(solution)/shard_map/ppermute | solution.py:53
  56.6 28.8 %collective-permute-start.18 = (bf16[512,768]{1,0:T(8,128)(2,1)}, bf16[512,768]{1,0:T(8,128)(2,1)S(1)}, u32[]{:S(2)}, u32[]{:S(2)}) collective-permute-start(bf16[512,768]{1,0:T(8,128)(2,1)} %constant_dynamic-update-slice_fusion.4.refs_0_), channel_id=1, source_target_pairs={{0,8},{1,65},{2,10},{3,67},{4,12},{5,69},{6,14},{7,71},{8,0},{9,73... | collective-permute-start | bytes 2359304 | tf_op jit(solution)/shard_map/ppermute | solution.py:53
  61.0 24.4 %collective-permute-start.19 = (bf16[512,768]{1,0:T(8,128)(2,1)}, bf16[512,768]{1,0:T(8,128)(2,1)S(1)}, u32[]{:S(2)}, u32[]{:S(2)}) collective-permute-start(bf16[512,768]{1,0:T(8,128)(2,1)} %constant_dynamic-update-slice_fusion.4.refs_0_), channel_id=1, source_target_pairs={{0,16},{1,129},{2,18},{3,131},{4,20},{5,133},{6,22},{7,135},{8,24}... | collective-permute-start | bytes 2359304 | tf_op jit(solution)/shard_map/ppermute | solution.py:53
  62.1 6.7 %collective-permute-start.6 = (bf16[4,192,128]{2,1,0:T(8,128)(2,1)S(1)}, bf16[4,192,128]{2,1,0:T(8,128)(2,1)S(1)}, u32[]{:S(2)}, u32[]{:S(2)}) collective-permute-start(bf16[4,192,128]{2,1,0:T(8,128)(2,1)S(1)} %get-tuple-element.15), channel_id=1, source_target_pairs={{0,6},{1,7},{2,4},{3,5},{4,2},{5,3},{6,0},{7,1},{8,14},{9,15},{10,... | collective-permute-start | bytes 589832 | tf_op jit(solution)/shard_map/ppermute | solution.py:53
  63.2 8.4 %collective-permute-start.9 = (bf16[128,768]{1,0:T(8,128)(2,1)S(1)}, bf16[128,768]{1,0:T(8,128)(2,1)S(1)}, u32[]{:S(2)}, u32[]{:S(2)}) collective-permute-start(bf16[128,768]{1,0:T(8,128)(2,1)S(1)} %copy-done.4), channel_id=1, source_target_pairs={{0,64},{1,9},{2,66},{3,11},{4,68},{5,13},{6,70},{7,15},{8,72},{9,1... | collective-permute-start | bytes 589832 | tf_op jit(solution)/shard_map/ppermute | solution.py:53
  68.8 8.4 %collective-permute-start.10 = (bf16[128,768]{1,0:T(8,128)(2,1)S(1)}, bf16[128,768]{1,0:T(8,128)(2,1)S(1)}, u32[]{:S(2)}, u32[]{:S(2)}) collective-permute-start(bf16[128,768]{1,0:T(8,128)(2,1)S(1)} %copy-done.4), channel_id=1, source_target_pairs={{0,128},{1,17},{2,130},{3,19},{4,132},{5,21},{6,134},{7,23},{8,136... | collective-permute-start | bytes 589832 | tf_op jit(solution)/shard_map/ppermute | solution.py:53
  71.6 12.4 %collective-permute-start.11 = (bf16[128,768]{1,0:T(8,128)(2,1)S(1)}, bf16[128,768]{1,0:T(8,128)(2,1)S(1)}, u32[]{:S(2)}, u32[]{:S(2)}) collective-permute-start(bf16[128,768]{1,0:T(8,128)(2,1)S(1)} %copy-done.4), channel_id=1, source_target_pairs={{0,192},{1,25},{2,194},{3,27},{4,196},{5,29},{6,198},{7,31},{8,200... | collective-permute-start | bytes 589832 | tf_op jit(solution)/shard_map/ppermute | solution.py:53
  73.3 24.7 %copy-start = (bf16[4,4,192,128]{3,2,1,0:T(8,128)(2,1)}, bf16[4,4,192,128]{3,2,1,0:T(8,128)(2,1)S(1)}, u32[]{:S(2)}) copy-start(bf16[4,4,192,128]{3,2,1,0:T(8,128)(2,1)S(1)} %pad_maximum_fusion.own) | copy-start | bytes 2359300
  77.2 20.8 %collective-permute-start.20 = (bf16[512,768]{1,0:T(8,128)(2,1)}, bf16[512,768]{1,0:T(8,128)(2,1)}, u32[]{:S(2)}, u32[]{:S(2)}) collective-permute-start(bf16[512,768]{1,0:T(8,128)(2,1)} %constant_dynamic-update-slice_fusion.4.refs_0_), channel_id=1, source_target_pairs={{0,24},{1,193},{2,26},{3,195},{4,28},{5,197},{6,30},{7,199},{8,16}... | collective-permute-start | bytes 2359304 | tf_op jit(solution)/shard_map/ppermute | solution.py:53
  84.0 18.7 %collective-permute-start.7 = (bf16[4,4,192,128]{3,2,1,0:T(8,128)(2,1)S(1)}, bf16[4,4,192,128]{3,2,1,0:T(8,128)(2,1)S(1)}, u32[]{:S(2)}, u32[]{:S(2)}) collective-permute-start(bf16[4,4,192,128]{3,2,1,0:T(8,128)(2,1)S(1)} %pad_maximum_fusion.own), channel_id=1, source_target_pairs={{0,1},{1,0},{2,3},{3,2},{4,5},{5,4},{6,7},{7,6},{8,9},{9,8},{10,11... | collective-permute-start | bytes 2359304 | tf_op jit(solution)/shard_map/ppermute | solution.py:53
  85.4 2.6 %copy-start.6 = (bf16[512,768]{1,0:T(8,128)(2,1)}, bf16[512,768]{1,0:T(8,128)(2,1)S(1)}, u32[]{:S(2)}) copy-start(bf16[512,768]{1,0:T(8,128)(2,1)S(1)} %collective-permute-done.18.refs_1_) | copy-start | bytes 2359300
  85.4 17.3 %collective-permute-start.12 = (bf16[512,768]{1,0:T(8,128)(2,1)}, bf16[512,768]{1,0:T(8,128)(2,1)}, u32[]{:S(2)}, u32[]{:S(2)}) collective-permute-start(bf16[512,768]{1,0:T(8,128)(2,1)} %constant_dynamic-update-slice_fusion.refs_0_), channel_id=1, source_target_pairs={{0,8},{1,65},{2,10},{3,67},{4,12},{5,69},{6,14},{7,71},{8,0},{9,73... | collective-permute-start | bytes 2359304 | tf_op jit(solution)/shard_map/ppermute | solution.py:53
  85.4 2.6 %copy-start.7 = (bf16[512,768]{1,0:T(8,128)(2,1)}, bf16[512,768]{1,0:T(8,128)(2,1)S(1)}, u32[]{:S(2)}) copy-start(bf16[512,768]{1,0:T(8,128)(2,1)S(1)} %collective-permute-done.19.refs_2_) | copy-start | bytes 2359300
  85.5 21.0 %collective-permute-start.13 = (bf16[512,768]{1,0:T(8,128)(2,1)}, bf16[512,768]{1,0:T(8,128)(2,1)}, u32[]{:S(2)}, u32[]{:S(2)}) collective-permute-start(bf16[512,768]{1,0:T(8,128)(2,1)} %constant_dynamic-update-slice_fusion.refs_0_), channel_id=1, source_target_pairs={{0,16},{1,129},{2,18},{3,131},{4,20},{5,133},{6,22},{7,135},{8,24}... | collective-permute-start | bytes 2359304 | tf_op jit(solution)/shard_map/ppermute | solution.py:53
  88.1 1.4 %copy-start.5 = (f32[8,384,128]{2,1,0:T(8,128)}, f32[8,384,128]{2,1,0:T(8,128)S(1)}, u32[]{:S(2)}) copy-start(f32[8,384,128]{2,1,0:T(8,128)S(1)} %collective-permute-done.21.taken) | copy-start | bytes 4718596
  88.1 25.8 %collective-permute-start.14 = (bf16[512,768]{1,0:T(8,128)(2,1)}, bf16[512,768]{1,0:T(8,128)(2,1)}, u32[]{:S(2)}, u32[]{:S(2)}) collective-permute-start(bf16[512,768]{1,0:T(8,128)(2,1)} %constant_dynamic-update-slice_fusion.refs_0_), channel_id=1, source_target_pairs={{0,24},{1,193},{2,26},{3,195},{4,28},{5,197},{6,30},{7,199},{8,16}... | collective-permute-start | bytes 2359304 | tf_op jit(solution)/shard_map/ppermute | solution.py:53
  98.0 23.4 %collective-permute-start.22 = (f32[768,128]{1,0:T(8,128)}, f32[768,128]{1,0:T(8,128)S(1)}, u32[]{:S(2)}, u32[]{:S(2)}) collective-permute-start(f32[768,128]{1,0:T(8,128)} %get-tuple-element.8), channel_id=1, source_target_pairs={{0,2},{1,3},{2,4},{3,5},{4,6},{5,7},{6,32},{7,33},{8,10},{9,11},{1... | collective-permute-start | bytes 1179656 | tf_op jit(solution)/shard_map/ppermute | solution.py:53
  102.7 7.2 %copy-start.1 = (bf16[4,4,192,128]{3,2,1,0:T(8,128)(2,1)}, bf16[4,4,192,128]{3,2,1,0:T(8,128)(2,1)S(1)}, u32[]{:S(2)}) copy-start(bf16[4,4,192,128]{3,2,1,0:T(8,128)(2,1)S(1)} %collective-permute-done.7.other) | copy-start | bytes 2359300
  102.7 18.7 %collective-permute-start.23 = (f32[768,128]{1,0:T(8,128)}, f32[768,128]{1,0:T(8,128)S(1)}, u32[]{:S(2)}, u32[]{:S(2)}) collective-permute-start(f32[768,128]{1,0:T(8,128)} %get-tuple-element.9), channel_id=1, source_target_pairs={{0,38},{1,39},{2,0},{3,1},{4,2},{5,3},{6,4},{7,5},{8,46},{9,47},{1... | collective-permute-start | bytes 1179656 | tf_op jit(solution)/shard_map/ppermute | solution.py:53
  102.7 16.4 %collective-permute-start.24 = (f32[384,128]{1,0:T(8,128)}, f32[384,128]{1,0:T(8,128)S(1)}, u32[]{:S(2)}, u32[]{:S(2)}) collective-permute-start(f32[384,128]{1,0:T(8,128)} %get-tuple-element.10), channel_id=1, source_target_pairs={{0,4},{1,5},{2,6},{3,7},{4,32},{5,33},{6,34},{7,35},{8,12},{9,13},... | collective-permute-start | bytes 589832 | tf_op jit(solution)/shard_map/ppermute | solution.py:53
  106.5 14.9 %collective-permute-start.25 = (f32[384,128]{1,0:T(8,128)}, f32[384,128]{1,0:T(8,128)S(1)}, u32[]{:S(2)}, u32[]{:S(2)}) collective-permute-start(f32[384,128]{1,0:T(8,128)} %get-tuple-element.11), channel_id=1, source_target_pairs={{0,36},{1,37},{2,38},{3,39},{4,0},{5,1},{6,2},{7,3},{8,44},{9,45},... | collective-permute-start | bytes 589832 | tf_op jit(solution)/shard_map/ppermute | solution.py:53
  119.0 2.4 %copy-start.10 = (f32[384,128]{1,0:T(8,128)}, f32[384,128]{1,0:T(8,128)S(1)}, u32[]{:S(2)}) copy-start(f32[384,128]{1,0:T(8,128)S(1)} %collective-permute-done.24.two_before) | copy-start | bytes 589828
  121.4 0.7 copy-start.11
  121.4 0.8 copy-start.8
  121.4 1.0 copy-start.9

commit v2 on v1

--- a/solution.py
+++ b/solution.py
@@ -2,6 +2,7 @@
 
 import jax
 import jax.numpy as jnp
+import numpy as np
 from jax import lax
 from jax.experimental import pallas as pl
 from jax.experimental.pallas import tpu as pltpu
@@ -14,7 +15,7 @@
 VMEM = pl.BlockSpec(memory_space=pltpu.VMEM)
 SMEM = pl.BlockSpec(memory_space=pltpu.SMEM)
 
-GIVEN, KEPT, PICK, LOW, MIXED, CORE = 0, 8, 16, 24, 25, 26
+GIVEN, KEPT, PICK, LOW, MIXED, CORE = 0, 4, 8, 16, 17, 18
 
 
 def place(x, h, y, l, c):
@@ -57,61 +58,76 @@
     return lax.dynamic_index_in_dim(stack, index, 0, keepdims=False)
 
 
-def product(weight, near, far, use_far):
-    right = jnp.where(use_far, far[...], near[...])
-    return lax.dot_general(
-        weight[...], right, (((1,), (1,)), ((), ())), preferred_element_type=F32
-    )
-
-
-def given_kernel(table, weight, near, far, out):
+def turn(i, near, far, turned):
+    @pl.when(i == 0)
+    def _():
+        turned[0] = near[...].T
+        turned[1] = far[...].T
+
+
+def product(table, i, weight, turned, half):
+    rows = weight.shape[0] // 2
+    return jnp.dot(
+        weight[pl.ds(half * rows, rows), :],
+        turned[table[PICK + 2 * i + half]],
+        preferred_element_type=F32,
+    )
+
+
+def given_kernel(table, weight, near, far, out, turned):
     i = pl.program_id(0)
-    out[0] = product(weight, near, far, table[PICK + i] == 1)
-
-
-def kept_kernel(table, weight, near, far, taken, here, after, before, skip_up, skip_down):
+    turn(i, near, far, turned)
+    rows = weight.shape[0] // 2
+    for half in range(2):
+        out[0, pl.ds(half * rows, rows), :] = product(table, i, weight, turned, half)
+
+
+def kept_kernel(table, weight, near, far, taken, here, after, before, up, down, turned):
     i = pl.program_id(0)
-    total = product(weight, near, far, table[PICK + i] == 1) + taken[0]
-    for j, out in enumerate((here, after, before)):
-
-        @pl.when(i // 2 == j)
-        def _(out=out):
-            out[...] = total
-
-    for j, out in ((6, skip_up), (7, skip_down)):
-
-        @pl.when(i == j)
-        def _(out=out):
+    turn(i, near, far, turned)
+    rows = weight.shape[0] // 2
+    for half in range(2):
+        part = pl.ds(half * rows, rows)
+        total = product(table, i, weight, turned, half) + taken[0, part, :]
+        for j, out in enumerate((here, after, before)):
+
+            @pl.when(i == j)
+            def _(out=out, part=part, total=total):
+                out[part, :] = total
+
+        @pl.when(i == 3)
+        def _(out=(up, down)[half], total=total):
             out[...] = total
 
 
 def products(start, table, weight, near, far, taken=None):
     tokens, depth = near.shape
-    rows = depth // 2
     whole = pl.BlockSpec((tokens, depth), lambda i, t: (0, 0))
-    specs = [pl.BlockSpec((rows, depth), lambda i, t: (t[start + i], 0)), whole, whole]
-    step = pl.BlockSpec((1, rows, tokens), lambda i, t: (i, 0, 0))
+    specs = [pl.BlockSpec((depth, depth), lambda i, t: (t[start + i], 0)), whole, whole]
+    block = pl.BlockSpec((1, depth, tokens), lambda i, t: (i, 0, 0))
     args = [table, weight, near, far]
     if taken is None:
-        kernel, shapes, outs = given_kernel, jax.ShapeDtypeStruct((8, rows, tokens), F32), step
+        kernel, shapes, outs = given_kernel, jax.ShapeDtypeStruct((4, depth, tokens), F32), block
     else:
         kernel = kept_kernel
-        specs.append(step)
+        specs.append(block)
         args.append(taken)
-        shapes = [jax.ShapeDtypeStruct((n * rows, tokens), F32) for n in (2, 2, 2, 1, 1)]
-        outs = [
-            pl.BlockSpec((rows, tokens), lambda i, t, j=j: (jnp.clip(i - 2 * j, 0, 1), 0))
-            for j in range(3)
-        ] + [pl.BlockSpec((rows, tokens), lambda i, t: (0, 0))] * 2
+        rows = [depth, depth, depth, depth // 2, depth // 2]
+        shapes = [jax.ShapeDtypeStruct((n, tokens), F32) for n in rows]
+        outs = [pl.BlockSpec((n, tokens), lambda i, t: (0, 0)) for n in rows]
     return pl.pallas_call(
         kernel,
         out_shape=shapes,
         grid_spec=pltpu.PrefetchScalarGridSpec(
-            num_scalar_prefetch=1, grid=(8,), in_specs=specs, out_specs=outs
+            num_scalar_prefetch=1,
+            grid=(4,),
+            in_specs=specs,
+            out_specs=outs,
+            scratch_shapes=[pltpu.VMEM((2, depth, tokens), BF16)],
         ),
         cost_estimate=pl.CostEstimate(
-            flops=16 * rows * tokens * depth,
-            bytes_accessed=8 * rows * depth * 2 + 8 * rows * tokens * 4,
+            flops=8 * depth * tokens * depth,
+            bytes_accessed=8 * depth * depth + 16 * depth * tokens,
             transcendentals=0,
         ),
     )(*args)
@@ -159,23 +175,27 @@
     )(table, own, other, *cots, *total)
 
 
-def scalars(h, l, c):
-    relative = jnp.array([0, 0, 1, 1, 3, 3, 2, 2], jnp.int32)
-    step = jnp.array([0, 0, 1, 1, -1, -1, 2, -2], jnp.int32)
-    half = jnp.array([0, 1] * 4, jnp.int32)
-    block = (l + relative) % 4 * 4 + half
-    pick = ((4 * h + l + step + 8) % 8 // 4 != h).astype(jnp.int32)
-    rest = jnp.stack([l, c ^ h, c])
-    return jnp.concatenate([block + 2 * (1 - c), block + 2 * c, pick, rest]).astype(jnp.int32)
+def scalars(device):
+    rows = []
+    for _ in range(4):
+        for h in range(2):
+            for _ in range(4):
+                for l in range(4):
+                    for c in range(2):
+                        block = [(l + r) % 4 * 2 for r in (0, 1, 3, 2)]
+                        step = (0, 0, 1, 1, -1, -1, 2, -2)
+                        pick = [int((4 * h + l + d) % 8 // 4 != h) for d in step]
+                        given = [b + 1 - c for b in block]
+                        kept = [b + c for b in block]
+                        rows.append(given + kept + pick + [l, c ^ h, c, 0, 0, 0, 0, 0])
+    return at(jnp.asarray(np.array(rows, np.int32)), device)
 
 
 def step(context, cotangent, out_weight):
     batch, y, mp = (lax.axis_index(a) for a in AXES)
-    h = batch % 2
-    l, c = mp // 2, mp % 2
     tokens, width = cotangent.shape
     quarter = width // 4
-    table = scalars(h, l, c)
+    table = scalars((batch * 4 + y) * 8 + mp)
 
     def gather(array):
         first = [array] + [send(array, crosswise(k, True)) for k in (1, 2, 3)]
@@ -186,11 +206,13 @@
     far_cot = send(cotangent, ring(4))
     far_cots = gather(far_cot)
 
-    turned = context.T.reshape(4, quarter, tokens)
+    block = send(context, lambda x, h, y, l, c: (l, c, y, l ^ x, h))
+    turned = block.T.reshape(4, quarter, tokens)
     mine = jnp.stack(
-        [
-            send(at(turned, y ^ s), lambda x, h, y, l, c, s=s: (l, c, y ^ s, l ^ x, h))
-            for s in range(4)
+        [at(turned, y)]
+        + [
+            send(at(turned, y ^ k), lambda x, h, y, l, c, k=k: (x, h, y ^ k, l, c))
+            for k in (1, 2, 3)
         ]
     )
     own = jnp.stack(

time: 125 us -> 116 us (0.928)
  the two profiles are of different devices: /device:TPU:1 before, /device:TPU:64 now
where the time goes in v2:
time: 116 us; the launch traced here: 115 us
  starting transfers between devices  45.5 us (39%)
  waiting for transfers between devices  33.8 us (29%)
  Pallas kernels  24 us (21%)
  local copies, waits for them, and re-layouts  11.2 us (10%)
    ppermute x26, starting transfers between devices, send(): return lax.ppermute(array, AXES, pairs(route))  45.5 us
    ppermute x26, waiting for transfers between devices, send(): return lax.ppermute(array, AXES, pairs(route))  33.8 us
    pallas_call x2, Pallas kernels, products(): pl.pallas_call(kernel, out_shape=shapes, grid_spec=pltpu.PrefetchScalarGr...  13.8 us
    unnamed x30, local copies, waits for them, and re-layouts  8.37 us
    pallas_call x2, Pallas kernels, weight_part(): pl.pallas_call(functools.partial(weight_kernel, far), out_shape=jax.Shape...  8.03 us
  transfers between devices with their start and end apart: 26, of which 9 were waited for; matrix products, arithmetic and copies ran while one was open for 6% of the time, Pallas kernels for 19%

profile of v2, /device:TPU:64, one launch (start us, length us, event | category | flops | bytes accessed | tf_op | source)
XLA Modules:
  0.0 115.4 jit_solution(7969120939350501744)
XLA Ops:
  0.6 5.5 %collective-permute-start.8 = (bf16[128,768]{1,0:T(8,128)(2,1)}, bf16[128,768]{1,0:T(8,128)(2,1)S(1)}, u32[]{:S(2)}, u32[]{:S(2)}) collective-permute-start(bf16[128,768]{1,0:T(8,128)(2,1)} %near.3), channel_id=1, source_target_pairs={{0,32},{1,33},{2,34},{3,35},{4,36},{5,37},{6,38},{7,39},{8,40},{9,... | collective-permute-start | bytes 589832 | tf_op jit(solution)/shard_map/ppermute | solution.py:54
  6.1 1.5 %collective-permute-start.15 = (bf16[128,768]{1,0:T(8,128)(2,1)}, bf16[128,768]{1,0:T(8,128)(2,1)S(1)}, u32[]{:S(2)}, u32[]{:S(2)}) collective-permute-start(bf16[128,768]{1,0:T(8,128)(2,1)} %near.3), channel_id=1, source_target_pairs={{0,64},{1,9},{2,66},{3,11},{4,68},{5,13},{6,70},{7,15},{8,72},{9,1... | collective-permute-start | bytes 589832 | tf_op jit(solution)/shard_map/ppermute | solution.py:54
  7.6 2.7 %collective-permute-start.16 = (bf16[128,768]{1,0:T(8,128)(2,1)}, bf16[128,768]{1,0:T(8,128)(2,1)S(1)}, u32[]{:S(2)}, u32[]{:S(2)}) collective-permute-start(bf16[128,768]{1,0:T(8,128)(2,1)} %near.3), channel_id=1, source_target_pairs={{0,128},{1,17},{2,130},{3,19},{4,132},{5,21},{6,134},{7,23},{8,136... | collective-permute-start | bytes 589832 | tf_op jit(solution)/shard_map/ppermute | solution.py:54
  10.3 0.5 collective-permute-start.17
  10.8 3.7 %collective-permute-start = (bf16[128,768]{1,0:T(8,128)(2,1)}, bf16[128,768]{1,0:T(8,128)(2,1)S(1)}, u32[]{:S(2)}, u32[]{:S(2)}) collective-permute-start(bf16[128,768]{1,0:T(8,128)(2,1)} %param.4), channel_id=1, source_target_pairs={{0,0},{1,32},{2,66},{3,98},{4,132},{5,164},{6,198},{7,230},{8,8},{... | collective-permute-start | bytes 589832 | tf_op jit(solution)/shard_map/ppermute | solution.py:54
  14.5 1.2 %fusion.table = s32[24]{0:T(128)} fusion(s32[256,24]{1,0:T(8,128)} %constant.40.clone, s32[]{:T(128)S(6)} %select_n.17), kind=kLoop, calls=%fused_computation.15 | loop fusion | bytes 196 | tf_op jit(solution)/shard_map/jit(dynamic_index_in_dim)/squeeze | solution.py:58
  15.8 0.7 copy-done.3
  16.5 6.0 %shard_map.61 = f32[4,768,128]{2,1,0:T(8,128)} custom-call(s32[24]{0:T(128)} %fusion.table, bf16[6144,768]{1,0:T(8,128)(2,1)} %weight.3, bf16[128,768]{1,0:T(8,128)(2,1)} %near.3, bf16[128,768]{1,0:T(8,128)(2,1)} %copy-done.3), custom_call_target="tpu_custom_call" | custom-call | flops 603979776 | bytes 6291456 | tf_op jit(solution)/shard_map/pallas_call | solution.py:118
  22.5 0.7 constant_dynamic-update-slice_fusion.7
  23.2 0.2 copy.6
  23.4 0.7 constant_dynamic-update-slice_fusion.6
  24.1 0.7 constant_dynamic-update-slice_fusion.5
  24.8 0.7 constant_dynamic-update-slice_fusion.4.refs_0_
  25.5 1.6 %collective-permute-start.18 = (bf16[512,768]{1,0:T(8,128)(2,1)}, bf16[512,768]{1,0:T(8,128)(2,1)S(1)}, u32[]{:S(2)}, u32[]{:S(2)}) collective-permute-start(bf16[512,768]{1,0:T(8,128)(2,1)} %constant_dynamic-update-slice_fusion.4.refs_0_), channel_id=1, source_target_pairs={{0,8},{1,65},{2,10},{3,67},{4,12},{5,69},{6,14},{7,71},{8,0},{9,73... | collective-permute-start | bytes 2359304 | tf_op jit(solution)/shard_map/ppermute | solution.py:54
  27.2 2.0 %collective-permute-start.9 = (bf16[128,768]{1,0:T(8,128)(2,1)S(1)}, bf16[128,768]{1,0:T(8,128)(2,1)S(1)}, u32[]{:S(2)}, u32[]{:S(2)}) collective-permute-start(bf16[128,768]{1,0:T(8,128)(2,1)S(1)} %copy-done.4), channel_id=1, source_target_pairs={{0,64},{1,9},{2,66},{3,11},{4,68},{5,13},{6,70},{7,15},{8,72},{9,1... | collective-permute-start | bytes 589832 | tf_op jit(solution)/shard_map/ppermute | solution.py:54
  29.3 3.6 %collective-permute-start.2 = (bf16[192,128]{1,0:T(8,128)(2,1)S(1)}, bf16[192,128]{1,0:T(8,128)(2,1)S(1)}, u32[]{:S(2)}, u32[]{:S(2)}) collective-permute-start(bf16[192,128]{1,0:T(8,128)(2,1)S(1)} %get-tuple-element.16), channel_id=1, source_target_pairs={{0,16},{1,17},{2,18},{3,19},{4,20},{5,21},{6,22},{7,23},{8,24},{9,... | collective-permute-start | bytes 147464 | tf_op jit(solution)/shard_map/ppermute | solution.py:54
  32.9 10.2 %collective-permute-done.1 = bf16[192,128]{1,0:T(8,128)(2,1)S(1)} collective-permute-done((bf16[192,128]{1,0:T(8,128)(2,1)S(1)}, bf16[192,128]{1,0:T(8,128)(2,1)S(1)}, u32[]{:S(2)}, u32[]{:S(2)}) %collective-permute-start.1) | collective-permute-done | bytes 49184 | tf_op jit(solution)/shard_map/ppermute | solution.py:54
  43.1 4.7 %collective-permute-start.10 = (bf16[128,768]{1,0:T(8,128)(2,1)S(1)}, bf16[128,768]{1,0:T(8,128)(2,1)S(1)}, u32[]{:S(2)}, u32[]{:S(2)}) collective-permute-start(bf16[128,768]{1,0:T(8,128)(2,1)S(1)} %copy-done.4), channel_id=1, source_target_pairs={{0,128},{1,17},{2,130},{3,19},{4,132},{5,21},{6,134},{7,23},{8,136... | collective-permute-start | bytes 589832 | tf_op jit(solution)/shard_map/ppermute | solution.py:54
  47.8 3.0 %collective-permute-start.3 = (bf16[192,128]{1,0:T(8,128)(2,1)S(1)}, bf16[192,128]{1,0:T(8,128)(2,1)S(1)}, u32[]{:S(2)}, u32[]{:S(2)}) collective-permute-start(bf16[192,128]{1,0:T(8,128)(2,1)S(1)} %get-tuple-element.15), channel_id=1, source_target_pairs={{0,24},{1,25},{2,26},{3,27},{4,28},{5,29},{6,30},{7,31},{8,16},{9,... | collective-permute-start | bytes 147464 | tf_op jit(solution)/shard_map/ppermute | solution.py:54
  50.8 2.9 %collective-permute-done.3 = bf16[192,128]{1,0:T(8,128)(2,1)S(1)} collective-permute-done((bf16[192,128]{1,0:T(8,128)(2,1)S(1)}, bf16[192,128]{1,0:T(8,128)(2,1)S(1)}, u32[]{:S(2)}, u32[]{:S(2)}) %collective-permute-start.3) | collective-permute-done | bytes 49184 | tf_op jit(solution)/shard_map/ppermute | solution.py:54
  53.7 1.4 %collective-permute-start.19 = (bf16[512,768]{1,0:T(8,128)(2,1)}, bf16[512,768]{1,0:T(8,128)(2,1)S(1)}, u32[]{:S(2)}, u32[]{:S(2)}) collective-permute-start(bf16[512,768]{1,0:T(8,128)(2,1)} %constant_dynamic-update-slice_fusion.4.refs_0_), channel_id=1, source_target_pairs={{0,16},{1,129},{2,18},{3,131},{4,20},{5,133},{6,22},{7,135},{8,24}... | collective-permute-start | bytes 2359304 | tf_op jit(solution)/shard_map/ppermute | solution.py:54
  55.1 0.3 collective-permute-start.11
  55.5 1.4 %collective-permute-start.4 = (bf16[4,192,128]{2,1,0:T(8,128)(2,1)S(1)}, bf16[4,192,128]{2,1,0:T(8,128)(2,1)S(1)}, u32[]{:S(2)}, u32[]{:S(2)}) collective-permute-start(bf16[4,192,128]{2,1,0:T(8,128)(2,1)S(1)} %get-tuple-element.13), channel_id=1, source_target_pairs={{0,2},{1,3},{2,0},{3,1},{4,6},{5,7},{6,4},{7,5},{8,10},{9,11},{10,... | collective-permute-start | bytes 589832 | tf_op jit(solution)/shard_map/ppermute | solution.py:54
  56.8 0.7 constant_dynamic-update-slice_fusion.3
  57.5 4.5 %collective-permute-done.11 = bf16[128,768]{1,0:T(8,128)(2,1)S(1)} collective-permute-done((bf16[128,768]{1,0:T(8,128)(2,1)S(1)}, bf16[128,768]{1,0:T(8,128)(2,1)S(1)}, u32[]{:S(2)}, u32[]{:S(2)}) %collective-permute-start.11) | collective-permute-done | bytes 196640 | tf_op jit(solution)/shard_map/ppermute | solution.py:54
  62.0 0.7 constant_dynamic-update-slice_fusion.2
  62.7 0.6 collective-permute-done.4
  63.3 1.1 collective-permute-start.6
  64.4 0.7 constant_dynamic-update-slice_fusion.1
  65.1 3.5 %collective-permute-done.5 = bf16[4,192,128]{2,1,0:T(8,128)(2,1)S(1)} collective-permute-done((bf16[4,192,128]{2,1,0:T(8,128)(2,1)S(1)}, bf16[4,192,128]{2,1,0:T(8,128)(2,1)S(1)}, u32[]{:S(2)}, u32[]{:S(2)}) %collective-permute-start.5) | collective-permute-done | bytes 196640 | tf_op jit(solution)/shard_map/ppermute | solution.py:54
  68.6 1.0 collective-permute-start.20
  69.7 0.7 constant_dynamic-update-slice_fusion.refs_0_
  70.4 3.3 %collective-permute-done.6 = bf16[4,192,128]{2,1,0:T(8,128)(2,1)S(1)} collective-permute-done((bf16[4,192,128]{2,1,0:T(8,128)(2,1)S(1)}, bf16[4,192,128]{2,1,0:T(8,128)(2,1)S(1)}, u32[]{:S(2)}, u32[]{:S(2)}) %collective-permute-start.6) | collective-permute-done | bytes 196640 | tf_op jit(solution)/shard_map/ppermute | solution.py:54
  73.6 3.9 %collective-permute-start.12 = (bf16[512,768]{1,0:T(8,128)(2,1)}, bf16[512,768]{1,0:T(8,128)(2,1)}, u32[]{:S(2)}, u32[]{:S(2)}) collective-permute-start(bf16[512,768]{1,0:T(8,128)(2,1)} %constant_dynamic-update-slice_fusion.refs_0_), channel_id=1, source_target_pairs={{0,8},{1,65},{2,10},{3,67},{4,12},{5,69},{6,14},{7,71},{8,0},{9,73... | collective-permute-start | bytes 2359304 | tf_op jit(solution)/shard_map/ppermute | solution.py:54
  77.6 0.9 copy-done.6
  78.7 0.8 copy-done.7
  79.5 1.9 %collective-permute-start.14 = (bf16[512,768]{1,0:T(8,128)(2,1)}, bf16[512,768]{1,0:T(8,128)(2,1)}, u32[]{:S(2)}, u32[]{:S(2)}) collective-permute-start(bf16[512,768]{1,0:T(8,128)(2,1)} %constant_dynamic-update-slice_fusion.refs_0_), channel_id=1, source_target_pairs={{0,24},{1,193},{2,26},{3,195},{4,28},{5,197},{6,30},{7,199},{8,16}... | collective-permute-start | bytes 2359304 | tf_op jit(solution)/shard_map/ppermute | solution.py:54
  81.4 7.8 %shard_map.62 = (f32[768,128]{1,0:T(8,128)}, f32[768,128]{1,0:T(8,128)}, f32[768,128]{1,0:T(8,128)}, f32[384,128]{1,0:T(8,128)}, f32[384,128]{1,0:T(8,128)}) custom-call(s32[24]{0:T(128)} %fusion.table, bf16[6144,768]{1,0:T(8,128)(2,1)} %weight.3, bf16[128,768]{1,0:T(8,128)(2,1)} %near.3, bf16[128,768]{1,0:T(8,128)(2,1)} %copy-done.3, f32[4,768,128]{2,1,0:T(8,128)} %copy-done.5), custom_call_target="tpu_custom_call" | custom-call | flops 603979776 | bytes 6291456 | tf_op jit(solution)/shard_map/pallas_call | solution.py:118
  89.3 2.0 %collective-permute-start.23 = (f32[768,128]{1,0:T(8,128)}, f32[768,128]{1,0:T(8,128)S(1)}, u32[]{:S(2)}, u32[]{:S(2)}) collective-permute-start(f32[768,128]{1,0:T(8,128)} %get-tuple-element.9), channel_id=1, source_target_pairs={{0,38},{1,39},{2,0},{3,1},{4,2},{5,3},{6,4},{7,5},{8,46},{9,47},{1... | collective-permute-start | bytes 1179656 | tf_op jit(solution)/shard_map/ppermute | solution.py:54
  91.3 4.6 %collective-permute-done.13.refs_2_ = bf16[512,768]{1,0:T(8,128)(2,1)} collective-permute-done((bf16[512,768]{1,0:T(8,128)(2,1)}, bf16[512,768]{1,0:T(8,128)(2,1)}, u32[]{:S(2)}, u32[]{:S(2)}) %collective-permute-start.13) | collective-permute-done | bytes 786464 | tf_op jit(solution)/shard_map/ppermute | solution.py:54
  95.9 3.3 %collective-permute-start.24 = (f32[384,128]{1,0:T(8,128)}, f32[384,128]{1,0:T(8,128)S(1)}, u32[]{:S(2)}, u32[]{:S(2)}) collective-permute-start(f32[384,128]{1,0:T(8,128)} %get-tuple-element.10), channel_id=1, source_target_pairs={{0,4},{1,5},{2,6},{3,7},{4,32},{5,33},{6,34},{7,35},{8,12},{9,13},... | collective-permute-start | bytes 589832 | tf_op jit(solution)/shard_map/ppermute | solution.py:54
  99.2 0.9 copy-done.1
  100.1 3.9 %shard_map.59.refs_4_ = f32[192,768]{1,0:T(8,128)} custom-call(s32[24]{0:T(128)} %fusion.table, bf16[4,4,192,128]{3,2,1,0:T(8,128)(2,1)} %copy-done, bf16[4,4,192,128]{3,2,1,0:T(8,128)(2,1)} %copy-done.1, bf16[512,768]{1,0:T(8,128)(2,1)} %constant_dynamic-update-slice_fusion.4.refs_0_, bf16[512,768]{1,0:T(8,128)(2,1)} %copy-done.6, ...), custom_call_target="tpu_custom_call" | custom-call | flops 603979776 | bytes 3145728 | tf_op jit(solution)/shard_map/pallas_call | solution.py:165
  104.0 4.1 %shard_map.60 = f32[192,768]{1,0:T(8,128)} custom-call(s32[24]{0:T(128)} %fusion.table, bf16[4,4,192,128]{3,2,1,0:T(8,128)(2,1)} %copy-done, bf16[4,4,192,128]{3,2,1,0:T(8,128)(2,1)} %copy-done.1, bf16[512,768]{1,0:T(8,128)(2,1)} %constant_dynamic-update-slice_fusion.refs_0_, bf16[512,768]{1,0:T(8,128)(2,1)} %collective-permute-done.12.refs_1_, ...), custom_call_target="tpu_custom_call" | custom-call | flops 603979776 | bytes 3145728 | tf_op jit(solution)/shard_map/pallas_call | solution.py:165
  108.1 4.1 %collective-permute-done.25.two_after = f32[384,128]{1,0:T(8,128)S(1)} collective-permute-done((f32[384,128]{1,0:T(8,128)}, f32[384,128]{1,0:T(8,128)S(1)}, u32[]{:S(2)}, u32[]{:S(2)}) %collective-permute-start.25) | collective-permute-done | bytes 196640 | tf_op jit(solution)/shard_map/ppermute | solution.py:54
  112.3 0.7 copy-done.11
  113.0 0.1 copy-done.8
  113.2 2.2 %shard_map.63 = bf16[128,768]{1,0:T(8,128)(2,1)} custom-call(f32[768,128]{1,0:T(8,128)} %get-tuple-element.7.here, f32[768,128]{1,0:T(8,128)} %copy-done.8, f32[768,128]{1,0:T(8,128)} %copy-done.9, f32[384,128]{1,0:T(8,128)} %copy-done.10, f32[384,128]{1,0:T(8,128)} %copy-done.11), custom_call_target="tpu_custom_call" | custom-call | flops 393216 | bytes 1769472 | tf_op jit(solution)/shard_map/pallas_call | solution.py:237
  (46 shorter events, 0.7 us)
Async XLA Ops:
  0.6 15.2 %collective-permute-start.8 = (bf16[128,768]{1,0:T(8,128)(2,1)}, bf16[128,768]{1,0:T(8,128)(2,1)S(1)}, u32[]{:S(2)}, u32[]{:S(2)}) collective-permute-start(bf16[128,768]{1,0:T(8,128)(2,1)} %near.3), channel_id=1, source_target_pairs={{0,32},{1,33},{2,34},{3,35},{4,36},{5,37},{6,38},{7,39},{8,40},{9,... | collective-permute-start | bytes 589832 | tf_op jit(solution)/shard_map/ppermute | solution.py:54
  6.1 17.3 %collective-permute-start.15 = (bf16[128,768]{1,0:T(8,128)(2,1)}, bf16[128,768]{1,0:T(8,128)(2,1)S(1)}, u32[]{:S(2)}, u32[]{:S(2)}) collective-permute-start(bf16[128,768]{1,0:T(8,128)(2,1)} %near.3), channel_id=1, source_target_pairs={{0,64},{1,9},{2,66},{3,11},{4,68},{5,13},{6,70},{7,15},{8,72},{9,1... | collective-permute-start | bytes 589832 | tf_op jit(solution)/shard_map/ppermute | solution.py:54
  7.6 16.5 %collective-permute-start.16 = (bf16[128,768]{1,0:T(8,128)(2,1)}, bf16[128,768]{1,0:T(8,128)(2,1)S(1)}, u32[]{:S(2)}, u32[]{:S(2)}) collective-permute-start(bf16[128,768]{1,0:T(8,128)(2,1)} %near.3), channel_id=1, source_target_pairs={{0,128},{1,17},{2,130},{3,19},{4,132},{5,21},{6,134},{7,23},{8,136... | collective-permute-start | bytes 589832 | tf_op jit(solution)/shard_map/ppermute | solution.py:54
  10.3 14.5 %collective-permute-start.17 = (bf16[128,768]{1,0:T(8,128)(2,1)}, bf16[128,768]{1,0:T(8,128)(2,1)S(1)}, u32[]{:S(2)}, u32[]{:S(2)}) collective-permute-start(bf16[128,768]{1,0:T(8,128)(2,1)} %near.3), channel_id=1, source_target_pairs={{0,192},{1,25},{2,194},{3,27},{4,196},{5,29},{6,198},{7,31},{8,200... | collective-permute-start | bytes 589832 | tf_op jit(solution)/shard_map/ppermute | solution.py:54
  10.8 12.4 %collective-permute-start = (bf16[128,768]{1,0:T(8,128)(2,1)}, bf16[128,768]{1,0:T(8,128)(2,1)S(1)}, u32[]{:S(2)}, u32[]{:S(2)}) collective-permute-start(bf16[128,768]{1,0:T(8,128)(2,1)} %param.4), channel_id=1, source_target_pairs={{0,0},{1,32},{2,66},{3,98},{4,132},{5,164},{6,198},{7,230},{8,8},{... | collective-permute-start | bytes 589832 | tf_op jit(solution)/shard_map/ppermute | solution.py:54
  15.8 6.8 %copy-start.2 = (bf16[128,768]{1,0:T(8,128)(2,1)S(1)}, bf16[128,768]{1,0:T(8,128)(2,1)}, u32[]{:S(2)}) copy-start(bf16[128,768]{1,0:T(8,128)(2,1)} %near.3) | copy-start | bytes 589828
  15.8 0.7 copy-start.3
  22.5 4.7 %copy-start.4 = (bf16[128,768]{1,0:T(8,128)(2,1)S(1)}, bf16[128,768]{1,0:T(8,128)(2,1)}, u32[]{:S(2)}) copy-start(bf16[128,768]{1,0:T(8,128)(2,1)} %copy-done.3) | copy-start | bytes 589828
  22.5 56.2 %collective-permute-start.21 = (f32[4,768,128]{2,1,0:T(8,128)}, f32[4,768,128]{2,1,0:T(8,128)S(1)}, u32[]{:S(2)}, u32[]{:S(2)}) collective-permute-start(f32[4,768,128]{2,1,0:T(8,128)} %shard_map.61), channel_id=1, source_target_pairs={{0,1},{1,0},{2,3},{3,2},{4,5},{5,4},{6,7},{7,6},{8,9},{9,8},{10,11... | collective-permute-start | bytes 4718600 | tf_op jit(solution)/shard_map/ppermute | solution.py:54
  25.5 52.0 %collective-permute-start.18 = (bf16[512,768]{1,0:T(8,128)(2,1)}, bf16[512,768]{1,0:T(8,128)(2,1)S(1)}, u32[]{:S(2)}, u32[]{:S(2)}) collective-permute-start(bf16[512,768]{1,0:T(8,128)(2,1)} %constant_dynamic-update-slice_fusion.4.refs_0_), channel_id=1, source_target_pairs={{0,8},{1,65},{2,10},{3,67},{4,12},{5,69},{6,14},{7,71},{8,0},{9,73... | collective-permute-start | bytes 2359304 | tf_op jit(solution)/shard_map/ppermute | solution.py:54
  27.2 27.9 %collective-permute-start.9 = (bf16[128,768]{1,0:T(8,128)(2,1)S(1)}, bf16[128,768]{1,0:T(8,128)(2,1)S(1)}, u32[]{:S(2)}, u32[]{:S(2)}) collective-permute-start(bf16[128,768]{1,0:T(8,128)(2,1)S(1)} %copy-done.4), channel_id=1, source_target_pairs={{0,64},{1,9},{2,66},{3,11},{4,68},{5,13},{6,70},{7,15},{8,72},{9,1... | collective-permute-start | bytes 589832 | tf_op jit(solution)/shard_map/ppermute | solution.py:54
  29.2 13.9 %collective-permute-start.1 = (bf16[192,128]{1,0:T(8,128)(2,1)S(1)}, bf16[192,128]{1,0:T(8,128)(2,1)S(1)}, u32[]{:S(2)}, u32[]{:S(2)}) collective-permute-start(bf16[192,128]{1,0:T(8,128)(2,1)S(1)} %get-tuple-element.17), channel_id=1, source_target_pairs={{0,8},{1,9},{2,10},{3,11},{4,12},{5,13},{6,14},{7,15},{8,0},{9,1},... | collective-permute-start | bytes 147464 | tf_op jit(solution)/shard_map/ppermute | solution.py:54
  29.3 18.5 %collective-permute-start.2 = (bf16[192,128]{1,0:T(8,128)(2,1)S(1)}, bf16[192,128]{1,0:T(8,128)(2,1)S(1)}, u32[]{:S(2)}, u32[]{:S(2)}) collective-permute-start(bf16[192,128]{1,0:T(8,128)(2,1)S(1)} %get-tuple-element.16), channel_id=1, source_target_pairs={{0,16},{1,17},{2,18},{3,19},{4,20},{5,21},{6,22},{7,23},{8,24},{9,... | collective-permute-start | bytes 147464 | tf_op jit(solution)/shard_map/ppermute | solution.py:54
  43.1 12.3 %collective-permute-start.10 = (bf16[128,768]{1,0:T(8,128)(2,1)S(1)}, bf16[128,768]{1,0:T(8,128)(2,1)S(1)}, u32[]{:S(2)}, u32[]{:S(2)}) collective-permute-start(bf16[128,768]{1,0:T(8,128)(2,1)S(1)} %copy-done.4), channel_id=1, source_target_pairs={{0,128},{1,17},{2,130},{3,19},{4,132},{5,21},{6,134},{7,23},{8,136... | collective-permute-start | bytes 589832 | tf_op jit(solution)/shard_map/ppermute | solution.py:54
  47.8 5.8 %collective-permute-start.3 = (bf16[192,128]{1,0:T(8,128)(2,1)S(1)}, bf16[192,128]{1,0:T(8,128)(2,1)S(1)}, u32[]{:S(2)}, u32[]{:S(2)}) collective-permute-start(bf16[192,128]{1,0:T(8,128)(2,1)S(1)} %get-tuple-element.15), channel_id=1, source_target_pairs={{0,24},{1,25},{2,26},{3,27},{4,28},{5,29},{6,30},{7,31},{8,16},{9,... | collective-permute-start | bytes 147464 | tf_op jit(solution)/shard_map/ppermute | solution.py:54
  53.7 24.9 %collective-permute-start.19 = (bf16[512,768]{1,0:T(8,128)(2,1)}, bf16[512,768]{1,0:T(8,128)(2,1)S(1)}, u32[]{:S(2)}, u32[]{:S(2)}) collective-permute-start(bf16[512,768]{1,0:T(8,128)(2,1)} %constant_dynamic-update-slice_fusion.4.refs_0_), channel_id=1, source_target_pairs={{0,16},{1,129},{2,18},{3,131},{4,20},{5,133},{6,22},{7,135},{8,24}... | collective-permute-start | bytes 2359304 | tf_op jit(solution)/shard_map/ppermute | solution.py:54
  55.1 6.9 %collective-permute-start.11 = (bf16[128,768]{1,0:T(8,128)(2,1)S(1)}, bf16[128,768]{1,0:T(8,128)(2,1)S(1)}, u32[]{:S(2)}, u32[]{:S(2)}) collective-permute-start(bf16[128,768]{1,0:T(8,128)(2,1)S(1)} %copy-done.4), channel_id=1, source_target_pairs={{0,192},{1,25},{2,194},{3,27},{4,196},{5,29},{6,198},{7,31},{8,200... | collective-permute-start | bytes 589832 | tf_op jit(solution)/shard_map/ppermute | solution.py:54
  55.5 7.8 %collective-permute-start.4 = (bf16[4,192,128]{2,1,0:T(8,128)(2,1)S(1)}, bf16[4,192,128]{2,1,0:T(8,128)(2,1)S(1)}, u32[]{:S(2)}, u32[]{:S(2)}) collective-permute-start(bf16[4,192,128]{2,1,0:T(8,128)(2,1)S(1)} %get-tuple-element.13), channel_id=1, source_target_pairs={{0,2},{1,3},{2,0},{3,1},{4,6},{5,7},{6,4},{7,5},{8,10},{9,11},{10,... | collective-permute-start | bytes 589832 | tf_op jit(solution)/shard_map/ppermute | solution.py:54
  62.0 6.7 %collective-permute-start.5 = (bf16[4,192,128]{2,1,0:T(8,128)(2,1)S(1)}, bf16[4,192,128]{2,1,0:T(8,128)(2,1)S(1)}, u32[]{:S(2)}, u32[]{:S(2)}) collective-permute-start(bf16[4,192,128]{2,1,0:T(8,128)(2,1)S(1)} %get-tuple-element.13), channel_id=1, source_target_pairs={{0,4},{1,5},{2,6},{3,7},{4,0},{5,1},{6,2},{7,3},{8,12},{9,13},{10,... | collective-permute-start | bytes 589832 | tf_op jit(solution)/shard_map/ppermute | solution.py:54
  63.3 10.4 %collective-permute-start.6 = (bf16[4,192,128]{2,1,0:T(8,128)(2,1)S(1)}, bf16[4,192,128]{2,1,0:T(8,128)(2,1)S(1)}, u32[]{:S(2)}, u32[]{:S(2)}) collective-permute-start(bf16[4,192,128]{2,1,0:T(8,128)(2,1)S(1)} %get-tuple-element.13), channel_id=1, source_target_pairs={{0,6},{1,7},{2,4},{3,5},{4,2},{5,3},{6,0},{7,1},{8,14},{9,15},{10,... | collective-permute-start | bytes 589832 | tf_op jit(solution)/shard_map/ppermute | solution.py:54
  68.6 20.5 %collective-permute-start.20 = (bf16[512,768]{1,0:T(8,128)(2,1)}, bf16[512,768]{1,0:T(8,128)(2,1)}, u32[]{:S(2)}, u32[]{:S(2)}) collective-permute-start(bf16[512,768]{1,0:T(8,128)(2,1)} %constant_dynamic-update-slice_fusion.4.refs_0_), channel_id=1, source_target_pairs={{0,24},{1,193},{2,26},{3,195},{4,28},{5,197},{6,30},{7,199},{8,16}... | collective-permute-start | bytes 2359304 | tf_op jit(solution)/shard_map/ppermute | solution.py:54
  73.6 15.6 %collective-permute-start.12 = (bf16[512,768]{1,0:T(8,128)(2,1)}, bf16[512,768]{1,0:T(8,128)(2,1)}, u32[]{:S(2)}, u32[]{:S(2)}) collective-permute-start(bf16[512,768]{1,0:T(8,128)(2,1)} %constant_dynamic-update-slice_fusion.refs_0_), channel_id=1, source_target_pairs={{0,8},{1,65},{2,10},{3,67},{4,12},{5,69},{6,14},{7,71},{8,0},{9,73... | collective-permute-start | bytes 2359304 | tf_op jit(solution)/shard_map/ppermute | solution.py:54
  77.6 0.9 copy-start.6
  77.6 18.3 %collective-permute-start.13 = (bf16[512,768]{1,0:T(8,128)(2,1)}, bf16[512,768]{1,0:T(8,128)(2,1)}, u32[]{:S(2)}, u32[]{:S(2)}) collective-permute-start(bf16[512,768]{1,0:T(8,128)(2,1)} %constant_dynamic-update-slice_fusion.refs_0_), channel_id=1, source_target_pairs={{0,16},{1,129},{2,18},{3,131},{4,20},{5,133},{6,22},{7,135},{8,24}... | collective-permute-start | bytes 2359304 | tf_op jit(solution)/shard_map/ppermute | solution.py:54
  78.6 10.6 %copy-start = (bf16[4,4,192,128]{3,2,1,0:T(8,128)(2,1)}, bf16[4,4,192,128]{3,2,1,0:T(8,128)(2,1)S(1)}, u32[]{:S(2)}) copy-start(bf16[4,4,192,128]{3,2,1,0:T(8,128)(2,1)S(1)} %pad_maximum_fusion.own) | copy-start | bytes 2359300
  78.6 0.9 copy-start.7
  78.6 20.6 %collective-permute-start.7 = (bf16[4,4,192,128]{3,2,1,0:T(8,128)(2,1)S(1)}, bf16[4,4,192,128]{3,2,1,0:T(8,128)(2,1)S(1)}, u32[]{:S(2)}, u32[]{:S(2)}) collective-permute-start(bf16[4,4,192,128]{3,2,1,0:T(8,128)(2,1)S(1)} %pad_maximum_fusion.own), channel_id=1, source_target_pairs={{0,1},{1,0},{2,3},{3,2},{4,5},{5,4},{6,7},{7,6},{8,9},{9,8},{10,11... | collective-permute-start | bytes 2359304 | tf_op jit(solution)/shard_map/ppermute | solution.py:54
  79.5 1.9 %copy-start.5 = (f32[4,768,128]{2,1,0:T(8,128)}, f32[4,768,128]{2,1,0:T(8,128)S(1)}, u32[]{:S(2)}) copy-start(f32[4,768,128]{2,1,0:T(8,128)S(1)} %collective-permute-done.21.taken) | copy-start | bytes 4718596
  79.5 24.5 %collective-permute-start.14 = (bf16[512,768]{1,0:T(8,128)(2,1)}, bf16[512,768]{1,0:T(8,128)(2,1)}, u32[]{:S(2)}, u32[]{:S(2)}) collective-permute-start(bf16[512,768]{1,0:T(8,128)(2,1)} %constant_dynamic-update-slice_fusion.refs_0_), channel_id=1, source_target_pairs={{0,24},{1,193},{2,26},{3,195},{4,28},{5,197},{6,30},{7,199},{8,16}... | collective-permute-start | bytes 2359304 | tf_op jit(solution)/shard_map/ppermute | solution.py:54
  89.2 23.1 %collective-permute-start.22 = (f32[768,128]{1,0:T(8,128)}, f32[768,128]{1,0:T(8,128)S(1)}, u32[]{:S(2)}, u32[]{:S(2)}) collective-permute-start(f32[768,128]{1,0:T(8,128)} %get-tuple-element.8), channel_id=1, source_target_pairs={{0,2},{1,3},{2,4},{3,5},{4,6},{5,7},{6,32},{7,33},{8,10},{9,11},{1... | collective-permute-start | bytes 1179656 | tf_op jit(solution)/shard_map/ppermute | solution.py:54
  89.3 23.0 %collective-permute-start.23 = (f32[768,128]{1,0:T(8,128)}, f32[768,128]{1,0:T(8,128)S(1)}, u32[]{:S(2)}, u32[]{:S(2)}) collective-permute-start(f32[768,128]{1,0:T(8,128)} %get-tuple-element.9), channel_id=1, source_target_pairs={{0,38},{1,39},{2,0},{3,1},{4,2},{5,3},{6,4},{7,5},{8,46},{9,47},{1... | collective-permute-start | bytes 1179656 | tf_op jit(solution)/shard_map/ppermute | solution.py:54
  95.9 12.3 %collective-permute-start.24 = (f32[384,128]{1,0:T(8,128)}, f32[384,128]{1,0:T(8,128)S(1)}, u32[]{:S(2)}, u32[]{:S(2)}) collective-permute-start(f32[384,128]{1,0:T(8,128)} %get-tuple-element.10), channel_id=1, source_target_pairs={{0,4},{1,5},{2,6},{3,7},{4,32},{5,33},{6,34},{7,35},{8,12},{9,13},... | collective-permute-start | bytes 589832 | tf_op jit(solution)/shard_map/ppermute | solution.py:54
  99.2 0.9 copy-start.1
  99.2 13.1 %collective-permute-start.25 = (f32[384,128]{1,0:T(8,128)}, f32[384,128]{1,0:T(8,128)S(1)}, u32[]{:S(2)}, u32[]{:S(2)}) collective-permute-start(f32[384,128]{1,0:T(8,128)} %get-tuple-element.11), channel_id=1, source_target_pairs={{0,36},{1,37},{2,38},{3,39},{4,0},{5,1},{6,2},{7,3},{8,44},{9,45},... | collective-permute-start | bytes 589832 | tf_op jit(solution)/shard_map/ppermute | solution.py:54
  108.1 4.2 %copy-start.10 = (f32[384,128]{1,0:T(8,128)}, f32[384,128]{1,0:T(8,128)S(1)}, u32[]{:S(2)}) copy-start(f32[384,128]{1,0:T(8,128)S(1)} %collective-permute-done.24.two_before) | copy-start | bytes 589828
  112.3 0.7 copy-start.11
  112.3 0.8 copy-start.8
  112.3 0.9 copy-start.9

commit v3 on v2

v3 whole, which is shorter than its diff:
```python
import functools

import jax
import jax.numpy as jnp
from jax import lax
from jax.experimental import pallas as pl
from jax.experimental.pallas import tpu as pltpu
from jax.sharding import PartitionSpec as P


AXES = ("batch", "seq", "mp")
F32 = jnp.float32
BF16 = jnp.bfloat16
VMEM = pl.BlockSpec(memory_space=pltpu.VMEM)

MIB = 1 << 20


def here():
    batch, mp = lax.axis_index("batch"), lax.axis_index("mp")
    return batch & 1, mp >> 1, mp & 1


def place(x, h, y, l, c):
    return ((x * 2 + h) * 4 + y) * 8 + l * 2 + c


def pairs(route):
    return [
        (place(x, h, y, l, c), place(*route(x, h, y, l, c)))
        for x in range(4)
        for h in range(2)
        for y in range(4)
        for l in range(4)
        for c in range(2)
    ]


def ring(step):
    def route(x, h, y, l, c):
        z = (4 * h + l + step) % 8
        return x, z // 4, y, z % 4, c

    return route


def crosswise(k, first):
    def route(x, h, y, l, c):
        if (c == 0) == first:
            return x ^ k, h, y, l, c
        return x, h, y ^ k, l, c

    return route


def send(array, route):
    return lax.ppermute(array, AXES, pairs(route))


def at(stack, index):
    return lax.dynamic_index_in_dim(stack, index, 0, keepdims=False)


def products_kernel(kept, weight, near, far, *refs):
    h, l, c = here()
    turned = refs[-1]
    turned[0] = near[...].T
    turned[1] = far[...].T
    depth = near.shape[1]
    rows = depth // 2
    core = c if kept else 1 - c
    for i, (block, steps) in enumerate(((0, (0, 0)), (1, (1, 1)), (3, (-1, -1)), (2, (2, -2)))):
        for half, step in enumerate(steps):
            target = (4 * h + l + step + 8) & 7
            use_far = (target >> 2) ^ h
            row = ((((l + block) & 3) * 2 + core) * 2 + half) * rows
            part = pl.ds(half * rows, rows)
            total = jnp.dot(
                weight[pl.ds(pl.multiple_of(row, rows), rows), :],
                turned[use_far],
                preferred_element_type=F32,
            )
            if not kept:
                refs[0][i, part, :] = total
                continue
            total += refs[0][i, part, :]
            if i < 3:
                refs[1 + i][part, :] = total
            else:
                refs[4 + half][...] = total


def products(weight, near, far, *taken):
    tokens, depth = near.shape
    kept = bool(taken)
    if kept:
        rows = [depth, depth, depth, depth // 2, depth // 2]
        shapes = [jax.ShapeDtypeStruct((n, tokens), F32) for n in rows]
    else:
        shapes = [jax.ShapeDtypeStruct((4, depth, tokens), F32)]
    return pl.pallas_call(
        functools.partial(products_kernel, kept),
        out_shape=shapes,
        in_specs=[VMEM] * (3 + kept),
        out_specs=[VMEM] * len(shapes),
        scratch_shapes=[pltpu.VMEM((2, depth, tokens), BF16)],
        compiler_params=pltpu.CompilerParams(vmem_limit_bytes=20 * MIB),
        cost_estimate=pl.CostEstimate(
            flops=8 * depth * tokens * depth,
            bytes_accessed=8 * depth * depth + 16 * depth * tokens,
            transcendentals=0,
        ),
    )(weight, near, far, *taken)


def finish_kernel(home, before, after, two_before, two_after, out):
    rows = two_before.shape[0]
    for i, skip in enumerate((two_before, two_after)):
        part = pl.ds(i * rows, rows)
        total = home[part, :] + before[part, :] + after[part, :] + skip[...]
        out[:, part] = total.T.astype(BF16)


def weight_kernel(far, own, other, *refs):
    h, low, core = here()
    cots, out = refs[:4], refs[-1]
    use_own = (core ^ h) == far
    total = refs[4][...] if far else jnp.zeros(out.shape, F32)
    for piece, cot in enumerate(cots):
        for half in range(2):
            lefts = []
            for m in (2 * half, 2 * half + 1):
                r = jnp.where(core == 0, m, piece)
                s = jnp.where(core == 0, piece, m)
                k = low ^ r
                lefts.append(jnp.where(use_own, own[k, s], other[k, s]))
            left = jnp.concatenate(lefts, axis=1)
            right = cot[pl.ds(256 * half, 256), :]
            total += jnp.dot(left, right, preferred_element_type=F32)
    out[...] = total


def weight_part(far, own, other, cots, *total):
    rows, width = own.shape[2], cots[0].shape[1]
    return pl.pallas_call(
        functools.partial(weight_kernel, far),
        out_shape=jax.ShapeDtypeStruct((rows, width), F32),
        in_specs=[VMEM] * (6 + len(total)),
        out_specs=VMEM,
        compiler_params=pltpu.CompilerParams(vmem_limit_bytes=16 * MIB),
        cost_estimate=pl.CostEstimate(
            flops=2 * rows * width * 512 * 4,
            bytes_accessed=4 * 512 * width * 2,
            transcendentals=0,
        ),
    )(own, other, *cots, *total)


def step(context, cotangent, out_weight):
    y = lax.axis_index("seq")
    tokens, width = cotangent.shape
    quarter = width // 4

    def gather(array):
        first = [array] + [send(array, crosswise(k, True)) for k in (1, 2, 3)]
        row = jnp.concatenate(first)
        return [row] + [send(row, crosswise(k, False)) for k in (1, 2, 3)]

    near_cots = gather(cotangent)
    far_cot = send(cotangent, ring(4))
    far_cots = gather(far_cot)

    turned = context.T.reshape(4, quarter, tokens)
    block = jnp.stack(
        [at(turned, y)]
        + [
            send(at(turned, y ^ k), lambda x, h, y, l, c, k=k: (x, h, y ^ k, l, c))
            for k in (1, 2, 3)
        ]
    )
    mine = send(block, lambda x, h, y, l, c: (l, c, y, l ^ x, h))
    gathered = [mine] + [
        send(mine, lambda x, h, y, l, c, k=k: (x, h, y, l ^ k, c)) for k in (1, 2, 3)
    ]
    own = jnp.stack(gathered)
    swap = lambda x, h, y, l, c: (x, h, y, l, 1 - c)
    other = send(own, swap)

    (given,) = products(out_weight, cotangent, far_cot)
    taken = send(given, swap)
    at_home, after, before, skip_up, skip_down = products(out_weight, cotangent, far_cot, taken)
    from_before = send(after, ring(1))
    from_after = send(before, ring(-1))
    from_two_before = send(skip_up, ring(2))
    from_two_after = send(skip_down, ring(-2))

    near_part = weight_part(0, own, other, near_cots)
    grad_weight = weight_part(1, own, other, far_cots, near_part)
    grad_context = pl.pallas_call(
        finish_kernel,
        out_shape=jax.ShapeDtypeStruct((tokens, width), BF16),
        in_specs=[VMEM] * 5,
        out_specs=VMEM,
        compiler_params=pltpu.CompilerParams(vmem_limit_bytes=8 * MIB),
        cost_estimate=pl.CostEstimate(
            flops=4 * tokens * width, bytes_accessed=18 * tokens * width, transcendentals=0
        ),
    )(at_home, from_before, from_after, from_two_before, from_two_after)
    return grad_weight, grad_context


def solution(mesh):
    return jax.shard_map(
        step,
        mesh=mesh,
        in_specs=(P(("batch", "seq"), "mp"), P(("batch", "seq"), "mp"), P(None, "mp")),
        out_specs=(P(("batch", "seq"), "mp"), P(("batch", "seq"), "mp")),
        check_vma=False,
    )
```

time: 116 us -> 103 us (0.89)
  Pallas kernels: 24 us -> 6.26 us
  waiting for transfers between devices: 33.8 us -> 40 us
  local copies, waits for them, and re-layouts: 11.2 us -> 5.83 us
  starting transfers between devices: 45.5 us -> 50 us
    pallas_call x2, Pallas kernels: 13.8 us -> 3.06 us  [products(): pl.pallas_call(functools.partial(products_kernel, kept), out_shape=shapes...]
    ppermute x26, waiting for transfers between devices: 33.8 us -> 40 us  [send(): return lax.ppermute(array, AXES, pairs(route))]
    pallas_call x2, Pallas kernels: 8.03 us -> 2.38 us  [weight_part(): pl.pallas_call(functools.partial(weight_kernel, far), out_shape=jax.Shape...]
    ppermute x26, starting transfers between devices: 45.5 us -> 50 us  [send(): return lax.ppermute(array, AXES, pairs(route))]
    unnamed x30 -> x10, local copies, waits for them, and re-layouts: 8.37 us -> 4.69 us
    concatenate x2, local copies, waits for them, and re-layouts: 1.42 us -> 0.03 us  [gather(): row = jnp.concatenate(first)]
    pallas_call x1, Pallas kernels: 2.19 us -> 0.82 us  [step(): pl.pallas_call(finish_kernel, out_shape=jax.ShapeDtypeStruct((tokens, wid...]
    squeeze x1 -> x0, local copies, waits for them, and re-layouts: 1.23 us -> none  [at(): return lax.dynamic_index_in_dim(stack, index, 0, keepdims=False)]
  transfers between devices with their start and end apart: 26 -> 26, of which waited for: 9 -> 13; matrix products, arithmetic and copies ran while one was open for 6% -> 1% of each run, Pallas kernels for 19% -> 5%
where the time goes in v3:
time: 103 us
  starting transfers between devices  50 us (49%)
  waiting for transfers between devices  40 us (39%)
  Pallas kernels  6.26 us (6%)
  local copies, waits for them, and re-layouts  5.83 us (6%)
    ppermute x26, starting transfers between devices, send(): return lax.ppermute(array, AXES, pairs(route))  50 us
    ppermute x26, waiting for transfers between devices, send(): return lax.ppermute(array, AXES, pairs(route))  40 us
    unnamed x10, local copies, waits for them, and re-layouts  4.69 us
    pallas_call x2, Pallas kernels, products(): pl.pallas_call(functools.partial(products_kernel, kept), out_shape=shapes...  3.06 us
    pallas_call x2, Pallas kernels, weight_part(): pl.pallas_call(functools.partial(weight_kernel, far), out_shape=jax.Shape...  2.38 us
  transfers between devices with their start and end apart: 26, of which 13 were waited for; matrix products, arithmetic and copies ran while one was open for 1% of the time, Pallas kernels for 5%

profile of v3, /device:TPU:64, one launch (start us, length us, event | category | flops | bytes accessed | tf_op | source)
XLA Modules:
  0.0 103.1 jit_solution(9841661375998028546)
XLA Ops:
  0.6 5.5 %collective-permute-start.8 = (bf16[128,768]{1,0:T(8,128)(2,1)}, bf16[128,768]{1,0:T(8,128)(2,1)S(1)}, u32[]{:S(2)}, u32[]{:S(2)}) collective-permute-start(bf16[128,768]{1,0:T(8,128)(2,1)} %near.3), channel_id=1, source_target_pairs={{0,32},{1,33},{2,34},{3,35},{4,36},{5,37},{6,38},{7,39},{8,40},{9,... | collective-permute-start | bytes 589832 | tf_op jit(solution)/shard_map/ppermute | solution.py:57
  6.1 1.5 %collective-permute-start.15 = (bf16[128,768]{1,0:T(8,128)(2,1)}, bf16[128,768]{1,0:T(8,128)(2,1)S(1)}, u32[]{:S(2)}, u32[]{:S(2)}) collective-permute-start(bf16[128,768]{1,0:T(8,128)(2,1)} %near.3), channel_id=1, source_target_pairs={{0,64},{1,9},{2,66},{3,11},{4,68},{5,13},{6,70},{7,15},{8,72},{9,1... | collective-permute-start | bytes 589832 | tf_op jit(solution)/shard_map/ppermute | solution.py:57
  7.6 1.1 %copy.5 = bf16[768,128]{1,0:T(8,128)(2,1)S(1)} copy(bf16[768,128]{0,1:T(8,128)(2,1)} %bitcast.20) | data formatting | bytes 393216 | tf_op jit(solution)/shard_map/transpose | solution.py:173
  8.7 1.7 %collective-permute-start = (bf16[192,128]{1,0:T(8,128)(2,1)S(1)}, bf16[192,128]{1,0:T(8,128)(2,1)S(1)}, u32[]{:S(2)}, u32[]{:S(2)}) collective-permute-start(bf16[192,128]{1,0:T(8,128)(2,1)S(1)} %get-tuple-element.15), channel_id=1, source_target_pairs={{0,8},{1,9},{2,10},{3,11},{4,12},{5,13},{6,14},{7,15},{8,0},{9,1},... | collective-permute-start | bytes 147464 | tf_op jit(solution)/shard_map/ppermute | solution.py:57
  10.4 2.9 %collective-permute-start.1 = (bf16[192,128]{1,0:T(8,128)(2,1)S(1)}, bf16[192,128]{1,0:T(8,128)(2,1)S(1)}, u32[]{:S(2)}, u32[]{:S(2)}) collective-permute-start(bf16[192,128]{1,0:T(8,128)(2,1)S(1)} %get-tuple-element.14), channel_id=1, source_target_pairs={{0,16},{1,17},{2,18},{3,19},{4,20},{5,21},{6,22},{7,23},{8,24},{9,... | collective-permute-start | bytes 147464 | tf_op jit(solution)/shard_map/ppermute | solution.py:57
  13.3 0.2 collective-permute-start.2
  13.5 2.3 %collective-permute-done.8.far = bf16[128,768]{1,0:T(8,128)(2,1)S(1)} collective-permute-done((bf16[128,768]{1,0:T(8,128)(2,1)}, bf16[128,768]{1,0:T(8,128)(2,1)S(1)}, u32[]{:S(2)}, u32[]{:S(2)}) %collective-permute-start.8) | collective-permute-done | bytes 196640 | tf_op jit(solution)/shard_map/ppermute | solution.py:57
  15.8 3.7 %copy-done = bf16[6144,768]{1,0:T(8,128)(2,1)S(1)} copy-done((bf16[6144,768]{1,0:T(8,128)(2,1)S(1)}, bf16[6144,768]{1,0:T(8,128)(2,1)}, u32[]{:S(2)}) %copy-start) | copy-done | bytes 9437208
  19.5 0.9 copy-done.1
  20.4 1.5 %shard_map.52 = f32[4,768,128]{2,1,0:T(8,128)S(1)} custom-call(bf16[6144,768]{1,0:T(8,128)(2,1)S(1)} %copy-done, bf16[128,768]{1,0:T(8,128)(2,1)S(1)} %copy-done.1, bf16[128,768]{1,0:T(8,128)(2,1)S(1)} %collective-permute-done.8.far), custom_call_target="tpu_custom_call" | custom-call | flops 603979776 | bytes 6291456 | tf_op jit(solution)/shard_map/pallas_call | solution.py:101
  22.0 0.1 collective-permute-start.21
  22.1 0.0 collective-permute-done
  22.1 3.1 %collective-permute-start.16 = (bf16[128,768]{1,0:T(8,128)(2,1)S(1)}, bf16[128,768]{1,0:T(8,128)(2,1)S(1)}, u32[]{:S(2)}, u32[]{:S(2)}) collective-permute-start(bf16[128,768]{1,0:T(8,128)(2,1)S(1)} %copy-done.1), channel_id=1, source_target_pairs={{0,128},{1,17},{2,130},{3,19},{4,132},{5,21},{6,134},{7,23},{8,136... | collective-permute-start | bytes 589832 | tf_op jit(solution)/shard_map/ppermute | solution.py:57
  25.2 0.0 collective-permute-done.1
  25.2 1.1 %collective-permute-start.17 = (bf16[128,768]{1,0:T(8,128)(2,1)S(1)}, bf16[128,768]{1,0:T(8,128)(2,1)S(1)}, u32[]{:S(2)}, u32[]{:S(2)}) collective-permute-start(bf16[128,768]{1,0:T(8,128)(2,1)S(1)} %copy-done.1), channel_id=1, source_target_pairs={{0,192},{1,25},{2,194},{3,27},{4,196},{5,29},{6,198},{7,31},{8,200... | collective-permute-start | bytes 589832 | tf_op jit(solution)/shard_map/ppermute | solution.py:57
  26.4 3.4 %collective-permute-start.3 = (bf16[4,192,128]{2,1,0:T(8,128)(2,1)S(1)}, bf16[4,192,128]{2,1,0:T(8,128)(2,1)S(1)}, u32[]{:S(2)}, u32[]{:S(2)}) collective-permute-start(bf16[4,192,128]{2,1,0:T(8,128)(2,1)S(1)} %pad_maximum_fusion.1), channel_id=1, source_target_pairs={{0,0},{1,32},{2,66},{3,98},{4,132},{5,164},{6,198},{7,230},{8,8},{... | collective-permute-start | bytes 589832 | tf_op jit(solution)/shard_map/ppermute | solution.py:57
  29.8 0.1 collective-permute-start.9
  30.0 0.0 collective-permute-done.16
  30.0 2.1 %collective-permute-done.17 = bf16[128,768]{1,0:T(8,128)(2,1)S(1)} collective-permute-done((bf16[128,768]{1,0:T(8,128)(2,1)S(1)}, bf16[128,768]{1,0:T(8,128)(2,1)S(1)}, u32[]{:S(2)}, u32[]{:S(2)}) %collective-permute-start.17) | collective-permute-done | bytes 196640 | tf_op jit(solution)/shard_map/ppermute | solution.py:57
  32.1 1.7 %collective-permute-start.18 = (bf16[512,768]{1,0:T(8,128)(2,1)S(1)}, bf16[512,768]{1,0:T(8,128)(2,1)S(1)}, u32[]{:S(2)}, u32[]{:S(2)}) collective-permute-start(bf16[512,768]{1,0:T(8,128)(2,1)S(1)} %constant_dynamic-update-slice_fusion.4.refs_0_), channel_id=1, source_target_pairs={{0,8},{1,65},{2,10},{3,67},{4,12},{5,69},{6,14},{7,71},{8,0},{9,73... | collective-permute-start | bytes 2359304 | tf_op jit(solution)/shard_map/ppermute | solution.py:57
  33.8 1.5 %collective-permute-start.10 = (bf16[128,768]{1,0:T(8,128)(2,1)S(1)}, bf16[128,768]{1,0:T(8,128)(2,1)S(1)}, u32[]{:S(2)}, u32[]{:S(2)}) collective-permute-start(bf16[128,768]{1,0:T(8,128)(2,1)S(1)} %collective-permute-done.8.far), channel_id=1, source_target_pairs={{0,128},{1,17},{2,130},{3,19},{4,132},{5,21},{6,134},{7,23},{8,136... | collective-permute-start | bytes 589832 | tf_op jit(solution)/shard_map/ppermute | solution.py:57
  35.3 2.1 %collective-permute-done.3 = bf16[4,192,128]{2,1,0:T(8,128)(2,1)S(1)} collective-permute-done((bf16[4,192,128]{2,1,0:T(8,128)(2,1)S(1)}, bf16[4,192,128]{2,1,0:T(8,128)(2,1)S(1)}, u32[]{:S(2)}, u32[]{:S(2)}) %collective-permute-start.3) | collective-permute-done | bytes 196640 | tf_op jit(solution)/shard_map/ppermute | solution.py:57
  37.5 5.2 %collective-permute-start.19 = (bf16[512,768]{1,0:T(8,128)(2,1)S(1)}, bf16[512,768]{1,0:T(8,128)(2,1)S(1)}, u32[]{:S(2)}, u32[]{:S(2)}) collective-permute-start(bf16[512,768]{1,0:T(8,128)(2,1)S(1)} %constant_dynamic-update-slice_fusion.4.refs_0_), channel_id=1, source_target_pairs={{0,16},{1,129},{2,18},{3,131},{4,20},{5,133},{6,22},{7,135},{8,24}... | collective-permute-start | bytes 2359304 | tf_op jit(solution)/shard_map/ppermute | solution.py:57
  42.7 1.8 %collective-permute-done.10 = bf16[128,768]{1,0:T(8,128)(2,1)S(1)} collective-permute-done((bf16[128,768]{1,0:T(8,128)(2,1)S(1)}, bf16[128,768]{1,0:T(8,128)(2,1)S(1)}, u32[]{:S(2)}, u32[]{:S(2)}) %collective-permute-start.10) | collective-permute-done | bytes 196640 | tf_op jit(solution)/shard_map/ppermute | solution.py:57
  44.5 0.0 collective-permute-start.5
  44.5 5.1 %collective-permute-done.11 = bf16[128,768]{1,0:T(8,128)(2,1)S(1)} collective-permute-done((bf16[128,768]{1,0:T(8,128)(2,1)S(1)}, bf16[128,768]{1,0:T(8,128)(2,1)S(1)}, u32[]{:S(2)}, u32[]{:S(2)}) %collective-permute-start.11) | collective-permute-done | bytes 196640 | tf_op jit(solution)/shard_map/ppermute | solution.py:57
  49.6 1.6 %collective-permute-done.5 = bf16[4,192,128]{2,1,0:T(8,128)(2,1)S(1)} collective-permute-done((bf16[4,192,128]{2,1,0:T(8,128)(2,1)S(1)}, bf16[4,192,128]{2,1,0:T(8,128)(2,1)S(1)}, u32[]{:S(2)}, u32[]{:S(2)}) %collective-permute-start.5) | collective-permute-done | bytes 196640 | tf_op jit(solution)/shard_map/ppermute | solution.py:57
  51.1 10.3 %collective-permute-start.4 = (bf16[4,192,128]{2,1,0:T(8,128)(2,1)S(1)}, bf16[4,192,128]{2,1,0:T(8,128)(2,1)S(1)}, u32[]{:S(2)}, u32[]{:S(2)}) collective-permute-start(bf16[4,192,128]{2,1,0:T(8,128)(2,1)S(1)} %collective-permute-done.3), channel_id=1, source_target_pairs={{0,2},{1,3},{2,0},{3,1},{4,6},{5,7},{6,4},{7,5},{8,10},{9,11},{10,... | collective-permute-start | bytes 589832 | tf_op jit(solution)/shard_map/ppermute | solution.py:57
  61.5 2.7 %collective-permute-done.6 = bf16[4,192,128]{2,1,0:T(8,128)(2,1)S(1)} collective-permute-done((bf16[4,192,128]{2,1,0:T(8,128)(2,1)S(1)}, bf16[4,192,128]{2,1,0:T(8,128)(2,1)S(1)}, u32[]{:S(2)}, u32[]{:S(2)}) %collective-permute-start.6) | collective-permute-done | bytes 196640 | tf_op jit(solution)/shard_map/ppermute | solution.py:57
  64.2 3.4 %collective-permute-start.20 = (bf16[512,768]{1,0:T(8,128)(2,1)S(1)}, bf16[512,768]{1,0:T(8,128)(2,1)S(1)}, u32[]{:S(2)}, u32[]{:S(2)}) collective-permute-start(bf16[512,768]{1,0:T(8,128)(2,1)S(1)} %constant_dynamic-update-slice_fusion.4.refs_0_), channel_id=1, source_target_pairs={{0,24},{1,193},{2,26},{3,195},{4,28},{5,197},{6,30},{7,199},{8,16}... | collective-permute-start | bytes 2359304 | tf_op jit(solution)/shard_map/ppermute | solution.py:57
  67.6 0.7 collective-permute-start.12
  68.3 2.8 %collective-permute-start.13 = (bf16[512,768]{1,0:T(8,128)(2,1)S(1)}, bf16[512,768]{1,0:T(8,128)(2,1)S(1)}, u32[]{:S(2)}, u32[]{:S(2)}) collective-permute-start(bf16[512,768]{1,0:T(8,128)(2,1)S(1)} %constant_dynamic-update-slice_fusion.refs_0_), channel_id=1, source_target_pairs={{0,16},{1,129},{2,18},{3,131},{4,20},{5,133},{6,22},{7,135},{8,24}... | collective-permute-start | bytes 2359304 | tf_op jit(solution)/shard_map/ppermute | solution.py:57
  71.2 0.1 pad_maximum_fusion.own
  71.3 0.3 collective-permute-start.7
  71.6 1.3 %collective-permute-start.14 = (bf16[512,768]{1,0:T(8,128)(2,1)S(1)}, bf16[512,768]{1,0:T(8,128)(2,1)S(1)}, u32[]{:S(2)}, u32[]{:S(2)}) collective-permute-start(bf16[512,768]{1,0:T(8,128)(2,1)S(1)} %constant_dynamic-update-slice_fusion.refs_0_), channel_id=1, source_target_pairs={{0,24},{1,193},{2,26},{3,195},{4,28},{5,197},{6,30},{7,199},{8,16}... | collective-permute-start | bytes 2359304 | tf_op jit(solution)/shard_map/ppermute | solution.py:57
  72.9 1.5 %shard_map.53 = (f32[768,128]{1,0:T(8,128)S(1)}, f32[768,128]{1,0:T(8,128)S(1)}, f32[768,128]{1,0:T(8,128)S(1)}, f32[384,128]{1,0:T(8,128)S(1)}, f32[384,128]{1,0:T(8,128)S(1)}) custom-call(bf16[6144,768]{1,0:T(8,128)(2,1)S(1)} %copy-done, bf16[128,768]{1,0:T(8,128)(2,1)S(1)} %copy-done.1, bf16[128,768]{1,0:T(8,128)(2,1)S(1)} %collective-permute-done.8.far, ...), custom_call_target="tpu_custom_call" | custom-call | flops 603979776 | bytes 6291456 | tf_op jit(solution)/shard_map/pallas_call | solution.py:101
  74.4 3.1 %collective-permute-done.20.refs_3_ = bf16[512,768]{1,0:T(8,128)(2,1)S(1)} collective-permute-done((bf16[512,768]{1,0:T(8,128)(2,1)S(1)}, bf16[512,768]{1,0:T(8,128)(2,1)S(1)}, u32[]{:S(2)}, u32[]{:S(2)}) %collective-permute-start.20) | collective-permute-done | bytes 786464 | tf_op jit(solution)/shard_map/ppermute | solution.py:57
  77.5 2.1 %collective-permute-done.12.refs_1_ = bf16[512,768]{1,0:T(8,128)(2,1)S(1)} collective-permute-done((bf16[512,768]{1,0:T(8,128)(2,1)S(1)}, bf16[512,768]{1,0:T(8,128)(2,1)S(1)}, u32[]{:S(2)}, u32[]{:S(2)}) %collective-permute-start.12) | collective-permute-done | bytes 786464 | tf_op jit(solution)/shard_map/ppermute | solution.py:57
  79.7 0.3 collective-permute-start.23
  79.9 9.7 %collective-permute-done.13.refs_2_ = bf16[512,768]{1,0:T(8,128)(2,1)S(1)} collective-permute-done((bf16[512,768]{1,0:T(8,128)(2,1)S(1)}, bf16[512,768]{1,0:T(8,128)(2,1)S(1)}, u32[]{:S(2)}, u32[]{:S(2)}) %collective-permute-start.13) | collective-permute-done | bytes 786464 | tf_op jit(solution)/shard_map/ppermute | solution.py:57
  89.7 2.2 %collective-permute-start.24 = (f32[384,128]{1,0:T(8,128)S(1)}, f32[384,128]{1,0:T(8,128)S(1)}, u32[]{:S(2)}, u32[]{:S(2)}) collective-permute-start(f32[384,128]{1,0:T(8,128)S(1)} %get-tuple-element.10), channel_id=1, source_target_pairs={{0,4},{1,5},{2,6},{3,7},{4,32},{5,33},{6,34},{7,35},{8,12},{9,13},... | collective-permute-start | bytes 589832 | tf_op jit(solution)/shard_map/ppermute | solution.py:57
  91.8 0.8 collective-permute-start.25
  92.6 0.8 shard_map.50.refs_4_
  93.4 1.0 collective-permute-done.14.refs_3_
  94.4 1.6 %shard_map.51 = f32[192,768]{1,0:T(8,128)} custom-call(bf16[4,4,192,128]{3,2,1,0:T(8,128)(2,1)S(1)} %pad_maximum_fusion.own, bf16[4,4,192,128]{3,2,1,0:T(8,128)(2,1)S(1)} %collective-permute-done.7.other, bf16[512,768]{1,0:T(8,128)(2,1)S(1)} %constant_dynamic-update-slice_fusion.refs_0_, bf16[512,768]{1,0:T(8,128)(2,1)S(1)} %collective-permute-done.12.refs_1_, ...), custom_call_target="tpu_custom_call" | custom-call | flops 603979776 | bytes 3145728 | tf_op jit(solution)/shard_map/pallas_call | solution.py:145
  96.0 1.9 %collective-permute-done.24.two_before = f32[384,128]{1,0:T(8,128)S(1)} collective-permute-done((f32[384,128]{1,0:T(8,128)S(1)}, f32[384,128]{1,0:T(8,128)S(1)}, u32[]{:S(2)}, u32[]{:S(2)}) %collective-permute-start.24) | collective-permute-done | bytes 196640 | tf_op jit(solution)/shard_map/ppermute | solution.py:57
  97.9 4.4 %collective-permute-done.25.two_after = f32[384,128]{1,0:T(8,128)S(1)} collective-permute-done((f32[384,128]{1,0:T(8,128)S(1)}, f32[384,128]{1,0:T(8,128)S(1)}, u32[]{:S(2)}, u32[]{:S(2)}) %collective-permute-start.25) | collective-permute-done | bytes 196640 | tf_op jit(solution)/shard_map/ppermute | solution.py:57
  102.3 0.8 shard_map.54
  (25 shorter events, 0.2 us)
Async XLA Ops:
  0.6 15.2 %collective-permute-start.8 = (bf16[128,768]{1,0:T(8,128)(2,1)}, bf16[128,768]{1,0:T(8,128)(2,1)S(1)}, u32[]{:S(2)}, u32[]{:S(2)}) collective-permute-start(bf16[128,768]{1,0:T(8,128)(2,1)} %near.3), channel_id=1, source_target_pairs={{0,32},{1,33},{2,34},{3,35},{4,36},{5,37},{6,38},{7,39},{8,40},{9,... | collective-permute-start | bytes 589832 | tf_op jit(solution)/shard_map/ppermute | solution.py:57
  6.1 23.7 %collective-permute-start.15 = (bf16[128,768]{1,0:T(8,128)(2,1)}, bf16[128,768]{1,0:T(8,128)(2,1)S(1)}, u32[]{:S(2)}, u32[]{:S(2)}) collective-permute-start(bf16[128,768]{1,0:T(8,128)(2,1)} %near.3), channel_id=1, source_target_pairs={{0,64},{1,9},{2,66},{3,11},{4,68},{5,13},{6,70},{7,15},{8,72},{9,1... | collective-permute-start | bytes 589832 | tf_op jit(solution)/shard_map/ppermute | solution.py:57
  8.7 13.4 %collective-permute-start = (bf16[192,128]{1,0:T(8,128)(2,1)S(1)}, bf16[192,128]{1,0:T(8,128)(2,1)S(1)}, u32[]{:S(2)}, u32[]{:S(2)}) collective-permute-start(bf16[192,128]{1,0:T(8,128)(2,1)S(1)} %get-tuple-element.15), channel_id=1, source_target_pairs={{0,8},{1,9},{2,10},{3,11},{4,12},{5,13},{6,14},{7,15},{8,0},{9,1},... | collective-permute-start | bytes 147464 | tf_op jit(solution)/shard_map/ppermute | solution.py:57
  10.4 14.8 %collective-permute-start.1 = (bf16[192,128]{1,0:T(8,128)(2,1)S(1)}, bf16[192,128]{1,0:T(8,128)(2,1)S(1)}, u32[]{:S(2)}, u32[]{:S(2)}) collective-permute-start(bf16[192,128]{1,0:T(8,128)(2,1)S(1)} %get-tuple-element.14), channel_id=1, source_target_pairs={{0,16},{1,17},{2,18},{3,19},{4,20},{5,21},{6,22},{7,23},{8,24},{9,... | collective-permute-start | bytes 147464 | tf_op jit(solution)/shard_map/ppermute | solution.py:57
  13.3 13.1 %collective-permute-start.2 = (bf16[192,128]{1,0:T(8,128)(2,1)S(1)}, bf16[192,128]{1,0:T(8,128)(2,1)S(1)}, u32[]{:S(2)}, u32[]{:S(2)}) collective-permute-start(bf16[192,128]{1,0:T(8,128)(2,1)S(1)} %get-tuple-element.13), channel_id=1, source_target_pairs={{0,24},{1,25},{2,26},{3,27},{4,28},{5,29},{6,30},{7,31},{8,16},{9,... | collective-permute-start | bytes 147464 | tf_op jit(solution)/shard_map/ppermute | solution.py:57
  15.8 3.7 %copy-start = (bf16[6144,768]{1,0:T(8,128)(2,1)S(1)}, bf16[6144,768]{1,0:T(8,128)(2,1)}, u32[]{:S(2)}) copy-start(bf16[6144,768]{1,0:T(8,128)(2,1)} %weight.3) | copy-start | bytes 28311556
  19.5 0.9 copy-start.1
  22.0 49.6 %collective-permute-start.21 = (f32[4,768,128]{2,1,0:T(8,128)S(1)}, f32[4,768,128]{2,1,0:T(8,128)S(1)}, u32[]{:S(2)}, u32[]{:S(2)}) collective-permute-start(f32[4,768,128]{2,1,0:T(8,128)S(1)} %shard_map.52), channel_id=1, source_target_pairs={{0,1},{1,0},{2,3},{3,2},{4,5},{5,4},{6,7},{7,6},{8,9},{9,8},{10,11... | collective-permute-start | bytes 4718600 | tf_op jit(solution)/shard_map/ppermute | solution.py:57
  22.1 7.9 %collective-permute-start.16 = (bf16[128,768]{1,0:T(8,128)(2,1)S(1)}, bf16[128,768]{1,0:T(8,128)(2,1)S(1)}, u32[]{:S(2)}, u32[]{:S(2)}) collective-permute-start(bf16[128,768]{1,0:T(8,128)(2,1)S(1)} %copy-done.1), channel_id=1, source_target_pairs={{0,128},{1,17},{2,130},{3,19},{4,132},{5,21},{6,134},{7,23},{8,136... | collective-permute-start | bytes 589832 | tf_op jit(solution)/shard_map/ppermute | solution.py:57
  25.2 6.9 %collective-permute-start.17 = (bf16[128,768]{1,0:T(8,128)(2,1)S(1)}, bf16[128,768]{1,0:T(8,128)(2,1)S(1)}, u32[]{:S(2)}, u32[]{:S(2)}) collective-permute-start(bf16[128,768]{1,0:T(8,128)(2,1)S(1)} %copy-done.1), channel_id=1, source_target_pairs={{0,192},{1,25},{2,194},{3,27},{4,196},{5,29},{6,198},{7,31},{8,200... | collective-permute-start | bytes 589832 | tf_op jit(solution)/shard_map/ppermute | solution.py:57
  26.4 11.1 %collective-permute-start.3 = (bf16[4,192,128]{2,1,0:T(8,128)(2,1)S(1)}, bf16[4,192,128]{2,1,0:T(8,128)(2,1)S(1)}, u32[]{:S(2)}, u32[]{:S(2)}) collective-permute-start(bf16[4,192,128]{2,1,0:T(8,128)(2,1)S(1)} %pad_maximum_fusion.1), channel_id=1, source_target_pairs={{0,0},{1,32},{2,66},{3,98},{4,132},{5,164},{6,198},{7,230},{8,8},{... | collective-permute-start | bytes 589832 | tf_op jit(solution)/shard_map/ppermute | solution.py:57
  29.8 12.8 %collective-permute-start.9 = (bf16[128,768]{1,0:T(8,128)(2,1)S(1)}, bf16[128,768]{1,0:T(8,128)(2,1)S(1)}, u32[]{:S(2)}, u32[]{:S(2)}) collective-permute-start(bf16[128,768]{1,0:T(8,128)(2,1)S(1)} %collective-permute-done.8.far), channel_id=1, source_target_pairs={{0,64},{1,9},{2,66},{3,11},{4,68},{5,13},{6,70},{7,15},{8,72},{9,1... | collective-permute-start | bytes 589832 | tf_op jit(solution)/shard_map/ppermute | solution.py:57
  32.1 36.2 %collective-permute-start.18 = (bf16[512,768]{1,0:T(8,128)(2,1)S(1)}, bf16[512,768]{1,0:T(8,128)(2,1)S(1)}, u32[]{:S(2)}, u32[]{:S(2)}) collective-permute-start(bf16[512,768]{1,0:T(8,128)(2,1)S(1)} %constant_dynamic-update-slice_fusion.4.refs_0_), channel_id=1, source_target_pairs={{0,8},{1,65},{2,10},{3,67},{4,12},{5,69},{6,14},{7,71},{8,0},{9,73... | collective-permute-start | bytes 2359304 | tf_op jit(solution)/shard_map/ppermute | solution.py:57
  33.8 10.7 %collective-permute-start.10 = (bf16[128,768]{1,0:T(8,128)(2,1)S(1)}, bf16[128,768]{1,0:T(8,128)(2,1)S(1)}, u32[]{:S(2)}, u32[]{:S(2)}) collective-permute-start(bf16[128,768]{1,0:T(8,128)(2,1)S(1)} %collective-permute-done.8.far), channel_id=1, source_target_pairs={{0,128},{1,17},{2,130},{3,19},{4,132},{5,21},{6,134},{7,23},{8,136... | collective-permute-start | bytes 589832 | tf_op jit(solution)/shard_map/ppermute | solution.py:57
  37.5 33.8 %collective-permute-start.19 = (bf16[512,768]{1,0:T(8,128)(2,1)S(1)}, bf16[512,768]{1,0:T(8,128)(2,1)S(1)}, u32[]{:S(2)}, u32[]{:S(2)}) collective-permute-start(bf16[512,768]{1,0:T(8,128)(2,1)S(1)} %constant_dynamic-update-slice_fusion.4.refs_0_), channel_id=1, source_target_pairs={{0,16},{1,129},{2,18},{3,131},{4,20},{5,133},{6,22},{7,135},{8,24}... | collective-permute-start | bytes 2359304 | tf_op jit(solution)/shard_map/ppermute | solution.py:57
  42.7 6.9 %collective-permute-start.11 = (bf16[128,768]{1,0:T(8,128)(2,1)S(1)}, bf16[128,768]{1,0:T(8,128)(2,1)S(1)}, u32[]{:S(2)}, u32[]{:S(2)}) collective-permute-start(bf16[128,768]{1,0:T(8,128)(2,1)S(1)} %collective-permute-done.8.far), channel_id=1, source_target_pairs={{0,192},{1,25},{2,194},{3,27},{4,196},{5,29},{6,198},{7,31},{8,200... | collective-permute-start | bytes 589832 | tf_op jit(solution)/shard_map/ppermute | solution.py:57
  44.5 6.7 %collective-permute-start.5 = (bf16[4,192,128]{2,1,0:T(8,128)(2,1)S(1)}, bf16[4,192,128]{2,1,0:T(8,128)(2,1)S(1)}, u32[]{:S(2)}, u32[]{:S(2)}) collective-permute-start(bf16[4,192,128]{2,1,0:T(8,128)(2,1)S(1)} %collective-permute-done.3), channel_id=1, source_target_pairs={{0,4},{1,5},{2,6},{3,7},{4,0},{5,1},{6,2},{7,3},{8,12},{9,13},{10,... | collective-permute-start | bytes 589832 | tf_op jit(solution)/shard_map/ppermute | solution.py:57
  49.6 14.7 %collective-permute-start.6 = (bf16[4,192,128]{2,1,0:T(8,128)(2,1)S(1)}, bf16[4,192,128]{2,1,0:T(8,128)(2,1)S(1)}, u32[]{:S(2)}, u32[]{:S(2)}) collective-permute-start(bf16[4,192,128]{2,1,0:T(8,128)(2,1)S(1)} %collective-permute-done.3), channel_id=1, source_target_pairs={{0,6},{1,7},{2,4},{3,5},{4,2},{5,3},{6,0},{7,1},{8,14},{9,15},{10,... | collective-permute-start | bytes 589832 | tf_op jit(solution)/shard_map/ppermute | solution.py:57
  51.1 16.4 %collective-permute-start.4 = (bf16[4,192,128]{2,1,0:T(8,128)(2,1)S(1)}, bf16[4,192,128]{2,1,0:T(8,128)(2,1)S(1)}, u32[]{:S(2)}, u32[]{:S(2)}) collective-permute-start(bf16[4,192,128]{2,1,0:T(8,128)(2,1)S(1)} %collective-permute-done.3), channel_id=1, source_target_pairs={{0,2},{1,3},{2,0},{3,1},{4,6},{5,7},{6,4},{7,5},{8,10},{9,11},{10,... | collective-permute-start | bytes 589832 | tf_op jit(solution)/shard_map/ppermute | solution.py:57
  64.2 13.3 %collective-permute-start.20 = (bf16[512,768]{1,0:T(8,128)(2,1)S(1)}, bf16[512,768]{1,0:T(8,128)(2,1)S(1)}, u32[]{:S(2)}, u32[]{:S(2)}) collective-permute-start(bf16[512,768]{1,0:T(8,128)(2,1)S(1)} %constant_dynamic-update-slice_fusion.4.refs_0_), channel_id=1, source_target_pairs={{0,24},{1,193},{2,26},{3,195},{4,28},{5,197},{6,30},{7,199},{8,16}... | collective-permute-start | bytes 2359304 | tf_op jit(solution)/shard_map/ppermute | solution.py:57
  67.6 12.1 %collective-permute-start.12 = (bf16[512,768]{1,0:T(8,128)(2,1)S(1)}, bf16[512,768]{1,0:T(8,128)(2,1)S(1)}, u32[]{:S(2)}, u32[]{:S(2)}) collective-permute-start(bf16[512,768]{1,0:T(8,128)(2,1)S(1)} %constant_dynamic-update-slice_fusion.refs_0_), channel_id=1, source_target_pairs={{0,8},{1,65},{2,10},{3,67},{4,12},{5,69},{6,14},{7,71},{8,0},{9,73... | collective-permute-start | bytes 2359304 | tf_op jit(solution)/shard_map/ppermute | solution.py:57
  68.3 21.3 %collective-permute-start.13 = (bf16[512,768]{1,0:T(8,128)(2,1)S(1)}, bf16[512,768]{1,0:T(8,128)(2,1)S(1)}, u32[]{:S(2)}, u32[]{:S(2)}) collective-permute-start(bf16[512,768]{1,0:T(8,128)(2,1)S(1)} %constant_dynamic-update-slice_fusion.refs_0_), channel_id=1, source_target_pairs={{0,16},{1,129},{2,18},{3,131},{4,20},{5,133},{6,22},{7,135},{8,24}... | collective-permute-start | bytes 2359304 | tf_op jit(solution)/shard_map/ppermute | solution.py:57
  71.3 20.6 %collective-permute-start.7 = (bf16[4,4,192,128]{3,2,1,0:T(8,128)(2,1)S(1)}, bf16[4,4,192,128]{3,2,1,0:T(8,128)(2,1)S(1)}, u32[]{:S(2)}, u32[]{:S(2)}) collective-permute-start(bf16[4,4,192,128]{3,2,1,0:T(8,128)(2,1)S(1)} %pad_maximum_fusion.own), channel_id=1, source_target_pairs={{0,1},{1,0},{2,3},{3,2},{4,5},{5,4},{6,7},{7,6},{8,9},{9,8},{10,11... | collective-permute-start | bytes 2359304 | tf_op jit(solution)/shard_map/ppermute | solution.py:57
  71.6 22.8 %collective-permute-start.14 = (bf16[512,768]{1,0:T(8,128)(2,1)S(1)}, bf16[512,768]{1,0:T(8,128)(2,1)S(1)}, u32[]{:S(2)}, u32[]{:S(2)}) collective-permute-start(bf16[512,768]{1,0:T(8,128)(2,1)S(1)} %constant_dynamic-update-slice_fusion.refs_0_), channel_id=1, source_target_pairs={{0,24},{1,193},{2,26},{3,195},{4,28},{5,197},{6,30},{7,199},{8,16}... | collective-permute-start | bytes 2359304 | tf_op jit(solution)/shard_map/ppermute | solution.py:57
  77.5 24.7 %collective-permute-start.22 = (f32[768,128]{1,0:T(8,128)S(1)}, f32[768,128]{1,0:T(8,128)S(1)}, u32[]{:S(2)}, u32[]{:S(2)}) collective-permute-start(f32[768,128]{1,0:T(8,128)S(1)} %get-tuple-element.8), channel_id=1, source_target_pairs={{0,2},{1,3},{2,4},{3,5},{4,6},{5,7},{6,32},{7,33},{8,10},{9,11},{1... | collective-permute-start | bytes 1179656 | tf_op jit(solution)/shard_map/ppermute | solution.py:57
  79.7 22.6 %collective-permute-start.23 = (f32[768,128]{1,0:T(8,128)S(1)}, f32[768,128]{1,0:T(8,128)S(1)}, u32[]{:S(2)}, u32[]{:S(2)}) collective-permute-start(f32[768,128]{1,0:T(8,128)S(1)} %get-tuple-element.9), channel_id=1, source_target_pairs={{0,38},{1,39},{2,0},{3,1},{4,2},{5,3},{6,4},{7,5},{8,46},{9,47},{1... | collective-permute-start | bytes 1179656 | tf_op jit(solution)/shard_map/ppermute | solution.py:57
  89.7 8.2 %collective-permute-start.24 = (f32[384,128]{1,0:T(8,128)S(1)}, f32[384,128]{1,0:T(8,128)S(1)}, u32[]{:S(2)}, u32[]{:S(2)}) collective-permute-start(f32[384,128]{1,0:T(8,128)S(1)} %get-tuple-element.10), channel_id=1, source_target_pairs={{0,4},{1,5},{2,6},{3,7},{4,32},{5,33},{6,34},{7,35},{8,12},{9,13},... | collective-permute-start | bytes 589832 | tf_op jit(solution)/shard_map/ppermute | solution.py:57
  91.8 10.4 %collective-permute-start.25 = (f32[384,128]{1,0:T(8,128)S(1)}, f32[384,128]{1,0:T(8,128)S(1)}, u32[]{:S(2)}, u32[]{:S(2)}) collective-permute-start(f32[384,128]{1,0:T(8,128)S(1)} %get-tuple-element.11), channel_id=1, source_target_pairs={{0,36},{1,37},{2,38},{3,39},{4,0},{5,1},{6,2},{7,3},{8,44},{9,45},... | collective-permute-start | bytes 589832 | tf_op jit(solution)/shard_map/ppermute | solution.py:57

commit v4 on v3

--- a/solution.py
+++ b/solution.py
@@ -63,22 +63,32 @@
 
 def products_kernel(kept, weight, near, far, *refs):
     h, l, c = here()
-    turned = refs[-1]
-    turned[0] = near[...].T
-    turned[1] = far[...].T
+    turned, blocks, arrived = refs[-3:]
     depth = near.shape[1]
     rows = depth // 2
     core = c if kept else 1 - c
-    for i, (block, steps) in enumerate(((0, (0, 0)), (1, (1, 1)), (3, (-1, -1)), (2, (2, -2)))):
+    copies = []
+    for i, block in enumerate((0, 1, 3, 2)):
+        for half in range(2):
+            row = ((((l + block) & 3) * 2 + core) * 2 + half) * rows
+            copies.append(
+                pltpu.make_async_copy(
+                    weight.at[pl.ds(pl.multiple_of(row, rows), rows), :],
+                    blocks.at[i, half],
+                    arrived.at[i, half],
+                )
+            )
+            copies[-1].start()
+    turned[0] = near[...].T
+    turned[1] = far[...].T
+    for i, steps in enumerate(((0, 0), (1, 1), (-1, -1), (2, -2))):
         for half, step in enumerate(steps):
             target = (4 * h + l + step + 8) & 7
             use_far = (target >> 2) ^ h
-            row = ((((l + block) & 3) * 2 + core) * 2 + half) * rows
             part = pl.ds(half * rows, rows)
+            copies[2 * i + half].wait()
             total = jnp.dot(
-                weight[pl.ds(pl.multiple_of(row, rows), rows), :],
-                turned[use_far],
-                preferred_element_type=F32,
+                blocks[i, half], turned[use_far], preferred_element_type=F32
             )
             if not kept:
                 refs[0][i, part, :] = total
@@ -101,10 +111,14 @@
     return pl.pallas_call(
         functools.partial(products_kernel, kept),
         out_shape=shapes,
-        in_specs=[VMEM] * (3 + kept),
+        in_specs=[pl.BlockSpec(memory_space=pltpu.HBM)] + [VMEM] * (2 + kept),
         out_specs=[VMEM] * len(shapes),
-        scratch_shapes=[pltpu.VMEM((2, depth, tokens), BF16)],
-        compiler_params=pltpu.CompilerParams(vmem_limit_bytes=20 * MIB),
+        scratch_shapes=[
+            pltpu.VMEM((2, depth, tokens), BF16),
+            pltpu.VMEM((4, 2, depth // 2, depth), BF16),
+            pltpu.SemaphoreType.DMA((4, 2)),
+        ],
+        compiler_params=pltpu.CompilerParams(vmem_limit_bytes=48 * MIB),
         cost_estimate=pl.CostEstimate(
             flops=8 * depth * tokens * depth,
             bytes_accessed=8 * depth * depth + 16 * depth * tokens,

time: 103 us -> 103 us (level)
  the two profiles are of different devices: /device:TPU:64 before, /device:TPU:1 now
where the time goes in v4:
time: 103 us; the launch traced here: 102 us
  starting transfers between devices  53.4 us (52%)
  waiting for transfers between devices  32.6 us (32%)
  Pallas kernels  12.8 us (12%)
  local copies, waits for them, and re-layouts  2.15 us (2%)
    ppermute x26, starting transfers between devices, send(): return lax.ppermute(array, AXES, pairs(route))  53.4 us
    ppermute x26, waiting for transfers between devices, send(): return lax.ppermute(array, AXES, pairs(route))  32.6 us
    pallas_call x2, Pallas kernels, products(): pl.pallas_call(functools.partial(products_kernel, kept), out_shape=shapes...  9.56 us
    pallas_call x2, Pallas kernels, weight_part(): pl.pallas_call(functools.partial(weight_kernel, far), out_shape=jax.Shape...  2.38 us
  transfers between devices with their start and end apart: 26, of which 8 were waited for; matrix products, arithmetic and copies ran while one was open for 1% of the time, Pallas kernels for 12%

profile of v4, /device:TPU:1, one launch (start us, length us, event | category | flops | bytes accessed | tf_op | source)
XLA Modules:
  0.0 101.9 jit_solution(307729562002096386)
XLA Ops:
  0.6 7.8 %collective-permute-start.8 = (bf16[128,768]{1,0:T(8,128)(2,1)}, bf16[128,768]{1,0:T(8,128)(2,1)S(1)}, u32[]{:S(2)}, u32[]{:S(2)}) collective-permute-start(bf16[128,768]{1,0:T(8,128)(2,1)} %near.3), channel_id=1, source_target_pairs={{0,32},{1,33},{2,34},{3,35},{4,36},{5,37},{6,38},{7,39},{8,40},{9,... | collective-permute-start | bytes 589832 | tf_op jit(solution)/shard_map/ppermute | solution.py:57
  8.4 1.3 %collective-permute-start.15 = (bf16[128,768]{1,0:T(8,128)(2,1)}, bf16[128,768]{1,0:T(8,128)(2,1)S(1)}, u32[]{:S(2)}, u32[]{:S(2)}) collective-permute-start(bf16[128,768]{1,0:T(8,128)(2,1)} %near.3), channel_id=1, source_target_pairs={{0,64},{1,9},{2,66},{3,11},{4,68},{5,13},{6,70},{7,15},{8,72},{9,1... | collective-permute-start | bytes 589832 | tf_op jit(solution)/shard_map/ppermute | solution.py:57
  9.7 1.1 %copy.5 = bf16[768,128]{1,0:T(8,128)(2,1)S(1)} copy(bf16[768,128]{0,1:T(8,128)(2,1)} %bitcast.20) | data formatting | bytes 393216 | tf_op jit(solution)/shard_map/transpose | solution.py:187
  10.9 0.3 collective-permute-start
  11.1 2.9 %collective-permute-start.1 = (bf16[192,128]{1,0:T(8,128)(2,1)S(1)}, bf16[192,128]{1,0:T(8,128)(2,1)S(1)}, u32[]{:S(2)}, u32[]{:S(2)}) collective-permute-start(bf16[192,128]{1,0:T(8,128)(2,1)S(1)} %get-tuple-element.14), channel_id=1, source_target_pairs={{0,16},{1,17},{2,18},{3,19},{4,20},{5,21},{6,22},{7,23},{8,24},{9,... | collective-permute-start | bytes 147464 | tf_op jit(solution)/shard_map/ppermute | solution.py:57
  14.0 0.8 collective-permute-start.2
  14.8 0.9 copy-done
  15.8 4.8 %shard_map.52 = f32[4,768,128]{2,1,0:T(8,128)S(1)} custom-call(bf16[6144,768]{1,0:T(8,128)(2,1)} %weight.3, bf16[128,768]{1,0:T(8,128)(2,1)S(1)} %copy-done, bf16[128,768]{1,0:T(8,128)(2,1)S(1)} %collective-permute-done.8.far), custom_call_target="tpu_custom_call" | custom-call | flops 603979776 | bytes 6291456 | tf_op jit(solution)/shard_map/pallas_call | solution.py:111
  20.5 2.1 %collective-permute-start.21 = (f32[4,768,128]{2,1,0:T(8,128)S(1)}, f32[4,768,128]{2,1,0:T(8,128)S(1)}, u32[]{:S(2)}, u32[]{:S(2)}) collective-permute-start(f32[4,768,128]{2,1,0:T(8,128)S(1)} %shard_map.52), channel_id=1, source_target_pairs={{0,1},{1,0},{2,3},{3,2},{4,5},{5,4},{6,7},{7,6},{8,9},{9,8},{10,11... | collective-permute-start | bytes 4718600 | tf_op jit(solution)/shard_map/ppermute | solution.py:57
  22.6 1.8 %collective-permute-start.16 = (bf16[128,768]{1,0:T(8,128)(2,1)S(1)}, bf16[128,768]{1,0:T(8,128)(2,1)S(1)}, u32[]{:S(2)}, u32[]{:S(2)}) collective-permute-start(bf16[128,768]{1,0:T(8,128)(2,1)S(1)} %copy-done), channel_id=1, source_target_pairs={{0,128},{1,17},{2,130},{3,19},{4,132},{5,21},{6,134},{7,23},{8,136... | collective-permute-start | bytes 589832 | tf_op jit(solution)/shard_map/ppermute | solution.py:57
  24.4 1.1 %collective-permute-start.17 = (bf16[128,768]{1,0:T(8,128)(2,1)S(1)}, bf16[128,768]{1,0:T(8,128)(2,1)S(1)}, u32[]{:S(2)}, u32[]{:S(2)}) collective-permute-start(bf16[128,768]{1,0:T(8,128)(2,1)S(1)} %copy-done), channel_id=1, source_target_pairs={{0,192},{1,25},{2,194},{3,27},{4,196},{5,29},{6,198},{7,31},{8,200... | collective-permute-start | bytes 589832 | tf_op jit(solution)/shard_map/ppermute | solution.py:57
  25.6 9.7 %collective-permute-start.3 = (bf16[4,192,128]{2,1,0:T(8,128)(2,1)S(1)}, bf16[4,192,128]{2,1,0:T(8,128)(2,1)S(1)}, u32[]{:S(2)}, u32[]{:S(2)}) collective-permute-start(bf16[4,192,128]{2,1,0:T(8,128)(2,1)S(1)} %pad_maximum_fusion.1), channel_id=1, source_target_pairs={{0,0},{1,32},{2,66},{3,98},{4,132},{5,164},{6,198},{7,230},{8,8},{... | collective-permute-start | bytes 589832 | tf_op jit(solution)/shard_map/ppermute | solution.py:57
  35.3 0.0 collective-permute-done.15
  35.3 1.4 %collective-permute-start.9 = (bf16[128,768]{1,0:T(8,128)(2,1)S(1)}, bf16[128,768]{1,0:T(8,128)(2,1)S(1)}, u32[]{:S(2)}, u32[]{:S(2)}) collective-permute-start(bf16[128,768]{1,0:T(8,128)(2,1)S(1)} %collective-permute-done.8.far), channel_id=1, source_target_pairs={{0,64},{1,9},{2,66},{3,11},{4,68},{5,13},{6,70},{7,15},{8,72},{9,1... | collective-permute-start | bytes 589832 | tf_op jit(solution)/shard_map/ppermute | solution.py:57
  36.8 0.0 collective-permute-done.17
  36.8 1.5 %collective-permute-start.18 = (bf16[512,768]{1,0:T(8,128)(2,1)S(1)}, bf16[512,768]{1,0:T(8,128)(2,1)S(1)}, u32[]{:S(2)}, u32[]{:S(2)}) collective-permute-start(bf16[512,768]{1,0:T(8,128)(2,1)S(1)} %constant_dynamic-update-slice_fusion.4.refs_0_), channel_id=1, source_target_pairs={{0,8},{1,65},{2,10},{3,67},{4,12},{5,69},{6,14},{7,71},{8,0},{9,73... | collective-permute-start | bytes 2359304 | tf_op jit(solution)/shard_map/ppermute | solution.py:57
  38.3 2.6 %collective-permute-start.10 = (bf16[128,768]{1,0:T(8,128)(2,1)S(1)}, bf16[128,768]{1,0:T(8,128)(2,1)S(1)}, u32[]{:S(2)}, u32[]{:S(2)}) collective-permute-start(bf16[128,768]{1,0:T(8,128)(2,1)S(1)} %collective-permute-done.8.far), channel_id=1, source_target_pairs={{0,128},{1,17},{2,130},{3,19},{4,132},{5,21},{6,134},{7,23},{8,136... | collective-permute-start | bytes 589832 | tf_op jit(solution)/shard_map/ppermute | solution.py:57
  41.0 0.0 collective-permute-done.3
  41.0 1.1 %collective-permute-start.19 = (bf16[512,768]{1,0:T(8,128)(2,1)S(1)}, bf16[512,768]{1,0:T(8,128)(2,1)S(1)}, u32[]{:S(2)}, u32[]{:S(2)}) collective-permute-start(bf16[512,768]{1,0:T(8,128)(2,1)S(1)} %constant_dynamic-update-slice_fusion.4.refs_0_), channel_id=1, source_target_pairs={{0,16},{1,129},{2,18},{3,131},{4,20},{5,133},{6,22},{7,135},{8,24}... | collective-permute-start | bytes 2359304 | tf_op jit(solution)/shard_map/ppermute | solution.py:57
  42.0 0.3 collective-permute-done.9
  42.4 2.7 %collective-permute-start.11 = (bf16[128,768]{1,0:T(8,128)(2,1)S(1)}, bf16[128,768]{1,0:T(8,128)(2,1)S(1)}, u32[]{:S(2)}, u32[]{:S(2)}) collective-permute-start(bf16[128,768]{1,0:T(8,128)(2,1)S(1)} %collective-permute-done.8.far), channel_id=1, source_target_pairs={{0,192},{1,25},{2,194},{3,27},{4,196},{5,29},{6,198},{7,31},{8,200... | collective-permute-start | bytes 589832 | tf_op jit(solution)/shard_map/ppermute | solution.py:57
  45.1 3.6 %collective-permute-done.10 = bf16[128,768]{1,0:T(8,128)(2,1)S(1)} collective-permute-done((bf16[128,768]{1,0:T(8,128)(2,1)S(1)}, bf16[128,768]{1,0:T(8,128)(2,1)S(1)}, u32[]{:S(2)}, u32[]{:S(2)}) %collective-permute-start.10) | collective-permute-done | bytes 196640 | tf_op jit(solution)/shard_map/ppermute | solution.py:57
  48.7 2.8 %collective-permute-start.5 = (bf16[4,192,128]{2,1,0:T(8,128)(2,1)S(1)}, bf16[4,192,128]{2,1,0:T(8,128)(2,1)S(1)}, u32[]{:S(2)}, u32[]{:S(2)}) collective-permute-start(bf16[4,192,128]{2,1,0:T(8,128)(2,1)S(1)} %collective-permute-done.3), channel_id=1, source_target_pairs={{0,4},{1,5},{2,6},{3,7},{4,0},{5,1},{6,2},{7,3},{8,12},{9,13},{10,... | collective-permute-start | bytes 589832 | tf_op jit(solution)/shard_map/ppermute | solution.py:57
  51.5 0.0 collective-permute-done.11
  51.5 1.0 collective-permute-start.6
  52.5 12.4 %collective-permute-done.5 = bf16[4,192,128]{2,1,0:T(8,128)(2,1)S(1)} collective-permute-done((bf16[4,192,128]{2,1,0:T(8,128)(2,1)S(1)}, bf16[4,192,128]{2,1,0:T(8,128)(2,1)S(1)}, u32[]{:S(2)}, u32[]{:S(2)}) %collective-permute-start.5) | collective-permute-done | bytes 196640 | tf_op jit(solution)/shard_map/ppermute | solution.py:57
  64.9 0.0 collective-permute-start.4
  65.0 0.0 collective-permute-done.6
  65.0 0.1 collective-permute-start.20
  65.1 4.7 %collective-permute-done.4 = bf16[4,192,128]{2,1,0:T(8,128)(2,1)S(1)} collective-permute-done((bf16[4,192,128]{2,1,0:T(8,128)(2,1)S(1)}, bf16[4,192,128]{2,1,0:T(8,128)(2,1)S(1)}, u32[]{:S(2)}, u32[]{:S(2)}) %collective-permute-start.4) | collective-permute-done | bytes 196640 | tf_op jit(solution)/shard_map/ppermute | solution.py:57
  69.8 1.7 %collective-permute-start.13 = (bf16[512,768]{1,0:T(8,128)(2,1)S(1)}, bf16[512,768]{1,0:T(8,128)(2,1)S(1)}, u32[]{:S(2)}, u32[]{:S(2)}) collective-permute-start(bf16[512,768]{1,0:T(8,128)(2,1)S(1)} %constant_dynamic-update-slice_fusion.refs_0_), channel_id=1, source_target_pairs={{0,16},{1,129},{2,18},{3,131},{4,20},{5,133},{6,22},{7,135},{8,24}... | collective-permute-start | bytes 2359304 | tf_op jit(solution)/shard_map/ppermute | solution.py:57
  71.4 0.1 pad_maximum_fusion.own
  71.6 3.0 %collective-permute-start.7 = (bf16[4,4,192,128]{3,2,1,0:T(8,128)(2,1)S(1)}, bf16[4,4,192,128]{3,2,1,0:T(8,128)(2,1)S(1)}, u32[]{:S(2)}, u32[]{:S(2)}) collective-permute-start(bf16[4,4,192,128]{3,2,1,0:T(8,128)(2,1)S(1)} %pad_maximum_fusion.own), channel_id=1, source_target_pairs={{0,1},{1,0},{2,3},{3,2},{4,5},{5,4},{6,7},{7,6},{8,9},{9,8},{10,11... | collective-permute-start | bytes 2359304 | tf_op jit(solution)/shard_map/ppermute | solution.py:57
  74.5 0.0 collective-permute-done.21.refs_0_
  74.5 4.8 %shard_map.53 = (f32[768,128]{1,0:T(8,128)S(1)}, f32[768,128]{1,0:T(8,128)S(1)}, f32[768,128]{1,0:T(8,128)S(1)}, f32[384,128]{1,0:T(8,128)S(1)}, f32[384,128]{1,0:T(8,128)S(1)}) custom-call(bf16[6144,768]{1,0:T(8,128)(2,1)} %weight.3, bf16[128,768]{1,0:T(8,128)(2,1)S(1)} %copy-done, bf16[128,768]{1,0:T(8,128)(2,1)S(1)} %collective-permute-done.8.far, ...), custom_call_target="tpu_custom_call" | custom-call | flops 603979776 | bytes 6291456 | tf_op jit(solution)/shard_map/pallas_call | solution.py:111
  79.3 0.0 collective-permute-done.20.refs_3_
  79.3 0.4 collective-permute-start.22
  79.8 1.1 %collective-permute-done.12.refs_1_ = bf16[512,768]{1,0:T(8,128)(2,1)S(1)} collective-permute-done((bf16[512,768]{1,0:T(8,128)(2,1)S(1)}, bf16[512,768]{1,0:T(8,128)(2,1)S(1)}, u32[]{:S(2)}, u32[]{:S(2)}) %collective-permute-start.12) | collective-permute-done | bytes 786464 | tf_op jit(solution)/shard_map/ppermute | solution.py:57
  80.9 3.8 %collective-permute-start.23 = (f32[768,128]{1,0:T(8,128)S(1)}, f32[768,128]{1,0:T(8,128)S(1)}, u32[]{:S(2)}, u32[]{:S(2)}) collective-permute-start(f32[768,128]{1,0:T(8,128)S(1)} %get-tuple-element.9), channel_id=1, source_target_pairs={{0,38},{1,39},{2,0},{3,1},{4,2},{5,3},{6,4},{7,5},{8,46},{9,47},{1... | collective-permute-start | bytes 1179656 | tf_op jit(solution)/shard_map/ppermute | solution.py:57
  84.7 4.9 %collective-permute-done.13.refs_2_ = bf16[512,768]{1,0:T(8,128)(2,1)S(1)} collective-permute-done((bf16[512,768]{1,0:T(8,128)(2,1)S(1)}, bf16[512,768]{1,0:T(8,128)(2,1)S(1)}, u32[]{:S(2)}, u32[]{:S(2)}) %collective-permute-start.13) | collective-permute-done | bytes 786464 | tf_op jit(solution)/shard_map/ppermute | solution.py:57
  89.6 1.9 %collective-permute-start.24 = (f32[384,128]{1,0:T(8,128)S(1)}, f32[384,128]{1,0:T(8,128)S(1)}, u32[]{:S(2)}, u32[]{:S(2)}) collective-permute-start(f32[384,128]{1,0:T(8,128)S(1)} %get-tuple-element.10), channel_id=1, source_target_pairs={{0,4},{1,5},{2,6},{3,7},{4,32},{5,33},{6,34},{7,35},{8,12},{9,13},... | collective-permute-start | bytes 589832 | tf_op jit(solution)/shard_map/ppermute | solution.py:57
  91.5 1.7 %collective-permute-start.25 = (f32[384,128]{1,0:T(8,128)S(1)}, f32[384,128]{1,0:T(8,128)S(1)}, u32[]{:S(2)}, u32[]{:S(2)}) collective-permute-start(f32[384,128]{1,0:T(8,128)S(1)} %get-tuple-element.11), channel_id=1, source_target_pairs={{0,36},{1,37},{2,38},{3,39},{4,0},{5,1},{6,2},{7,3},{8,44},{9,45},... | collective-permute-start | bytes 589832 | tf_op jit(solution)/shard_map/ppermute | solution.py:57
  93.2 0.8 shard_map.50.refs_4_
  93.9 1.3 %collective-permute-done.14.refs_3_ = bf16[512,768]{1,0:T(8,128)(2,1)S(1)} collective-permute-done((bf16[512,768]{1,0:T(8,128)(2,1)S(1)}, bf16[512,768]{1,0:T(8,128)(2,1)S(1)}, u32[]{:S(2)}, u32[]{:S(2)}) %collective-permute-start.14) | collective-permute-done | bytes 786464 | tf_op jit(solution)/shard_map/ppermute | solution.py:57
  95.3 1.6 %shard_map.51 = f32[192,768]{1,0:T(8,128)} custom-call(bf16[4,4,192,128]{3,2,1,0:T(8,128)(2,1)S(1)} %pad_maximum_fusion.own, bf16[4,4,192,128]{3,2,1,0:T(8,128)(2,1)S(1)} %collective-permute-done.7.other, bf16[512,768]{1,0:T(8,128)(2,1)S(1)} %constant_dynamic-update-slice_fusion.refs_0_, bf16[512,768]{1,0:T(8,128)(2,1)S(1)} %collective-permute-done.12.refs_1_, ...), custom_call_target="tpu_custom_call" | custom-call | flops 603979776 | bytes 3145728 | tf_op jit(solution)/shard_map/pallas_call | solution.py:159
  96.9 4.2 %collective-permute-done.24.two_before = f32[384,128]{1,0:T(8,128)S(1)} collective-permute-done((f32[384,128]{1,0:T(8,128)S(1)}, f32[384,128]{1,0:T(8,128)S(1)}, u32[]{:S(2)}, u32[]{:S(2)}) %collective-permute-start.24) | collective-permute-done | bytes 196640 | tf_op jit(solution)/shard_map/ppermute | solution.py:57
  101.1 0.0 collective-permute-done.25.two_after
  101.1 0.8 shard_map.54
  (23 shorter events, 0.2 us)
Async XLA Ops:
  0.6 14.2 %collective-permute-start.8 = (bf16[128,768]{1,0:T(8,128)(2,1)}, bf16[128,768]{1,0:T(8,128)(2,1)S(1)}, u32[]{:S(2)}, u32[]{:S(2)}) collective-permute-start(bf16[128,768]{1,0:T(8,128)(2,1)} %near.3), channel_id=1, source_target_pairs={{0,32},{1,33},{2,34},{3,35},{4,36},{5,37},{6,38},{7,39},{8,40},{9,... | collective-permute-start | bytes 589832 | tf_op jit(solution)/shard_map/ppermute | solution.py:57
  8.4 26.9 %collective-permute-start.15 = (bf16[128,768]{1,0:T(8,128)(2,1)}, bf16[128,768]{1,0:T(8,128)(2,1)S(1)}, u32[]{:S(2)}, u32[]{:S(2)}) collective-permute-start(bf16[128,768]{1,0:T(8,128)(2,1)} %near.3), channel_id=1, source_target_pairs={{0,64},{1,9},{2,66},{3,11},{4,68},{5,13},{6,70},{7,15},{8,72},{9,1... | collective-permute-start | bytes 589832 | tf_op jit(solution)/shard_map/ppermute | solution.py:57
  10.9 11.8 %collective-permute-start = (bf16[192,128]{1,0:T(8,128)(2,1)S(1)}, bf16[192,128]{1,0:T(8,128)(2,1)S(1)}, u32[]{:S(2)}, u32[]{:S(2)}) collective-permute-start(bf16[192,128]{1,0:T(8,128)(2,1)S(1)} %get-tuple-element.15), channel_id=1, source_target_pairs={{0,8},{1,9},{2,10},{3,11},{4,12},{5,13},{6,14},{7,15},{8,0},{9,1},... | collective-permute-start | bytes 147464 | tf_op jit(solution)/shard_map/ppermute | solution.py:57
  11.1 13.3 %collective-permute-start.1 = (bf16[192,128]{1,0:T(8,128)(2,1)S(1)}, bf16[192,128]{1,0:T(8,128)(2,1)S(1)}, u32[]{:S(2)}, u32[]{:S(2)}) collective-permute-start(bf16[192,128]{1,0:T(8,128)(2,1)S(1)} %get-tuple-element.14), channel_id=1, source_target_pairs={{0,16},{1,17},{2,18},{3,19},{4,20},{5,21},{6,22},{7,23},{8,24},{9,... | collective-permute-start | bytes 147464 | tf_op jit(solution)/shard_map/ppermute | solution.py:57
  14.0 11.5 %collective-permute-start.2 = (bf16[192,128]{1,0:T(8,128)(2,1)S(1)}, bf16[192,128]{1,0:T(8,128)(2,1)S(1)}, u32[]{:S(2)}, u32[]{:S(2)}) collective-permute-start(bf16[192,128]{1,0:T(8,128)(2,1)S(1)} %get-tuple-element.13), channel_id=1, source_target_pairs={{0,24},{1,25},{2,26},{3,27},{4,28},{5,29},{6,30},{7,31},{8,16},{9,... | collective-permute-start | bytes 147464 | tf_op jit(solution)/shard_map/ppermute | solution.py:57
  14.8 0.9 copy-start
  20.5 54.0 %collective-permute-start.21 = (f32[4,768,128]{2,1,0:T(8,128)S(1)}, f32[4,768,128]{2,1,0:T(8,128)S(1)}, u32[]{:S(2)}, u32[]{:S(2)}) collective-permute-start(f32[4,768,128]{2,1,0:T(8,128)S(1)} %shard_map.52), channel_id=1, source_target_pairs={{0,1},{1,0},{2,3},{3,2},{4,5},{5,4},{6,7},{7,6},{8,9},{9,8},{10,11... | collective-permute-start | bytes 4718600 | tf_op jit(solution)/shard_map/ppermute | solution.py:57
  22.6 14.1 %collective-permute-start.16 = (bf16[128,768]{1,0:T(8,128)(2,1)S(1)}, bf16[128,768]{1,0:T(8,128)(2,1)S(1)}, u32[]{:S(2)}, u32[]{:S(2)}) collective-permute-start(bf16[128,768]{1,0:T(8,128)(2,1)S(1)} %copy-done), channel_id=1, source_target_pairs={{0,128},{1,17},{2,130},{3,19},{4,132},{5,21},{6,134},{7,23},{8,136... | collective-permute-start | bytes 589832 | tf_op jit(solution)/shard_map/ppermute | solution.py:57
  24.4 12.3 %collective-permute-start.17 = (bf16[128,768]{1,0:T(8,128)(2,1)S(1)}, bf16[128,768]{1,0:T(8,128)(2,1)S(1)}, u32[]{:S(2)}, u32[]{:S(2)}) collective-permute-start(bf16[128,768]{1,0:T(8,128)(2,1)S(1)} %copy-done), channel_id=1, source_target_pairs={{0,192},{1,25},{2,194},{3,27},{4,196},{5,29},{6,198},{7,31},{8,200... | collective-permute-start | bytes 589832 | tf_op jit(solution)/shard_map/ppermute | solution.py:57
  25.6 15.3 %collective-permute-start.3 = (bf16[4,192,128]{2,1,0:T(8,128)(2,1)S(1)}, bf16[4,192,128]{2,1,0:T(8,128)(2,1)S(1)}, u32[]{:S(2)}, u32[]{:S(2)}) collective-permute-start(bf16[4,192,128]{2,1,0:T(8,128)(2,1)S(1)} %pad_maximum_fusion.1), channel_id=1, source_target_pairs={{0,0},{1,32},{2,66},{3,98},{4,132},{5,164},{6,198},{7,230},{8,8},{... | collective-permute-start | bytes 589832 | tf_op jit(solution)/shard_map/ppermute | solution.py:57
  35.3 7.0 %collective-permute-start.9 = (bf16[128,768]{1,0:T(8,128)(2,1)S(1)}, bf16[128,768]{1,0:T(8,128)(2,1)S(1)}, u32[]{:S(2)}, u32[]{:S(2)}) collective-permute-start(bf16[128,768]{1,0:T(8,128)(2,1)S(1)} %collective-permute-done.8.far), channel_id=1, source_target_pairs={{0,64},{1,9},{2,66},{3,11},{4,68},{5,13},{6,70},{7,15},{8,72},{9,1... | collective-permute-start | bytes 589832 | tf_op jit(solution)/shard_map/ppermute | solution.py:57
  36.8 32.9 %collective-permute-start.18 = (bf16[512,768]{1,0:T(8,128)(2,1)S(1)}, bf16[512,768]{1,0:T(8,128)(2,1)S(1)}, u32[]{:S(2)}, u32[]{:S(2)}) collective-permute-start(bf16[512,768]{1,0:T(8,128)(2,1)S(1)} %constant_dynamic-update-slice_fusion.4.refs_0_), channel_id=1, source_target_pairs={{0,8},{1,65},{2,10},{3,67},{4,12},{5,69},{6,14},{7,71},{8,0},{9,73... | collective-permute-start | bytes 2359304 | tf_op jit(solution)/shard_map/ppermute | solution.py:57
  38.3 10.4 %collective-permute-start.10 = (bf16[128,768]{1,0:T(8,128)(2,1)S(1)}, bf16[128,768]{1,0:T(8,128)(2,1)S(1)}, u32[]{:S(2)}, u32[]{:S(2)}) collective-permute-start(bf16[128,768]{1,0:T(8,128)(2,1)S(1)} %collective-permute-done.8.far), channel_id=1, source_target_pairs={{0,128},{1,17},{2,130},{3,19},{4,132},{5,21},{6,134},{7,23},{8,136... | collective-permute-start | bytes 589832 | tf_op jit(solution)/shard_map/ppermute | solution.py:57
  41.0 30.6 %collective-permute-start.19 = (bf16[512,768]{1,0:T(8,128)(2,1)S(1)}, bf16[512,768]{1,0:T(8,128)(2,1)S(1)}, u32[]{:S(2)}, u32[]{:S(2)}) collective-permute-start(bf16[512,768]{1,0:T(8,128)(2,1)S(1)} %constant_dynamic-update-slice_fusion.4.refs_0_), channel_id=1, source_target_pairs={{0,16},{1,129},{2,18},{3,131},{4,20},{5,133},{6,22},{7,135},{8,24}... | collective-permute-start | bytes 2359304 | tf_op jit(solution)/shard_map/ppermute | solution.py:57
  42.4 9.2 %collective-permute-start.11 = (bf16[128,768]{1,0:T(8,128)(2,1)S(1)}, bf16[128,768]{1,0:T(8,128)(2,1)S(1)}, u32[]{:S(2)}, u32[]{:S(2)}) collective-permute-start(bf16[128,768]{1,0:T(8,128)(2,1)S(1)} %collective-permute-done.8.far), channel_id=1, source_target_pairs={{0,192},{1,25},{2,194},{3,27},{4,196},{5,29},{6,198},{7,31},{8,200... | collective-permute-start | bytes 589832 | tf_op jit(solution)/shard_map/ppermute | solution.py:57
  48.7 16.2 %collective-permute-start.5 = (bf16[4,192,128]{2,1,0:T(8,128)(2,1)S(1)}, bf16[4,192,128]{2,1,0:T(8,128)(2,1)S(1)}, u32[]{:S(2)}, u32[]{:S(2)}) collective-permute-start(bf16[4,192,128]{2,1,0:T(8,128)(2,1)S(1)} %collective-permute-done.3), channel_id=1, source_target_pairs={{0,4},{1,5},{2,6},{3,7},{4,0},{5,1},{6,2},{7,3},{8,12},{9,13},{10,... | collective-permute-start | bytes 589832 | tf_op jit(solution)/shard_map/ppermute | solution.py:57
  51.5 13.4 %collective-permute-start.6 = (bf16[4,192,128]{2,1,0:T(8,128)(2,1)S(1)}, bf16[4,192,128]{2,1,0:T(8,128)(2,1)S(1)}, u32[]{:S(2)}, u32[]{:S(2)}) collective-permute-start(bf16[4,192,128]{2,1,0:T(8,128)(2,1)S(1)} %collective-permute-done.3), channel_id=1, source_target_pairs={{0,6},{1,7},{2,4},{3,5},{4,2},{5,3},{6,0},{7,1},{8,14},{9,15},{10,... | collective-permute-start | bytes 589832 | tf_op jit(solution)/shard_map/ppermute | solution.py:57
  64.9 4.8 %collective-permute-start.4 = (bf16[4,192,128]{2,1,0:T(8,128)(2,1)S(1)}, bf16[4,192,128]{2,1,0:T(8,128)(2,1)S(1)}, u32[]{:S(2)}, u32[]{:S(2)}) collective-permute-start(bf16[4,192,128]{2,1,0:T(8,128)(2,1)S(1)} %collective-permute-done.3), channel_id=1, source_target_pairs={{0,2},{1,3},{2,0},{3,1},{4,6},{5,7},{6,4},{7,5},{8,10},{9,11},{10,... | collective-permute-start | bytes 589832 | tf_op jit(solution)/shard_map/ppermute | solution.py:57
  65.0 14.4 %collective-permute-start.20 = (bf16[512,768]{1,0:T(8,128)(2,1)S(1)}, bf16[512,768]{1,0:T(8,128)(2,1)S(1)}, u32[]{:S(2)}, u32[]{:S(2)}) collective-permute-start(bf16[512,768]{1,0:T(8,128)(2,1)S(1)} %constant_dynamic-update-slice_fusion.4.refs_0_), channel_id=1, source_target_pairs={{0,24},{1,193},{2,26},{3,195},{4,28},{5,197},{6,30},{7,199},{8,16}... | collective-permute-start | bytes 2359304 | tf_op jit(solution)/shard_map/ppermute | solution.py:57
  69.7 11.1 %collective-permute-start.12 = (bf16[512,768]{1,0:T(8,128)(2,1)S(1)}, bf16[512,768]{1,0:T(8,128)(2,1)S(1)}, u32[]{:S(2)}, u32[]{:S(2)}) collective-permute-start(bf16[512,768]{1,0:T(8,128)(2,1)S(1)} %constant_dynamic-update-slice_fusion.refs_0_), channel_id=1, source_target_pairs={{0,8},{1,65},{2,10},{3,67},{4,12},{5,69},{6,14},{7,71},{8,0},{9,73... | collective-permute-start | bytes 2359304 | tf_op jit(solution)/shard_map/ppermute | solution.py:57
  69.8 19.8 %collective-permute-start.13 = (bf16[512,768]{1,0:T(8,128)(2,1)S(1)}, bf16[512,768]{1,0:T(8,128)(2,1)S(1)}, u32[]{:S(2)}, u32[]{:S(2)}) collective-permute-start(bf16[512,768]{1,0:T(8,128)(2,1)S(1)} %constant_dynamic-update-slice_fusion.refs_0_), channel_id=1, source_target_pairs={{0,16},{1,129},{2,18},{3,131},{4,20},{5,133},{6,22},{7,135},{8,24}... | collective-permute-start | bytes 2359304 | tf_op jit(solution)/shard_map/ppermute | solution.py:57
  71.6 19.9 %collective-permute-start.7 = (bf16[4,4,192,128]{3,2,1,0:T(8,128)(2,1)S(1)}, bf16[4,4,192,128]{3,2,1,0:T(8,128)(2,1)S(1)}, u32[]{:S(2)}, u32[]{:S(2)}) collective-permute-start(bf16[4,4,192,128]{3,2,1,0:T(8,128)(2,1)S(1)} %pad_maximum_fusion.own), channel_id=1, source_target_pairs={{0,1},{1,0},{2,3},{3,2},{4,5},{5,4},{6,7},{7,6},{8,9},{9,8},{10,11... | collective-permute-start | bytes 2359304 | tf_op jit(solution)/shard_map/ppermute | solution.py:57
  74.5 20.8 %collective-permute-start.14 = (bf16[512,768]{1,0:T(8,128)(2,1)S(1)}, bf16[512,768]{1,0:T(8,128)(2,1)S(1)}, u32[]{:S(2)}, u32[]{:S(2)}) collective-permute-start(bf16[512,768]{1,0:T(8,128)(2,1)S(1)} %constant_dynamic-update-slice_fusion.refs_0_), channel_id=1, source_target_pairs={{0,24},{1,193},{2,26},{3,195},{4,28},{5,197},{6,30},{7,199},{8,16}... | collective-permute-start | bytes 2359304 | tf_op jit(solution)/shard_map/ppermute | solution.py:57
  79.3 21.8 %collective-permute-start.22 = (f32[768,128]{1,0:T(8,128)S(1)}, f32[768,128]{1,0:T(8,128)S(1)}, u32[]{:S(2)}, u32[]{:S(2)}) collective-permute-start(f32[768,128]{1,0:T(8,128)S(1)} %get-tuple-element.8), channel_id=1, source_target_pairs={{0,2},{1,3},{2,4},{3,5},{4,6},{5,7},{6,32},{7,33},{8,10},{9,11},{1... | collective-permute-start | bytes 1179656 | tf_op jit(solution)/shard_map/ppermute | solution.py:57
  80.9 20.2 %collective-permute-start.23 = (f32[768,128]{1,0:T(8,128)S(1)}, f32[768,128]{1,0:T(8,128)S(1)}, u32[]{:S(2)}, u32[]{:S(2)}) collective-permute-start(f32[768,128]{1,0:T(8,128)S(1)} %get-tuple-element.9), channel_id=1, source_target_pairs={{0,38},{1,39},{2,0},{3,1},{4,2},{5,3},{6,4},{7,5},{8,46},{9,47},{1... | collective-permute-start | bytes 1179656 | tf_op jit(solution)/shard_map/ppermute | solution.py:57
  89.6 11.5 %collective-permute-start.24 = (f32[384,128]{1,0:T(8,128)S(1)}, f32[384,128]{1,0:T(8,128)S(1)}, u32[]{:S(2)}, u32[]{:S(2)}) collective-permute-start(f32[384,128]{1,0:T(8,128)S(1)} %get-tuple-element.10), channel_id=1, source_target_pairs={{0,4},{1,5},{2,6},{3,7},{4,32},{5,33},{6,34},{7,35},{8,12},{9,13},... | collective-permute-start | bytes 589832 | tf_op jit(solution)/shard_map/ppermute | solution.py:57
  91.5 9.7 %collective-permute-start.25 = (f32[384,128]{1,0:T(8,128)S(1)}, f32[384,128]{1,0:T(8,128)S(1)}, u32[]{:S(2)}, u32[]{:S(2)}) collective-permute-start(f32[384,128]{1,0:T(8,128)S(1)} %get-tuple-element.11), channel_id=1, source_target_pairs={{0,36},{1,37},{2,38},{3,39},{4,0},{5,1},{6,2},{7,3},{8,44},{9,45},... | collective-permute-start | bytes 589832 | tf_op jit(solution)/shard_map/ppermute | solution.py:57

commit v5 on v3

--- a/solution.py
+++ b/solution.py
@@ -121,39 +121,39 @@
         out[:, part] = total.T.astype(BF16)
 
 
-def weight_kernel(far, own, other, *refs):
+def weight_kernel(items, own, other, *refs):
     h, low, core = here()
-    cots, out = refs[:4], refs[-1]
-    use_own = (core ^ h) == far
-    total = refs[4][...] if far else jnp.zeros(out.shape, F32)
-    for piece, cot in enumerate(cots):
-        for half in range(2):
-            lefts = []
-            for m in (2 * half, 2 * half + 1):
-                r = jnp.where(core == 0, m, piece)
-                s = jnp.where(core == 0, piece, m)
-                k = low ^ r
-                lefts.append(jnp.where(use_own, own[k, s], other[k, s]))
-            left = jnp.concatenate(lefts, axis=1)
-            right = cot[pl.ds(256 * half, 256), :]
-            total += jnp.dot(left, right, preferred_element_type=F32)
+    swapped = core != h
+    arrays = max(a for a, _, _, _ in items) + 1
+    out = refs[-1]
+    total = refs[arrays][...] if len(refs) > arrays + 1 else jnp.zeros(out.shape, F32)
+    for a, row, i, j in items:
+        r = jnp.where(core == 0, i, j)
+        s = jnp.where(core == 0, j, i)
+        mine, theirs = own[low ^ r, s], other[low ^ r, s]
+        near = jnp.where(swapped, theirs, mine)
+        far = jnp.where(swapped, mine, theirs)
+        left = jnp.concatenate([near, far], axis=1)
+        right = refs[a][pl.ds(row, left.shape[1]), :]
+        total += jnp.dot(left, right, preferred_element_type=F32)
     out[...] = total
 
 
-def weight_part(far, own, other, cots, *total):
-    rows, width = own.shape[2], cots[0].shape[1]
+def weight_part(items, own, other, arrays, *total):
+    rows, width = own.shape[2], arrays[0].shape[1]
+    depth = 2 * own.shape[3] * len(items)
     return pl.pallas_call(
-        functools.partial(weight_kernel, far),
+        functools.partial(weight_kernel, items),
         out_shape=jax.ShapeDtypeStruct((rows, width), F32),
-        in_specs=[VMEM] * (6 + len(total)),
+        in_specs=[VMEM] * (2 + len(arrays) + len(total)),
         out_specs=VMEM,
         compiler_params=pltpu.CompilerParams(vmem_limit_bytes=16 * MIB),
         cost_estimate=pl.CostEstimate(
-            flops=2 * rows * width * 512 * 4,
-            bytes_accessed=4 * 512 * width * 2,
+            flops=2 * rows * width * depth,
+            bytes_accessed=2 * depth * (width + rows) + 8 * rows * width,
             transcendentals=0,
         ),
-    )(own, other, *cots, *total)
+    )(own, other, *arrays, *total)
 
 
 def step(context, cotangent, out_weight):
@@ -161,14 +161,14 @@
     tokens, width = cotangent.shape
     quarter = width // 4
 
-    def gather(array):
-        first = [array] + [send(array, crosswise(k, True)) for k in (1, 2, 3)]
-        row = jnp.concatenate(first)
-        return [row] + [send(row, crosswise(k, False)) for k in (1, 2, 3)]
-
-    near_cots = gather(cotangent)
+    others = (1, 2, 3)
+
     far_cot = send(cotangent, ring(4))
-    far_cots = gather(far_cot)
+    pair = jnp.concatenate([cotangent, far_cot])
+    first = [send(pair, crosswise(k, True)) for k in others]
+    second = [send(pair, crosswise(k, False)) for k in others]
+    row = jnp.concatenate(first)
+    both = [send(row, crosswise(k, False)) for k in others]
 
     turned = context.T.reshape(4, quarter, tokens)
     block = jnp.stack(
@@ -194,8 +194,11 @@
     from_two_before = send(skip_up, ring(2))
     from_two_after = send(skip_down, ring(-2))
 
-    near_part = weight_part(0, own, other, near_cots)
-    grad_weight = weight_part(1, own, other, far_cots, near_part)
+    deep = 2 * tokens
+    early = [(0, 0, 0, 0)] + [(k, 0, k, 0) for k in others] + [(3 + k, 0, 0, k) for k in others]
+    late = [(k - 1, deep * (i - 1), i, k) for k in others for i in others]
+    early_part = weight_part(early, own, other, [pair] + first + second)
+    grad_weight = weight_part(late, own, other, both, early_part)
     grad_context = pl.pallas_call(
         finish_kernel,
         out_shape=jax.ShapeDtypeStruct((tokens, width), BF16),

time: 103 us -> 118 us (1.15)
  the two profiles are of different devices: /device:TPU:64 before, /device:TPU:80 now
where the time goes in v5:
time: 118 us
  waiting for transfers between devices  73.9 us (63%)
  starting transfers between devices  31.2 us (26%)
  Pallas kernels  6.27 us (5%)
  local copies, waits for them, and re-layouts  5.83 us (5%)
    ppermute x23, waiting for transfers between devices, send(): return lax.ppermute(array, AXES, pairs(route))  73.9 us
    ppermute x23, starting transfers between devices, send(): return lax.ppermute(array, AXES, pairs(route))  31.2 us
    unnamed x7, local copies, waits for them, and re-layouts  4.67 us
    pallas_call x2, Pallas kernels, products(): pl.pallas_call(functools.partial(products_kernel, kept), out_shape=shapes...  3.06 us
    pallas_call x2, Pallas kernels, weight_part(): pl.pallas_call(functools.partial(weight_kernel, items), out_shape=jax.Sha...  2.39 us
  transfers between devices with their start and end apart: 23, of which 9 were waited for; matrix products, arithmetic and copies ran while one was open for 1% of the time, Pallas kernels for 5%

profile of v5, /device:TPU:80, one launch (start us, length us, event | category | flops | bytes accessed | tf_op | source)
XLA Modules:
  0.0 118.1 jit_solution(219942672220679483)
XLA Ops:
  0.6 5.5 %collective-permute-start.8 = (bf16[128,768]{1,0:T(8,128)(2,1)}, bf16[128,768]{1,0:T(8,128)(2,1)S(1)}, u32[]{:S(2)}, u32[]{:S(2)}) collective-permute-start(bf16[128,768]{1,0:T(8,128)(2,1)} %near.3), channel_id=1, source_target_pairs={{0,32},{1,33},{2,34},{3,35},{4,36},{5,37},{6,38},{7,39},{8,40},{9,... | collective-permute-start | bytes 589832 | tf_op jit(solution)/shard_map/ppermute | solution.py:57
  6.1 1.1 copy.5
  7.2 0.5 collective-permute-start.2
  7.8 2.9 %collective-permute-start.1 = (bf16[192,128]{1,0:T(8,128)(2,1)S(1)}, bf16[192,128]{1,0:T(8,128)(2,1)S(1)}, u32[]{:S(2)}, u32[]{:S(2)}) collective-permute-start(bf16[192,128]{1,0:T(8,128)(2,1)S(1)} %get-tuple-element.14), channel_id=1, source_target_pairs={{0,16},{1,17},{2,18},{3,19},{4,20},{5,21},{6,22},{7,23},{8,24},{9,... | collective-permute-start | bytes 147464 | tf_op jit(solution)/shard_map/ppermute | solution.py:57
  10.7 0.7 collective-permute-start
  11.4 4.4 %collective-permute-done.8.far = bf16[128,768]{1,0:T(8,128)(2,1)S(1)} collective-permute-done((bf16[128,768]{1,0:T(8,128)(2,1)}, bf16[128,768]{1,0:T(8,128)(2,1)S(1)}, u32[]{:S(2)}, u32[]{:S(2)}) %collective-permute-start.8) | collective-permute-done | bytes 196640 | tf_op jit(solution)/shard_map/ppermute | solution.py:57
  15.8 3.7 %copy-done = bf16[6144,768]{1,0:T(8,128)(2,1)S(1)} copy-done((bf16[6144,768]{1,0:T(8,128)(2,1)S(1)}, bf16[6144,768]{1,0:T(8,128)(2,1)}, u32[]{:S(2)}) %copy-start) | copy-done | bytes 9437208
  19.5 0.9 copy-done.1
  20.4 1.5 %shard_map.52 = f32[4,768,128]{2,1,0:T(8,128)S(1)} custom-call(bf16[6144,768]{1,0:T(8,128)(2,1)S(1)} %copy-done, bf16[128,768]{1,0:T(8,128)(2,1)S(1)} %copy-done.1, bf16[128,768]{1,0:T(8,128)(2,1)S(1)} %collective-permute-done.8.far), custom_call_target="tpu_custom_call" | custom-call | flops 603979776 | bytes 6291456 | tf_op jit(solution)/shard_map/pallas_call | solution.py:101
  22.0 0.1 collective-permute-start.18
  22.1 1.6 %collective-permute-start.9 = (bf16[256,768]{1,0:T(8,128)(2,1)S(1)}, bf16[256,768]{1,0:T(8,128)(2,1)S(1)}, u32[]{:S(2)}, u32[]{:S(2)}) collective-permute-start(bf16[256,768]{1,0:T(8,128)(2,1)S(1)} %constant_dynamic-update-slice_fusion.refs_0_), channel_id=1, source_target_pairs={{0,64},{1,9},{2,66},{3,11},{4,68},{5,13},{6,70},{7,15},{8,72},{9,1... | collective-permute-start | bytes 1179656 | tf_op jit(solution)/shard_map/ppermute | solution.py:57
  23.7 0.0 collective-permute-done.2
  23.7 0.0 collective-permute-done.1
  23.7 0.0 collective-permute-done
  23.8 4.6 %collective-permute-start.3 = (bf16[4,192,128]{2,1,0:T(8,128)(2,1)S(1)}, bf16[4,192,128]{2,1,0:T(8,128)(2,1)S(1)}, u32[]{:S(2)}, u32[]{:S(2)}) collective-permute-start(bf16[4,192,128]{2,1,0:T(8,128)(2,1)S(1)} %pad_maximum_fusion.1), channel_id=1, source_target_pairs={{0,0},{1,32},{2,66},{3,98},{4,132},{5,164},{6,198},{7,230},{8,8},{... | collective-permute-start | bytes 589832 | tf_op jit(solution)/shard_map/ppermute | solution.py:57
  28.4 0.7 collective-permute-start.11
  29.1 0.4 collective-permute-start.10
  29.5 7.4 %collective-permute-done.3 = bf16[4,192,128]{2,1,0:T(8,128)(2,1)S(1)} collective-permute-done((bf16[4,192,128]{2,1,0:T(8,128)(2,1)S(1)}, bf16[4,192,128]{2,1,0:T(8,128)(2,1)S(1)}, u32[]{:S(2)}, u32[]{:S(2)}) %collective-permute-start.3) | collective-permute-done | bytes 196640 | tf_op jit(solution)/shard_map/ppermute | solution.py:57
  36.9 0.0 collective-permute-start.6
  36.9 0.0 collective-permute-done.9.refs_1_
  36.9 0.5 collective-permute-start.17
  37.4 10.1 %collective-permute-done.6 = bf16[4,192,128]{2,1,0:T(8,128)(2,1)S(1)} collective-permute-done((bf16[4,192,128]{2,1,0:T(8,128)(2,1)S(1)}, bf16[4,192,128]{2,1,0:T(8,128)(2,1)S(1)}, u32[]{:S(2)}, u32[]{:S(2)}) %collective-permute-start.6) | collective-permute-done | bytes 196640 | tf_op jit(solution)/shard_map/ppermute | solution.py:57
  47.5 0.0 collective-permute-start.16
  47.5 1.6 %collective-permute-done.11.refs_3_ = bf16[256,768]{1,0:T(8,128)(2,1)S(1)} collective-permute-done((bf16[256,768]{1,0:T(8,128)(2,1)S(1)}, bf16[256,768]{1,0:T(8,128)(2,1)S(1)}, u32[]{:S(2)}, u32[]{:S(2)}) %collective-permute-start.11) | collective-permute-done | bytes 393248 | tf_op jit(solution)/shard_map/ppermute | solution.py:57
  49.2 0.6 collective-permute-start.4
  49.9 7.2 %collective-permute-done.5 = bf16[4,192,128]{2,1,0:T(8,128)(2,1)S(1)} collective-permute-done((bf16[4,192,128]{2,1,0:T(8,128)(2,1)S(1)}, bf16[4,192,128]{2,1,0:T(8,128)(2,1)S(1)}, u32[]{:S(2)}, u32[]{:S(2)}) %collective-permute-start.5) | collective-permute-done | bytes 196640 | tf_op jit(solution)/shard_map/ppermute | solution.py:57
  57.1 0.5 collective-permute-start.14
  57.6 1.4 %collective-permute-done.4 = bf16[4,192,128]{2,1,0:T(8,128)(2,1)S(1)} collective-permute-done((bf16[4,192,128]{2,1,0:T(8,128)(2,1)S(1)}, bf16[4,192,128]{2,1,0:T(8,128)(2,1)S(1)}, u32[]{:S(2)}, u32[]{:S(2)}) %collective-permute-start.4) | collective-permute-done | bytes 196640 | tf_op jit(solution)/shard_map/ppermute | solution.py:57
  58.9 2.4 %collective-permute-start.13 = (bf16[768,768]{1,0:T(8,128)(2,1)S(1)}, bf16[768,768]{1,0:T(8,128)(2,1)S(1)}, u32[]{:S(2)}, u32[]{:S(2)}) collective-permute-start(bf16[768,768]{1,0:T(8,128)(2,1)S(1)} %constant_dynamic-update-slice_fusion.2), channel_id=1, source_target_pairs={{0,16},{1,129},{2,18},{3,131},{4,20},{5,133},{6,22},{7,135},{8,24}... | collective-permute-start | bytes 3538952 | tf_op jit(solution)/shard_map/ppermute | solution.py:57
  61.3 0.0 collective-permute-done.17.refs_6_
  61.3 0.0 collective-permute-start.12
  61.4 0.1 pad_maximum_fusion.own
  61.5 0.0 collective-permute-done.16.refs_5_
  61.5 0.1 collective-permute-start.7
  61.6 2.3 %collective-permute-start.15 = (bf16[256,768]{1,0:T(8,128)(2,1)S(1)}, bf16[256,768]{1,0:T(8,128)(2,1)S(1)}, u32[]{:S(2)}, u32[]{:S(2)}) collective-permute-start(bf16[256,768]{1,0:T(8,128)(2,1)S(1)} %constant_dynamic-update-slice_fusion.refs_0_), channel_id=1, source_target_pairs={{0,8},{1,65},{2,10},{3,67},{4,12},{5,69},{6,14},{7,71},{8,0},{9,73... | collective-permute-start | bytes 1179656 | tf_op jit(solution)/shard_map/ppermute | solution.py:57
  63.9 1.5 %shard_map.53 = (f32[768,128]{1,0:T(8,128)S(1)}, f32[768,128]{1,0:T(8,128)S(1)}, f32[768,128]{1,0:T(8,128)S(1)}, f32[384,128]{1,0:T(8,128)S(1)}, f32[384,128]{1,0:T(8,128)S(1)}) custom-call(bf16[6144,768]{1,0:T(8,128)(2,1)S(1)} %copy-done, bf16[128,768]{1,0:T(8,128)(2,1)S(1)} %copy-done.1, bf16[128,768]{1,0:T(8,128)(2,1)S(1)} %collective-permute-done.8.far, ...), custom_call_target="tpu_custom_call" | custom-call | flops 603979776 | bytes 6291456 | tf_op jit(solution)/shard_map/pallas_call | solution.py:101
  65.4 26.9 %collective-permute-done.15.refs_4_ = bf16[256,768]{1,0:T(8,128)(2,1)S(1)} collective-permute-done((bf16[256,768]{1,0:T(8,128)(2,1)S(1)}, bf16[256,768]{1,0:T(8,128)(2,1)S(1)}, u32[]{:S(2)}, u32[]{:S(2)}) %collective-permute-start.15) | collective-permute-done | bytes 393248 | tf_op jit(solution)/shard_map/ppermute | solution.py:57
  92.3 2.1 %collective-permute-start.19 = (f32[768,128]{1,0:T(8,128)S(1)}, f32[768,128]{1,0:T(8,128)S(1)}, u32[]{:S(2)}, u32[]{:S(2)}) collective-permute-start(f32[768,128]{1,0:T(8,128)S(1)} %get-tuple-element.8), channel_id=1, source_target_pairs={{0,2},{1,3},{2,4},{3,5},{4,6},{5,7},{6,32},{7,33},{8,10},{9,11},{1... | collective-permute-start | bytes 1179656 | tf_op jit(solution)/shard_map/ppermute | solution.py:57
  94.4 5.6 %collective-permute-start.21 = (f32[384,128]{1,0:T(8,128)S(1)}, f32[384,128]{1,0:T(8,128)S(1)}, u32[]{:S(2)}, u32[]{:S(2)}) collective-permute-start(f32[384,128]{1,0:T(8,128)S(1)} %get-tuple-element.10), channel_id=1, source_target_pairs={{0,4},{1,5},{2,6},{3,7},{4,32},{5,33},{6,34},{7,35},{8,12},{9,13},... | collective-permute-start | bytes 589832 | tf_op jit(solution)/shard_map/ppermute | solution.py:57
  100.0 0.0 collective-permute-done.13.refs_1_
  100.0 0.0 collective-permute-start.22
  100.0 0.7 shard_map.50.refs_3_
  100.7 1.7 %shard_map.51 = f32[192,768]{1,0:T(8,128)} custom-call(bf16[4,4,192,128]{3,2,1,0:T(8,128)(2,1)S(1)} %pad_maximum_fusion.own, bf16[4,4,192,128]{3,2,1,0:T(8,128)(2,1)S(1)} %collective-permute-done.7.other, bf16[768,768]{1,0:T(8,128)(2,1)S(1)} %collective-permute-done.12.refs_0_, bf16[768,768]{1,0:T(8,128)(2,1)S(1)} %collective-permute-done.13.refs_1_, ...), custom_call_target="tpu_custom_call" | custom-call | flops 679477248 | bytes 5603328 | tf_op jit(solution)/shard_map/pallas_call | solution.py:145
  102.4 8.0 %collective-permute-done.21.two_before = f32[384,128]{1,0:T(8,128)S(1)} collective-permute-done((f32[384,128]{1,0:T(8,128)S(1)}, f32[384,128]{1,0:T(8,128)S(1)}, u32[]{:S(2)}, u32[]{:S(2)}) %collective-permute-start.21) | collective-permute-done | bytes 196640 | tf_op jit(solution)/shard_map/ppermute | solution.py:57
  110.4 6.8 %collective-permute-done.22.two_after = f32[384,128]{1,0:T(8,128)S(1)} collective-permute-done((f32[384,128]{1,0:T(8,128)S(1)}, f32[384,128]{1,0:T(8,128)S(1)}, u32[]{:S(2)}, u32[]{:S(2)}) %collective-permute-start.22) | collective-permute-done | bytes 196640 | tf_op jit(solution)/shard_map/ppermute | solution.py:57
  117.2 0.0 collective-permute-done.19.before
  117.2 0.0 collective-permute-done.20.after
  117.3 0.8 shard_map.54
  (16 shorter events, 0.2 us)
Async XLA Ops:
  0.6 15.2 %collective-permute-start.8 = (bf16[128,768]{1,0:T(8,128)(2,1)}, bf16[128,768]{1,0:T(8,128)(2,1)S(1)}, u32[]{:S(2)}, u32[]{:S(2)}) collective-permute-start(bf16[128,768]{1,0:T(8,128)(2,1)} %near.3), channel_id=1, source_target_pairs={{0,32},{1,33},{2,34},{3,35},{4,36},{5,37},{6,38},{7,39},{8,40},{9,... | collective-permute-start | bytes 589832 | tf_op jit(solution)/shard_map/ppermute | solution.py:57
  7.2 16.5 %collective-permute-start.2 = (bf16[192,128]{1,0:T(8,128)(2,1)S(1)}, bf16[192,128]{1,0:T(8,128)(2,1)S(1)}, u32[]{:S(2)}, u32[]{:S(2)}) collective-permute-start(bf16[192,128]{1,0:T(8,128)(2,1)S(1)} %get-tuple-element.13), channel_id=1, source_target_pairs={{0,24},{1,25},{2,26},{3,27},{4,28},{5,29},{6,30},{7,31},{8,16},{9,... | collective-permute-start | bytes 147464 | tf_op jit(solution)/shard_map/ppermute | solution.py:57
  7.8 15.9 %collective-permute-start.1 = (bf16[192,128]{1,0:T(8,128)(2,1)S(1)}, bf16[192,128]{1,0:T(8,128)(2,1)S(1)}, u32[]{:S(2)}, u32[]{:S(2)}) collective-permute-start(bf16[192,128]{1,0:T(8,128)(2,1)S(1)} %get-tuple-element.14), channel_id=1, source_target_pairs={{0,16},{1,17},{2,18},{3,19},{4,20},{5,21},{6,22},{7,23},{8,24},{9,... | collective-permute-start | bytes 147464 | tf_op jit(solution)/shard_map/ppermute | solution.py:57
  10.7 13.0 %collective-permute-start = (bf16[192,128]{1,0:T(8,128)(2,1)S(1)}, bf16[192,128]{1,0:T(8,128)(2,1)S(1)}, u32[]{:S(2)}, u32[]{:S(2)}) collective-permute-start(bf16[192,128]{1,0:T(8,128)(2,1)S(1)} %get-tuple-element.15), channel_id=1, source_target_pairs={{0,8},{1,9},{2,10},{3,11},{4,12},{5,13},{6,14},{7,15},{8,0},{9,1},... | collective-permute-start | bytes 147464 | tf_op jit(solution)/shard_map/ppermute | solution.py:57
  15.8 3.7 %copy-start = (bf16[6144,768]{1,0:T(8,128)(2,1)S(1)}, bf16[6144,768]{1,0:T(8,128)(2,1)}, u32[]{:S(2)}) copy-start(bf16[6144,768]{1,0:T(8,128)(2,1)} %weight.3) | copy-start | bytes 28311556
  19.5 0.9 copy-start.1
  22.0 39.6 %collective-permute-start.18 = (f32[4,768,128]{2,1,0:T(8,128)S(1)}, f32[4,768,128]{2,1,0:T(8,128)S(1)}, u32[]{:S(2)}, u32[]{:S(2)}) collective-permute-start(f32[4,768,128]{2,1,0:T(8,128)S(1)} %shard_map.52), channel_id=1, source_target_pairs={{0,1},{1,0},{2,3},{3,2},{4,5},{5,4},{6,7},{7,6},{8,9},{9,8},{10,11... | collective-permute-start | bytes 4718600 | tf_op jit(solution)/shard_map/ppermute | solution.py:57
  22.1 14.8 %collective-permute-start.9 = (bf16[256,768]{1,0:T(8,128)(2,1)S(1)}, bf16[256,768]{1,0:T(8,128)(2,1)S(1)}, u32[]{:S(2)}, u32[]{:S(2)}) collective-permute-start(bf16[256,768]{1,0:T(8,128)(2,1)S(1)} %constant_dynamic-update-slice_fusion.refs_0_), channel_id=1, source_target_pairs={{0,64},{1,9},{2,66},{3,11},{4,68},{5,13},{6,70},{7,15},{8,72},{9,1... | collective-permute-start | bytes 1179656 | tf_op jit(solution)/shard_map/ppermute | solution.py:57
  23.8 13.2 %collective-permute-start.3 = (bf16[4,192,128]{2,1,0:T(8,128)(2,1)S(1)}, bf16[4,192,128]{2,1,0:T(8,128)(2,1)S(1)}, u32[]{:S(2)}, u32[]{:S(2)}) collective-permute-start(bf16[4,192,128]{2,1,0:T(8,128)(2,1)S(1)} %pad_maximum_fusion.1), channel_id=1, source_target_pairs={{0,0},{1,32},{2,66},{3,98},{4,132},{5,164},{6,198},{7,230},{8,8},{... | collective-permute-start | bytes 589832 | tf_op jit(solution)/shard_map/ppermute | solution.py:57
  28.4 20.8 %collective-permute-start.11 = (bf16[256,768]{1,0:T(8,128)(2,1)S(1)}, bf16[256,768]{1,0:T(8,128)(2,1)S(1)}, u32[]{:S(2)}, u32[]{:S(2)}) collective-permute-start(bf16[256,768]{1,0:T(8,128)(2,1)S(1)} %constant_dynamic-update-slice_fusion.refs_0_), channel_id=1, source_target_pairs={{0,192},{1,25},{2,194},{3,27},{4,196},{5,29},{6,198},{7,31},{8,200... | collective-permute-start | bytes 1179656 | tf_op jit(solution)/shard_map/ppermute | solution.py:57
  29.1 20.0 %collective-permute-start.10 = (bf16[256,768]{1,0:T(8,128)(2,1)S(1)}, bf16[256,768]{1,0:T(8,128)(2,1)S(1)}, u32[]{:S(2)}, u32[]{:S(2)}) collective-permute-start(bf16[256,768]{1,0:T(8,128)(2,1)S(1)} %constant_dynamic-update-slice_fusion.refs_0_), channel_id=1, source_target_pairs={{0,128},{1,17},{2,130},{3,19},{4,132},{5,21},{6,134},{7,23},{8,136... | collective-permute-start | bytes 1179656 | tf_op jit(solution)/shard_map/ppermute | solution.py:57
  36.9 10.6 %collective-permute-start.6 = (bf16[4,192,128]{2,1,0:T(8,128)(2,1)S(1)}, bf16[4,192,128]{2,1,0:T(8,128)(2,1)S(1)}, u32[]{:S(2)}, u32[]{:S(2)}) collective-permute-start(bf16[4,192,128]{2,1,0:T(8,128)(2,1)S(1)} %collective-permute-done.3), channel_id=1, source_target_pairs={{0,6},{1,7},{2,4},{3,5},{4,2},{5,3},{6,0},{7,1},{8,14},{9,15},{10,... | collective-permute-start | bytes 589832 | tf_op jit(solution)/shard_map/ppermute | solution.py:57
  36.9 24.4 %collective-permute-start.17 = (bf16[256,768]{1,0:T(8,128)(2,1)S(1)}, bf16[256,768]{1,0:T(8,128)(2,1)S(1)}, u32[]{:S(2)}, u32[]{:S(2)}) collective-permute-start(bf16[256,768]{1,0:T(8,128)(2,1)S(1)} %constant_dynamic-update-slice_fusion.refs_0_), channel_id=1, source_target_pairs={{0,24},{1,193},{2,26},{3,195},{4,28},{5,197},{6,30},{7,199},{8,16}... | collective-permute-start | bytes 1179656 | tf_op jit(solution)/shard_map/ppermute | solution.py:57
  47.5 13.9 %collective-permute-start.16 = (bf16[256,768]{1,0:T(8,128)(2,1)S(1)}, bf16[256,768]{1,0:T(8,128)(2,1)S(1)}, u32[]{:S(2)}, u32[]{:S(2)}) collective-permute-start(bf16[256,768]{1,0:T(8,128)(2,1)S(1)} %constant_dynamic-update-slice_fusion.refs_0_), channel_id=1, source_target_pairs={{0,16},{1,129},{2,18},{3,131},{4,20},{5,133},{6,22},{7,135},{8,24}... | collective-permute-start | bytes 1179656 | tf_op jit(solution)/shard_map/ppermute | solution.py:57
  49.2 7.9 %collective-permute-start.5 = (bf16[4,192,128]{2,1,0:T(8,128)(2,1)S(1)}, bf16[4,192,128]{2,1,0:T(8,128)(2,1)S(1)}, u32[]{:S(2)}, u32[]{:S(2)}) collective-permute-start(bf16[4,192,128]{2,1,0:T(8,128)(2,1)S(1)} %collective-permute-done.3), channel_id=1, source_target_pairs={{0,4},{1,5},{2,6},{3,7},{4,0},{5,1},{6,2},{7,3},{8,12},{9,13},{10,... | collective-permute-start | bytes 589832 | tf_op jit(solution)/shard_map/ppermute | solution.py:57
  49.2 9.8 %collective-permute-start.4 = (bf16[4,192,128]{2,1,0:T(8,128)(2,1)S(1)}, bf16[4,192,128]{2,1,0:T(8,128)(2,1)S(1)}, u32[]{:S(2)}, u32[]{:S(2)}) collective-permute-start(bf16[4,192,128]{2,1,0:T(8,128)(2,1)S(1)} %collective-permute-done.3), channel_id=1, source_target_pairs={{0,2},{1,3},{2,0},{3,1},{4,6},{5,7},{6,4},{7,5},{8,10},{9,11},{10,... | collective-permute-start | bytes 589832 | tf_op jit(solution)/shard_map/ppermute | solution.py:57
  57.1 37.3 %collective-permute-start.14 = (bf16[768,768]{1,0:T(8,128)(2,1)S(1)}, bf16[768,768]{1,0:T(8,128)(2,1)S(1)}, u32[]{:S(2)}, u32[]{:S(2)}) collective-permute-start(bf16[768,768]{1,0:T(8,128)(2,1)S(1)} %constant_dynamic-update-slice_fusion.2), channel_id=1, source_target_pairs={{0,24},{1,193},{2,26},{3,195},{4,28},{5,197},{6,30},{7,199},{8,16}... | collective-permute-start | bytes 3538952 | tf_op jit(solution)/shard_map/ppermute | solution.py:57
  58.9 41.1 %collective-permute-start.13 = (bf16[768,768]{1,0:T(8,128)(2,1)S(1)}, bf16[768,768]{1,0:T(8,128)(2,1)S(1)}, u32[]{:S(2)}, u32[]{:S(2)}) collective-permute-start(bf16[768,768]{1,0:T(8,128)(2,1)S(1)} %constant_dynamic-update-slice_fusion.2), channel_id=1, source_target_pairs={{0,16},{1,129},{2,18},{3,131},{4,20},{5,133},{6,22},{7,135},{8,24}... | collective-permute-start | bytes 3538952 | tf_op jit(solution)/shard_map/ppermute | solution.py:57
  61.3 39.4 %collective-permute-start.12 = (bf16[768,768]{1,0:T(8,128)(2,1)S(1)}, bf16[768,768]{1,0:T(8,128)(2,1)S(1)}, u32[]{:S(2)}, u32[]{:S(2)}) collective-permute-start(bf16[768,768]{1,0:T(8,128)(2,1)S(1)} %constant_dynamic-update-slice_fusion.2), channel_id=1, source_target_pairs={{0,8},{1,65},{2,10},{3,67},{4,12},{5,69},{6,14},{7,71},{8,0},{9,73... | collective-permute-start | bytes 3538952 | tf_op jit(solution)/shard_map/ppermute | solution.py:57
  61.5 32.9 %collective-permute-start.7 = (bf16[4,4,192,128]{3,2,1,0:T(8,128)(2,1)S(1)}, bf16[4,4,192,128]{3,2,1,0:T(8,128)(2,1)S(1)}, u32[]{:S(2)}, u32[]{:S(2)}) collective-permute-start(bf16[4,4,192,128]{3,2,1,0:T(8,128)(2,1)S(1)} %pad_maximum_fusion.own), channel_id=1, source_target_pairs={{0,1},{1,0},{2,3},{3,2},{4,5},{5,4},{6,7},{7,6},{8,9},{9,8},{10,11... | collective-permute-start | bytes 2359304 | tf_op jit(solution)/shard_map/ppermute | solution.py:57
  61.6 30.7 %collective-permute-start.15 = (bf16[256,768]{1,0:T(8,128)(2,1)S(1)}, bf16[256,768]{1,0:T(8,128)(2,1)S(1)}, u32[]{:S(2)}, u32[]{:S(2)}) collective-permute-start(bf16[256,768]{1,0:T(8,128)(2,1)S(1)} %constant_dynamic-update-slice_fusion.refs_0_), channel_id=1, source_target_pairs={{0,8},{1,65},{2,10},{3,67},{4,12},{5,69},{6,14},{7,71},{8,0},{9,73... | collective-permute-start | bytes 1179656 | tf_op jit(solution)/shard_map/ppermute | solution.py:57
  92.3 25.0 %collective-permute-start.19 = (f32[768,128]{1,0:T(8,128)S(1)}, f32[768,128]{1,0:T(8,128)S(1)}, u32[]{:S(2)}, u32[]{:S(2)}) collective-permute-start(f32[768,128]{1,0:T(8,128)S(1)} %get-tuple-element.8), channel_id=1, source_target_pairs={{0,2},{1,3},{2,4},{3,5},{4,6},{5,7},{6,32},{7,33},{8,10},{9,11},{1... | collective-permute-start | bytes 1179656 | tf_op jit(solution)/shard_map/ppermute | solution.py:57
  94.4 22.9 %collective-permute-start.20 = (f32[768,128]{1,0:T(8,128)S(1)}, f32[768,128]{1,0:T(8,128)S(1)}, u32[]{:S(2)}, u32[]{:S(2)}) collective-permute-start(f32[768,128]{1,0:T(8,128)S(1)} %get-tuple-element.9), channel_id=1, source_target_pairs={{0,38},{1,39},{2,0},{3,1},{4,2},{5,3},{6,4},{7,5},{8,46},{9,47},{1... | collective-permute-start | bytes 1179656 | tf_op jit(solution)/shard_map/ppermute | solution.py:57
  94.4 16.1 %collective-permute-start.21 = (f32[384,128]{1,0:T(8,128)S(1)}, f32[384,128]{1,0:T(8,128)S(1)}, u32[]{:S(2)}, u32[]{:S(2)}) collective-permute-start(f32[384,128]{1,0:T(8,128)S(1)} %get-tuple-element.10), channel_id=1, source_target_pairs={{0,4},{1,5},{2,6},{3,7},{4,32},{5,33},{6,34},{7,35},{8,12},{9,13},... | collective-permute-start | bytes 589832 | tf_op jit(solution)/shard_map/ppermute | solution.py:57
  100.0 17.2 %collective-permute-start.22 = (f32[384,128]{1,0:T(8,128)S(1)}, f32[384,128]{1,0:T(8,128)S(1)}, u32[]{:S(2)}, u32[]{:S(2)}) collective-permute-start(f32[384,128]{1,0:T(8,128)S(1)} %get-tuple-element.11), channel_id=1, source_target_pairs={{0,36},{1,37},{2,38},{3,39},{4,0},{5,1},{6,2},{7,3},{8,44},{9,45},... | collective-permute-start | bytes 589832 | tf_op jit(solution)/shard_map/ppermute | solution.py:57

commit v6 on v5

--- a/solution.py
+++ b/solution.py
@@ -55,10 +55,6 @@
 
 def send(array, route):
     return lax.ppermute(array, AXES, pairs(route))
-
-
-def at(stack, index):
-    return lax.dynamic_index_in_dim(stack, index, 0, keepdims=False)
 
 
 def products_kernel(kept, weight, near, far, *refs):
@@ -124,17 +120,21 @@
 def weight_kernel(items, own, other, *refs):
     h, low, core = here()
     swapped = core != h
-    arrays = max(a for a, _, _, _ in items) + 1
+    y = lax.axis_index("seq")
+    arrays = 1 + max(max(item[0], item[2]) for item in items)
+    tokens = own.shape[3]
     out = refs[-1]
     total = refs[arrays][...] if len(refs) > arrays + 1 else jnp.zeros(out.shape, F32)
-    for a, row, i, j in items:
-        r = jnp.where(core == 0, i, j)
-        s = jnp.where(core == 0, j, i)
-        mine, theirs = own[low ^ r, s], other[low ^ r, s]
+    for a, row, b, far_row, i, j in items:
+        k = low ^ jnp.where(core == 0, i, j)
+        s = y ^ jnp.where(core == 0, j, i)
+        mine, theirs = own[k, s], other[k, s]
         near = jnp.where(swapped, theirs, mine)
         far = jnp.where(swapped, mine, theirs)
         left = jnp.concatenate([near, far], axis=1)
-        right = refs[a][pl.ds(row, left.shape[1]), :]
+        right = jnp.concatenate(
+            [refs[a][pl.ds(row, tokens), :], refs[b][pl.ds(far_row, tokens), :]]
+        )
         total += jnp.dot(left, right, preferred_element_type=F32)
     out[...] = total
 
@@ -157,7 +157,6 @@
 
 
 def step(context, cotangent, out_weight):
-    y = lax.axis_index("seq")
     tokens, width = cotangent.shape
     quarter = width // 4
 
@@ -166,18 +165,12 @@
     far_cot = send(cotangent, ring(4))
     pair = jnp.concatenate([cotangent, far_cot])
     first = [send(pair, crosswise(k, True)) for k in others]
-    second = [send(pair, crosswise(k, False)) for k in others]
-    row = jnp.concatenate(first)
+    second = [send(cotangent, crosswise(k, False)) for k in others]
+    row = jnp.concatenate([*first, far_cot])
     both = [send(row, crosswise(k, False)) for k in others]
 
     turned = context.T.reshape(4, quarter, tokens)
-    block = jnp.stack(
-        [at(turned, y)]
-        + [
-            send(at(turned, y ^ k), lambda x, h, y, l, c, k=k: (x, h, y ^ k, l, c))
-            for k in (1, 2, 3)
-        ]
-    )
+    block = lax.all_to_all(turned, "seq", split_axis=0, concat_axis=0, tiled=True)
     mine = send(block, lambda x, h, y, l, c: (l, c, y, l ^ x, h))
     gathered = [mine] + [
         send(mine, lambda x, h, y, l, c, k=k: (x, h, y, l ^ k, c)) for k in (1, 2, 3)
@@ -194,11 +187,14 @@
     from_two_before = send(skip_up, ring(2))
     from_two_after = send(skip_down, ring(-2))
 
-    deep = 2 * tokens
-    early = [(0, 0, 0, 0)] + [(k, 0, k, 0) for k in others] + [(3 + k, 0, 0, k) for k in others]
-    late = [(k - 1, deep * (i - 1), i, k) for k in others for i in others]
-    early_part = weight_part(early, own, other, [pair] + first + second)
-    grad_weight = weight_part(late, own, other, both, early_part)
+    early = [(k, 0, k, tokens, k, 0) for k in range(4)]
+    late = [(2 + k, 0, k - 1, 6 * tokens, 0, k) for k in others] + [
+        (k - 1, 2 * tokens * (i - 1), k - 1, 2 * tokens * (i - 1) + tokens, i, k)
+        for k in others
+        for i in others
+    ]
+    early_part = weight_part(early, own, other, [pair] + first)
+    grad_weight = weight_part(late, own, other, both + second, early_part)
     grad_context = pl.pallas_call(
         finish_kernel,
         out_shape=jax.ShapeDtypeStruct((tokens, width), BF16),

time: 118 us -> 118 us (level)
  the two profiles are of different devices: /device:TPU:80 before, /device:TPU:1 now
where the time goes in v6:
time: 118 us
  starting transfers between devices  56.1 us (48%)
  waiting for transfers between devices  48.2 us (41%)
  local copies, waits for them, and re-layouts  6.51 us (6%)
  Pallas kernels  6.26 us (5%)
    ppermute x20, starting transfers between devices, send(): return lax.ppermute(array, AXES, pairs(route))  52.2 us
    ppermute x20, waiting for transfers between devices, send(): return lax.ppermute(array, AXES, pairs(route))  46 us
    unnamed x8, local copies, waits for them, and re-layouts  4.74 us
    all_to_all x1, starting transfers between devices, step(): lax.all_to_all(turned, 'seq', split_axis=0, concat_axis=0, tiled=True)  3.89 us
    pallas_call x2, Pallas kernels, products(): pl.pallas_call(functools.partial(products_kernel, kept), out_shape=shapes...  3.06 us
    pallas_call x2, Pallas kernels, weight_part(): pl.pallas_call(functools.partial(weight_kernel, items), out_shape=jax.Sha...  2.38 us
  transfers between devices with their start and end apart: 21, of which 8 were waited for; matrix products, arithmetic and copies ran while one was open for 2% of the time, Pallas kernels for 5%

profile of v6, /device:TPU:1, one launch (start us, length us, event | category | flops | bytes accessed | tf_op | source)
XLA Modules:
  0.0 117.9 jit_solution(13034387107613410280)
XLA Ops:
  0.6 7.8 %collective-permute-start.5 = (bf16[128,768]{1,0:T(8,128)(2,1)}, bf16[128,768]{1,0:T(8,128)(2,1)S(1)}, u32[]{:S(2)}, u32[]{:S(2)}) collective-permute-start(bf16[128,768]{1,0:T(8,128)(2,1)} %near.3), channel_id=1, source_target_pairs={{0,32},{1,33},{2,34},{3,35},{4,36},{5,37},{6,38},{7,39},{8,40},{9,... | collective-permute-start | bytes 589832 | tf_op jit(solution)/shard_map/ppermute | solution.py:57
  8.5 1.0 constant_dynamic-update-slice_fusion.1
  9.4 3.4 %collective-permute-done.5.far = bf16[128,768]{1,0:T(8,128)(2,1)S(1)} collective-permute-done((bf16[128,768]{1,0:T(8,128)(2,1)}, bf16[128,768]{1,0:T(8,128)(2,1)S(1)}, u32[]{:S(2)}, u32[]{:S(2)}) %collective-permute-start.5) | collective-permute-done | bytes 196640 | tf_op jit(solution)/shard_map/ppermute | solution.py:57
  12.8 1.8 %collective-permute-start.6 = (bf16[256,768]{1,0:T(8,128)(2,1)S(1)}, bf16[256,768]{1,0:T(8,128)(2,1)S(1)}, u32[]{:S(2)}, u32[]{:S(2)}) collective-permute-start(bf16[256,768]{1,0:T(8,128)(2,1)S(1)} %constant_dynamic-update-slice_fusion.refs_0_), channel_id=1, source_target_pairs={{0,64},{1,9},{2,66},{3,11},{4,68},{5,13},{6,70},{7,15},{8,72},{9,1... | collective-permute-start | bytes 1179656 | tf_op jit(solution)/shard_map/ppermute | solution.py:57
  14.7 1.7 %copy.5 = bf16[768,128]{1,0:T(8,128)(2,1)} copy(bf16[768,128]{0,1:T(8,128)(2,1)} %bitcast.10) | data formatting | bytes 393216 | tf_op jit(solution)/shard_map/transpose | solution.py:172
  16.4 3.9 %all-to-all-start = ((bf16[4,192,128]{2,1,0:T(8,128)(2,1)}), bf16[4,192,128]{2,1,0:T(8,128)(2,1)S(1)}, u32[]{:S(2)}, u32[]{:S(2)}) async-start(bf16[4,192,128]{2,1,0:T(8,128)(2,1)} %bitcast.1), calls=%async_computation | async-start | bytes 393216 | tf_op jit(solution)/shard_map/all_to_all | solution.py:173
  20.3 3.0 %collective-permute-start.7 = (bf16[256,768]{1,0:T(8,128)(2,1)S(1)}, bf16[256,768]{1,0:T(8,128)(2,1)S(1)}, u32[]{:S(2)}, u32[]{:S(2)}) collective-permute-start(bf16[256,768]{1,0:T(8,128)(2,1)S(1)} %constant_dynamic-update-slice_fusion.refs_0_), channel_id=1, source_target_pairs={{0,128},{1,17},{2,130},{3,19},{4,132},{5,21},{6,134},{7,23},{8,136... | collective-permute-start | bytes 1179656 | tf_op jit(solution)/shard_map/ppermute | solution.py:57
  23.3 2.2 %all-to-all-done = bf16[4,192,128]{2,1,0:T(8,128)(2,1)S(1)} async-done(((bf16[4,192,128]{2,1,0:T(8,128)(2,1)}), bf16[4,192,128]{2,1,0:T(8,128)(2,1)S(1)}, u32[]{:S(2)}, u32[]{:S(2)}) %all-to-all-start) | async-done | bytes 196640 | tf_op jit(solution)/shard_map/all_to_all | solution.py:173
  25.5 14.1 %collective-permute-start = (bf16[4,192,128]{2,1,0:T(8,128)(2,1)S(1)}, bf16[4,192,128]{2,1,0:T(8,128)(2,1)S(1)}, u32[]{:S(2)}, u32[]{:S(2)}) collective-permute-start(bf16[4,192,128]{2,1,0:T(8,128)(2,1)S(1)} %all-to-all-done), channel_id=1, source_target_pairs={{0,0},{1,32},{2,66},{3,98},{4,132},{5,164},{6,198},{7,230},{8,8},{... | collective-permute-start | bytes 589832 | tf_op jit(solution)/shard_map/ppermute | solution.py:57
  39.6 0.7 collective-permute-start.8
  40.3 3.7 %copy-done = bf16[6144,768]{1,0:T(8,128)(2,1)S(1)} copy-done((bf16[6144,768]{1,0:T(8,128)(2,1)S(1)}, bf16[6144,768]{1,0:T(8,128)(2,1)}, u32[]{:S(2)}) %copy-start) | copy-done | bytes 9437208
  44.0 1.5 %shard_map.52 = f32[4,768,128]{2,1,0:T(8,128)S(1)} custom-call(bf16[6144,768]{1,0:T(8,128)(2,1)S(1)} %copy-done, bf16[128,768]{1,0:T(8,128)(2,1)S(1)} %copy-done.1, bf16[128,768]{1,0:T(8,128)(2,1)S(1)} %collective-permute-done.5.far), custom_call_target="tpu_custom_call" | custom-call | flops 603979776 | bytes 6291456 | tf_op jit(solution)/shard_map/pallas_call | solution.py:97
  45.5 0.1 collective-permute-start.15
  45.6 0.0 collective-permute-done
  45.6 2.6 %collective-permute-start.12 = (bf16[128,768]{1,0:T(8,128)(2,1)S(1)}, bf16[128,768]{1,0:T(8,128)(2,1)S(1)}, u32[]{:S(2)}, u32[]{:S(2)}) collective-permute-start(bf16[128,768]{1,0:T(8,128)(2,1)S(1)} %copy-done.1), channel_id=1, source_target_pairs={{0,8},{1,65},{2,10},{3,67},{4,12},{5,69},{6,14},{7,71},{8,0},{9,73... | collective-permute-start | bytes 589832 | tf_op jit(solution)/shard_map/ppermute | solution.py:57
  48.2 0.0 collective-permute-done.6.refs_1_
  48.2 0.1 collective-permute-start.1
  48.3 0.0 collective-permute-done.7.refs_2_
  48.3 2.8 %collective-permute-start.2 = (bf16[4,192,128]{2,1,0:T(8,128)(2,1)S(1)}, bf16[4,192,128]{2,1,0:T(8,128)(2,1)S(1)}, u32[]{:S(2)}, u32[]{:S(2)}) collective-permute-start(bf16[4,192,128]{2,1,0:T(8,128)(2,1)S(1)} %collective-permute-done), channel_id=1, source_target_pairs={{0,4},{1,5},{2,6},{3,7},{4,0},{5,1},{6,2},{7,3},{8,12},{9,13},{10,... | collective-permute-start | bytes 589832 | tf_op jit(solution)/shard_map/ppermute | solution.py:57
  51.1 0.0 collective-permute-done.8.refs_3_
  51.2 0.9 collective-permute-start.10
  52.2 0.0 collective-permute-done.12.refs_3_
  52.2 1.9 %collective-permute-start.3 = (bf16[4,192,128]{2,1,0:T(8,128)(2,1)S(1)}, bf16[4,192,128]{2,1,0:T(8,128)(2,1)S(1)}, u32[]{:S(2)}, u32[]{:S(2)}) collective-permute-start(bf16[4,192,128]{2,1,0:T(8,128)(2,1)S(1)} %collective-permute-done), channel_id=1, source_target_pairs={{0,6},{1,7},{2,4},{3,5},{4,2},{5,3},{6,0},{7,1},{8,14},{9,15},{10,... | collective-permute-start | bytes 589832 | tf_op jit(solution)/shard_map/ppermute | solution.py:57
  54.0 1.6 %collective-permute-done.1 = bf16[4,192,128]{2,1,0:T(8,128)(2,1)S(1)} collective-permute-done((bf16[4,192,128]{2,1,0:T(8,128)(2,1)S(1)}, bf16[4,192,128]{2,1,0:T(8,128)(2,1)S(1)}, u32[]{:S(2)}, u32[]{:S(2)}) %collective-permute-start.1) | collective-permute-done | bytes 196640 | tf_op jit(solution)/shard_map/ppermute | solution.py:57
  55.7 0.5 collective-permute-start.11
  56.1 0.0 collective-permute-done.2
  56.1 1.2 %collective-permute-start.9 = (bf16[896,768]{1,0:T(8,128)(2,1)S(1)}, bf16[896,768]{1,0:T(8,128)(2,1)S(1)}, u32[]{:S(2)}, u32[]{:S(2)}) collective-permute-start(bf16[896,768]{1,0:T(8,128)(2,1)S(1)} %constant_dynamic-update-slice_fusion.2), channel_id=1, source_target_pairs={{0,8},{1,65},{2,10},{3,67},{4,12},{5,69},{6,14},{7,71},{8,0},{9,73... | collective-permute-start | bytes 4128776 | tf_op jit(solution)/shard_map/ppermute | solution.py:57
  57.3 4.9 %collective-permute-done.3 = bf16[4,192,128]{2,1,0:T(8,128)(2,1)S(1)} collective-permute-done((bf16[4,192,128]{2,1,0:T(8,128)(2,1)S(1)}, bf16[4,192,128]{2,1,0:T(8,128)(2,1)S(1)}, u32[]{:S(2)}, u32[]{:S(2)}) %collective-permute-start.3) | collective-permute-done | bytes 196640 | tf_op jit(solution)/shard_map/ppermute | solution.py:57
  62.3 4.0 %collective-permute-start.13 = (bf16[128,768]{1,0:T(8,128)(2,1)S(1)}, bf16[128,768]{1,0:T(8,128)(2,1)S(1)}, u32[]{:S(2)}, u32[]{:S(2)}) collective-permute-start(bf16[128,768]{1,0:T(8,128)(2,1)S(1)} %copy-done.1), channel_id=1, source_target_pairs={{0,16},{1,129},{2,18},{3,131},{4,20},{5,133},{6,22},{7,135},{8,24}... | collective-permute-start | bytes 589832 | tf_op jit(solution)/shard_map/ppermute | solution.py:57
  66.3 0.1 pad_maximum_fusion.own
  66.4 20.5 %collective-permute-done.13.refs_4_ = bf16[128,768]{1,0:T(8,128)(2,1)S(1)} collective-permute-done((bf16[128,768]{1,0:T(8,128)(2,1)S(1)}, bf16[128,768]{1,0:T(8,128)(2,1)S(1)}, u32[]{:S(2)}, u32[]{:S(2)}) %collective-permute-start.13) | collective-permute-done | bytes 196640 | tf_op jit(solution)/shard_map/ppermute | solution.py:57
  86.9 4.5 %collective-permute-start.4 = (bf16[4,4,192,128]{3,2,1,0:T(8,128)(2,1)S(1)}, bf16[4,4,192,128]{3,2,1,0:T(8,128)(2,1)S(1)}, u32[]{:S(2)}, u32[]{:S(2)}) collective-permute-start(bf16[4,4,192,128]{3,2,1,0:T(8,128)(2,1)S(1)} %pad_maximum_fusion.own), channel_id=1, source_target_pairs={{0,1},{1,0},{2,3},{3,2},{4,5},{5,4},{6,7},{7,6},{8,9},{9,8},{10,11... | collective-permute-start | bytes 2359304 | tf_op jit(solution)/shard_map/ppermute | solution.py:57
  91.4 0.0 collective-permute-done.15.refs_0_
  91.4 0.0 collective-permute-start.14
  91.4 1.5 %shard_map.53 = (f32[768,128]{1,0:T(8,128)S(1)}, f32[768,128]{1,0:T(8,128)S(1)}, f32[768,128]{1,0:T(8,128)S(1)}, f32[384,128]{1,0:T(8,128)S(1)}, f32[384,128]{1,0:T(8,128)S(1)}) custom-call(bf16[6144,768]{1,0:T(8,128)(2,1)S(1)} %copy-done, bf16[128,768]{1,0:T(8,128)(2,1)S(1)} %copy-done.1, bf16[128,768]{1,0:T(8,128)(2,1)S(1)} %collective-permute-done.5.far, ...), custom_call_target="tpu_custom_call" | custom-call | flops 603979776 | bytes 6291456 | tf_op jit(solution)/shard_map/pallas_call | solution.py:97
  92.9 4.5 %collective-permute-done.14.refs_5_ = bf16[128,768]{1,0:T(8,128)(2,1)S(1)} collective-permute-done((bf16[128,768]{1,0:T(8,128)(2,1)S(1)}, bf16[128,768]{1,0:T(8,128)(2,1)S(1)}, u32[]{:S(2)}, u32[]{:S(2)}) %collective-permute-start.14) | collective-permute-done | bytes 196640 | tf_op jit(solution)/shard_map/ppermute | solution.py:57
  97.4 1.7 %collective-permute-start.16 = (f32[768,128]{1,0:T(8,128)S(1)}, f32[768,128]{1,0:T(8,128)S(1)}, u32[]{:S(2)}, u32[]{:S(2)}) collective-permute-start(f32[768,128]{1,0:T(8,128)S(1)} %get-tuple-element.8), channel_id=1, source_target_pairs={{0,2},{1,3},{2,4},{3,5},{4,6},{5,7},{6,32},{7,33},{8,10},{9,11},{1... | collective-permute-start | bytes 1179656 | tf_op jit(solution)/shard_map/ppermute | solution.py:57
  99.2 0.9 collective-permute-start.17
  100.1 0.0 collective-permute-done.10.refs_1_
  100.1 0.3 collective-permute-start.18
  100.3 3.3 %collective-permute-start.19 = (f32[384,128]{1,0:T(8,128)S(1)}, f32[384,128]{1,0:T(8,128)S(1)}, u32[]{:S(2)}, u32[]{:S(2)}) collective-permute-start(f32[384,128]{1,0:T(8,128)S(1)} %get-tuple-element.11), channel_id=1, source_target_pairs={{0,36},{1,37},{2,38},{3,39},{4,0},{5,1},{6,2},{7,3},{8,44},{9,45},... | collective-permute-start | bytes 589832 | tf_op jit(solution)/shard_map/ppermute | solution.py:57
  103.7 0.5 shard_map.50.refs_6_
  104.2 1.9 %shard_map.51 = f32[192,768]{1,0:T(8,128)} custom-call(bf16[4,4,192,128]{3,2,1,0:T(8,128)(2,1)S(1)} %pad_maximum_fusion.own, bf16[4,4,192,128]{3,2,1,0:T(8,128)(2,1)S(1)} %collective-permute-done.4.other, bf16[896,768]{1,0:T(8,128)(2,1)S(1)} %collective-permute-done.9.refs_0_, bf16[896,768]{1,0:T(8,128)(2,1)S(1)} %collective-permute-done.10.refs_1_, ...), custom_call_target="tpu_custom_call" | custom-call | flops 905969664 | bytes 7077888 | tf_op jit(solution)/shard_map/pallas_call | solution.py:145
  106.1 6.1 %collective-permute-done.18.two_before = f32[384,128]{1,0:T(8,128)S(1)} collective-permute-done((f32[384,128]{1,0:T(8,128)S(1)}, f32[384,128]{1,0:T(8,128)S(1)}, u32[]{:S(2)}, u32[]{:S(2)}) %collective-permute-start.18) | collective-permute-done | bytes 196640 | tf_op jit(solution)/shard_map/ppermute | solution.py:57
  112.2 4.9 %collective-permute-done.19.two_after = f32[384,128]{1,0:T(8,128)S(1)} collective-permute-done((f32[384,128]{1,0:T(8,128)S(1)}, f32[384,128]{1,0:T(8,128)S(1)}, u32[]{:S(2)}, u32[]{:S(2)}) %collective-permute-start.19) | collective-permute-done | bytes 196640 | tf_op jit(solution)/shard_map/ppermute | solution.py:57
  117.1 0.0 collective-permute-done.16.before
  117.1 0.0 collective-permute-done.17.after
  117.1 0.8 shard_map.54
  (11 shorter events, 0.1 us)
Async XLA Ops:
  0.6 39.7 %copy-start.1 = (bf16[128,768]{1,0:T(8,128)(2,1)S(1)}, bf16[128,768]{1,0:T(8,128)(2,1)}, u32[]{:S(2)}) copy-start(bf16[128,768]{1,0:T(8,128)(2,1)} %near.3) | copy-start | bytes 589828
  0.6 12.2 %collective-permute-start.5 = (bf16[128,768]{1,0:T(8,128)(2,1)}, bf16[128,768]{1,0:T(8,128)(2,1)S(1)}, u32[]{:S(2)}, u32[]{:S(2)}) collective-permute-start(bf16[128,768]{1,0:T(8,128)(2,1)} %near.3), channel_id=1, source_target_pairs={{0,32},{1,33},{2,34},{3,35},{4,36},{5,37},{6,38},{7,39},{8,40},{9,... | collective-permute-start | bytes 589832 | tf_op jit(solution)/shard_map/ppermute | solution.py:57
  12.8 35.4 %collective-permute-start.6 = (bf16[256,768]{1,0:T(8,128)(2,1)S(1)}, bf16[256,768]{1,0:T(8,128)(2,1)S(1)}, u32[]{:S(2)}, u32[]{:S(2)}) collective-permute-start(bf16[256,768]{1,0:T(8,128)(2,1)S(1)} %constant_dynamic-update-slice_fusion.refs_0_), channel_id=1, source_target_pairs={{0,64},{1,9},{2,66},{3,11},{4,68},{5,13},{6,70},{7,15},{8,72},{9,1... | collective-permute-start | bytes 1179656 | tf_op jit(solution)/shard_map/ppermute | solution.py:57
  16.4 9.1 %all-to-all-start = ((bf16[4,192,128]{2,1,0:T(8,128)(2,1)}), bf16[4,192,128]{2,1,0:T(8,128)(2,1)S(1)}, u32[]{:S(2)}, u32[]{:S(2)}) async-start(bf16[4,192,128]{2,1,0:T(8,128)(2,1)} %bitcast.1), calls=%async_computation | async-start | bytes 393216 | tf_op jit(solution)/shard_map/all_to_all | solution.py:173
  20.3 28.0 %collective-permute-start.7 = (bf16[256,768]{1,0:T(8,128)(2,1)S(1)}, bf16[256,768]{1,0:T(8,128)(2,1)S(1)}, u32[]{:S(2)}, u32[]{:S(2)}) collective-permute-start(bf16[256,768]{1,0:T(8,128)(2,1)S(1)} %constant_dynamic-update-slice_fusion.refs_0_), channel_id=1, source_target_pairs={{0,128},{1,17},{2,130},{3,19},{4,132},{5,21},{6,134},{7,23},{8,136... | collective-permute-start | bytes 1179656 | tf_op jit(solution)/shard_map/ppermute | solution.py:57
  25.5 20.1 %collective-permute-start = (bf16[4,192,128]{2,1,0:T(8,128)(2,1)S(1)}, bf16[4,192,128]{2,1,0:T(8,128)(2,1)S(1)}, u32[]{:S(2)}, u32[]{:S(2)}) collective-permute-start(bf16[4,192,128]{2,1,0:T(8,128)(2,1)S(1)} %all-to-all-done), channel_id=1, source_target_pairs={{0,0},{1,32},{2,66},{3,98},{4,132},{5,164},{6,198},{7,230},{8,8},{... | collective-permute-start | bytes 589832 | tf_op jit(solution)/shard_map/ppermute | solution.py:57
  39.6 11.6 %collective-permute-start.8 = (bf16[256,768]{1,0:T(8,128)(2,1)S(1)}, bf16[256,768]{1,0:T(8,128)(2,1)S(1)}, u32[]{:S(2)}, u32[]{:S(2)}) collective-permute-start(bf16[256,768]{1,0:T(8,128)(2,1)S(1)} %constant_dynamic-update-slice_fusion.refs_0_), channel_id=1, source_target_pairs={{0,192},{1,25},{2,194},{3,27},{4,196},{5,29},{6,198},{7,31},{8,200... | collective-permute-start | bytes 1179656 | tf_op jit(solution)/shard_map/ppermute | solution.py:57
  40.3 3.7 %copy-start = (bf16[6144,768]{1,0:T(8,128)(2,1)S(1)}, bf16[6144,768]{1,0:T(8,128)(2,1)}, u32[]{:S(2)}) copy-start(bf16[6144,768]{1,0:T(8,128)(2,1)} %weight.3) | copy-start | bytes 28311556
  45.5 45.9 %collective-permute-start.15 = (f32[4,768,128]{2,1,0:T(8,128)S(1)}, f32[4,768,128]{2,1,0:T(8,128)S(1)}, u32[]{:S(2)}, u32[]{:S(2)}) collective-permute-start(f32[4,768,128]{2,1,0:T(8,128)S(1)} %shard_map.52), channel_id=1, source_target_pairs={{0,1},{1,0},{2,3},{3,2},{4,5},{5,4},{6,7},{7,6},{8,9},{9,8},{10,11... | collective-permute-start | bytes 4718600 | tf_op jit(solution)/shard_map/ppermute | solution.py:57
  45.6 6.5 %collective-permute-start.12 = (bf16[128,768]{1,0:T(8,128)(2,1)S(1)}, bf16[128,768]{1,0:T(8,128)(2,1)S(1)}, u32[]{:S(2)}, u32[]{:S(2)}) collective-permute-start(bf16[128,768]{1,0:T(8,128)(2,1)S(1)} %copy-done.1), channel_id=1, source_target_pairs={{0,8},{1,65},{2,10},{3,67},{4,12},{5,69},{6,14},{7,71},{8,0},{9,73... | collective-permute-start | bytes 589832 | tf_op jit(solution)/shard_map/ppermute | solution.py:57
  48.2 7.5 %collective-permute-start.1 = (bf16[4,192,128]{2,1,0:T(8,128)(2,1)S(1)}, bf16[4,192,128]{2,1,0:T(8,128)(2,1)S(1)}, u32[]{:S(2)}, u32[]{:S(2)}) collective-permute-start(bf16[4,192,128]{2,1,0:T(8,128)(2,1)S(1)} %collective-permute-done), channel_id=1, source_target_pairs={{0,2},{1,3},{2,0},{3,1},{4,6},{5,7},{6,4},{7,5},{8,10},{9,11},{10,... | collective-permute-start | bytes 589832 | tf_op jit(solution)/shard_map/ppermute | solution.py:57
  48.3 7.8 %collective-permute-start.2 = (bf16[4,192,128]{2,1,0:T(8,128)(2,1)S(1)}, bf16[4,192,128]{2,1,0:T(8,128)(2,1)S(1)}, u32[]{:S(2)}, u32[]{:S(2)}) collective-permute-start(bf16[4,192,128]{2,1,0:T(8,128)(2,1)S(1)} %collective-permute-done), channel_id=1, source_target_pairs={{0,4},{1,5},{2,6},{3,7},{4,0},{5,1},{6,2},{7,3},{8,12},{9,13},{10,... | collective-permute-start | bytes 589832 | tf_op jit(solution)/shard_map/ppermute | solution.py:57
  51.2 48.9 %collective-permute-start.10 = (bf16[896,768]{1,0:T(8,128)(2,1)S(1)}, bf16[896,768]{1,0:T(8,128)(2,1)S(1)}, u32[]{:S(2)}, u32[]{:S(2)}) collective-permute-start(bf16[896,768]{1,0:T(8,128)(2,1)S(1)} %constant_dynamic-update-slice_fusion.2), channel_id=1, source_target_pairs={{0,16},{1,129},{2,18},{3,131},{4,20},{5,133},{6,22},{7,135},{8,24}... | collective-permute-start | bytes 4128776 | tf_op jit(solution)/shard_map/ppermute | solution.py:57
  52.2 10.1 %collective-permute-start.3 = (bf16[4,192,128]{2,1,0:T(8,128)(2,1)S(1)}, bf16[4,192,128]{2,1,0:T(8,128)(2,1)S(1)}, u32[]{:S(2)}, u32[]{:S(2)}) collective-permute-start(bf16[4,192,128]{2,1,0:T(8,128)(2,1)S(1)} %collective-permute-done), channel_id=1, source_target_pairs={{0,6},{1,7},{2,4},{3,5},{4,2},{5,3},{6,0},{7,1},{8,14},{9,15},{10,... | collective-permute-start | bytes 589832 | tf_op jit(solution)/shard_map/ppermute | solution.py:57
  55.7 44.7 %collective-permute-start.11 = (bf16[896,768]{1,0:T(8,128)(2,1)S(1)}, bf16[896,768]{1,0:T(8,128)(2,1)S(1)}, u32[]{:S(2)}, u32[]{:S(2)}) collective-permute-start(bf16[896,768]{1,0:T(8,128)(2,1)S(1)} %constant_dynamic-update-slice_fusion.2), channel_id=1, source_target_pairs={{0,24},{1,193},{2,26},{3,195},{4,28},{5,197},{6,30},{7,199},{8,16}... | collective-permute-start | bytes 4128776 | tf_op jit(solution)/shard_map/ppermute | solution.py:57
  56.1 48.0 %collective-permute-start.9 = (bf16[896,768]{1,0:T(8,128)(2,1)S(1)}, bf16[896,768]{1,0:T(8,128)(2,1)S(1)}, u32[]{:S(2)}, u32[]{:S(2)}) collective-permute-start(bf16[896,768]{1,0:T(8,128)(2,1)S(1)} %constant_dynamic-update-slice_fusion.2), channel_id=1, source_target_pairs={{0,8},{1,65},{2,10},{3,67},{4,12},{5,69},{6,14},{7,71},{8,0},{9,73... | collective-permute-start | bytes 4128776 | tf_op jit(solution)/shard_map/ppermute | solution.py:57
  62.3 24.6 %collective-permute-start.13 = (bf16[128,768]{1,0:T(8,128)(2,1)S(1)}, bf16[128,768]{1,0:T(8,128)(2,1)S(1)}, u32[]{:S(2)}, u32[]{:S(2)}) collective-permute-start(bf16[128,768]{1,0:T(8,128)(2,1)S(1)} %copy-done.1), channel_id=1, source_target_pairs={{0,16},{1,129},{2,18},{3,131},{4,20},{5,133},{6,22},{7,135},{8,24}... | collective-permute-start | bytes 589832 | tf_op jit(solution)/shard_map/ppermute | solution.py:57
  86.9 12.3 %collective-permute-start.4 = (bf16[4,4,192,128]{3,2,1,0:T(8,128)(2,1)S(1)}, bf16[4,4,192,128]{3,2,1,0:T(8,128)(2,1)S(1)}, u32[]{:S(2)}, u32[]{:S(2)}) collective-permute-start(bf16[4,4,192,128]{3,2,1,0:T(8,128)(2,1)S(1)} %pad_maximum_fusion.own), channel_id=1, source_target_pairs={{0,1},{1,0},{2,3},{3,2},{4,5},{5,4},{6,7},{7,6},{8,9},{9,8},{10,11... | collective-permute-start | bytes 2359304 | tf_op jit(solution)/shard_map/ppermute | solution.py:57
  91.4 6.0 %collective-permute-start.14 = (bf16[128,768]{1,0:T(8,128)(2,1)S(1)}, bf16[128,768]{1,0:T(8,128)(2,1)S(1)}, u32[]{:S(2)}, u32[]{:S(2)}) collective-permute-start(bf16[128,768]{1,0:T(8,128)(2,1)S(1)} %copy-done.1), channel_id=1, source_target_pairs={{0,24},{1,193},{2,26},{3,195},{4,28},{5,197},{6,30},{7,199},{8,16}... | collective-permute-start | bytes 589832 | tf_op jit(solution)/shard_map/ppermute | solution.py:57
  97.4 19.7 %collective-permute-start.16 = (f32[768,128]{1,0:T(8,128)S(1)}, f32[768,128]{1,0:T(8,128)S(1)}, u32[]{:S(2)}, u32[]{:S(2)}) collective-permute-start(f32[768,128]{1,0:T(8,128)S(1)} %get-tuple-element.8), channel_id=1, source_target_pairs={{0,2},{1,3},{2,4},{3,5},{4,6},{5,7},{6,32},{7,33},{8,10},{9,11},{1... | collective-permute-start | bytes 1179656 | tf_op jit(solution)/shard_map/ppermute | solution.py:57
  99.2 18.0 %collective-permute-start.17 = (f32[768,128]{1,0:T(8,128)S(1)}, f32[768,128]{1,0:T(8,128)S(1)}, u32[]{:S(2)}, u32[]{:S(2)}) collective-permute-start(f32[768,128]{1,0:T(8,128)S(1)} %get-tuple-element.9), channel_id=1, source_target_pairs={{0,38},{1,39},{2,0},{3,1},{4,2},{5,3},{6,4},{7,5},{8,46},{9,47},{1... | collective-permute-start | bytes 1179656 | tf_op jit(solution)/shard_map/ppermute | solution.py:57
  100.1 12.1 %collective-permute-start.18 = (f32[384,128]{1,0:T(8,128)S(1)}, f32[384,128]{1,0:T(8,128)S(1)}, u32[]{:S(2)}, u32[]{:S(2)}) collective-permute-start(f32[384,128]{1,0:T(8,128)S(1)} %get-tuple-element.10), channel_id=1, source_target_pairs={{0,4},{1,5},{2,6},{3,7},{4,32},{5,33},{6,34},{7,35},{8,12},{9,13},... | collective-permute-start | bytes 589832 | tf_op jit(solution)/shard_map/ppermute | solution.py:57
  100.3 16.8 %collective-permute-start.19 = (f32[384,128]{1,0:T(8,128)S(1)}, f32[384,128]{1,0:T(8,128)S(1)}, u32[]{:S(2)}, u32[]{:S(2)}) collective-permute-start(f32[384,128]{1,0:T(8,128)S(1)} %get-tuple-element.11), channel_id=1, source_target_pairs={{0,36},{1,37},{2,38},{3,39},{4,0},{5,1},{6,2},{7,3},{8,44},{9,45},... | collective-permute-start | bytes 589832 | tf_op jit(solution)/shard_map/ppermute | solution.py:57

commit v7 on v6

--- a/solution.py
+++ b/solution.py
@@ -109,6 +109,12 @@
     )(weight, near, far, *taken)
 
 
+def pair_kernel(near, far, out):
+    tokens = near.shape[0]
+    out[pl.ds(0, tokens), :] = near[...]
+    out[pl.ds(tokens, tokens), :] = far[...]
+
+
 def finish_kernel(home, before, after, two_before, two_after, out):
     rows = two_before.shape[0]
     for i, skip in enumerate((two_before, two_after)):
@@ -163,11 +169,22 @@
     others = (1, 2, 3)
 
     far_cot = send(cotangent, ring(4))
-    pair = jnp.concatenate([cotangent, far_cot])
+    pair = pl.pallas_call(
+        pair_kernel,
+        out_shape=jax.ShapeDtypeStruct((2 * tokens, width), BF16),
+        in_specs=[VMEM] * 2,
+        out_specs=VMEM,
+        compiler_params=pltpu.CompilerParams(vmem_limit_bytes=4 * MIB),
+        cost_estimate=pl.CostEstimate(
+            flops=0, bytes_accessed=8 * tokens * width, transcendentals=0
+        ),
+    )(cotangent, far_cot)
     first = [send(pair, crosswise(k, True)) for k in others]
     second = [send(cotangent, crosswise(k, False)) for k in others]
     row = jnp.concatenate([*first, far_cot])
-    both = [send(row, crosswise(k, False)) for k in others]
+    one, three = (send(row, crosswise(k, False)) for k in (1, 3))
+    cut = 4 * tokens
+    two = [send(three[:cut], crosswise(1, False)), send(one[cut:], crosswise(3, False))]
 
     turned = context.T.reshape(4, quarter, tokens)
     block = lax.all_to_all(turned, "seq", split_axis=0, concat_axis=0, tiled=True)
@@ -188,13 +205,22 @@
     from_two_after = send(skip_down, ring(-2))
 
     early = [(k, 0, k, tokens, k, 0) for k in range(4)]
-    late = [(2 + k, 0, k - 1, 6 * tokens, 0, k) for k in others] + [
-        (k - 1, 2 * tokens * (i - 1), k - 1, 2 * tokens * (i - 1) + tokens, i, k)
-        for k in others
-        for i in others
-    ]
-    early_part = weight_part(early, own, other, [pair] + first)
-    grad_weight = weight_part(late, own, other, both + second, early_part)
+    both = [one, three, second[0], second[2]]
+    late = [
+        (2 + a, 0, a, 6 * tokens, 0, k) if i == 0 else (a, at_row, a, at_row + tokens, i, k)
+        for a, k in ((0, 1), (1, 3))
+        for i in range(4)
+        for at_row in (2 * tokens * (i - 1),)
+    ]
+    last = [
+        (0, 0, 0, tokens, 1, 2),
+        (0, 2 * tokens, 0, 3 * tokens, 2, 2),
+        (1, 0, 1, tokens, 3, 2),
+        (2, 0, 1, 2 * tokens, 0, 2),
+    ]
+    total = weight_part(early, own, other, [pair] + first)
+    total = weight_part(late, own, other, both, total)
+    grad_weight = weight_part(last, own, other, two + [second[1]], total)
     grad_context = pl.pallas_call(
         finish_kernel,
         out_shape=jax.ShapeDtypeStruct((tokens, width), BF16),

time: 118 us -> 135 us (1.14)
  the two profiles are of different devices: /device:TPU:1 before, /device:TPU:24 now
where the time goes in v7:
time: 135 us; the launch traced here: 134 us
  starting transfers between devices  61.9 us (46%)
  waiting for transfers between devices  49.1 us (36%)
  local copies, waits for them, and re-layouts  13.3 us (10%)
  Pallas kernels  9.06 us (7%)
    ppermute x21, starting transfers between devices, send(): return lax.ppermute(array, AXES, pairs(route))  54.9 us
    ppermute x21, waiting for transfers between devices, send(): return lax.ppermute(array, AXES, pairs(route))  36 us
    all_to_all x1, waiting for transfers between devices, step(): lax.all_to_all(turned, 'seq', split_axis=0, concat_axis=0, tiled=True)  13.1 us
    unnamed x27, local copies, waits for them, and re-layouts  11.6 us
    all_to_all x1, starting transfers between devices, step(): lax.all_to_all(turned, 'seq', split_axis=0, concat_axis=0, tiled=True)  6.97 us
    pallas_call x2, Pallas kernels, products(): pl.pallas_call(functools.partial(products_kernel, kept), out_shape=shapes...  5.66 us
  transfers between devices with their start and end apart: 22, of which 8 were waited for; matrix products, arithmetic and copies ran while one was open for 3% of the time, Pallas kernels for 6%

profile of v7, /device:TPU:24, one launch (start us, length us, event | category | flops | bytes accessed | tf_op | source)
XLA Modules:
  0.0 134.2 jit_solution(5984027536396617381)
XLA Ops:
  0.6 7.3 %collective-permute-start.5 = (bf16[128,768]{1,0:T(8,128)(2,1)}, bf16[128,768]{1,0:T(8,128)(2,1)S(1)}, u32[]{:S(2)}, u32[]{:S(2)}) collective-permute-start(bf16[128,768]{1,0:T(8,128)(2,1)} %near.5), channel_id=1, source_target_pairs={{0,32},{1,33},{2,34},{3,35},{4,36},{5,37},{6,38},{7,39},{8,40},{9,... | collective-permute-start | bytes 589832 | tf_op jit(solution)/shard_map/ppermute | solution.py:57
  7.9 5.2 %collective-permute-done.5.far = bf16[128,768]{1,0:T(8,128)(2,1)S(1)} collective-permute-done((bf16[128,768]{1,0:T(8,128)(2,1)}, bf16[128,768]{1,0:T(8,128)(2,1)S(1)}, u32[]{:S(2)}, u32[]{:S(2)}) %collective-permute-start.5) | collective-permute-done | bytes 196640 | tf_op jit(solution)/shard_map/ppermute | solution.py:57
  13.1 0.9 copy-done.2
  14.1 1.6 %collective-permute-start.6 = (bf16[256,768]{1,0:T(8,128)(2,1)S(1)}, bf16[256,768]{1,0:T(8,128)(2,1)S(1)}, u32[]{:S(2)}, u32[]{:S(2)}) collective-permute-start(bf16[256,768]{1,0:T(8,128)(2,1)S(1)} %shard_map.50.refs_0_), channel_id=1, source_target_pairs={{0,64},{1,9},{2,66},{3,11},{4,68},{5,13},{6,70},{7,15},{8,72},{9,1... | collective-permute-start | bytes 1179656 | tf_op jit(solution)/shard_map/ppermute | solution.py:57
  15.7 2.7 %collective-permute-start.7 = (bf16[256,768]{1,0:T(8,128)(2,1)S(1)}, bf16[256,768]{1,0:T(8,128)(2,1)S(1)}, u32[]{:S(2)}, u32[]{:S(2)}) collective-permute-start(bf16[256,768]{1,0:T(8,128)(2,1)S(1)} %shard_map.50.refs_0_), channel_id=1, source_target_pairs={{0,128},{1,17},{2,130},{3,19},{4,132},{5,21},{6,134},{7,23},{8,136... | collective-permute-start | bytes 1179656 | tf_op jit(solution)/shard_map/ppermute | solution.py:57
  18.4 0.5 collective-permute-start.8
  18.9 3.7 %copy-done = bf16[6144,768]{1,0:T(8,128)(2,1)S(1)} copy-done((bf16[6144,768]{1,0:T(8,128)(2,1)S(1)}, bf16[6144,768]{1,0:T(8,128)(2,1)}, u32[]{:S(2)}) %copy-start) | copy-done | bytes 9437208
  22.5 0.9 copy-done.3
  23.5 2.7 %shard_map.54 = f32[4,768,128]{2,1,0:T(8,128)} custom-call(bf16[6144,768]{1,0:T(8,128)(2,1)S(1)} %copy-done, bf16[128,768]{1,0:T(8,128)(2,1)S(1)} %copy-done.3, bf16[128,768]{1,0:T(8,128)(2,1)S(1)} %collective-permute-done.5.far), custom_call_target="tpu_custom_call" | custom-call | flops 603979776 | bytes 6291456 | tf_op jit(solution)/shard_map/pallas_call | solution.py:97
  26.2 0.0 collective-permute-start.16
  26.2 0.0 collective-permute-done.6.refs_1_
  26.2 0.0 copy-start.5
  26.2 0.8 constant_dynamic-update-slice_fusion.3
  27.0 1.5 %collective-permute-done.7.refs_2_ = bf16[256,768]{1,0:T(8,128)(2,1)S(1)} collective-permute-done((bf16[256,768]{1,0:T(8,128)(2,1)S(1)}, bf16[256,768]{1,0:T(8,128)(2,1)S(1)}, u32[]{:S(2)}, u32[]{:S(2)}) %collective-permute-start.7) | collective-permute-done | bytes 393248 | tf_op jit(solution)/shard_map/ppermute | solution.py:57
  28.5 0.8 constant_dynamic-update-slice_fusion.2
  29.3 2.3 %collective-permute-done.8.refs_3_ = bf16[256,768]{1,0:T(8,128)(2,1)S(1)} collective-permute-done((bf16[256,768]{1,0:T(8,128)(2,1)S(1)}, bf16[256,768]{1,0:T(8,128)(2,1)S(1)}, u32[]{:S(2)}, u32[]{:S(2)}) %collective-permute-start.8) | collective-permute-done | bytes 393248 | tf_op jit(solution)/shard_map/ppermute | solution.py:57
  31.6 0.8 constant_dynamic-update-slice_fusion.1
  32.4 0.7 constant_dynamic-update-slice_fusion
  33.1 0.2 collective-permute-start.9
  33.3 0.8 copy.5
  34.1 7.0 %all-to-all-start = ((bf16[4,192,128]{2,1,0:T(8,128)(2,1)}), bf16[4,192,128]{2,1,0:T(8,128)(2,1)}, u32[]{:S(2)}, u32[]{:S(2)}) async-start(bf16[4,192,128]{2,1,0:T(8,128)(2,1)} %bitcast.1), calls=%async_computation | async-start | bytes 393216 | tf_op jit(solution)/shard_map/all_to_all | solution.py:190
  41.1 0.9 collective-permute-start.11
  42.0 13.1 %all-to-all-done = bf16[4,192,128]{2,1,0:T(8,128)(2,1)} async-done(((bf16[4,192,128]{2,1,0:T(8,128)(2,1)}), bf16[4,192,128]{2,1,0:T(8,128)(2,1)}, u32[]{:S(2)}, u32[]{:S(2)}) %all-to-all-start) | async-done | bytes 196640 | tf_op jit(solution)/shard_map/all_to_all | solution.py:190
  55.0 1.6 %collective-permute-start = (bf16[4,192,128]{2,1,0:T(8,128)(2,1)}, bf16[4,192,128]{2,1,0:T(8,128)(2,1)S(1)}, u32[]{:S(2)}, u32[]{:S(2)}) collective-permute-start(bf16[4,192,128]{2,1,0:T(8,128)(2,1)} %all-to-all-done), channel_id=1, source_target_pairs={{0,0},{1,32},{2,66},{3,98},{4,132},{5,164},{6,198},{7,230},{8,8},{... | collective-permute-start | bytes 589832 | tf_op jit(solution)/shard_map/ppermute | solution.py:57
  56.6 14.0 %collective-permute-start.1 = (bf16[4,192,128]{2,1,0:T(8,128)(2,1)S(1)}, bf16[4,192,128]{2,1,0:T(8,128)(2,1)S(1)}, u32[]{:S(2)}, u32[]{:S(2)}) collective-permute-start(bf16[4,192,128]{2,1,0:T(8,128)(2,1)S(1)} %collective-permute-done), channel_id=1, source_target_pairs={{0,2},{1,3},{2,0},{3,1},{4,6},{5,7},{6,4},{7,5},{8,10},{9,11},{10,... | collective-permute-start | bytes 589832 | tf_op jit(solution)/shard_map/ppermute | solution.py:57
  70.6 3.8 %collective-permute-start.2 = (bf16[4,192,128]{2,1,0:T(8,128)(2,1)S(1)}, bf16[4,192,128]{2,1,0:T(8,128)(2,1)S(1)}, u32[]{:S(2)}, u32[]{:S(2)}) collective-permute-start(bf16[4,192,128]{2,1,0:T(8,128)(2,1)S(1)} %collective-permute-done), channel_id=1, source_target_pairs={{0,4},{1,5},{2,6},{3,7},{4,0},{5,1},{6,2},{7,3},{8,12},{9,13},{10,... | collective-permute-start | bytes 589832 | tf_op jit(solution)/shard_map/ppermute | solution.py:57
  74.4 7.2 %collective-permute-start.3 = (bf16[4,192,128]{2,1,0:T(8,128)(2,1)S(1)}, bf16[4,192,128]{2,1,0:T(8,128)(2,1)S(1)}, u32[]{:S(2)}, u32[]{:S(2)}) collective-permute-start(bf16[4,192,128]{2,1,0:T(8,128)(2,1)S(1)} %collective-permute-done), channel_id=1, source_target_pairs={{0,6},{1,7},{2,4},{3,5},{4,2},{5,3},{6,0},{7,1},{8,14},{9,15},{10,... | collective-permute-start | bytes 589832 | tf_op jit(solution)/shard_map/ppermute | solution.py:57
  81.6 6.3 %collective-permute-done.2 = bf16[4,192,128]{2,1,0:T(8,128)(2,1)S(1)} collective-permute-done((bf16[4,192,128]{2,1,0:T(8,128)(2,1)S(1)}, bf16[4,192,128]{2,1,0:T(8,128)(2,1)S(1)}, u32[]{:S(2)}, u32[]{:S(2)}) %collective-permute-start.2) | collective-permute-done | bytes 196640 | tf_op jit(solution)/shard_map/ppermute | solution.py:57
  88.0 0.1 pad_maximum_fusion.own
  88.1 1.3 collective-permute-start.4
  89.4 0.1 slice.8
  89.5 2.1 %collective-permute-start.10 = (bf16[512,768]{1,0:T(8,128)(2,1)S(1)}, bf16[512,768]{1,0:T(8,128)(2,1)S(1)}, u32[]{:S(2)}, u32[]{:S(2)}) collective-permute-start(bf16[512,768]{1,0:T(8,128)(2,1)S(1)} %slice.8), channel_id=1, source_target_pairs={{0,8},{1,65},{2,10},{3,67},{4,12},{5,69},{6,14},{7,71},{8,0},{9,73... | collective-permute-start | bytes 2359304 | tf_op jit(solution)/shard_map/ppermute | solution.py:57
  91.6 0.2 collective-permute-start.15
  91.8 3.7 %copy-done.1 = bf16[6144,768]{1,0:T(8,128)(2,1)S(1)} copy-done((bf16[6144,768]{1,0:T(8,128)(2,1)S(1)}, bf16[6144,768]{1,0:T(8,128)(2,1)}, u32[]{:S(2)}) %copy-start.1) | copy-done | bytes 9437208
  95.4 2.9 %shard_map.55 = (f32[768,128]{1,0:T(8,128)S(1)}, f32[768,128]{1,0:T(8,128)S(1)}, f32[768,128]{1,0:T(8,128)S(1)}, f32[384,128]{1,0:T(8,128)S(1)}, f32[384,128]{1,0:T(8,128)S(1)}) custom-call(bf16[6144,768]{1,0:T(8,128)(2,1)S(1)} %copy-done.1, bf16[128,768]{1,0:T(8,128)(2,1)S(1)} %copy-done.4, bf16[128,768]{1,0:T(8,128)(2,1)S(1)} %collective-permute-done.5.far, ...), custom_call_target="tpu_custom_call" | custom-call | flops 603979776 | bytes 6291456 | tf_op jit(solution)/shard_map/pallas_call | solution.py:97
  98.4 0.0 copy-start.6
  98.4 5.1 %collective-permute-start.19 = (f32[384,128]{1,0:T(8,128)S(1)}, f32[384,128]{1,0:T(8,128)S(1)}, u32[]{:S(2)}, u32[]{:S(2)}) collective-permute-start(f32[384,128]{1,0:T(8,128)S(1)} %get-tuple-element.10), channel_id=1, source_target_pairs={{0,4},{1,5},{2,6},{3,7},{4,32},{5,33},{6,34},{7,35},{8,12},{9,13},... | collective-permute-start | bytes 589832 | tf_op jit(solution)/shard_map/ppermute | solution.py:57
  103.6 3.1 %collective-permute-start.12 = (bf16[384,768]{1,0:T(8,128)(2,1)S(1)}, bf16[384,768]{1,0:T(8,128)(2,1)S(1)}, u32[]{:S(2)}, u32[]{:S(2)}) collective-permute-start(bf16[384,768]{1,0:T(8,128)(2,1)S(1)} %slice.9), channel_id=1, source_target_pairs={{0,24},{1,193},{2,26},{3,195},{4,28},{5,197},{6,30},{7,199},{8,16}... | collective-permute-start | bytes 1769480 | tf_op jit(solution)/shard_map/ppermute | solution.py:57
  106.8 0.0 collective-permute-start.17
  106.8 3.2 %collective-permute-start.18 = (f32[768,128]{1,0:T(8,128)S(1)}, f32[768,128]{1,0:T(8,128)S(1)}, u32[]{:S(2)}, u32[]{:S(2)}) collective-permute-start(f32[768,128]{1,0:T(8,128)S(1)} %get-tuple-element.9), channel_id=1, source_target_pairs={{0,38},{1,39},{2,0},{3,1},{4,2},{5,3},{6,4},{7,5},{8,46},{9,47},{1... | collective-permute-start | bytes 1179656 | tf_op jit(solution)/shard_map/ppermute | solution.py:57
  110.0 2.0 %collective-permute-done.19.two_before = f32[384,128]{1,0:T(8,128)S(1)} collective-permute-done((f32[384,128]{1,0:T(8,128)S(1)}, f32[384,128]{1,0:T(8,128)S(1)}, u32[]{:S(2)}, u32[]{:S(2)}) %collective-permute-start.19) | collective-permute-done | bytes 196640 | tf_op jit(solution)/shard_map/ppermute | solution.py:57
  112.0 13.7 %collective-permute-done.20.two_after = f32[384,128]{1,0:T(8,128)S(1)} collective-permute-done((f32[384,128]{1,0:T(8,128)S(1)}, f32[384,128]{1,0:T(8,128)S(1)}, u32[]{:S(2)}, u32[]{:S(2)}) %collective-permute-start.20) | collective-permute-done | bytes 196640 | tf_op jit(solution)/shard_map/ppermute | solution.py:57
  125.7 0.0 collective-permute-start.13
  125.7 0.5 shard_map.51.refs_4_
  126.2 0.8 shard_map.52.refs_3_
  127.0 0.8 shard_map.56
  127.9 5.0 %collective-permute-done.13.refs_2_ = bf16[128,768]{1,0:T(8,128)(2,1)S(1)} collective-permute-done((bf16[128,768]{1,0:T(8,128)(2,1)S(1)}, bf16[128,768]{1,0:T(8,128)(2,1)S(1)}, u32[]{:S(2)}, u32[]{:S(2)}) %collective-permute-start.13) | collective-permute-done | bytes 196640 | tf_op jit(solution)/shard_map/ppermute | solution.py:57
  132.9 1.3 shard_map.53
  (35 shorter events, 0.1 us)
Async XLA Ops:
  0.6 12.5 %collective-permute-start.5 = (bf16[128,768]{1,0:T(8,128)(2,1)}, bf16[128,768]{1,0:T(8,128)(2,1)S(1)}, u32[]{:S(2)}, u32[]{:S(2)}) collective-permute-start(bf16[128,768]{1,0:T(8,128)(2,1)} %near.5), channel_id=1, source_target_pairs={{0,32},{1,33},{2,34},{3,35},{4,36},{5,37},{6,38},{7,39},{8,40},{9,... | collective-permute-start | bytes 589832 | tf_op jit(solution)/shard_map/ppermute | solution.py:57
  13.1 0.9 copy-start.2
  14.1 12.1 %collective-permute-start.6 = (bf16[256,768]{1,0:T(8,128)(2,1)S(1)}, bf16[256,768]{1,0:T(8,128)(2,1)S(1)}, u32[]{:S(2)}, u32[]{:S(2)}) collective-permute-start(bf16[256,768]{1,0:T(8,128)(2,1)S(1)} %shard_map.50.refs_0_), channel_id=1, source_target_pairs={{0,64},{1,9},{2,66},{3,11},{4,68},{5,13},{6,70},{7,15},{8,72},{9,1... | collective-permute-start | bytes 1179656 | tf_op jit(solution)/shard_map/ppermute | solution.py:57
  15.7 12.8 %collective-permute-start.7 = (bf16[256,768]{1,0:T(8,128)(2,1)S(1)}, bf16[256,768]{1,0:T(8,128)(2,1)S(1)}, u32[]{:S(2)}, u32[]{:S(2)}) collective-permute-start(bf16[256,768]{1,0:T(8,128)(2,1)S(1)} %shard_map.50.refs_0_), channel_id=1, source_target_pairs={{0,128},{1,17},{2,130},{3,19},{4,132},{5,21},{6,134},{7,23},{8,136... | collective-permute-start | bytes 1179656 | tf_op jit(solution)/shard_map/ppermute | solution.py:57
  18.4 13.2 %collective-permute-start.8 = (bf16[256,768]{1,0:T(8,128)(2,1)S(1)}, bf16[256,768]{1,0:T(8,128)(2,1)S(1)}, u32[]{:S(2)}, u32[]{:S(2)}) collective-permute-start(bf16[256,768]{1,0:T(8,128)(2,1)S(1)} %shard_map.50.refs_0_), channel_id=1, source_target_pairs={{0,192},{1,25},{2,194},{3,27},{4,196},{5,29},{6,198},{7,31},{8,200... | collective-permute-start | bytes 1179656 | tf_op jit(solution)/shard_map/ppermute | solution.py:57
  18.9 3.7 %copy-start = (bf16[6144,768]{1,0:T(8,128)(2,1)S(1)}, bf16[6144,768]{1,0:T(8,128)(2,1)}, u32[]{:S(2)}) copy-start(bf16[6144,768]{1,0:T(8,128)(2,1)} %weight.3) | copy-start | bytes 28311556
  22.5 0.9 copy-start.3
  26.2 7.1 %copy-start.11 = (bf16[128,768]{1,0:T(8,128)(2,1)S(1)}, bf16[128,768]{1,0:T(8,128)(2,1)}, u32[]{:S(2)}) copy-start(bf16[128,768]{1,0:T(8,128)(2,1)} %param.3) | copy-start | bytes 589828
  26.2 65.4 %collective-permute-start.16 = (f32[4,768,128]{2,1,0:T(8,128)}, f32[4,768,128]{2,1,0:T(8,128)}, u32[]{:S(2)}, u32[]{:S(2)}) collective-permute-start(f32[4,768,128]{2,1,0:T(8,128)} %shard_map.54), channel_id=1, source_target_pairs={{0,1},{1,0},{2,3},{3,2},{4,5},{5,4},{6,7},{7,6},{8,9},{9,8},{10,11... | collective-permute-start | bytes 4718600 | tf_op jit(solution)/shard_map/ppermute | solution.py:57
  26.2 6.9 %copy-start.5 = (bf16[256,768]{1,0:T(8,128)(2,1)}, bf16[256,768]{1,0:T(8,128)(2,1)S(1)}, u32[]{:S(2)}) copy-start(bf16[256,768]{1,0:T(8,128)(2,1)S(1)} %collective-permute-done.6.refs_1_) | copy-start | bytes 1179652
  28.4 5.7 %copy-start.7 = (bf16[256,768]{1,0:T(8,128)(2,1)}, bf16[256,768]{1,0:T(8,128)(2,1)S(1)}, u32[]{:S(2)}) copy-start(bf16[256,768]{1,0:T(8,128)(2,1)S(1)} %collective-permute-done.7.refs_2_) | copy-start | bytes 1179652
  31.6 2.6 %copy-start.9 = (bf16[256,768]{1,0:T(8,128)(2,1)}, bf16[256,768]{1,0:T(8,128)(2,1)S(1)}, u32[]{:S(2)}) copy-start(bf16[256,768]{1,0:T(8,128)(2,1)S(1)} %collective-permute-done.8.refs_3_) | copy-start | bytes 1179652
  32.4 57.0 %copy-start.4 = (bf16[128,768]{1,0:T(8,128)(2,1)S(1)}, bf16[128,768]{1,0:T(8,128)(2,1)}, u32[]{:S(2)}) copy-start(bf16[128,768]{1,0:T(8,128)(2,1)} %near.5) | copy-start | bytes 589828
  33.1 56.3 %collective-permute-start.9 = (bf16[896,768]{1,0:T(8,128)(2,1)}, bf16[896,768]{1,0:T(8,128)(2,1)S(1)}, u32[]{:S(2)}, u32[]{:S(2)}) collective-permute-start(bf16[896,768]{1,0:T(8,128)(2,1)} %constant_dynamic-update-slice_fusion), channel_id=1, source_target_pairs={{0,24},{1,193},{2,26},{3,195},{4,28},{5,197},{6,30},{7,199},{8,16}... | collective-permute-start | bytes 4128776 | tf_op jit(solution)/shard_map/ppermute | solution.py:57
  34.1 20.9 %all-to-all-start = ((bf16[4,192,128]{2,1,0:T(8,128)(2,1)}), bf16[4,192,128]{2,1,0:T(8,128)(2,1)}, u32[]{:S(2)}, u32[]{:S(2)}) async-start(bf16[4,192,128]{2,1,0:T(8,128)(2,1)} %bitcast.1), calls=%async_computation | async-start | bytes 393216 | tf_op jit(solution)/shard_map/all_to_all | solution.py:190
  41.1 57.3 %collective-permute-start.11 = (bf16[896,768]{1,0:T(8,128)(2,1)}, bf16[896,768]{1,0:T(8,128)(2,1)S(1)}, u32[]{:S(2)}, u32[]{:S(2)}) collective-permute-start(bf16[896,768]{1,0:T(8,128)(2,1)} %constant_dynamic-update-slice_fusion), channel_id=1, source_target_pairs={{0,8},{1,65},{2,10},{3,67},{4,12},{5,69},{6,14},{7,71},{8,0},{9,73... | collective-permute-start | bytes 4128776 | tf_op jit(solution)/shard_map/ppermute | solution.py:57
  55.0 1.6 %collective-permute-start = (bf16[4,192,128]{2,1,0:T(8,128)(2,1)}, bf16[4,192,128]{2,1,0:T(8,128)(2,1)S(1)}, u32[]{:S(2)}, u32[]{:S(2)}) collective-permute-start(bf16[4,192,128]{2,1,0:T(8,128)(2,1)} %all-to-all-done), channel_id=1, source_target_pairs={{0,0},{1,32},{2,66},{3,98},{4,132},{5,164},{6,198},{7,230},{8,8},{... | collective-permute-start | bytes 589832 | tf_op jit(solution)/shard_map/ppermute | solution.py:57
  56.6 17.8 %collective-permute-start.1 = (bf16[4,192,128]{2,1,0:T(8,128)(2,1)S(1)}, bf16[4,192,128]{2,1,0:T(8,128)(2,1)S(1)}, u32[]{:S(2)}, u32[]{:S(2)}) collective-permute-start(bf16[4,192,128]{2,1,0:T(8,128)(2,1)S(1)} %collective-permute-done), channel_id=1, source_target_pairs={{0,2},{1,3},{2,0},{3,1},{4,6},{5,7},{6,4},{7,5},{8,10},{9,11},{10,... | collective-permute-start | bytes 589832 | tf_op jit(solution)/shard_map/ppermute | solution.py:57
  70.6 17.3 %collective-permute-start.2 = (bf16[4,192,128]{2,1,0:T(8,128)(2,1)S(1)}, bf16[4,192,128]{2,1,0:T(8,128)(2,1)S(1)}, u32[]{:S(2)}, u32[]{:S(2)}) collective-permute-start(bf16[4,192,128]{2,1,0:T(8,128)(2,1)S(1)} %collective-permute-done), channel_id=1, source_target_pairs={{0,4},{1,5},{2,6},{3,7},{4,0},{5,1},{6,2},{7,3},{8,12},{9,13},{10,... | collective-permute-start | bytes 589832 | tf_op jit(solution)/shard_map/ppermute | solution.py:57
  74.4 13.5 %collective-permute-start.3 = (bf16[4,192,128]{2,1,0:T(8,128)(2,1)S(1)}, bf16[4,192,128]{2,1,0:T(8,128)(2,1)S(1)}, u32[]{:S(2)}, u32[]{:S(2)}) collective-permute-start(bf16[4,192,128]{2,1,0:T(8,128)(2,1)S(1)} %collective-permute-done), channel_id=1, source_target_pairs={{0,6},{1,7},{2,4},{3,5},{4,2},{5,3},{6,0},{7,1},{8,14},{9,15},{10,... | collective-permute-start | bytes 589832 | tf_op jit(solution)/shard_map/ppermute | solution.py:57
  88.1 18.7 %collective-permute-start.4 = (bf16[4,4,192,128]{3,2,1,0:T(8,128)(2,1)S(1)}, bf16[4,4,192,128]{3,2,1,0:T(8,128)(2,1)S(1)}, u32[]{:S(2)}, u32[]{:S(2)}) collective-permute-start(bf16[4,4,192,128]{3,2,1,0:T(8,128)(2,1)S(1)} %pad_maximum_fusion.own), channel_id=1, source_target_pairs={{0,1},{1,0},{2,3},{3,2},{4,5},{5,4},{6,7},{7,6},{8,9},{9,8},{10,11... | collective-permute-start | bytes 2359304 | tf_op jit(solution)/shard_map/ppermute | solution.py:57
  89.4 14.2 %collective-permute-start.14 = (bf16[128,768]{1,0:T(8,128)(2,1)S(1)}, bf16[128,768]{1,0:T(8,128)(2,1)S(1)}, u32[]{:S(2)}, u32[]{:S(2)}) collective-permute-start(bf16[128,768]{1,0:T(8,128)(2,1)S(1)} %copy-done.4), channel_id=1, source_target_pairs={{0,8},{1,65},{2,10},{3,67},{4,12},{5,69},{6,14},{7,71},{8,0},{9,73... | collective-permute-start | bytes 589832 | tf_op jit(solution)/shard_map/ppermute | solution.py:57
  89.5 43.4 %collective-permute-start.10 = (bf16[512,768]{1,0:T(8,128)(2,1)S(1)}, bf16[512,768]{1,0:T(8,128)(2,1)S(1)}, u32[]{:S(2)}, u32[]{:S(2)}) collective-permute-start(bf16[512,768]{1,0:T(8,128)(2,1)S(1)} %slice.8), channel_id=1, source_target_pairs={{0,8},{1,65},{2,10},{3,67},{4,12},{5,69},{6,14},{7,71},{8,0},{9,73... | collective-permute-start | bytes 2359304 | tf_op jit(solution)/shard_map/ppermute | solution.py:57
  91.6 15.2 %collective-permute-start.15 = (bf16[128,768]{1,0:T(8,128)(2,1)S(1)}, bf16[128,768]{1,0:T(8,128)(2,1)S(1)}, u32[]{:S(2)}, u32[]{:S(2)}) collective-permute-start(bf16[128,768]{1,0:T(8,128)(2,1)S(1)} %copy-done.4), channel_id=1, source_target_pairs={{0,24},{1,193},{2,26},{3,195},{4,28},{5,197},{6,30},{7,199},{8,16}... | collective-permute-start | bytes 589832 | tf_op jit(solution)/shard_map/ppermute | solution.py:57
  91.8 3.7 %copy-start.1 = (bf16[6144,768]{1,0:T(8,128)(2,1)S(1)}, bf16[6144,768]{1,0:T(8,128)(2,1)}, u32[]{:S(2)}) copy-start(bf16[6144,768]{1,0:T(8,128)(2,1)} %weight.3) | copy-start | bytes 28311556
  98.4 27.3 %copy-start.6 = (bf16[256,768]{1,0:T(8,128)(2,1)S(1)}, bf16[256,768]{1,0:T(8,128)(2,1)}, u32[]{:S(2)}) copy-start(bf16[256,768]{1,0:T(8,128)(2,1)} %copy-done.5) | copy-start | bytes 1179652
  98.4 27.3 %copy-start.8 = (bf16[256,768]{1,0:T(8,128)(2,1)S(1)}, bf16[256,768]{1,0:T(8,128)(2,1)}, u32[]{:S(2)}) copy-start(bf16[256,768]{1,0:T(8,128)(2,1)} %copy-done.7) | copy-start | bytes 1179652
  98.4 27.3 %copy-start.10 = (bf16[256,768]{1,0:T(8,128)(2,1)S(1)}, bf16[256,768]{1,0:T(8,128)(2,1)}, u32[]{:S(2)}) copy-start(bf16[256,768]{1,0:T(8,128)(2,1)} %copy-done.9) | copy-start | bytes 1179652
  98.4 13.6 %collective-permute-start.19 = (f32[384,128]{1,0:T(8,128)S(1)}, f32[384,128]{1,0:T(8,128)S(1)}, u32[]{:S(2)}, u32[]{:S(2)}) collective-permute-start(f32[384,128]{1,0:T(8,128)S(1)} %get-tuple-element.10), channel_id=1, source_target_pairs={{0,4},{1,5},{2,6},{3,7},{4,32},{5,33},{6,34},{7,35},{8,12},{9,13},... | collective-permute-start | bytes 589832 | tf_op jit(solution)/shard_map/ppermute | solution.py:57
  103.6 29.2 %collective-permute-start.12 = (bf16[384,768]{1,0:T(8,128)(2,1)S(1)}, bf16[384,768]{1,0:T(8,128)(2,1)S(1)}, u32[]{:S(2)}, u32[]{:S(2)}) collective-permute-start(bf16[384,768]{1,0:T(8,128)(2,1)S(1)} %slice.9), channel_id=1, source_target_pairs={{0,24},{1,193},{2,26},{3,195},{4,28},{5,197},{6,30},{7,199},{8,16}... | collective-permute-start | bytes 1769480 | tf_op jit(solution)/shard_map/ppermute | solution.py:57
  106.8 20.3 %collective-permute-start.17 = (f32[768,128]{1,0:T(8,128)S(1)}, f32[768,128]{1,0:T(8,128)S(1)}, u32[]{:S(2)}, u32[]{:S(2)}) collective-permute-start(f32[768,128]{1,0:T(8,128)S(1)} %get-tuple-element.8), channel_id=1, source_target_pairs={{0,2},{1,3},{2,4},{3,5},{4,6},{5,7},{6,32},{7,33},{8,10},{9,11},{1... | collective-permute-start | bytes 1179656 | tf_op jit(solution)/shard_map/ppermute | solution.py:57
  106.8 20.3 %collective-permute-start.18 = (f32[768,128]{1,0:T(8,128)S(1)}, f32[768,128]{1,0:T(8,128)S(1)}, u32[]{:S(2)}, u32[]{:S(2)}) collective-permute-start(f32[768,128]{1,0:T(8,128)S(1)} %get-tuple-element.9), channel_id=1, source_target_pairs={{0,38},{1,39},{2,0},{3,1},{4,2},{5,3},{6,4},{7,5},{8,46},{9,47},{1... | collective-permute-start | bytes 1179656 | tf_op jit(solution)/shard_map/ppermute | solution.py:57
  112.0 13.7 %collective-permute-start.20 = (f32[384,128]{1,0:T(8,128)S(1)}, f32[384,128]{1,0:T(8,128)S(1)}, u32[]{:S(2)}, u32[]{:S(2)}) collective-permute-start(f32[384,128]{1,0:T(8,128)S(1)} %get-tuple-element.11), channel_id=1, source_target_pairs={{0,36},{1,37},{2,38},{3,39},{4,0},{5,1},{6,2},{7,3},{8,44},{9,45},... | collective-permute-start | bytes 589832 | tf_op jit(solution)/shard_map/ppermute | solution.py:57
  125.7 7.2 %collective-permute-start.13 = (bf16[128,768]{1,0:T(8,128)(2,1)S(1)}, bf16[128,768]{1,0:T(8,128)(2,1)S(1)}, u32[]{:S(2)}, u32[]{:S(2)}) collective-permute-start(bf16[128,768]{1,0:T(8,128)(2,1)S(1)} %copy-done.4), channel_id=1, source_target_pairs={{0,16},{1,129},{2,18},{3,131},{4,20},{5,133},{6,22},{7,135},{8,24}... | collective-permute-start | bytes 589832 | tf_op jit(solution)/shard_map/ppermute | solution.py:57

commit v8 on v6

--- a/solution.py
+++ b/solution.py
@@ -55,6 +55,10 @@
 
 def send(array, route):
     return lax.ppermute(array, AXES, pairs(route))
+
+
+def at(stack, index):
+    return lax.dynamic_index_in_dim(stack, index, 0, keepdims=False)
 
 
 def products_kernel(kept, weight, near, far, *refs):
@@ -120,14 +124,13 @@
 def weight_kernel(items, own, other, *refs):
     h, low, core = here()
     swapped = core != h
-    y = lax.axis_index("seq")
     arrays = 1 + max(max(item[0], item[2]) for item in items)
     tokens = own.shape[3]
     out = refs[-1]
     total = refs[arrays][...] if len(refs) > arrays + 1 else jnp.zeros(out.shape, F32)
     for a, row, b, far_row, i, j in items:
         k = low ^ jnp.where(core == 0, i, j)
-        s = y ^ jnp.where(core == 0, j, i)
+        s = jnp.where(core == 0, j, i)
         mine, theirs = own[k, s], other[k, s]
         near = jnp.where(swapped, theirs, mine)
         far = jnp.where(swapped, mine, theirs)
@@ -157,6 +160,7 @@
 
 
 def step(context, cotangent, out_weight):
+    y = lax.axis_index("seq")
     tokens, width = cotangent.shape
     quarter = width // 4
 
@@ -165,12 +169,16 @@
     far_cot = send(cotangent, ring(4))
     pair = jnp.concatenate([cotangent, far_cot])
     first = [send(pair, crosswise(k, True)) for k in others]
-    second = [send(cotangent, crosswise(k, False)) for k in others]
-    row = jnp.concatenate([*first, far_cot])
-    both = [send(row, crosswise(k, False)) for k in others]
+    row = jnp.concatenate([*first, pair])
+    one, three = (send(row, crosswise(k, False)) for k in (1, 3))
+    cut = 4 * tokens
+    two = [send(three[:cut], crosswise(1, False)), send(one[cut:], crosswise(3, False))]
 
     turned = context.T.reshape(4, quarter, tokens)
-    block = lax.all_to_all(turned, "seq", split_axis=0, concat_axis=0, tiled=True)
+    block = jnp.stack(
+        [at(turned, y)]
+        + [send(at(turned, y ^ k), lambda x, h, y, l, c, k=k: (x, h, y ^ k, l, c)) for k in others]
+    )
     mine = send(block, lambda x, h, y, l, c: (l, c, y, l ^ x, h))
     gathered = [mine] + [
         send(mine, lambda x, h, y, l, c, k=k: (x, h, y, l ^ k, c)) for k in (1, 2, 3)
@@ -188,13 +196,19 @@
     from_two_after = send(skip_down, ring(-2))
 
     early = [(k, 0, k, tokens, k, 0) for k in range(4)]
-    late = [(2 + k, 0, k - 1, 6 * tokens, 0, k) for k in others] + [
-        (k - 1, 2 * tokens * (i - 1), k - 1, 2 * tokens * (i - 1) + tokens, i, k)
-        for k in others
-        for i in others
-    ]
-    early_part = weight_part(early, own, other, [pair] + first)
-    grad_weight = weight_part(late, own, other, both + second, early_part)
+    late = [
+        (a, at_row, a, at_row + tokens, i, k)
+        for a, k in ((0, 1), (1, 3))
+        for i in range(4)
+        for at_row in (2 * tokens * ((i + 3) % 4),)
+    ]
+    last = [
+        (a, at_row, a, at_row + tokens, i, 2)
+        for a, at_row, i in ((0, 0, 1), (0, 2 * tokens, 2), (1, 0, 3), (1, 2 * tokens, 0))
+    ]
+    total = weight_part(early, own, other, [pair] + first)
+    total = weight_part(late, own, other, [one, three], total)
+    grad_weight = weight_part(last, own, other, two, total)
     grad_context = pl.pallas_call(
         finish_kernel,
         out_shape=jax.ShapeDtypeStruct((tokens, width), BF16),

time: 118 us -> 127 us (1.076)
  the two profiles are of different devices: /device:TPU:1 before, /device:TPU:3 now
where the time goes in v8:
time: 127 us
  starting transfers between devices  56.9 us (45%)
  waiting for transfers between devices  51.4 us (40%)
  local copies, waits for them, and re-layouts  11.3 us (9%)
  Pallas kernels  6.44 us (5%)
    ppermute x21, starting transfers between devices, send(): return lax.ppermute(array, AXES, pairs(route))  56.9 us
    ppermute x21, waiting for transfers between devices, send(): return lax.ppermute(array, AXES, pairs(route))  51.4 us
    unnamed x25, local copies, waits for them, and re-layouts  7.87 us
    pallas_call x2, Pallas kernels, products(): pl.pallas_call(functools.partial(products_kernel, kept), out_shape=shapes...  3.06 us
    pallas_call x3, Pallas kernels, weight_part(): pl.pallas_call(functools.partial(weight_kernel, items), out_shape=jax.Sha...  2.56 us
  transfers between devices with their start and end apart: 21, of which 9 were waited for; matrix products, arithmetic and copies ran while one was open for 4% of the time, Pallas kernels for 4%

profile of v8, /device:TPU:3, one launch (start us, length us, event | category | flops | bytes accessed | tf_op | source)
XLA Modules:
  0.0 127.0 jit_solution(8240716185933287439)
XLA Ops:
  0.6 7.0 %collective-permute-start.8 = (bf16[128,768]{1,0:T(8,128)(2,1)}, bf16[128,768]{1,0:T(8,128)(2,1)S(1)}, u32[]{:S(2)}, u32[]{:S(2)}) collective-permute-start(bf16[128,768]{1,0:T(8,128)(2,1)} %near.3), channel_id=1, source_target_pairs={{0,32},{1,33},{2,34},{3,35},{4,36},{5,37},{6,38},{7,39},{8,40},{9,... | collective-permute-start | bytes 589832 | tf_op jit(solution)/shard_map/ppermute | solution.py:57
  7.6 1.0 constant_dynamic-update-slice_fusion.1
  8.6 3.8 %collective-permute-done.8.far = bf16[128,768]{1,0:T(8,128)(2,1)S(1)} collective-permute-done((bf16[128,768]{1,0:T(8,128)(2,1)}, bf16[128,768]{1,0:T(8,128)(2,1)S(1)}, u32[]{:S(2)}, u32[]{:S(2)}) %collective-permute-start.8) | collective-permute-done | bytes 196640 | tf_op jit(solution)/shard_map/ppermute | solution.py:57
  12.5 0.0 copy-start.8
  12.5 1.4 %collective-permute-start.9 = (bf16[256,768]{1,0:T(8,128)(2,1)S(1)}, bf16[256,768]{1,0:T(8,128)(2,1)S(1)}, u32[]{:S(2)}, u32[]{:S(2)}) collective-permute-start(bf16[256,768]{1,0:T(8,128)(2,1)S(1)} %constant_dynamic-update-slice_fusion.refs_0_), channel_id=1, source_target_pairs={{0,64},{1,9},{2,66},{3,11},{4,68},{5,13},{6,70},{7,15},{8,72},{9,1... | collective-permute-start | bytes 1179656 | tf_op jit(solution)/shard_map/ppermute | solution.py:57
  13.9 2.6 %collective-permute-start.10 = (bf16[256,768]{1,0:T(8,128)(2,1)S(1)}, bf16[256,768]{1,0:T(8,128)(2,1)S(1)}, u32[]{:S(2)}, u32[]{:S(2)}) collective-permute-start(bf16[256,768]{1,0:T(8,128)(2,1)S(1)} %constant_dynamic-update-slice_fusion.refs_0_), channel_id=1, source_target_pairs={{0,128},{1,17},{2,130},{3,19},{4,132},{5,21},{6,134},{7,23},{8,136... | collective-permute-start | bytes 1179656 | tf_op jit(solution)/shard_map/ppermute | solution.py:57
  16.5 3.0 %collective-permute-done.9.refs_1_ = bf16[256,768]{1,0:T(8,128)(2,1)S(1)} collective-permute-done((bf16[256,768]{1,0:T(8,128)(2,1)S(1)}, bf16[256,768]{1,0:T(8,128)(2,1)S(1)}, u32[]{:S(2)}, u32[]{:S(2)}) %collective-permute-start.9) | collective-permute-done | bytes 393248 | tf_op jit(solution)/shard_map/ppermute | solution.py:57
  19.5 0.8 constant_dynamic-update-slice_fusion.6
  20.3 5.6 %collective-permute-done.10.refs_2_ = bf16[256,768]{1,0:T(8,128)(2,1)S(1)} collective-permute-done((bf16[256,768]{1,0:T(8,128)(2,1)S(1)}, bf16[256,768]{1,0:T(8,128)(2,1)S(1)}, u32[]{:S(2)}, u32[]{:S(2)}) %collective-permute-start.10) | collective-permute-done | bytes 393248 | tf_op jit(solution)/shard_map/ppermute | solution.py:57
  26.0 0.8 constant_dynamic-update-slice_fusion.5
  26.8 1.8 %collective-permute-done.11.refs_3_ = bf16[256,768]{1,0:T(8,128)(2,1)S(1)} collective-permute-done((bf16[256,768]{1,0:T(8,128)(2,1)S(1)}, bf16[256,768]{1,0:T(8,128)(2,1)S(1)}, u32[]{:S(2)}, u32[]{:S(2)}) %collective-permute-start.11) | collective-permute-done | bytes 393248 | tf_op jit(solution)/shard_map/ppermute | solution.py:57
  28.5 0.8 constant_dynamic-update-slice_fusion.4
  29.4 0.7 constant_dynamic-update-slice_fusion.3
  30.1 0.7 constant_dynamic-update-slice_fusion.2
  30.8 1.2 collective-permute-start.12
  32.0 1.7 %collective-permute-start.14 = (bf16[1024,768]{1,0:T(8,128)(2,1)}, bf16[1024,768]{1,0:T(8,128)(2,1)S(1)}, u32[]{:S(2)}, u32[]{:S(2)}) collective-permute-start(bf16[1024,768]{1,0:T(8,128)(2,1)} %constant_dynamic-update-slice_fusion.2), channel_id=1, source_target_pairs={{0,8},{1,65},{2,10},{3,67},{4,12},{5,69},{6,14},{7,71},{8,0},{9,73... | collective-permute-start | bytes 4718600 | tf_op jit(solution)/shard_map/ppermute | solution.py:57
  33.6 1.7 %copy.5 = bf16[768,128]{1,0:T(8,128)(2,1)} copy(bf16[768,128]{0,1:T(8,128)(2,1)} %bitcast.20) | data formatting | bytes 393216 | tf_op jit(solution)/shard_map/transpose | solution.py:177
  35.4 0.9 constant_dynamic-slice_fusion
  36.3 0.1 collective-permute-start
  36.4 1.3 %collective-permute-start.1 = (bf16[192,128]{1,0:T(8,128)(2,1)S(1)}, bf16[192,128]{1,0:T(8,128)(2,1)S(1)}, u32[]{:S(2)}, u32[]{:S(2)}) collective-permute-start(bf16[192,128]{1,0:T(8,128)(2,1)S(1)} %get-tuple-element.14), channel_id=1, source_target_pairs={{0,16},{1,17},{2,18},{3,19},{4,20},{5,21},{6,22},{7,23},{8,24},{9,... | collective-permute-start | bytes 147464 | tf_op jit(solution)/shard_map/ppermute | solution.py:57
  37.7 2.5 %collective-permute-start.2 = (bf16[192,128]{1,0:T(8,128)(2,1)S(1)}, bf16[192,128]{1,0:T(8,128)(2,1)S(1)}, u32[]{:S(2)}, u32[]{:S(2)}) collective-permute-start(bf16[192,128]{1,0:T(8,128)(2,1)S(1)} %get-tuple-element.13), channel_id=1, source_target_pairs={{0,24},{1,25},{2,26},{3,27},{4,28},{5,29},{6,30},{7,31},{8,16},{9,... | collective-permute-start | bytes 147464 | tf_op jit(solution)/shard_map/ppermute | solution.py:57
  40.2 3.7 %copy-done = bf16[6144,768]{1,0:T(8,128)(2,1)S(1)} copy-done((bf16[6144,768]{1,0:T(8,128)(2,1)S(1)}, bf16[6144,768]{1,0:T(8,128)(2,1)}, u32[]{:S(2)}) %copy-start) | copy-done | bytes 9437208
  43.9 1.5 %shard_map.53 = f32[4,768,128]{2,1,0:T(8,128)S(1)} custom-call(bf16[6144,768]{1,0:T(8,128)(2,1)S(1)} %copy-done, bf16[128,768]{1,0:T(8,128)(2,1)S(1)} %copy-done.1, bf16[128,768]{1,0:T(8,128)(2,1)S(1)} %collective-permute-done.8.far), custom_call_target="tpu_custom_call" | custom-call | flops 603979776 | bytes 6291456 | tf_op jit(solution)/shard_map/pallas_call | solution.py:101
  45.4 10.9 %collective-permute-start.16 = (f32[4,768,128]{2,1,0:T(8,128)S(1)}, f32[4,768,128]{2,1,0:T(8,128)S(1)}, u32[]{:S(2)}, u32[]{:S(2)}) collective-permute-start(f32[4,768,128]{2,1,0:T(8,128)S(1)} %shard_map.53), channel_id=1, source_target_pairs={{0,1},{1,0},{2,3},{3,2},{4,5},{5,4},{6,7},{7,6},{8,9},{9,8},{10,11... | collective-permute-start | bytes 4718600 | tf_op jit(solution)/shard_map/ppermute | solution.py:57
  56.4 12.7 %collective-permute-start.3 = (bf16[4,192,128]{2,1,0:T(8,128)(2,1)S(1)}, bf16[4,192,128]{2,1,0:T(8,128)(2,1)S(1)}, u32[]{:S(2)}, u32[]{:S(2)}) collective-permute-start(bf16[4,192,128]{2,1,0:T(8,128)(2,1)S(1)} %pad_maximum_fusion.1), channel_id=1, source_target_pairs={{0,0},{1,32},{2,66},{3,98},{4,132},{5,164},{6,198},{7,230},{8,8},{... | collective-permute-start | bytes 589832 | tf_op jit(solution)/shard_map/ppermute | solution.py:57
  69.1 2.7 %collective-permute-done.3 = bf16[4,192,128]{2,1,0:T(8,128)(2,1)S(1)} collective-permute-done((bf16[4,192,128]{2,1,0:T(8,128)(2,1)S(1)}, bf16[4,192,128]{2,1,0:T(8,128)(2,1)S(1)}, u32[]{:S(2)}, u32[]{:S(2)}) %collective-permute-start.3) | collective-permute-done | bytes 196640 | tf_op jit(solution)/shard_map/ppermute | solution.py:57
  71.8 4.8 %collective-permute-start.5 = (bf16[4,192,128]{2,1,0:T(8,128)(2,1)S(1)}, bf16[4,192,128]{2,1,0:T(8,128)(2,1)S(1)}, u32[]{:S(2)}, u32[]{:S(2)}) collective-permute-start(bf16[4,192,128]{2,1,0:T(8,128)(2,1)S(1)} %collective-permute-done.3), channel_id=1, source_target_pairs={{0,4},{1,5},{2,6},{3,7},{4,0},{5,1},{6,2},{7,3},{8,12},{9,13},{10,... | collective-permute-start | bytes 589832 | tf_op jit(solution)/shard_map/ppermute | solution.py:57
  76.7 1.3 collective-permute-start.6
  77.9 10.2 %collective-permute-done.5 = bf16[4,192,128]{2,1,0:T(8,128)(2,1)S(1)} collective-permute-done((bf16[4,192,128]{2,1,0:T(8,128)(2,1)S(1)}, bf16[4,192,128]{2,1,0:T(8,128)(2,1)S(1)}, u32[]{:S(2)}, u32[]{:S(2)}) %collective-permute-start.5) | collective-permute-done | bytes 196640 | tf_op jit(solution)/shard_map/ppermute | solution.py:57
  88.1 5.2 %collective-permute-done.4 = bf16[4,192,128]{2,1,0:T(8,128)(2,1)S(1)} collective-permute-done((bf16[4,192,128]{2,1,0:T(8,128)(2,1)S(1)}, bf16[4,192,128]{2,1,0:T(8,128)(2,1)S(1)}, u32[]{:S(2)}, u32[]{:S(2)}) %collective-permute-start.4) | collective-permute-done | bytes 196640 | tf_op jit(solution)/shard_map/ppermute | solution.py:57
  93.3 0.1 pad_maximum_fusion.own
  93.4 0.1 collective-permute-start.7
  93.5 0.1 slice.8
  93.6 5.3 %collective-permute-start.13 = (bf16[512,768]{1,0:T(8,128)(2,1)S(1)}, bf16[512,768]{1,0:T(8,128)(2,1)S(1)}, u32[]{:S(2)}, u32[]{:S(2)}) collective-permute-start(bf16[512,768]{1,0:T(8,128)(2,1)S(1)} %slice.8), channel_id=1, source_target_pairs={{0,8},{1,65},{2,10},{3,67},{4,12},{5,69},{6,14},{7,71},{8,0},{9,73... | collective-permute-start | bytes 2359304 | tf_op jit(solution)/shard_map/ppermute | solution.py:57
  98.9 0.1 slice.9
  99.0 0.0 copy-start.9
  99.0 0.1 collective-permute-start.15
  99.1 1.5 %shard_map.54 = (f32[768,128]{1,0:T(8,128)S(1)}, f32[768,128]{1,0:T(8,128)S(1)}, f32[768,128]{1,0:T(8,128)S(1)}, f32[384,128]{1,0:T(8,128)S(1)}, f32[384,128]{1,0:T(8,128)S(1)}) custom-call(bf16[6144,768]{1,0:T(8,128)(2,1)S(1)} %copy-done, bf16[128,768]{1,0:T(8,128)(2,1)S(1)} %copy-done.1, bf16[128,768]{1,0:T(8,128)(2,1)S(1)} %collective-permute-done.8.far, ...), custom_call_target="tpu_custom_call" | custom-call | flops 603979776 | bytes 6291456 | tf_op jit(solution)/shard_map/pallas_call | solution.py:101
  100.7 0.3 collective-permute-start.19
  100.9 1.5 %collective-permute-start.17 = (f32[768,128]{1,0:T(8,128)S(1)}, f32[768,128]{1,0:T(8,128)S(1)}, u32[]{:S(2)}, u32[]{:S(2)}) collective-permute-start(f32[768,128]{1,0:T(8,128)S(1)} %get-tuple-element.8), channel_id=1, source_target_pairs={{0,2},{1,3},{2,4},{3,5},{4,6},{5,7},{6,32},{7,33},{8,10},{9,11},{1... | collective-permute-start | bytes 1179656 | tf_op jit(solution)/shard_map/ppermute | solution.py:57
  102.5 1.2 collective-permute-start.18
  103.7 10.2 %collective-permute-done.19.two_before = f32[384,128]{1,0:T(8,128)S(1)} collective-permute-done((f32[384,128]{1,0:T(8,128)S(1)}, f32[384,128]{1,0:T(8,128)S(1)}, u32[]{:S(2)}, u32[]{:S(2)}) %collective-permute-start.19) | collective-permute-done | bytes 196640 | tf_op jit(solution)/shard_map/ppermute | solution.py:57
  113.9 0.8 collective-permute-start.20
  114.7 0.5 shard_map.50.refs_2_
  115.2 8.9 %collective-permute-done.20.two_after = f32[384,128]{1,0:T(8,128)S(1)} collective-permute-done((f32[384,128]{1,0:T(8,128)S(1)}, f32[384,128]{1,0:T(8,128)S(1)}, u32[]{:S(2)}, u32[]{:S(2)}) %collective-permute-start.20) | collective-permute-done | bytes 196640 | tf_op jit(solution)/shard_map/ppermute | solution.py:57
  124.1 0.8 shard_map.55
  124.9 0.8 shard_map.51.refs_2_
  125.7 1.3 %shard_map.52 = f32[192,768]{1,0:T(8,128)} custom-call(bf16[4,4,192,128]{3,2,1,0:T(8,128)(2,1)S(1)} %pad_maximum_fusion.own, bf16[4,4,192,128]{3,2,1,0:T(8,128)(2,1)S(1)} %collective-permute-done.7.other, bf16[512,768]{1,0:T(8,128)(2,1)S(1)} %collective-permute-done.13.refs_0_, bf16[512,768]{1,0:T(8,128)(2,1)S(1)} %collective-permute-done.15.refs_1_, ...), custom_call_target="tpu_custom_call" | custom-call | flops 301989888 | bytes 3145728 | tf_op jit(solution)/shard_map/pallas_call | solution.py:148
  (33 shorter events, 0.1 us)
Async XLA Ops:
  0.6 28.7 %copy-start.1 = (bf16[128,768]{1,0:T(8,128)(2,1)S(1)}, bf16[128,768]{1,0:T(8,128)(2,1)}, u32[]{:S(2)}) copy-start(bf16[128,768]{1,0:T(8,128)(2,1)} %near.3) | copy-start | bytes 589828
  0.6 11.8 %collective-permute-start.8 = (bf16[128,768]{1,0:T(8,128)(2,1)}, bf16[128,768]{1,0:T(8,128)(2,1)S(1)}, u32[]{:S(2)}, u32[]{:S(2)}) collective-permute-start(bf16[128,768]{1,0:T(8,128)(2,1)} %near.3), channel_id=1, source_target_pairs={{0,32},{1,33},{2,34},{3,35},{4,36},{5,37},{6,38},{7,39},{8,40},{9,... | collective-permute-start | bytes 589832 | tf_op jit(solution)/shard_map/ppermute | solution.py:57
  12.5 18.3 %copy-start.8 = (bf16[256,768]{1,0:T(8,128)(2,1)}, bf16[256,768]{1,0:T(8,128)(2,1)S(1)}, u32[]{:S(2)}) copy-start(bf16[256,768]{1,0:T(8,128)(2,1)S(1)} %constant_dynamic-update-slice_fusion.refs_0_) | copy-start | bytes 1179652
  12.5 7.0 %collective-permute-start.9 = (bf16[256,768]{1,0:T(8,128)(2,1)S(1)}, bf16[256,768]{1,0:T(8,128)(2,1)S(1)}, u32[]{:S(2)}, u32[]{:S(2)}) collective-permute-start(bf16[256,768]{1,0:T(8,128)(2,1)S(1)} %constant_dynamic-update-slice_fusion.refs_0_), channel_id=1, source_target_pairs={{0,64},{1,9},{2,66},{3,11},{4,68},{5,13},{6,70},{7,15},{8,72},{9,1... | collective-permute-start | bytes 1179656 | tf_op jit(solution)/shard_map/ppermute | solution.py:57
  13.9 12.1 %collective-permute-start.10 = (bf16[256,768]{1,0:T(8,128)(2,1)S(1)}, bf16[256,768]{1,0:T(8,128)(2,1)S(1)}, u32[]{:S(2)}, u32[]{:S(2)}) collective-permute-start(bf16[256,768]{1,0:T(8,128)(2,1)S(1)} %constant_dynamic-update-slice_fusion.refs_0_), channel_id=1, source_target_pairs={{0,128},{1,17},{2,130},{3,19},{4,132},{5,21},{6,134},{7,23},{8,136... | collective-permute-start | bytes 1179656 | tf_op jit(solution)/shard_map/ppermute | solution.py:57
  16.5 12.1 %collective-permute-start.11 = (bf16[256,768]{1,0:T(8,128)(2,1)S(1)}, bf16[256,768]{1,0:T(8,128)(2,1)S(1)}, u32[]{:S(2)}, u32[]{:S(2)}) collective-permute-start(bf16[256,768]{1,0:T(8,128)(2,1)S(1)} %constant_dynamic-update-slice_fusion.refs_0_), channel_id=1, source_target_pairs={{0,192},{1,25},{2,194},{3,27},{4,196},{5,29},{6,198},{7,31},{8,200... | collective-permute-start | bytes 1179656 | tf_op jit(solution)/shard_map/ppermute | solution.py:57
  19.5 11.3 %copy-start.2 = (bf16[256,768]{1,0:T(8,128)(2,1)}, bf16[256,768]{1,0:T(8,128)(2,1)S(1)}, u32[]{:S(2)}) copy-start(bf16[256,768]{1,0:T(8,128)(2,1)S(1)} %collective-permute-done.9.refs_1_) | copy-start | bytes 1179652
  26.0 6.0 %copy-start.4 = (bf16[256,768]{1,0:T(8,128)(2,1)}, bf16[256,768]{1,0:T(8,128)(2,1)S(1)}, u32[]{:S(2)}) copy-start(bf16[256,768]{1,0:T(8,128)(2,1)S(1)} %collective-permute-done.10.refs_2_) | copy-start | bytes 1179652
  28.5 5.1 %copy-start.6 = (bf16[256,768]{1,0:T(8,128)(2,1)}, bf16[256,768]{1,0:T(8,128)(2,1)S(1)}, u32[]{:S(2)}) copy-start(bf16[256,768]{1,0:T(8,128)(2,1)S(1)} %collective-permute-done.11.refs_3_) | copy-start | bytes 1179652
  30.8 62.8 %collective-permute-start.12 = (bf16[1024,768]{1,0:T(8,128)(2,1)}, bf16[1024,768]{1,0:T(8,128)(2,1)S(1)}, u32[]{:S(2)}, u32[]{:S(2)}) collective-permute-start(bf16[1024,768]{1,0:T(8,128)(2,1)} %constant_dynamic-update-slice_fusion.2), channel_id=1, source_target_pairs={{0,24},{1,193},{2,26},{3,195},{4,28},{5,197},{6,30},{7,199},{8,16}... | collective-permute-start | bytes 4718600 | tf_op jit(solution)/shard_map/ppermute | solution.py:57
  32.0 66.9 %collective-permute-start.14 = (bf16[1024,768]{1,0:T(8,128)(2,1)}, bf16[1024,768]{1,0:T(8,128)(2,1)S(1)}, u32[]{:S(2)}, u32[]{:S(2)}) collective-permute-start(bf16[1024,768]{1,0:T(8,128)(2,1)} %constant_dynamic-update-slice_fusion.2), channel_id=1, source_target_pairs={{0,8},{1,65},{2,10},{3,67},{4,12},{5,69},{6,14},{7,71},{8,0},{9,73... | collective-permute-start | bytes 4718600 | tf_op jit(solution)/shard_map/ppermute | solution.py:57
  36.3 9.2 %collective-permute-start = (bf16[192,128]{1,0:T(8,128)(2,1)S(1)}, bf16[192,128]{1,0:T(8,128)(2,1)S(1)}, u32[]{:S(2)}, u32[]{:S(2)}) collective-permute-start(bf16[192,128]{1,0:T(8,128)(2,1)S(1)} %get-tuple-element.15), channel_id=1, source_target_pairs={{0,8},{1,9},{2,10},{3,11},{4,12},{5,13},{6,14},{7,15},{8,0},{9,1},... | collective-permute-start | bytes 147464 | tf_op jit(solution)/shard_map/ppermute | solution.py:57
  36.4 20.0 %collective-permute-start.1 = (bf16[192,128]{1,0:T(8,128)(2,1)S(1)}, bf16[192,128]{1,0:T(8,128)(2,1)S(1)}, u32[]{:S(2)}, u32[]{:S(2)}) collective-permute-start(bf16[192,128]{1,0:T(8,128)(2,1)S(1)} %get-tuple-element.14), channel_id=1, source_target_pairs={{0,16},{1,17},{2,18},{3,19},{4,20},{5,21},{6,22},{7,23},{8,24},{9,... | collective-permute-start | bytes 147464 | tf_op jit(solution)/shard_map/ppermute | solution.py:57
  37.7 18.6 %collective-permute-start.2 = (bf16[192,128]{1,0:T(8,128)(2,1)S(1)}, bf16[192,128]{1,0:T(8,128)(2,1)S(1)}, u32[]{:S(2)}, u32[]{:S(2)}) collective-permute-start(bf16[192,128]{1,0:T(8,128)(2,1)S(1)} %get-tuple-element.13), channel_id=1, source_target_pairs={{0,24},{1,25},{2,26},{3,27},{4,28},{5,29},{6,30},{7,31},{8,16},{9,... | collective-permute-start | bytes 147464 | tf_op jit(solution)/shard_map/ppermute | solution.py:57
  40.2 3.7 %copy-start = (bf16[6144,768]{1,0:T(8,128)(2,1)S(1)}, bf16[6144,768]{1,0:T(8,128)(2,1)}, u32[]{:S(2)}) copy-start(bf16[6144,768]{1,0:T(8,128)(2,1)} %weight.3) | copy-start | bytes 28311556
  45.4 53.7 %collective-permute-start.16 = (f32[4,768,128]{2,1,0:T(8,128)S(1)}, f32[4,768,128]{2,1,0:T(8,128)S(1)}, u32[]{:S(2)}, u32[]{:S(2)}) collective-permute-start(f32[4,768,128]{2,1,0:T(8,128)S(1)} %shard_map.53), channel_id=1, source_target_pairs={{0,1},{1,0},{2,3},{3,2},{4,5},{5,4},{6,7},{7,6},{8,9},{9,8},{10,11... | collective-permute-start | bytes 4718600 | tf_op jit(solution)/shard_map/ppermute | solution.py:57
  56.4 15.5 %collective-permute-start.3 = (bf16[4,192,128]{2,1,0:T(8,128)(2,1)S(1)}, bf16[4,192,128]{2,1,0:T(8,128)(2,1)S(1)}, u32[]{:S(2)}, u32[]{:S(2)}) collective-permute-start(bf16[4,192,128]{2,1,0:T(8,128)(2,1)S(1)} %pad_maximum_fusion.1), channel_id=1, source_target_pairs={{0,0},{1,32},{2,66},{3,98},{4,132},{5,164},{6,198},{7,230},{8,8},{... | collective-permute-start | bytes 589832 | tf_op jit(solution)/shard_map/ppermute | solution.py:57
  71.8 16.3 %collective-permute-start.5 = (bf16[4,192,128]{2,1,0:T(8,128)(2,1)S(1)}, bf16[4,192,128]{2,1,0:T(8,128)(2,1)S(1)}, u32[]{:S(2)}, u32[]{:S(2)}) collective-permute-start(bf16[4,192,128]{2,1,0:T(8,128)(2,1)S(1)} %collective-permute-done.3), channel_id=1, source_target_pairs={{0,4},{1,5},{2,6},{3,7},{4,0},{5,1},{6,2},{7,3},{8,12},{9,13},{10,... | collective-permute-start | bytes 589832 | tf_op jit(solution)/shard_map/ppermute | solution.py:57
  76.7 11.5 %collective-permute-start.6 = (bf16[4,192,128]{2,1,0:T(8,128)(2,1)S(1)}, bf16[4,192,128]{2,1,0:T(8,128)(2,1)S(1)}, u32[]{:S(2)}, u32[]{:S(2)}) collective-permute-start(bf16[4,192,128]{2,1,0:T(8,128)(2,1)S(1)} %collective-permute-done.3), channel_id=1, source_target_pairs={{0,6},{1,7},{2,4},{3,5},{4,2},{5,3},{6,0},{7,1},{8,14},{9,15},{10,... | collective-permute-start | bytes 589832 | tf_op jit(solution)/shard_map/ppermute | solution.py:57
  88.1 5.2 %collective-permute-start.4 = (bf16[4,192,128]{2,1,0:T(8,128)(2,1)S(1)}, bf16[4,192,128]{2,1,0:T(8,128)(2,1)S(1)}, u32[]{:S(2)}, u32[]{:S(2)}) collective-permute-start(bf16[4,192,128]{2,1,0:T(8,128)(2,1)S(1)} %collective-permute-done.3), channel_id=1, source_target_pairs={{0,2},{1,3},{2,0},{3,1},{4,6},{5,7},{6,4},{7,5},{8,10},{9,11},{10,... | collective-permute-start | bytes 589832 | tf_op jit(solution)/shard_map/ppermute | solution.py:57
  93.4 9.0 %collective-permute-start.7 = (bf16[4,4,192,128]{3,2,1,0:T(8,128)(2,1)S(1)}, bf16[4,4,192,128]{3,2,1,0:T(8,128)(2,1)S(1)}, u32[]{:S(2)}, u32[]{:S(2)}) collective-permute-start(bf16[4,4,192,128]{3,2,1,0:T(8,128)(2,1)S(1)} %pad_maximum_fusion.own), channel_id=1, source_target_pairs={{0,1},{1,0},{2,3},{3,2},{4,5},{5,4},{6,7},{7,6},{8,9},{9,8},{10,11... | collective-permute-start | bytes 2359304 | tf_op jit(solution)/shard_map/ppermute | solution.py:57
  93.6 32.1 %collective-permute-start.13 = (bf16[512,768]{1,0:T(8,128)(2,1)S(1)}, bf16[512,768]{1,0:T(8,128)(2,1)S(1)}, u32[]{:S(2)}, u32[]{:S(2)}) collective-permute-start(bf16[512,768]{1,0:T(8,128)(2,1)S(1)} %slice.8), channel_id=1, source_target_pairs={{0,8},{1,65},{2,10},{3,67},{4,12},{5,69},{6,14},{7,71},{8,0},{9,73... | collective-permute-start | bytes 2359304 | tf_op jit(solution)/shard_map/ppermute | solution.py:57
  99.0 15.7 %copy-start.3 = (bf16[256,768]{1,0:T(8,128)(2,1)S(1)}, bf16[256,768]{1,0:T(8,128)(2,1)}, u32[]{:S(2)}) copy-start(bf16[256,768]{1,0:T(8,128)(2,1)} %copy-done.2) | copy-start | bytes 1179652
  99.0 15.7 %copy-start.5 = (bf16[256,768]{1,0:T(8,128)(2,1)S(1)}, bf16[256,768]{1,0:T(8,128)(2,1)}, u32[]{:S(2)}) copy-start(bf16[256,768]{1,0:T(8,128)(2,1)} %copy-done.4) | copy-start | bytes 1179652
  99.0 15.7 %copy-start.7 = (bf16[256,768]{1,0:T(8,128)(2,1)S(1)}, bf16[256,768]{1,0:T(8,128)(2,1)}, u32[]{:S(2)}) copy-start(bf16[256,768]{1,0:T(8,128)(2,1)} %copy-done.6) | copy-start | bytes 1179652
  99.0 15.7 %copy-start.9 = (bf16[256,768]{1,0:T(8,128)(2,1)S(1)}, bf16[256,768]{1,0:T(8,128)(2,1)}, u32[]{:S(2)}) copy-start(bf16[256,768]{1,0:T(8,128)(2,1)} %copy-done.8) | copy-start | bytes 1179652
  99.0 26.7 %collective-permute-start.15 = (bf16[512,768]{1,0:T(8,128)(2,1)S(1)}, bf16[512,768]{1,0:T(8,128)(2,1)S(1)}, u32[]{:S(2)}, u32[]{:S(2)}) collective-permute-start(bf16[512,768]{1,0:T(8,128)(2,1)S(1)} %slice.9), channel_id=1, source_target_pairs={{0,24},{1,193},{2,26},{3,195},{4,28},{5,197},{6,30},{7,199},{8,16}... | collective-permute-start | bytes 2359304 | tf_op jit(solution)/shard_map/ppermute | solution.py:57
  100.7 13.2 %collective-permute-start.19 = (f32[384,128]{1,0:T(8,128)S(1)}, f32[384,128]{1,0:T(8,128)S(1)}, u32[]{:S(2)}, u32[]{:S(2)}) collective-permute-start(f32[384,128]{1,0:T(8,128)S(1)} %get-tuple-element.10), channel_id=1, source_target_pairs={{0,4},{1,5},{2,6},{3,7},{4,32},{5,33},{6,34},{7,35},{8,12},{9,13},... | collective-permute-start | bytes 589832 | tf_op jit(solution)/shard_map/ppermute | solution.py:57
  100.9 23.1 %collective-permute-start.17 = (f32[768,128]{1,0:T(8,128)S(1)}, f32[768,128]{1,0:T(8,128)S(1)}, u32[]{:S(2)}, u32[]{:S(2)}) collective-permute-start(f32[768,128]{1,0:T(8,128)S(1)} %get-tuple-element.8), channel_id=1, source_target_pairs={{0,2},{1,3},{2,4},{3,5},{4,6},{5,7},{6,32},{7,33},{8,10},{9,11},{1... | collective-permute-start | bytes 1179656 | tf_op jit(solution)/shard_map/ppermute | solution.py:57
  102.5 21.6 %collective-permute-start.18 = (f32[768,128]{1,0:T(8,128)S(1)}, f32[768,128]{1,0:T(8,128)S(1)}, u32[]{:S(2)}, u32[]{:S(2)}) collective-permute-start(f32[768,128]{1,0:T(8,128)S(1)} %get-tuple-element.9), channel_id=1, source_target_pairs={{0,38},{1,39},{2,0},{3,1},{4,2},{5,3},{6,4},{7,5},{8,46},{9,47},{1... | collective-permute-start | bytes 1179656 | tf_op jit(solution)/shard_map/ppermute | solution.py:57
  113.9 10.2 %collective-permute-start.20 = (f32[384,128]{1,0:T(8,128)S(1)}, f32[384,128]{1,0:T(8,128)S(1)}, u32[]{:S(2)}, u32[]{:S(2)}) collective-permute-start(f32[384,128]{1,0:T(8,128)S(1)} %get-tuple-element.11), channel_id=1, source_target_pairs={{0,36},{1,37},{2,38},{3,39},{4,0},{5,1},{6,2},{7,3},{8,44},{9,45},... | collective-permute-start | bytes 589832 | tf_op jit(solution)/shard_map/ppermute | solution.py:57

commit v9 on v8

--- a/solution.py
+++ b/solution.py
@@ -64,6 +64,8 @@
 def products_kernel(kept, weight, near, far, *refs):
     h, l, c = here()
     turned = refs[-1]
+    if not kept:
+        refs = refs[1:]
     turned[0] = near[...].T
     turned[1] = far[...].T
     depth = near.shape[1]
@@ -90,9 +92,11 @@
                 refs[4 + half][...] = total
 
 
-def products(weight, near, far, *taken):
+def products(weight, near, far, *taken, after=None):
     tokens, depth = near.shape
     kept = bool(taken)
+    if after is not None:
+        taken = (after,)
     if kept:
         rows = [depth, depth, depth, depth // 2, depth // 2]
         shapes = [jax.ShapeDtypeStruct((n, tokens), F32) for n in rows]
@@ -101,7 +105,7 @@
     return pl.pallas_call(
         functools.partial(products_kernel, kept),
         out_shape=shapes,
-        in_specs=[VMEM] * (3 + kept),
+        in_specs=[VMEM] * (3 + len(taken)),
         out_specs=[VMEM] * len(shapes),
         scratch_shapes=[pltpu.VMEM((2, depth, tokens), BF16)],
         compiler_params=pltpu.CompilerParams(vmem_limit_bytes=20 * MIB),
@@ -111,6 +115,10 @@
             transcendentals=0,
         ),
     )(weight, near, far, *taken)
+
+
+def touch_kernel(weight, out):
+    out[...] = weight[pl.ds(0, 16), pl.ds(0, 128)]
 
 
 def finish_kernel(home, before, after, two_before, two_after, out):
@@ -169,10 +177,14 @@
     far_cot = send(cotangent, ring(4))
     pair = jnp.concatenate([cotangent, far_cot])
     first = [send(pair, crosswise(k, True)) for k in others]
-    row = jnp.concatenate([*first, pair])
-    one, three = (send(row, crosswise(k, False)) for k in (1, 3))
-    cut = 4 * tokens
-    two = [send(three[:cut], crosswise(1, False)), send(one[cut:], crosswise(3, False))]
+    low_half = jnp.concatenate(first[:2])
+    high_half = jnp.concatenate([first[2], pair])
+    low3 = send(low_half, crosswise(3, False))
+    high1 = send(high_half, crosswise(1, False))
+    high3 = send(high_half, crosswise(3, False))
+    low1 = send(low_half, crosswise(1, False))
+    low2 = send(low3, crosswise(1, False))
+    high2 = send(high1, crosswise(3, False))
 
     turned = context.T.reshape(4, quarter, tokens)
     block = jnp.stack(
@@ -187,7 +199,15 @@
     swap = lambda x, h, y, l, c: (x, h, y, l, 1 - c)
     other = send(own, swap)
 
-    (given,) = products(out_weight, cotangent, far_cot)
+    corner = pl.pallas_call(
+        touch_kernel,
+        out_shape=jax.ShapeDtypeStruct((16, 128), BF16),
+        in_specs=[VMEM],
+        out_specs=VMEM,
+        compiler_params=pltpu.CompilerParams(vmem_limit_bytes=12 * MIB),
+        cost_estimate=pl.CostEstimate(flops=0, bytes_accessed=8192, transcendentals=0),
+    )(out_weight)
+    (given,) = products(out_weight, cotangent, far_cot, after=corner)
     taken = send(given, swap)
     at_home, after, before, skip_up, skip_down = products(out_weight, cotangent, far_cot, taken)
     from_before = send(after, ring(1))
@@ -196,19 +216,14 @@
     from_two_after = send(skip_down, ring(-2))
 
     early = [(k, 0, k, tokens, k, 0) for k in range(4)]
-    late = [
-        (a, at_row, a, at_row + tokens, i, k)
-        for a, k in ((0, 1), (1, 3))
-        for i in range(4)
-        for at_row in (2 * tokens * ((i + 3) % 4),)
-    ]
-    last = [
-        (a, at_row, a, at_row + tokens, i, 2)
-        for a, at_row, i in ((0, 0, 1), (0, 2 * tokens, 2), (1, 0, 3), (1, 2 * tokens, 0))
+    halves = lambda a, k: [
+        (a + n // 2, deep, a + n // 2, deep + tokens, i, k)
+        for n, i in enumerate((1, 2, 3, 0))
+        for deep in (n % 2 * 2 * tokens,)
     ]
     total = weight_part(early, own, other, [pair] + first)
-    total = weight_part(late, own, other, [one, three], total)
-    grad_weight = weight_part(last, own, other, two, total)
+    total = weight_part(halves(0, 1) + halves(2, 3), own, other, [low1, high1, low3, high3], total)
+    grad_weight = weight_part(halves(0, 2), own, other, [low2, high2], total)
     grad_context = pl.pallas_call(
         finish_kernel,
         out_shape=jax.ShapeDtypeStruct((tokens, width), BF16),

time: 127 us -> 106 us (0.83)
  the two profiles are of different devices: /device:TPU:3 before, /device:TPU:1 now
where the time goes in v9:
time: 106 us
  starting transfers between devices  48.9 us (46%)
  waiting for transfers between devices  42.7 us (40%)
  local copies, waits for them, and re-layouts  6.82 us (6%)
  Pallas kernels  6.46 us (6%)
    ppermute x23, starting transfers between devices, send(): return lax.ppermute(array, AXES, pairs(route))  48.9 us
    ppermute x23, waiting for transfers between devices, send(): return lax.ppermute(array, AXES, pairs(route))  42.7 us
    unnamed x10, local copies, waits for them, and re-layouts  5.67 us
    pallas_call x2, Pallas kernels, products(): pl.pallas_call(functools.partial(products_kernel, kept), out_shape=shapes...  3.06 us
    pallas_call x3, Pallas kernels, weight_part(): pl.pallas_call(functools.partial(weight_kernel, items), out_shape=jax.Sha...  2.58 us
  transfers between devices with their start and end apart: 23, of which 7 were waited for; matrix products, arithmetic and copies ran while one was open for 2% of the time, Pallas kernels for 5%

profile of v9, /device:TPU:1, one launch (start us, length us, event | category | flops | bytes accessed | tf_op | source)
XLA Modules:
  0.0 105.9 jit_solution(7308202160172210669)
XLA Ops:
  0.6 7.8 %collective-permute-start.8 = (bf16[128,768]{1,0:T(8,128)(2,1)}, bf16[128,768]{1,0:T(8,128)(2,1)S(1)}, u32[]{:S(2)}, u32[]{:S(2)}) collective-permute-start(bf16[128,768]{1,0:T(8,128)(2,1)} %near.3), channel_id=1, source_target_pairs={{0,32},{1,33},{2,34},{3,35},{4,36},{5,37},{6,38},{7,39},{8,40},{9,... | collective-permute-start | bytes 589832 | tf_op jit(solution)/shard_map/ppermute | solution.py:57
  8.4 1.0 constant_dynamic-update-slice_fusion.1
  9.4 3.4 %collective-permute-done.8.far = bf16[128,768]{1,0:T(8,128)(2,1)S(1)} collective-permute-done((bf16[128,768]{1,0:T(8,128)(2,1)}, bf16[128,768]{1,0:T(8,128)(2,1)S(1)}, u32[]{:S(2)}, u32[]{:S(2)}) %collective-permute-start.8) | collective-permute-done | bytes 196640 | tf_op jit(solution)/shard_map/ppermute | solution.py:57
  12.8 1.8 %collective-permute-start.9 = (bf16[256,768]{1,0:T(8,128)(2,1)S(1)}, bf16[256,768]{1,0:T(8,128)(2,1)S(1)}, u32[]{:S(2)}, u32[]{:S(2)}) collective-permute-start(bf16[256,768]{1,0:T(8,128)(2,1)S(1)} %constant_dynamic-update-slice_fusion.refs_0_), channel_id=1, source_target_pairs={{0,64},{1,9},{2,66},{3,11},{4,68},{5,13},{6,70},{7,15},{8,72},{9,1... | collective-permute-start | bytes 1179656 | tf_op jit(solution)/shard_map/ppermute | solution.py:57
  14.7 1.1 %copy.5 = bf16[768,128]{1,0:T(8,128)(2,1)S(1)} copy(bf16[768,128]{0,1:T(8,128)(2,1)} %bitcast.20) | data formatting | bytes 393216 | tf_op jit(solution)/shard_map/transpose | solution.py:189
  15.8 2.7 %collective-permute-start.10 = (bf16[256,768]{1,0:T(8,128)(2,1)S(1)}, bf16[256,768]{1,0:T(8,128)(2,1)S(1)}, u32[]{:S(2)}, u32[]{:S(2)}) collective-permute-start(bf16[256,768]{1,0:T(8,128)(2,1)S(1)} %constant_dynamic-update-slice_fusion.refs_0_), channel_id=1, source_target_pairs={{0,128},{1,17},{2,130},{3,19},{4,132},{5,21},{6,134},{7,23},{8,136... | collective-permute-start | bytes 1179656 | tf_op jit(solution)/shard_map/ppermute | solution.py:57
  18.5 0.1 collective-permute-start
  18.6 1.0 collective-permute-start.1
  19.6 2.9 %collective-permute-start.2 = (bf16[192,128]{1,0:T(8,128)(2,1)S(1)}, bf16[192,128]{1,0:T(8,128)(2,1)S(1)}, u32[]{:S(2)}, u32[]{:S(2)}) collective-permute-start(bf16[192,128]{1,0:T(8,128)(2,1)S(1)} %get-tuple-element.13), channel_id=1, source_target_pairs={{0,24},{1,25},{2,26},{3,27},{4,28},{5,29},{6,30},{7,31},{8,16},{9,... | collective-permute-start | bytes 147464 | tf_op jit(solution)/shard_map/ppermute | solution.py:57
  22.4 3.7 %copy-done = bf16[6144,768]{1,0:T(8,128)(2,1)S(1)} copy-done((bf16[6144,768]{1,0:T(8,128)(2,1)S(1)}, bf16[6144,768]{1,0:T(8,128)(2,1)}, u32[]{:S(2)}) %copy-start) | copy-done | bytes 9437208
  26.1 0.0 collective-permute-done
  26.1 2.7 %collective-permute-start.13 = (bf16[256,768]{1,0:T(8,128)(2,1)S(1)}, bf16[256,768]{1,0:T(8,128)(2,1)S(1)}, u32[]{:S(2)}, u32[]{:S(2)}) collective-permute-start(bf16[256,768]{1,0:T(8,128)(2,1)S(1)} %constant_dynamic-update-slice_fusion.refs_0_), channel_id=1, source_target_pairs={{0,192},{1,25},{2,194},{3,27},{4,196},{5,29},{6,198},{7,31},{8,200... | collective-permute-start | bytes 1179656 | tf_op jit(solution)/shard_map/ppermute | solution.py:57
  28.9 0.9 copy-done.1
  29.8 1.5 %shard_map.54 = f32[4,768,128]{2,1,0:T(8,128)S(1)} custom-call(bf16[6144,768]{1,0:T(8,128)(2,1)S(1)} %copy-done.1, bf16[128,768]{1,0:T(8,128)(2,1)S(1)} %copy-done.2, bf16[128,768]{1,0:T(8,128)(2,1)S(1)} %collective-permute-done.8.far, bf16[16,128]{1,0:T(8,128)(2,1)S(1)} %shard_map.53.refs_0_), custom_call_target="tpu_custom_call" | custom-call | flops 603979776 | bytes 6291456 | tf_op jit(solution)/shard_map/pallas_call | solution.py:105
  31.3 0.0 collective-permute-done.1
  31.3 2.6 %collective-permute-start.18 = (f32[4,768,128]{2,1,0:T(8,128)S(1)}, f32[4,768,128]{2,1,0:T(8,128)S(1)}, u32[]{:S(2)}, u32[]{:S(2)}) collective-permute-start(f32[4,768,128]{2,1,0:T(8,128)S(1)} %shard_map.54), channel_id=1, source_target_pairs={{0,1},{1,0},{2,3},{3,2},{4,5},{5,4},{6,7},{7,6},{8,9},{9,8},{10,11... | collective-permute-start | bytes 4718600 | tf_op jit(solution)/shard_map/ppermute | solution.py:57
  33.9 0.0 collective-permute-done.2
  34.0 10.6 %collective-permute-start.3 = (bf16[4,192,128]{2,1,0:T(8,128)(2,1)S(1)}, bf16[4,192,128]{2,1,0:T(8,128)(2,1)S(1)}, u32[]{:S(2)}, u32[]{:S(2)}) collective-permute-start(bf16[4,192,128]{2,1,0:T(8,128)(2,1)S(1)} %pad_maximum_fusion.1), channel_id=1, source_target_pairs={{0,0},{1,32},{2,66},{3,98},{4,132},{5,164},{6,198},{7,230},{8,8},{... | collective-permute-start | bytes 589832 | tf_op jit(solution)/shard_map/ppermute | solution.py:57
  44.6 0.0 collective-permute-done.9.refs_1_
  44.6 0.0 collective-permute-done.10.refs_2_
  44.7 0.7 collective-permute-start.11
  45.3 0.0 collective-permute-done.13.refs_3_
  45.4 1.6 %collective-permute-start.14 = (bf16[512,768]{1,0:T(8,128)(2,1)S(1)}, bf16[512,768]{1,0:T(8,128)(2,1)S(1)}, u32[]{:S(2)}, u32[]{:S(2)}) collective-permute-start(bf16[512,768]{1,0:T(8,128)(2,1)S(1)} %constant_dynamic-update-slice_fusion.4), channel_id=1, source_target_pairs={{0,8},{1,65},{2,10},{3,67},{4,12},{5,69},{6,14},{7,71},{8,0},{9,73... | collective-permute-start | bytes 2359304 | tf_op jit(solution)/shard_map/ppermute | solution.py:57
  47.0 1.0 collective-permute-done.3
  48.0 5.0 %collective-permute-start.5 = (bf16[4,192,128]{2,1,0:T(8,128)(2,1)S(1)}, bf16[4,192,128]{2,1,0:T(8,128)(2,1)S(1)}, u32[]{:S(2)}, u32[]{:S(2)}) collective-permute-start(bf16[4,192,128]{2,1,0:T(8,128)(2,1)S(1)} %collective-permute-done.3), channel_id=1, source_target_pairs={{0,4},{1,5},{2,6},{3,7},{4,0},{5,1},{6,2},{7,3},{8,12},{9,13},{10,... | collective-permute-start | bytes 589832 | tf_op jit(solution)/shard_map/ppermute | solution.py:57
  53.0 0.8 collective-permute-start.6
  53.8 12.6 %collective-permute-done.5 = bf16[4,192,128]{2,1,0:T(8,128)(2,1)S(1)} collective-permute-done((bf16[4,192,128]{2,1,0:T(8,128)(2,1)S(1)}, bf16[4,192,128]{2,1,0:T(8,128)(2,1)S(1)}, u32[]{:S(2)}, u32[]{:S(2)}) %collective-permute-start.5) | collective-permute-done | bytes 196640 | tf_op jit(solution)/shard_map/ppermute | solution.py:57
  66.5 6.0 %collective-permute-done.4 = bf16[4,192,128]{2,1,0:T(8,128)(2,1)S(1)} collective-permute-done((bf16[4,192,128]{2,1,0:T(8,128)(2,1)S(1)}, bf16[4,192,128]{2,1,0:T(8,128)(2,1)S(1)}, u32[]{:S(2)}, u32[]{:S(2)}) %collective-permute-start.4) | collective-permute-done | bytes 196640 | tf_op jit(solution)/shard_map/ppermute | solution.py:57
  72.5 0.1 pad_maximum_fusion.own
  72.6 1.4 %collective-permute-start.7 = (bf16[4,4,192,128]{3,2,1,0:T(8,128)(2,1)S(1)}, bf16[4,4,192,128]{3,2,1,0:T(8,128)(2,1)S(1)}, u32[]{:S(2)}, u32[]{:S(2)}) collective-permute-start(bf16[4,4,192,128]{3,2,1,0:T(8,128)(2,1)S(1)} %pad_maximum_fusion.own), channel_id=1, source_target_pairs={{0,1},{1,0},{2,3},{3,2},{4,5},{5,4},{6,7},{7,6},{8,9},{9,8},{10,11... | collective-permute-start | bytes 2359304 | tf_op jit(solution)/shard_map/ppermute | solution.py:57
  74.0 0.0 collective-permute-done.14.refs_1_
  74.0 1.5 %collective-permute-start.12 = (bf16[512,768]{1,0:T(8,128)(2,1)S(1)}, bf16[512,768]{1,0:T(8,128)(2,1)S(1)}, u32[]{:S(2)}, u32[]{:S(2)}) collective-permute-start(bf16[512,768]{1,0:T(8,128)(2,1)S(1)} %collective-permute-done.11.refs_2_), channel_id=1, source_target_pairs={{0,8},{1,65},{2,10},{3,67},{4,12},{5,69},{6,14},{7,71},{8,0},{9,73... | collective-permute-start | bytes 2359304 | tf_op jit(solution)/shard_map/ppermute | solution.py:57
  75.5 0.0 collective-permute-done.18.refs_0_
  75.5 2.0 %collective-permute-start.15 = (bf16[512,768]{1,0:T(8,128)(2,1)S(1)}, bf16[512,768]{1,0:T(8,128)(2,1)S(1)}, u32[]{:S(2)}, u32[]{:S(2)}) collective-permute-start(bf16[512,768]{1,0:T(8,128)(2,1)S(1)} %collective-permute-done.14.refs_1_), channel_id=1, source_target_pairs={{0,24},{1,193},{2,26},{3,195},{4,28},{5,197},{6,30},{7,199},{8,16}... | collective-permute-start | bytes 2359304 | tf_op jit(solution)/shard_map/ppermute | solution.py:57
  77.5 1.5 %shard_map.55 = (f32[768,128]{1,0:T(8,128)S(1)}, f32[768,128]{1,0:T(8,128)S(1)}, f32[768,128]{1,0:T(8,128)S(1)}, f32[384,128]{1,0:T(8,128)S(1)}, f32[384,128]{1,0:T(8,128)S(1)}) custom-call(bf16[6144,768]{1,0:T(8,128)(2,1)S(1)} %copy-done.1, bf16[128,768]{1,0:T(8,128)(2,1)S(1)} %copy-done.2, bf16[128,768]{1,0:T(8,128)(2,1)S(1)} %collective-permute-done.8.far, ...), custom_call_target="tpu_custom_call" | custom-call | flops 603979776 | bytes 6291456 | tf_op jit(solution)/shard_map/pallas_call | solution.py:105
  79.1 0.1 collective-permute-start.19
  79.2 5.9 %collective-permute-done.16.refs_0_ = bf16[512,768]{1,0:T(8,128)(2,1)S(1)} collective-permute-done((bf16[512,768]{1,0:T(8,128)(2,1)S(1)}, bf16[512,768]{1,0:T(8,128)(2,1)S(1)}, u32[]{:S(2)}, u32[]{:S(2)}) %collective-permute-start.16) | collective-permute-done | bytes 786464 | tf_op jit(solution)/shard_map/ppermute | solution.py:57
  85.1 2.1 %collective-permute-start.20 = (f32[768,128]{1,0:T(8,128)S(1)}, f32[768,128]{1,0:T(8,128)S(1)}, u32[]{:S(2)}, u32[]{:S(2)}) collective-permute-start(f32[768,128]{1,0:T(8,128)S(1)} %get-tuple-element.9), channel_id=1, source_target_pairs={{0,38},{1,39},{2,0},{3,1},{4,2},{5,3},{6,4},{7,5},{8,46},{9,47},{1... | collective-permute-start | bytes 1179656 | tf_op jit(solution)/shard_map/ppermute | solution.py:57
  87.2 0.0 collective-permute-done.17.refs_3_
  87.2 0.0 collective-permute-start.21
  87.2 6.3 %collective-permute-done.12.refs_0_ = bf16[512,768]{1,0:T(8,128)(2,1)S(1)} collective-permute-done((bf16[512,768]{1,0:T(8,128)(2,1)S(1)}, bf16[512,768]{1,0:T(8,128)(2,1)S(1)}, u32[]{:S(2)}, u32[]{:S(2)}) %collective-permute-start.12) | collective-permute-done | bytes 786464 | tf_op jit(solution)/shard_map/ppermute | solution.py:57
  93.5 1.5 %collective-permute-start.22 = (f32[384,128]{1,0:T(8,128)S(1)}, f32[384,128]{1,0:T(8,128)S(1)}, u32[]{:S(2)}, u32[]{:S(2)}) collective-permute-start(f32[384,128]{1,0:T(8,128)S(1)} %get-tuple-element.11), channel_id=1, source_target_pairs={{0,36},{1,37},{2,38},{3,39},{4,0},{5,1},{6,2},{7,3},{8,44},{9,45},... | collective-permute-start | bytes 589832 | tf_op jit(solution)/shard_map/ppermute | solution.py:57
  95.1 0.5 shard_map.50.refs_4_
  95.6 0.8 shard_map.51.refs_2_
  96.4 1.3 %shard_map.52 = f32[192,768]{1,0:T(8,128)} custom-call(bf16[4,4,192,128]{3,2,1,0:T(8,128)(2,1)S(1)} %pad_maximum_fusion.own, bf16[4,4,192,128]{3,2,1,0:T(8,128)(2,1)S(1)} %collective-permute-done.7.other, bf16[512,768]{1,0:T(8,128)(2,1)S(1)} %collective-permute-done.12.refs_0_, bf16[512,768]{1,0:T(8,128)(2,1)S(1)} %collective-permute-done.15.refs_1_, ...), custom_call_target="tpu_custom_call" | custom-call | flops 301989888 | bytes 3145728 | tf_op jit(solution)/shard_map/pallas_call | solution.py:156
  97.7 0.0 collective-permute-done.21.two_before
  97.7 7.4 %collective-permute-done.22.two_after = f32[384,128]{1,0:T(8,128)S(1)} collective-permute-done((f32[384,128]{1,0:T(8,128)S(1)}, f32[384,128]{1,0:T(8,128)S(1)}, u32[]{:S(2)}, u32[]{:S(2)}) %collective-permute-start.22) | collective-permute-done | bytes 196640 | tf_op jit(solution)/shard_map/ppermute | solution.py:57
  105.1 0.8 shard_map.56
  (22 shorter events, 0.2 us)
Async XLA Ops:
  0.6 12.2 %collective-permute-start.8 = (bf16[128,768]{1,0:T(8,128)(2,1)}, bf16[128,768]{1,0:T(8,128)(2,1)S(1)}, u32[]{:S(2)}, u32[]{:S(2)}) collective-permute-start(bf16[128,768]{1,0:T(8,128)(2,1)} %near.3), channel_id=1, source_target_pairs={{0,32},{1,33},{2,34},{3,35},{4,36},{5,37},{6,38},{7,39},{8,40},{9,... | collective-permute-start | bytes 589832 | tf_op jit(solution)/shard_map/ppermute | solution.py:57
  12.8 31.7 %collective-permute-start.9 = (bf16[256,768]{1,0:T(8,128)(2,1)S(1)}, bf16[256,768]{1,0:T(8,128)(2,1)S(1)}, u32[]{:S(2)}, u32[]{:S(2)}) collective-permute-start(bf16[256,768]{1,0:T(8,128)(2,1)S(1)} %constant_dynamic-update-slice_fusion.refs_0_), channel_id=1, source_target_pairs={{0,64},{1,9},{2,66},{3,11},{4,68},{5,13},{6,70},{7,15},{8,72},{9,1... | collective-permute-start | bytes 1179656 | tf_op jit(solution)/shard_map/ppermute | solution.py:57
  15.8 28.9 %collective-permute-start.10 = (bf16[256,768]{1,0:T(8,128)(2,1)S(1)}, bf16[256,768]{1,0:T(8,128)(2,1)S(1)}, u32[]{:S(2)}, u32[]{:S(2)}) collective-permute-start(bf16[256,768]{1,0:T(8,128)(2,1)S(1)} %constant_dynamic-update-slice_fusion.refs_0_), channel_id=1, source_target_pairs={{0,128},{1,17},{2,130},{3,19},{4,132},{5,21},{6,134},{7,23},{8,136... | collective-permute-start | bytes 1179656 | tf_op jit(solution)/shard_map/ppermute | solution.py:57
  18.5 10.4 %copy-start.2 = (bf16[128,768]{1,0:T(8,128)(2,1)S(1)}, bf16[128,768]{1,0:T(8,128)(2,1)}, u32[]{:S(2)}) copy-start(bf16[128,768]{1,0:T(8,128)(2,1)} %near.3) | copy-start | bytes 589828
  18.5 7.6 %collective-permute-start = (bf16[192,128]{1,0:T(8,128)(2,1)S(1)}, bf16[192,128]{1,0:T(8,128)(2,1)S(1)}, u32[]{:S(2)}, u32[]{:S(2)}) collective-permute-start(bf16[192,128]{1,0:T(8,128)(2,1)S(1)} %get-tuple-element.15), channel_id=1, source_target_pairs={{0,8},{1,9},{2,10},{3,11},{4,12},{5,13},{6,14},{7,15},{8,0},{9,1},... | collective-permute-start | bytes 147464 | tf_op jit(solution)/shard_map/ppermute | solution.py:57
  18.6 12.7 %collective-permute-start.1 = (bf16[192,128]{1,0:T(8,128)(2,1)S(1)}, bf16[192,128]{1,0:T(8,128)(2,1)S(1)}, u32[]{:S(2)}, u32[]{:S(2)}) collective-permute-start(bf16[192,128]{1,0:T(8,128)(2,1)S(1)} %get-tuple-element.14), channel_id=1, source_target_pairs={{0,16},{1,17},{2,18},{3,19},{4,20},{5,21},{6,22},{7,23},{8,24},{9,... | collective-permute-start | bytes 147464 | tf_op jit(solution)/shard_map/ppermute | solution.py:57
  19.6 14.4 %collective-permute-start.2 = (bf16[192,128]{1,0:T(8,128)(2,1)S(1)}, bf16[192,128]{1,0:T(8,128)(2,1)S(1)}, u32[]{:S(2)}, u32[]{:S(2)}) collective-permute-start(bf16[192,128]{1,0:T(8,128)(2,1)S(1)} %get-tuple-element.13), channel_id=1, source_target_pairs={{0,24},{1,25},{2,26},{3,27},{4,28},{5,29},{6,30},{7,31},{8,16},{9,... | collective-permute-start | bytes 147464 | tf_op jit(solution)/shard_map/ppermute | solution.py:57
  22.4 3.7 %copy-start = (bf16[6144,768]{1,0:T(8,128)(2,1)S(1)}, bf16[6144,768]{1,0:T(8,128)(2,1)}, u32[]{:S(2)}) copy-start(bf16[6144,768]{1,0:T(8,128)(2,1)} %weight.5) | copy-start | bytes 28311556
  26.1 3.7 %copy-start.1 = (bf16[6144,768]{1,0:T(8,128)(2,1)S(1)}, bf16[6144,768]{1,0:T(8,128)(2,1)}, u32[]{:S(2)}) copy-start(bf16[6144,768]{1,0:T(8,128)(2,1)} %weight.5) | copy-start | bytes 28311556
  26.1 19.2 %collective-permute-start.13 = (bf16[256,768]{1,0:T(8,128)(2,1)S(1)}, bf16[256,768]{1,0:T(8,128)(2,1)S(1)}, u32[]{:S(2)}, u32[]{:S(2)}) collective-permute-start(bf16[256,768]{1,0:T(8,128)(2,1)S(1)} %constant_dynamic-update-slice_fusion.refs_0_), channel_id=1, source_target_pairs={{0,192},{1,25},{2,194},{3,27},{4,196},{5,29},{6,198},{7,31},{8,200... | collective-permute-start | bytes 1179656 | tf_op jit(solution)/shard_map/ppermute | solution.py:57
  31.3 44.2 %collective-permute-start.18 = (f32[4,768,128]{2,1,0:T(8,128)S(1)}, f32[4,768,128]{2,1,0:T(8,128)S(1)}, u32[]{:S(2)}, u32[]{:S(2)}) collective-permute-start(f32[4,768,128]{2,1,0:T(8,128)S(1)} %shard_map.54), channel_id=1, source_target_pairs={{0,1},{1,0},{2,3},{3,2},{4,5},{5,4},{6,7},{7,6},{8,9},{9,8},{10,11... | collective-permute-start | bytes 4718600 | tf_op jit(solution)/shard_map/ppermute | solution.py:57
  34.0 14.1 %collective-permute-start.3 = (bf16[4,192,128]{2,1,0:T(8,128)(2,1)S(1)}, bf16[4,192,128]{2,1,0:T(8,128)(2,1)S(1)}, u32[]{:S(2)}, u32[]{:S(2)}) collective-permute-start(bf16[4,192,128]{2,1,0:T(8,128)(2,1)S(1)} %pad_maximum_fusion.1), channel_id=1, source_target_pairs={{0,0},{1,32},{2,66},{3,98},{4,132},{5,164},{6,198},{7,230},{8,8},{... | collective-permute-start | bytes 589832 | tf_op jit(solution)/shard_map/ppermute | solution.py:57
  44.7 29.3 %collective-permute-start.11 = (bf16[512,768]{1,0:T(8,128)(2,1)S(1)}, bf16[512,768]{1,0:T(8,128)(2,1)S(1)}, u32[]{:S(2)}, u32[]{:S(2)}) collective-permute-start(bf16[512,768]{1,0:T(8,128)(2,1)S(1)} %constant_dynamic-update-slice_fusion.2), channel_id=1, source_target_pairs={{0,24},{1,193},{2,26},{3,195},{4,28},{5,197},{6,30},{7,199},{8,16}... | collective-permute-start | bytes 2359304 | tf_op jit(solution)/shard_map/ppermute | solution.py:57
  45.4 28.6 %collective-permute-start.14 = (bf16[512,768]{1,0:T(8,128)(2,1)S(1)}, bf16[512,768]{1,0:T(8,128)(2,1)S(1)}, u32[]{:S(2)}, u32[]{:S(2)}) collective-permute-start(bf16[512,768]{1,0:T(8,128)(2,1)S(1)} %constant_dynamic-update-slice_fusion.4), channel_id=1, source_target_pairs={{0,8},{1,65},{2,10},{3,67},{4,12},{5,69},{6,14},{7,71},{8,0},{9,73... | collective-permute-start | bytes 2359304 | tf_op jit(solution)/shard_map/ppermute | solution.py:57
  48.0 18.4 %collective-permute-start.5 = (bf16[4,192,128]{2,1,0:T(8,128)(2,1)S(1)}, bf16[4,192,128]{2,1,0:T(8,128)(2,1)S(1)}, u32[]{:S(2)}, u32[]{:S(2)}) collective-permute-start(bf16[4,192,128]{2,1,0:T(8,128)(2,1)S(1)} %collective-permute-done.3), channel_id=1, source_target_pairs={{0,4},{1,5},{2,6},{3,7},{4,0},{5,1},{6,2},{7,3},{8,12},{9,13},{10,... | collective-permute-start | bytes 589832 | tf_op jit(solution)/shard_map/ppermute | solution.py:57
  53.0 13.5 %collective-permute-start.6 = (bf16[4,192,128]{2,1,0:T(8,128)(2,1)S(1)}, bf16[4,192,128]{2,1,0:T(8,128)(2,1)S(1)}, u32[]{:S(2)}, u32[]{:S(2)}) collective-permute-start(bf16[4,192,128]{2,1,0:T(8,128)(2,1)S(1)} %collective-permute-done.3), channel_id=1, source_target_pairs={{0,6},{1,7},{2,4},{3,5},{4,2},{5,3},{6,0},{7,1},{8,14},{9,15},{10,... | collective-permute-start | bytes 589832 | tf_op jit(solution)/shard_map/ppermute | solution.py:57
  66.5 6.0 %collective-permute-start.4 = (bf16[4,192,128]{2,1,0:T(8,128)(2,1)S(1)}, bf16[4,192,128]{2,1,0:T(8,128)(2,1)S(1)}, u32[]{:S(2)}, u32[]{:S(2)}) collective-permute-start(bf16[4,192,128]{2,1,0:T(8,128)(2,1)S(1)} %collective-permute-done.3), channel_id=1, source_target_pairs={{0,2},{1,3},{2,0},{3,1},{4,6},{5,7},{6,4},{7,5},{8,10},{9,11},{10,... | collective-permute-start | bytes 589832 | tf_op jit(solution)/shard_map/ppermute | solution.py:57
  72.6 6.4 %collective-permute-start.7 = (bf16[4,4,192,128]{3,2,1,0:T(8,128)(2,1)S(1)}, bf16[4,4,192,128]{3,2,1,0:T(8,128)(2,1)S(1)}, u32[]{:S(2)}, u32[]{:S(2)}) collective-permute-start(bf16[4,4,192,128]{3,2,1,0:T(8,128)(2,1)S(1)} %pad_maximum_fusion.own), channel_id=1, source_target_pairs={{0,1},{1,0},{2,3},{3,2},{4,5},{5,4},{6,7},{7,6},{8,9},{9,8},{10,11... | collective-permute-start | bytes 2359304 | tf_op jit(solution)/shard_map/ppermute | solution.py:57
  74.0 11.1 %collective-permute-start.16 = (bf16[512,768]{1,0:T(8,128)(2,1)S(1)}, bf16[512,768]{1,0:T(8,128)(2,1)S(1)}, u32[]{:S(2)}, u32[]{:S(2)}) collective-permute-start(bf16[512,768]{1,0:T(8,128)(2,1)S(1)} %constant_dynamic-update-slice_fusion.2), channel_id=1, source_target_pairs={{0,8},{1,65},{2,10},{3,67},{4,12},{5,69},{6,14},{7,71},{8,0},{9,73... | collective-permute-start | bytes 2359304 | tf_op jit(solution)/shard_map/ppermute | solution.py:57
  74.0 13.2 %collective-permute-start.17 = (bf16[512,768]{1,0:T(8,128)(2,1)S(1)}, bf16[512,768]{1,0:T(8,128)(2,1)S(1)}, u32[]{:S(2)}, u32[]{:S(2)}) collective-permute-start(bf16[512,768]{1,0:T(8,128)(2,1)S(1)} %constant_dynamic-update-slice_fusion.4), channel_id=1, source_target_pairs={{0,24},{1,193},{2,26},{3,195},{4,28},{5,197},{6,30},{7,199},{8,16}... | collective-permute-start | bytes 2359304 | tf_op jit(solution)/shard_map/ppermute | solution.py:57
  74.0 19.5 %collective-permute-start.12 = (bf16[512,768]{1,0:T(8,128)(2,1)S(1)}, bf16[512,768]{1,0:T(8,128)(2,1)S(1)}, u32[]{:S(2)}, u32[]{:S(2)}) collective-permute-start(bf16[512,768]{1,0:T(8,128)(2,1)S(1)} %collective-permute-done.11.refs_2_), channel_id=1, source_target_pairs={{0,8},{1,65},{2,10},{3,67},{4,12},{5,69},{6,14},{7,71},{8,0},{9,73... | collective-permute-start | bytes 2359304 | tf_op jit(solution)/shard_map/ppermute | solution.py:57
  75.5 20.8 %collective-permute-start.15 = (bf16[512,768]{1,0:T(8,128)(2,1)S(1)}, bf16[512,768]{1,0:T(8,128)(2,1)S(1)}, u32[]{:S(2)}, u32[]{:S(2)}) collective-permute-start(bf16[512,768]{1,0:T(8,128)(2,1)S(1)} %collective-permute-done.14.refs_1_), channel_id=1, source_target_pairs={{0,24},{1,193},{2,26},{3,195},{4,28},{5,197},{6,30},{7,199},{8,16}... | collective-permute-start | bytes 2359304 | tf_op jit(solution)/shard_map/ppermute | solution.py:57
  79.1 26.0 %collective-permute-start.19 = (f32[768,128]{1,0:T(8,128)S(1)}, f32[768,128]{1,0:T(8,128)S(1)}, u32[]{:S(2)}, u32[]{:S(2)}) collective-permute-start(f32[768,128]{1,0:T(8,128)S(1)} %get-tuple-element.8), channel_id=1, source_target_pairs={{0,2},{1,3},{2,4},{3,5},{4,6},{5,7},{6,32},{7,33},{8,10},{9,11},{1... | collective-permute-start | bytes 1179656 | tf_op jit(solution)/shard_map/ppermute | solution.py:57
  85.1 20.0 %collective-permute-start.20 = (f32[768,128]{1,0:T(8,128)S(1)}, f32[768,128]{1,0:T(8,128)S(1)}, u32[]{:S(2)}, u32[]{:S(2)}) collective-permute-start(f32[768,128]{1,0:T(8,128)S(1)} %get-tuple-element.9), channel_id=1, source_target_pairs={{0,38},{1,39},{2,0},{3,1},{4,2},{5,3},{6,4},{7,5},{8,46},{9,47},{1... | collective-permute-start | bytes 1179656 | tf_op jit(solution)/shard_map/ppermute | solution.py:57
  87.2 10.5 %collective-permute-start.21 = (f32[384,128]{1,0:T(8,128)S(1)}, f32[384,128]{1,0:T(8,128)S(1)}, u32[]{:S(2)}, u32[]{:S(2)}) collective-permute-start(f32[384,128]{1,0:T(8,128)S(1)} %get-tuple-element.10), channel_id=1, source_target_pairs={{0,4},{1,5},{2,6},{3,7},{4,32},{5,33},{6,34},{7,35},{8,12},{9,13},... | collective-permute-start | bytes 589832 | tf_op jit(solution)/shard_map/ppermute | solution.py:57
  93.5 11.5 %collective-permute-start.22 = (f32[384,128]{1,0:T(8,128)S(1)}, f32[384,128]{1,0:T(8,128)S(1)}, u32[]{:S(2)}, u32[]{:S(2)}) collective-permute-start(f32[384,128]{1,0:T(8,128)S(1)} %get-tuple-element.11), channel_id=1, source_target_pairs={{0,36},{1,37},{2,38},{3,39},{4,0},{5,1},{6,2},{7,3},{8,44},{9,45},... | collective-permute-start | bytes 589832 | tf_op jit(solution)/shard_map/ppermute | solution.py:57

commit v10 on v9

--- a/solution.py
+++ b/solution.py
@@ -177,14 +177,14 @@
     far_cot = send(cotangent, ring(4))
     pair = jnp.concatenate([cotangent, far_cot])
     first = [send(pair, crosswise(k, True)) for k in others]
-    low_half = jnp.concatenate(first[:2])
-    high_half = jnp.concatenate([first[2], pair])
-    low3 = send(low_half, crosswise(3, False))
-    high1 = send(high_half, crosswise(1, False))
-    high3 = send(high_half, crosswise(3, False))
-    low1 = send(low_half, crosswise(1, False))
-    low2 = send(low3, crosswise(1, False))
-    high2 = send(high1, crosswise(3, False))
+    half_a = jnp.concatenate([pair, first[0]])
+    half_b = jnp.concatenate([first[2], first[1]])
+    a1 = send(half_a, crosswise(1, False))
+    a3 = send(half_a, crosswise(3, False))
+    b3 = send(half_b, crosswise(3, False))
+    b1 = send(half_b, crosswise(1, False))
+    a2 = send(a3, crosswise(1, False))
+    b2 = send(b1, crosswise(3, False))
 
     turned = context.T.reshape(4, quarter, tokens)
     block = jnp.stack(
@@ -192,9 +192,10 @@
         + [send(at(turned, y ^ k), lambda x, h, y, l, c, k=k: (x, h, y ^ k, l, c)) for k in others]
     )
     mine = send(block, lambda x, h, y, l, c: (l, c, y, l ^ x, h))
-    gathered = [mine] + [
-        send(mine, lambda x, h, y, l, c, k=k: (x, h, y, l ^ k, c)) for k in (1, 2, 3)
-    ]
+    along = lambda k: lambda x, h, y, l, c: (x, h, y, l ^ k, c)
+    three_away = send(mine, along(3))
+    next_one = send(mine, along(1))
+    gathered = [mine, next_one, send(three_away, along(1)), three_away]
     own = jnp.stack(gathered)
     swap = lambda x, h, y, l, c: (x, h, y, l, 1 - c)
     other = send(own, swap)
@@ -218,12 +219,12 @@
     early = [(k, 0, k, tokens, k, 0) for k in range(4)]
     halves = lambda a, k: [
         (a + n // 2, deep, a + n // 2, deep + tokens, i, k)
-        for n, i in enumerate((1, 2, 3, 0))
+        for n, i in enumerate((0, 1, 3, 2))
         for deep in (n % 2 * 2 * tokens,)
     ]
     total = weight_part(early, own, other, [pair] + first)
-    total = weight_part(halves(0, 1) + halves(2, 3), own, other, [low1, high1, low3, high3], total)
-    grad_weight = weight_part(halves(0, 2), own, other, [low2, high2], total)
+    total = weight_part(halves(0, 1) + halves(2, 3), own, other, [a1, b1, a3, b3], total)
+    grad_weight = weight_part(halves(0, 2), own, other, [a2, b2], total)
     grad_context = pl.pallas_call(
         finish_kernel,
         out_shape=jax.ShapeDtypeStruct((tokens, width), BF16),

time: 106 us -> 103 us (0.972)
  the two profiles are of different devices: /device:TPU:1 before, /device:TPU:24 now
where the time goes in v10:
time: 103 us
  waiting for transfers between devices  43.7 us (42%)
  starting transfers between devices  41.9 us (41%)
  local copies, waits for them, and re-layouts  9.7 us (9%)
  Pallas kernels  6.44 us (6%)
    ppermute x23, waiting for transfers between devices, send(): return lax.ppermute(array, AXES, pairs(route))  43.7 us
    ppermute x23, starting transfers between devices, send(): return lax.ppermute(array, AXES, pairs(route))  41.9 us
    unnamed x8, local copies, waits for them, and re-layouts  8.5 us
    pallas_call x2, Pallas kernels, products(): pl.pallas_call(functools.partial(products_kernel, kept), out_shape=shapes...  3.06 us
    pallas_call x3, Pallas kernels, weight_part(): pl.pallas_call(functools.partial(weight_kernel, items), out_shape=jax.Sha...  2.55 us
  transfers between devices with their start and end apart: 23, of which 13 were waited for; matrix products, arithmetic and copies ran while one was open for 2% of the time, Pallas kernels for 5%

profile of v10, /device:TPU:24, one launch (start us, length us, event | category | flops | bytes accessed | tf_op | source)
XLA Modules:
  0.0 102.7 jit_solution(15135679503424443236)
XLA Ops:
  0.6 7.3 %collective-permute-start.8 = (bf16[128,768]{1,0:T(8,128)(2,1)}, bf16[128,768]{1,0:T(8,128)(2,1)S(1)}, u32[]{:S(2)}, u32[]{:S(2)}) collective-permute-start(bf16[128,768]{1,0:T(8,128)(2,1)} %near.3), channel_id=1, source_target_pairs={{0,32},{1,33},{2,34},{3,35},{4,36},{5,37},{6,38},{7,39},{8,40},{9,... | collective-permute-start | bytes 589832 | tf_op jit(solution)/shard_map/ppermute | solution.py:57
  7.9 1.0 constant_dynamic-update-slice_fusion.1
  8.9 4.2 %collective-permute-done.8.far = bf16[128,768]{1,0:T(8,128)(2,1)S(1)} collective-permute-done((bf16[128,768]{1,0:T(8,128)(2,1)}, bf16[128,768]{1,0:T(8,128)(2,1)S(1)}, u32[]{:S(2)}, u32[]{:S(2)}) %collective-permute-start.8) | collective-permute-done | bytes 196640 | tf_op jit(solution)/shard_map/ppermute | solution.py:57
  13.1 2.8 %collective-permute-start.12 = (bf16[256,768]{1,0:T(8,128)(2,1)S(1)}, bf16[256,768]{1,0:T(8,128)(2,1)S(1)}, u32[]{:S(2)}, u32[]{:S(2)}) collective-permute-start(bf16[256,768]{1,0:T(8,128)(2,1)S(1)} %get-tuple-element.12.refs_0_), channel_id=1, source_target_pairs={{0,192},{1,25},{2,194},{3,27},{4,196},{5,29},{6,198},{7,31},{8,200... | collective-permute-start | bytes 1179656 | tf_op jit(solution)/shard_map/ppermute | solution.py:57
  16.0 1.1 %copy.5 = bf16[768,128]{1,0:T(8,128)(2,1)S(1)} copy(bf16[768,128]{0,1:T(8,128)(2,1)} %bitcast.20) | data formatting | bytes 393216 | tf_op jit(solution)/shard_map/transpose | solution.py:189
  17.1 0.0 copy-start
  17.1 3.7 %copy-done = bf16[6144,768]{1,0:T(8,128)(2,1)S(1)} copy-done((bf16[6144,768]{1,0:T(8,128)(2,1)S(1)}, bf16[6144,768]{1,0:T(8,128)(2,1)}, u32[]{:S(2)}) %copy-start) | copy-done | bytes 9437208
  20.8 0.8 collective-permute-start.13
  21.6 0.1 copy-done.2
  21.7 3.7 %copy-done.1 = bf16[6144,768]{1,0:T(8,128)(2,1)S(1)} copy-done((bf16[6144,768]{1,0:T(8,128)(2,1)S(1)}, bf16[6144,768]{1,0:T(8,128)(2,1)}, u32[]{:S(2)}) %copy-start.1) | copy-done | bytes 9437208
  25.4 1.5 %shard_map.54 = f32[4,768,128]{2,1,0:T(8,128)S(1)} custom-call(bf16[6144,768]{1,0:T(8,128)(2,1)S(1)} %copy-done.1, bf16[128,768]{1,0:T(8,128)(2,1)S(1)} %copy-done.2, bf16[128,768]{1,0:T(8,128)(2,1)S(1)} %collective-permute-done.8.far, bf16[16,128]{1,0:T(8,128)(2,1)S(1)} %shard_map.53.refs_0_), custom_call_target="tpu_custom_call" | custom-call | flops 603979776 | bytes 6291456 | tf_op jit(solution)/shard_map/pallas_call | solution.py:105
  26.9 0.1 collective-permute-start.18
  27.1 0.8 collective-permute-start
  27.9 0.9 collective-permute-start.1
  28.8 2.9 %collective-permute-done = bf16[192,128]{1,0:T(8,128)(2,1)S(1)} collective-permute-done((bf16[192,128]{1,0:T(8,128)(2,1)S(1)}, bf16[192,128]{1,0:T(8,128)(2,1)S(1)}, u32[]{:S(2)}, u32[]{:S(2)}) %collective-permute-start) | collective-permute-done | bytes 49184 | tf_op jit(solution)/shard_map/ppermute | solution.py:57
  31.8 0.1 collective-permute-start.2
  31.9 1.6 %collective-permute-done.1 = bf16[192,128]{1,0:T(8,128)(2,1)S(1)} collective-permute-done((bf16[192,128]{1,0:T(8,128)(2,1)S(1)}, bf16[192,128]{1,0:T(8,128)(2,1)S(1)}, u32[]{:S(2)}, u32[]{:S(2)}) %collective-permute-start.1) | collective-permute-done | bytes 49184 | tf_op jit(solution)/shard_map/ppermute | solution.py:57
  33.5 0.4 collective-permute-start.9
  33.9 3.2 %collective-permute-done.2 = bf16[192,128]{1,0:T(8,128)(2,1)S(1)} collective-permute-done((bf16[192,128]{1,0:T(8,128)(2,1)S(1)}, bf16[192,128]{1,0:T(8,128)(2,1)S(1)}, u32[]{:S(2)}, u32[]{:S(2)}) %collective-permute-start.2) | collective-permute-done | bytes 49184 | tf_op jit(solution)/shard_map/ppermute | solution.py:57
  37.1 0.7 collective-permute-start.3
  37.9 0.1 collective-permute-start.14
  38.0 3.3 %collective-permute-done.9.refs_1_ = bf16[256,768]{1,0:T(8,128)(2,1)S(1)} collective-permute-done((bf16[256,768]{1,0:T(8,128)(2,1)S(1)}, bf16[256,768]{1,0:T(8,128)(2,1)S(1)}, u32[]{:S(2)}, u32[]{:S(2)}) %collective-permute-start.9) | collective-permute-done | bytes 393248 | tf_op jit(solution)/shard_map/ppermute | solution.py:57
  41.3 1.6 %collective-permute-start.10 = (bf16[512,768]{1,0:T(8,128)(2,1)S(1)}, bf16[512,768]{1,0:T(8,128)(2,1)S(1)}, u32[]{:S(2)}, u32[]{:S(2)}) collective-permute-start(bf16[512,768]{1,0:T(8,128)(2,1)S(1)} %constant_dynamic-update-slice_fusion.2), channel_id=1, source_target_pairs={{0,24},{1,193},{2,26},{3,195},{4,28},{5,197},{6,30},{7,199},{8,16}... | collective-permute-start | bytes 2359304 | tf_op jit(solution)/shard_map/ppermute | solution.py:57
  42.9 12.9 %collective-permute-start.5 = (bf16[4,192,128]{2,1,0:T(8,128)(2,1)S(1)}, bf16[4,192,128]{2,1,0:T(8,128)(2,1)S(1)}, u32[]{:S(2)}, u32[]{:S(2)}) collective-permute-start(bf16[4,192,128]{2,1,0:T(8,128)(2,1)S(1)} %collective-permute-done.3), channel_id=1, source_target_pairs={{0,6},{1,7},{2,4},{3,5},{4,2},{5,3},{6,0},{7,1},{8,14},{9,15},{10,... | collective-permute-start | bytes 589832 | tf_op jit(solution)/shard_map/ppermute | solution.py:57
  55.8 0.7 collective-permute-start.4
  56.5 5.1 %collective-permute-done.5 = bf16[4,192,128]{2,1,0:T(8,128)(2,1)S(1)} collective-permute-done((bf16[4,192,128]{2,1,0:T(8,128)(2,1)S(1)}, bf16[4,192,128]{2,1,0:T(8,128)(2,1)S(1)}, u32[]{:S(2)}, u32[]{:S(2)}) %collective-permute-start.5) | collective-permute-done | bytes 196640 | tf_op jit(solution)/shard_map/ppermute | solution.py:57
  61.6 3.9 %collective-permute-start.6 = (bf16[4,192,128]{2,1,0:T(8,128)(2,1)S(1)}, bf16[4,192,128]{2,1,0:T(8,128)(2,1)S(1)}, u32[]{:S(2)}, u32[]{:S(2)}) collective-permute-start(bf16[4,192,128]{2,1,0:T(8,128)(2,1)S(1)} %collective-permute-done.5), channel_id=1, source_target_pairs={{0,2},{1,3},{2,0},{3,1},{4,6},{5,7},{6,4},{7,5},{8,10},{9,11},{10,... | collective-permute-start | bytes 589832 | tf_op jit(solution)/shard_map/ppermute | solution.py:57
  65.5 0.2 collective-permute-start.17
  65.7 4.9 %collective-permute-done.6 = bf16[4,192,128]{2,1,0:T(8,128)(2,1)S(1)} collective-permute-done((bf16[4,192,128]{2,1,0:T(8,128)(2,1)S(1)}, bf16[4,192,128]{2,1,0:T(8,128)(2,1)S(1)}, u32[]{:S(2)}, u32[]{:S(2)}) %collective-permute-start.6) | collective-permute-done | bytes 196640 | tf_op jit(solution)/shard_map/ppermute | solution.py:57
  70.7 0.1 pad_maximum_fusion.own
  70.8 0.1 collective-permute-start.7
  70.9 0.3 collective-permute-start.15
  71.2 2.1 %collective-permute-start.11 = (bf16[512,768]{1,0:T(8,128)(2,1)S(1)}, bf16[512,768]{1,0:T(8,128)(2,1)S(1)}, u32[]{:S(2)}, u32[]{:S(2)}) collective-permute-start(bf16[512,768]{1,0:T(8,128)(2,1)S(1)} %collective-permute-done.10.refs_2_), channel_id=1, source_target_pairs={{0,8},{1,65},{2,10},{3,67},{4,12},{5,69},{6,14},{7,71},{8,0},{9,73... | collective-permute-start | bytes 2359304 | tf_op jit(solution)/shard_map/ppermute | solution.py:57
  73.3 1.5 %shard_map.55 = (f32[768,128]{1,0:T(8,128)S(1)}, f32[768,128]{1,0:T(8,128)S(1)}, f32[768,128]{1,0:T(8,128)S(1)}, f32[384,128]{1,0:T(8,128)S(1)}, f32[384,128]{1,0:T(8,128)S(1)}) custom-call(bf16[6144,768]{1,0:T(8,128)(2,1)S(1)} %copy-done.1, bf16[128,768]{1,0:T(8,128)(2,1)S(1)} %copy-done.2, bf16[128,768]{1,0:T(8,128)(2,1)S(1)} %collective-permute-done.8.far, ...), custom_call_target="tpu_custom_call" | custom-call | flops 603979776 | bytes 6291456 | tf_op jit(solution)/shard_map/pallas_call | solution.py:105
  74.8 3.9 %collective-permute-done.17.refs_3_ = bf16[512,768]{1,0:T(8,128)(2,1)S(1)} collective-permute-done((bf16[512,768]{1,0:T(8,128)(2,1)S(1)}, bf16[512,768]{1,0:T(8,128)(2,1)S(1)}, u32[]{:S(2)}, u32[]{:S(2)}) %collective-permute-start.17) | collective-permute-done | bytes 786464 | tf_op jit(solution)/shard_map/ppermute | solution.py:57
  78.7 1.2 %collective-permute-start.19 = (f32[768,128]{1,0:T(8,128)S(1)}, f32[768,128]{1,0:T(8,128)S(1)}, u32[]{:S(2)}, u32[]{:S(2)}) collective-permute-start(f32[768,128]{1,0:T(8,128)S(1)} %get-tuple-element.8), channel_id=1, source_target_pairs={{0,2},{1,3},{2,4},{3,5},{4,6},{5,7},{6,32},{7,33},{8,10},{9,11},{1... | collective-permute-start | bytes 1179656 | tf_op jit(solution)/shard_map/ppermute | solution.py:57
  79.9 2.7 %collective-permute-done.16.refs_0_ = bf16[512,768]{1,0:T(8,128)(2,1)S(1)} collective-permute-done((bf16[512,768]{1,0:T(8,128)(2,1)S(1)}, bf16[512,768]{1,0:T(8,128)(2,1)S(1)}, u32[]{:S(2)}, u32[]{:S(2)}) %collective-permute-start.16) | collective-permute-done | bytes 786464 | tf_op jit(solution)/shard_map/ppermute | solution.py:57
  82.7 1.1 %collective-permute-start.20 = (f32[768,128]{1,0:T(8,128)S(1)}, f32[768,128]{1,0:T(8,128)S(1)}, u32[]{:S(2)}, u32[]{:S(2)}) collective-permute-start(f32[768,128]{1,0:T(8,128)S(1)} %get-tuple-element.9), channel_id=1, source_target_pairs={{0,38},{1,39},{2,0},{3,1},{4,2},{5,3},{6,4},{7,5},{8,46},{9,47},{1... | collective-permute-start | bytes 1179656 | tf_op jit(solution)/shard_map/ppermute | solution.py:57
  83.8 2.2 %collective-permute-start.21 = (f32[384,128]{1,0:T(8,128)S(1)}, f32[384,128]{1,0:T(8,128)S(1)}, u32[]{:S(2)}, u32[]{:S(2)}) collective-permute-start(f32[384,128]{1,0:T(8,128)S(1)} %get-tuple-element.10), channel_id=1, source_target_pairs={{0,4},{1,5},{2,6},{3,7},{4,32},{5,33},{6,34},{7,35},{8,12},{9,13},... | collective-permute-start | bytes 589832 | tf_op jit(solution)/shard_map/ppermute | solution.py:57
  86.0 1.1 %collective-permute-done.15.refs_1_ = bf16[512,768]{1,0:T(8,128)(2,1)S(1)} collective-permute-done((bf16[512,768]{1,0:T(8,128)(2,1)S(1)}, bf16[512,768]{1,0:T(8,128)(2,1)S(1)}, u32[]{:S(2)}, u32[]{:S(2)}) %collective-permute-start.15) | collective-permute-done | bytes 786464 | tf_op jit(solution)/shard_map/ppermute | solution.py:57
  87.1 1.4 %collective-permute-start.22 = (f32[384,128]{1,0:T(8,128)S(1)}, f32[384,128]{1,0:T(8,128)S(1)}, u32[]{:S(2)}, u32[]{:S(2)}) collective-permute-start(f32[384,128]{1,0:T(8,128)S(1)} %get-tuple-element.11), channel_id=1, source_target_pairs={{0,36},{1,37},{2,38},{3,39},{4,0},{5,1},{6,2},{7,3},{8,44},{9,45},... | collective-permute-start | bytes 589832 | tf_op jit(solution)/shard_map/ppermute | solution.py:57
  88.6 0.5 shard_map.50.refs_4_
  89.0 0.8 shard_map.51.refs_2_
  89.8 1.2 %collective-permute-done.11.refs_0_ = bf16[512,768]{1,0:T(8,128)(2,1)S(1)} collective-permute-done((bf16[512,768]{1,0:T(8,128)(2,1)S(1)}, bf16[512,768]{1,0:T(8,128)(2,1)S(1)}, u32[]{:S(2)}, u32[]{:S(2)}) %collective-permute-start.11) | collective-permute-done | bytes 786464 | tf_op jit(solution)/shard_map/ppermute | solution.py:57
  91.1 1.3 %shard_map.52 = f32[192,768]{1,0:T(8,128)} custom-call(bf16[4,4,192,128]{3,2,1,0:T(8,128)(2,1)S(1)} %pad_maximum_fusion.own, bf16[4,4,192,128]{3,2,1,0:T(8,128)(2,1)S(1)} %collective-permute-done.7.other, bf16[512,768]{1,0:T(8,128)(2,1)S(1)} %collective-permute-done.11.refs_0_, bf16[512,768]{1,0:T(8,128)(2,1)S(1)} %collective-permute-done.15.refs_1_, ...), custom_call_target="tpu_custom_call" | custom-call | flops 301989888 | bytes 3145728 | tf_op jit(solution)/shard_map/pallas_call | solution.py:156
  92.4 5.4 %collective-permute-done.21.two_before = f32[384,128]{1,0:T(8,128)S(1)} collective-permute-done((f32[384,128]{1,0:T(8,128)S(1)}, f32[384,128]{1,0:T(8,128)S(1)}, u32[]{:S(2)}, u32[]{:S(2)}) %collective-permute-start.21) | collective-permute-done | bytes 196640 | tf_op jit(solution)/shard_map/ppermute | solution.py:57
  97.8 4.0 %collective-permute-done.22.two_after = f32[384,128]{1,0:T(8,128)S(1)} collective-permute-done((f32[384,128]{1,0:T(8,128)S(1)}, f32[384,128]{1,0:T(8,128)S(1)}, u32[]{:S(2)}, u32[]{:S(2)}) %collective-permute-start.22) | collective-permute-done | bytes 196640 | tf_op jit(solution)/shard_map/ppermute | solution.py:57
  101.8 0.8 shard_map.56
  (20 shorter events, 0.2 us)
Async XLA Ops:
  0.6 12.5 %collective-permute-start.8 = (bf16[128,768]{1,0:T(8,128)(2,1)}, bf16[128,768]{1,0:T(8,128)(2,1)S(1)}, u32[]{:S(2)}, u32[]{:S(2)}) collective-permute-start(bf16[128,768]{1,0:T(8,128)(2,1)} %near.3), channel_id=1, source_target_pairs={{0,32},{1,33},{2,34},{3,35},{4,36},{5,37},{6,38},{7,39},{8,40},{9,... | collective-permute-start | bytes 589832 | tf_op jit(solution)/shard_map/ppermute | solution.py:57
  13.1 24.6 %collective-permute-start.12 = (bf16[256,768]{1,0:T(8,128)(2,1)S(1)}, bf16[256,768]{1,0:T(8,128)(2,1)S(1)}, u32[]{:S(2)}, u32[]{:S(2)}) collective-permute-start(bf16[256,768]{1,0:T(8,128)(2,1)S(1)} %get-tuple-element.12.refs_0_), channel_id=1, source_target_pairs={{0,192},{1,25},{2,194},{3,27},{4,196},{5,29},{6,198},{7,31},{8,200... | collective-permute-start | bytes 1179656 | tf_op jit(solution)/shard_map/ppermute | solution.py:57
  17.1 3.7 %copy-start = (bf16[6144,768]{1,0:T(8,128)(2,1)S(1)}, bf16[6144,768]{1,0:T(8,128)(2,1)}, u32[]{:S(2)}) copy-start(bf16[6144,768]{1,0:T(8,128)(2,1)} %weight.5) | copy-start | bytes 28311556
  20.8 0.9 copy-start.2
  20.8 17.0 %collective-permute-start.13 = (bf16[256,768]{1,0:T(8,128)(2,1)S(1)}, bf16[256,768]{1,0:T(8,128)(2,1)S(1)}, u32[]{:S(2)}, u32[]{:S(2)}) collective-permute-start(bf16[256,768]{1,0:T(8,128)(2,1)S(1)} %get-tuple-element.12.refs_0_), channel_id=1, source_target_pairs={{0,128},{1,17},{2,130},{3,19},{4,132},{5,21},{6,134},{7,23},{8,136... | collective-permute-start | bytes 1179656 | tf_op jit(solution)/shard_map/ppermute | solution.py:57
  21.7 3.7 %copy-start.1 = (bf16[6144,768]{1,0:T(8,128)(2,1)S(1)}, bf16[6144,768]{1,0:T(8,128)(2,1)}, u32[]{:S(2)}) copy-start(bf16[6144,768]{1,0:T(8,128)(2,1)} %weight.5) | copy-start | bytes 28311556
  26.9 44.3 %collective-permute-start.18 = (f32[4,768,128]{2,1,0:T(8,128)S(1)}, f32[4,768,128]{2,1,0:T(8,128)S(1)}, u32[]{:S(2)}, u32[]{:S(2)}) collective-permute-start(f32[4,768,128]{2,1,0:T(8,128)S(1)} %shard_map.54), channel_id=1, source_target_pairs={{0,1},{1,0},{2,3},{3,2},{4,5},{5,4},{6,7},{7,6},{8,9},{9,8},{10,11... | collective-permute-start | bytes 4718600 | tf_op jit(solution)/shard_map/ppermute | solution.py:57
  27.1 4.7 %collective-permute-start = (bf16[192,128]{1,0:T(8,128)(2,1)S(1)}, bf16[192,128]{1,0:T(8,128)(2,1)S(1)}, u32[]{:S(2)}, u32[]{:S(2)}) collective-permute-start(bf16[192,128]{1,0:T(8,128)(2,1)S(1)} %get-tuple-element.19), channel_id=1, source_target_pairs={{0,8},{1,9},{2,10},{3,11},{4,12},{5,13},{6,14},{7,15},{8,0},{9,1},... | collective-permute-start | bytes 147464 | tf_op jit(solution)/shard_map/ppermute | solution.py:57
  27.9 5.6 %collective-permute-start.1 = (bf16[192,128]{1,0:T(8,128)(2,1)S(1)}, bf16[192,128]{1,0:T(8,128)(2,1)S(1)}, u32[]{:S(2)}, u32[]{:S(2)}) collective-permute-start(bf16[192,128]{1,0:T(8,128)(2,1)S(1)} %get-tuple-element.18), channel_id=1, source_target_pairs={{0,16},{1,17},{2,18},{3,19},{4,20},{5,21},{6,22},{7,23},{8,24},{9,... | collective-permute-start | bytes 147464 | tf_op jit(solution)/shard_map/ppermute | solution.py:57
  31.8 5.3 %collective-permute-start.2 = (bf16[192,128]{1,0:T(8,128)(2,1)S(1)}, bf16[192,128]{1,0:T(8,128)(2,1)S(1)}, u32[]{:S(2)}, u32[]{:S(2)}) collective-permute-start(bf16[192,128]{1,0:T(8,128)(2,1)S(1)} %get-tuple-element.17), channel_id=1, source_target_pairs={{0,24},{1,25},{2,26},{3,27},{4,28},{5,29},{6,30},{7,31},{8,16},{9,... | collective-permute-start | bytes 147464 | tf_op jit(solution)/shard_map/ppermute | solution.py:57
  33.5 7.8 %collective-permute-start.9 = (bf16[256,768]{1,0:T(8,128)(2,1)S(1)}, bf16[256,768]{1,0:T(8,128)(2,1)S(1)}, u32[]{:S(2)}, u32[]{:S(2)}) collective-permute-start(bf16[256,768]{1,0:T(8,128)(2,1)S(1)} %get-tuple-element.12.refs_0_), channel_id=1, source_target_pairs={{0,64},{1,9},{2,66},{3,11},{4,68},{5,13},{6,70},{7,15},{8,72},{9,1... | collective-permute-start | bytes 1179656 | tf_op jit(solution)/shard_map/ppermute | solution.py:57
  37.1 5.8 %collective-permute-start.3 = (bf16[4,192,128]{2,1,0:T(8,128)(2,1)S(1)}, bf16[4,192,128]{2,1,0:T(8,128)(2,1)S(1)}, u32[]{:S(2)}, u32[]{:S(2)}) collective-permute-start(bf16[4,192,128]{2,1,0:T(8,128)(2,1)S(1)} %pad_maximum_fusion.1), channel_id=1, source_target_pairs={{0,0},{1,32},{2,66},{3,98},{4,132},{5,164},{6,198},{7,230},{8,8},{... | collective-permute-start | bytes 589832 | tf_op jit(solution)/shard_map/ppermute | solution.py:57
  37.9 32.9 %collective-permute-start.14 = (bf16[512,768]{1,0:T(8,128)(2,1)S(1)}, bf16[512,768]{1,0:T(8,128)(2,1)S(1)}, u32[]{:S(2)}, u32[]{:S(2)}) collective-permute-start(bf16[512,768]{1,0:T(8,128)(2,1)S(1)} %constant_dynamic-update-slice_fusion.5), channel_id=1, source_target_pairs={{0,8},{1,65},{2,10},{3,67},{4,12},{5,69},{6,14},{7,71},{8,0},{9,73... | collective-permute-start | bytes 2359304 | tf_op jit(solution)/shard_map/ppermute | solution.py:57
  41.3 29.6 %collective-permute-start.10 = (bf16[512,768]{1,0:T(8,128)(2,1)S(1)}, bf16[512,768]{1,0:T(8,128)(2,1)S(1)}, u32[]{:S(2)}, u32[]{:S(2)}) collective-permute-start(bf16[512,768]{1,0:T(8,128)(2,1)S(1)} %constant_dynamic-update-slice_fusion.2), channel_id=1, source_target_pairs={{0,24},{1,193},{2,26},{3,195},{4,28},{5,197},{6,30},{7,199},{8,16}... | collective-permute-start | bytes 2359304 | tf_op jit(solution)/shard_map/ppermute | solution.py:57
  42.9 18.7 %collective-permute-start.5 = (bf16[4,192,128]{2,1,0:T(8,128)(2,1)S(1)}, bf16[4,192,128]{2,1,0:T(8,128)(2,1)S(1)}, u32[]{:S(2)}, u32[]{:S(2)}) collective-permute-start(bf16[4,192,128]{2,1,0:T(8,128)(2,1)S(1)} %collective-permute-done.3), channel_id=1, source_target_pairs={{0,6},{1,7},{2,4},{3,5},{4,2},{5,3},{6,0},{7,1},{8,14},{9,15},{10,... | collective-permute-start | bytes 589832 | tf_op jit(solution)/shard_map/ppermute | solution.py:57
  55.8 9.7 %collective-permute-start.4 = (bf16[4,192,128]{2,1,0:T(8,128)(2,1)S(1)}, bf16[4,192,128]{2,1,0:T(8,128)(2,1)S(1)}, u32[]{:S(2)}, u32[]{:S(2)}) collective-permute-start(bf16[4,192,128]{2,1,0:T(8,128)(2,1)S(1)} %collective-permute-done.3), channel_id=1, source_target_pairs={{0,2},{1,3},{2,0},{3,1},{4,6},{5,7},{6,4},{7,5},{8,10},{9,11},{10,... | collective-permute-start | bytes 589832 | tf_op jit(solution)/shard_map/ppermute | solution.py:57
  61.6 9.1 %collective-permute-start.6 = (bf16[4,192,128]{2,1,0:T(8,128)(2,1)S(1)}, bf16[4,192,128]{2,1,0:T(8,128)(2,1)S(1)}, u32[]{:S(2)}, u32[]{:S(2)}) collective-permute-start(bf16[4,192,128]{2,1,0:T(8,128)(2,1)S(1)} %collective-permute-done.5), channel_id=1, source_target_pairs={{0,2},{1,3},{2,0},{3,1},{4,6},{5,7},{6,4},{7,5},{8,10},{9,11},{10,... | collective-permute-start | bytes 589832 | tf_op jit(solution)/shard_map/ppermute | solution.py:57
  65.5 13.2 %collective-permute-start.17 = (bf16[512,768]{1,0:T(8,128)(2,1)S(1)}, bf16[512,768]{1,0:T(8,128)(2,1)S(1)}, u32[]{:S(2)}, u32[]{:S(2)}) collective-permute-start(bf16[512,768]{1,0:T(8,128)(2,1)S(1)} %constant_dynamic-update-slice_fusion.5), channel_id=1, source_target_pairs={{0,24},{1,193},{2,26},{3,195},{4,28},{5,197},{6,30},{7,199},{8,16}... | collective-permute-start | bytes 2359304 | tf_op jit(solution)/shard_map/ppermute | solution.py:57
  70.7 12.0 %collective-permute-start.16 = (bf16[512,768]{1,0:T(8,128)(2,1)S(1)}, bf16[512,768]{1,0:T(8,128)(2,1)S(1)}, u32[]{:S(2)}, u32[]{:S(2)}) collective-permute-start(bf16[512,768]{1,0:T(8,128)(2,1)S(1)} %constant_dynamic-update-slice_fusion.2), channel_id=1, source_target_pairs={{0,8},{1,65},{2,10},{3,67},{4,12},{5,69},{6,14},{7,71},{8,0},{9,73... | collective-permute-start | bytes 2359304 | tf_op jit(solution)/shard_map/ppermute | solution.py:57
  70.8 13.0 %collective-permute-start.7 = (bf16[4,4,192,128]{3,2,1,0:T(8,128)(2,1)S(1)}, bf16[4,4,192,128]{3,2,1,0:T(8,128)(2,1)S(1)}, u32[]{:S(2)}, u32[]{:S(2)}) collective-permute-start(bf16[4,4,192,128]{3,2,1,0:T(8,128)(2,1)S(1)} %pad_maximum_fusion.own), channel_id=1, source_target_pairs={{0,1},{1,0},{2,3},{3,2},{4,5},{5,4},{6,7},{7,6},{8,9},{9,8},{10,11... | collective-permute-start | bytes 2359304 | tf_op jit(solution)/shard_map/ppermute | solution.py:57
  70.9 16.2 %collective-permute-start.15 = (bf16[512,768]{1,0:T(8,128)(2,1)S(1)}, bf16[512,768]{1,0:T(8,128)(2,1)S(1)}, u32[]{:S(2)}, u32[]{:S(2)}) collective-permute-start(bf16[512,768]{1,0:T(8,128)(2,1)S(1)} %collective-permute-done.14.refs_1_), channel_id=1, source_target_pairs={{0,24},{1,193},{2,26},{3,195},{4,28},{5,197},{6,30},{7,199},{8,16}... | collective-permute-start | bytes 2359304 | tf_op jit(solution)/shard_map/ppermute | solution.py:57
  71.2 19.9 %collective-permute-start.11 = (bf16[512,768]{1,0:T(8,128)(2,1)S(1)}, bf16[512,768]{1,0:T(8,128)(2,1)S(1)}, u32[]{:S(2)}, u32[]{:S(2)}) collective-permute-start(bf16[512,768]{1,0:T(8,128)(2,1)S(1)} %collective-permute-done.10.refs_2_), channel_id=1, source_target_pairs={{0,8},{1,65},{2,10},{3,67},{4,12},{5,69},{6,14},{7,71},{8,0},{9,73... | collective-permute-start | bytes 2359304 | tf_op jit(solution)/shard_map/ppermute | solution.py:57
  78.7 23.1 %collective-permute-start.19 = (f32[768,128]{1,0:T(8,128)S(1)}, f32[768,128]{1,0:T(8,128)S(1)}, u32[]{:S(2)}, u32[]{:S(2)}) collective-permute-start(f32[768,128]{1,0:T(8,128)S(1)} %get-tuple-element.8), channel_id=1, source_target_pairs={{0,2},{1,3},{2,4},{3,5},{4,6},{5,7},{6,32},{7,33},{8,10},{9,11},{1... | collective-permute-start | bytes 1179656 | tf_op jit(solution)/shard_map/ppermute | solution.py:57
  82.7 19.2 %collective-permute-start.20 = (f32[768,128]{1,0:T(8,128)S(1)}, f32[768,128]{1,0:T(8,128)S(1)}, u32[]{:S(2)}, u32[]{:S(2)}) collective-permute-start(f32[768,128]{1,0:T(8,128)S(1)} %get-tuple-element.9), channel_id=1, source_target_pairs={{0,38},{1,39},{2,0},{3,1},{4,2},{5,3},{6,4},{7,5},{8,46},{9,47},{1... | collective-permute-start | bytes 1179656 | tf_op jit(solution)/shard_map/ppermute | solution.py:57
  83.8 14.0 %collective-permute-start.21 = (f32[384,128]{1,0:T(8,128)S(1)}, f32[384,128]{1,0:T(8,128)S(1)}, u32[]{:S(2)}, u32[]{:S(2)}) collective-permute-start(f32[384,128]{1,0:T(8,128)S(1)} %get-tuple-element.10), channel_id=1, source_target_pairs={{0,4},{1,5},{2,6},{3,7},{4,32},{5,33},{6,34},{7,35},{8,12},{9,13},... | collective-permute-start | bytes 589832 | tf_op jit(solution)/shard_map/ppermute | solution.py:57
  87.1 14.7 %collective-permute-start.22 = (f32[384,128]{1,0:T(8,128)S(1)}, f32[384,128]{1,0:T(8,128)S(1)}, u32[]{:S(2)}, u32[]{:S(2)}) collective-permute-start(f32[384,128]{1,0:T(8,128)S(1)} %get-tuple-element.11), channel_id=1, source_target_pairs={{0,36},{1,37},{2,38},{3,39},{4,0},{5,1},{6,2},{7,3},{8,44},{9,45},... | collective-permute-start | bytes 589832 | tf_op jit(solution)/shard_map/ppermute | solution.py:57

commit v11 on v10

--- a/solution.py
+++ b/solution.py
@@ -192,10 +192,9 @@
         + [send(at(turned, y ^ k), lambda x, h, y, l, c, k=k: (x, h, y ^ k, l, c)) for k in others]
     )
     mine = send(block, lambda x, h, y, l, c: (l, c, y, l ^ x, h))
-    along = lambda k: lambda x, h, y, l, c: (x, h, y, l ^ k, c)
-    three_away = send(mine, along(3))
-    next_one = send(mine, along(1))
-    gathered = [mine, next_one, send(three_away, along(1)), three_away]
+    gathered = [mine] + [
+        send(mine, lambda x, h, y, l, c, k=k: (x, h, y, l ^ k, c)) for k in (1, 2, 3)
+    ]
     own = jnp.stack(gathered)
     swap = lambda x, h, y, l, c: (x, h, y, l, 1 - c)
     other = send(own, swap)

time: 103 us -> 112 us (1.087)
  the two profiles are of different devices: /device:TPU:24 before, /device:TPU:1 now
where the time goes in v11:
time: 112 us; the launch traced here: 111 us
  starting transfers between devices  47 us (42%)
  waiting for transfers between devices  46.9 us (42%)
  local copies, waits for them, and re-layouts  10.1 us (9%)
  Pallas kernels  6.44 us (6%)
    ppermute x23, starting transfers between devices, send(): return lax.ppermute(array, AXES, pairs(route))  47 us
    ppermute x23, waiting for transfers between devices, send(): return lax.ppermute(array, AXES, pairs(route))  46.9 us
    unnamed x8, local copies, waits for them, and re-layouts  8.95 us
    pallas_call x2, Pallas kernels, products(): pl.pallas_call(functools.partial(products_kernel, kept), out_shape=shapes...  3.06 us
    pallas_call x3, Pallas kernels, weight_part(): pl.pallas_call(functools.partial(weight_kernel, items), out_shape=jax.Sha...  2.56 us
  transfers between devices with their start and end apart: 23, of which 10 were waited for; matrix products, arithmetic and copies ran while one was open for 2% of the time, Pallas kernels for 5%

profile of v11, /device:TPU:1, one launch (start us, length us, event | category | flops | bytes accessed | tf_op | source)
XLA Modules:
  0.0 111.4 jit_solution(13214716312089165362)
XLA Ops:
  0.6 7.8 %collective-permute-start.8 = (bf16[128,768]{1,0:T(8,128)(2,1)}, bf16[128,768]{1,0:T(8,128)(2,1)S(1)}, u32[]{:S(2)}, u32[]{:S(2)}) collective-permute-start(bf16[128,768]{1,0:T(8,128)(2,1)} %near.3), channel_id=1, source_target_pairs={{0,32},{1,33},{2,34},{3,35},{4,36},{5,37},{6,38},{7,39},{8,40},{9,... | collective-permute-start | bytes 589832 | tf_op jit(solution)/shard_map/ppermute | solution.py:57
  8.4 1.0 constant_dynamic-update-slice_fusion.1
  9.4 3.4 %collective-permute-done.8.far = bf16[128,768]{1,0:T(8,128)(2,1)S(1)} collective-permute-done((bf16[128,768]{1,0:T(8,128)(2,1)}, bf16[128,768]{1,0:T(8,128)(2,1)S(1)}, u32[]{:S(2)}, u32[]{:S(2)}) %collective-permute-start.8) | collective-permute-done | bytes 196640 | tf_op jit(solution)/shard_map/ppermute | solution.py:57
  12.8 3.3 %collective-permute-start.12 = (bf16[256,768]{1,0:T(8,128)(2,1)S(1)}, bf16[256,768]{1,0:T(8,128)(2,1)S(1)}, u32[]{:S(2)}, u32[]{:S(2)}) collective-permute-start(bf16[256,768]{1,0:T(8,128)(2,1)S(1)} %get-tuple-element.12.refs_0_), channel_id=1, source_target_pairs={{0,192},{1,25},{2,194},{3,27},{4,196},{5,29},{6,198},{7,31},{8,200... | collective-permute-start | bytes 1179656 | tf_op jit(solution)/shard_map/ppermute | solution.py:57
  16.1 1.1 copy.5
  17.2 0.0 copy-start
  17.2 3.7 %copy-done = bf16[6144,768]{1,0:T(8,128)(2,1)S(1)} copy-done((bf16[6144,768]{1,0:T(8,128)(2,1)S(1)}, bf16[6144,768]{1,0:T(8,128)(2,1)}, u32[]{:S(2)}) %copy-start) | copy-done | bytes 9437208
  20.9 0.3 collective-permute-start.13
  21.3 0.6 copy-done.2
  21.8 3.7 %copy-done.1 = bf16[6144,768]{1,0:T(8,128)(2,1)S(1)} copy-done((bf16[6144,768]{1,0:T(8,128)(2,1)S(1)}, bf16[6144,768]{1,0:T(8,128)(2,1)}, u32[]{:S(2)}) %copy-start.1) | copy-done | bytes 9437208
  25.5 1.5 %shard_map.54 = f32[4,768,128]{2,1,0:T(8,128)S(1)} custom-call(bf16[6144,768]{1,0:T(8,128)(2,1)S(1)} %copy-done.1, bf16[128,768]{1,0:T(8,128)(2,1)S(1)} %copy-done.2, bf16[128,768]{1,0:T(8,128)(2,1)S(1)} %collective-permute-done.8.far, bf16[16,128]{1,0:T(8,128)(2,1)S(1)} %shard_map.53.refs_0_), custom_call_target="tpu_custom_call" | custom-call | flops 603979776 | bytes 6291456 | tf_op jit(solution)/shard_map/pallas_call | solution.py:105
  27.0 1.5 %collective-permute-start.18 = (f32[4,768,128]{2,1,0:T(8,128)S(1)}, f32[4,768,128]{2,1,0:T(8,128)S(1)}, u32[]{:S(2)}, u32[]{:S(2)}) collective-permute-start(f32[4,768,128]{2,1,0:T(8,128)S(1)} %shard_map.54), channel_id=1, source_target_pairs={{0,1},{1,0},{2,3},{3,2},{4,5},{5,4},{6,7},{7,6},{8,9},{9,8},{10,11... | collective-permute-start | bytes 4718600 | tf_op jit(solution)/shard_map/ppermute | solution.py:57
  28.5 1.4 %collective-permute-start = (bf16[192,128]{1,0:T(8,128)(2,1)S(1)}, bf16[192,128]{1,0:T(8,128)(2,1)S(1)}, u32[]{:S(2)}, u32[]{:S(2)}) collective-permute-start(bf16[192,128]{1,0:T(8,128)(2,1)S(1)} %get-tuple-element.19), channel_id=1, source_target_pairs={{0,8},{1,9},{2,10},{3,11},{4,12},{5,13},{6,14},{7,15},{8,0},{9,1},... | collective-permute-start | bytes 147464 | tf_op jit(solution)/shard_map/ppermute | solution.py:57
  29.9 2.6 %collective-permute-start.1 = (bf16[192,128]{1,0:T(8,128)(2,1)S(1)}, bf16[192,128]{1,0:T(8,128)(2,1)S(1)}, u32[]{:S(2)}, u32[]{:S(2)}) collective-permute-start(bf16[192,128]{1,0:T(8,128)(2,1)S(1)} %get-tuple-element.18), channel_id=1, source_target_pairs={{0,16},{1,17},{2,18},{3,19},{4,20},{5,21},{6,22},{7,23},{8,24},{9,... | collective-permute-start | bytes 147464 | tf_op jit(solution)/shard_map/ppermute | solution.py:57
  32.5 2.1 %collective-permute-start.2 = (bf16[192,128]{1,0:T(8,128)(2,1)S(1)}, bf16[192,128]{1,0:T(8,128)(2,1)S(1)}, u32[]{:S(2)}, u32[]{:S(2)}) collective-permute-start(bf16[192,128]{1,0:T(8,128)(2,1)S(1)} %get-tuple-element.17), channel_id=1, source_target_pairs={{0,24},{1,25},{2,26},{3,27},{4,28},{5,29},{6,30},{7,31},{8,16},{9,... | collective-permute-start | bytes 147464 | tf_op jit(solution)/shard_map/ppermute | solution.py:57
  34.6 0.8 collective-permute-done.1
  35.4 1.3 %collective-permute-done.2 = bf16[192,128]{1,0:T(8,128)(2,1)S(1)} collective-permute-done((bf16[192,128]{1,0:T(8,128)(2,1)S(1)}, bf16[192,128]{1,0:T(8,128)(2,1)S(1)}, u32[]{:S(2)}, u32[]{:S(2)}) %collective-permute-start.2) | collective-permute-done | bytes 49184 | tf_op jit(solution)/shard_map/ppermute | solution.py:57
  36.7 12.3 %collective-permute-start.3 = (bf16[4,192,128]{2,1,0:T(8,128)(2,1)S(1)}, bf16[4,192,128]{2,1,0:T(8,128)(2,1)S(1)}, u32[]{:S(2)}, u32[]{:S(2)}) collective-permute-start(bf16[4,192,128]{2,1,0:T(8,128)(2,1)S(1)} %pad_maximum_fusion.1), channel_id=1, source_target_pairs={{0,0},{1,32},{2,66},{3,98},{4,132},{5,164},{6,198},{7,230},{8,8},{... | collective-permute-start | bytes 589832 | tf_op jit(solution)/shard_map/ppermute | solution.py:57
  49.0 0.0 collective-permute-done.12.refs_3_
  49.1 1.5 %collective-permute-start.14 = (bf16[512,768]{1,0:T(8,128)(2,1)S(1)}, bf16[512,768]{1,0:T(8,128)(2,1)S(1)}, u32[]{:S(2)}, u32[]{:S(2)}) collective-permute-start(bf16[512,768]{1,0:T(8,128)(2,1)S(1)} %constant_dynamic-update-slice_fusion.5), channel_id=1, source_target_pairs={{0,8},{1,65},{2,10},{3,67},{4,12},{5,69},{6,14},{7,71},{8,0},{9,73... | collective-permute-start | bytes 2359304 | tf_op jit(solution)/shard_map/ppermute | solution.py:57
  50.7 1.4 %collective-permute-start.10 = (bf16[512,768]{1,0:T(8,128)(2,1)S(1)}, bf16[512,768]{1,0:T(8,128)(2,1)S(1)}, u32[]{:S(2)}, u32[]{:S(2)}) collective-permute-start(bf16[512,768]{1,0:T(8,128)(2,1)S(1)} %constant_dynamic-update-slice_fusion.2), channel_id=1, source_target_pairs={{0,24},{1,193},{2,26},{3,195},{4,28},{5,197},{6,30},{7,199},{8,16}... | collective-permute-start | bytes 2359304 | tf_op jit(solution)/shard_map/ppermute | solution.py:57
  52.0 0.4 collective-permute-done.3
  52.5 4.3 %collective-permute-start.5 = (bf16[4,192,128]{2,1,0:T(8,128)(2,1)S(1)}, bf16[4,192,128]{2,1,0:T(8,128)(2,1)S(1)}, u32[]{:S(2)}, u32[]{:S(2)}) collective-permute-start(bf16[4,192,128]{2,1,0:T(8,128)(2,1)S(1)} %collective-permute-done.3), channel_id=1, source_target_pairs={{0,4},{1,5},{2,6},{3,7},{4,0},{5,1},{6,2},{7,3},{8,12},{9,13},{10,... | collective-permute-start | bytes 589832 | tf_op jit(solution)/shard_map/ppermute | solution.py:57
  56.8 13.8 %collective-permute-done.5 = bf16[4,192,128]{2,1,0:T(8,128)(2,1)S(1)} collective-permute-done((bf16[4,192,128]{2,1,0:T(8,128)(2,1)S(1)}, bf16[4,192,128]{2,1,0:T(8,128)(2,1)S(1)}, u32[]{:S(2)}, u32[]{:S(2)}) %collective-permute-start.5) | collective-permute-done | bytes 196640 | tf_op jit(solution)/shard_map/ppermute | solution.py:57
  70.7 6.0 %collective-permute-done.4 = bf16[4,192,128]{2,1,0:T(8,128)(2,1)S(1)} collective-permute-done((bf16[4,192,128]{2,1,0:T(8,128)(2,1)S(1)}, bf16[4,192,128]{2,1,0:T(8,128)(2,1)S(1)}, u32[]{:S(2)}, u32[]{:S(2)}) %collective-permute-start.4) | collective-permute-done | bytes 196640 | tf_op jit(solution)/shard_map/ppermute | solution.py:57
  76.6 0.1 pad_maximum_fusion.own
  76.7 1.4 %collective-permute-start.7 = (bf16[4,4,192,128]{3,2,1,0:T(8,128)(2,1)S(1)}, bf16[4,4,192,128]{3,2,1,0:T(8,128)(2,1)S(1)}, u32[]{:S(2)}, u32[]{:S(2)}) collective-permute-start(bf16[4,4,192,128]{3,2,1,0:T(8,128)(2,1)S(1)} %pad_maximum_fusion.own), channel_id=1, source_target_pairs={{0,1},{1,0},{2,3},{3,2},{4,5},{5,4},{6,7},{7,6},{8,9},{9,8},{10,11... | collective-permute-start | bytes 2359304 | tf_op jit(solution)/shard_map/ppermute | solution.py:57
  78.2 0.5 collective-permute-start.17
  78.6 0.0 collective-permute-done.14.refs_1_
  78.6 0.0 collective-permute-start.16
  78.6 0.0 collective-permute-done.10.refs_2_
  78.7 2.3 %collective-permute-start.15 = (bf16[512,768]{1,0:T(8,128)(2,1)S(1)}, bf16[512,768]{1,0:T(8,128)(2,1)S(1)}, u32[]{:S(2)}, u32[]{:S(2)}) collective-permute-start(bf16[512,768]{1,0:T(8,128)(2,1)S(1)} %collective-permute-done.14.refs_1_), channel_id=1, source_target_pairs={{0,24},{1,193},{2,26},{3,195},{4,28},{5,197},{6,30},{7,199},{8,16}... | collective-permute-start | bytes 2359304 | tf_op jit(solution)/shard_map/ppermute | solution.py:57
  80.9 0.8 collective-permute-start.11
  81.7 1.5 %shard_map.55 = (f32[768,128]{1,0:T(8,128)S(1)}, f32[768,128]{1,0:T(8,128)S(1)}, f32[768,128]{1,0:T(8,128)S(1)}, f32[384,128]{1,0:T(8,128)S(1)}, f32[384,128]{1,0:T(8,128)S(1)}) custom-call(bf16[6144,768]{1,0:T(8,128)(2,1)S(1)} %copy-done.1, bf16[128,768]{1,0:T(8,128)(2,1)S(1)} %copy-done.2, bf16[128,768]{1,0:T(8,128)(2,1)S(1)} %collective-permute-done.8.far, ...), custom_call_target="tpu_custom_call" | custom-call | flops 603979776 | bytes 6291456 | tf_op jit(solution)/shard_map/pallas_call | solution.py:105
  83.2 0.0 collective-permute-done.7.other
  83.3 0.1 collective-permute-start.19
  83.3 7.2 %collective-permute-done.17.refs_3_ = bf16[512,768]{1,0:T(8,128)(2,1)S(1)} collective-permute-done((bf16[512,768]{1,0:T(8,128)(2,1)S(1)}, bf16[512,768]{1,0:T(8,128)(2,1)S(1)}, u32[]{:S(2)}, u32[]{:S(2)}) %collective-permute-start.17) | collective-permute-done | bytes 786464 | tf_op jit(solution)/shard_map/ppermute | solution.py:57
  90.5 1.9 %collective-permute-start.20 = (f32[768,128]{1,0:T(8,128)S(1)}, f32[768,128]{1,0:T(8,128)S(1)}, u32[]{:S(2)}, u32[]{:S(2)}) collective-permute-start(f32[768,128]{1,0:T(8,128)S(1)} %get-tuple-element.9), channel_id=1, source_target_pairs={{0,38},{1,39},{2,0},{3,1},{4,2},{5,3},{6,4},{7,5},{8,46},{9,47},{1... | collective-permute-start | bytes 1179656 | tf_op jit(solution)/shard_map/ppermute | solution.py:57
  92.4 0.0 collective-permute-done.16.refs_0_
  92.4 0.0 collective-permute-start.21
  92.4 6.6 %collective-permute-done.15.refs_1_ = bf16[512,768]{1,0:T(8,128)(2,1)S(1)} collective-permute-done((bf16[512,768]{1,0:T(8,128)(2,1)S(1)}, bf16[512,768]{1,0:T(8,128)(2,1)S(1)}, u32[]{:S(2)}, u32[]{:S(2)}) %collective-permute-start.15) | collective-permute-done | bytes 786464 | tf_op jit(solution)/shard_map/ppermute | solution.py:57
  98.9 1.6 %collective-permute-start.22 = (f32[384,128]{1,0:T(8,128)S(1)}, f32[384,128]{1,0:T(8,128)S(1)}, u32[]{:S(2)}, u32[]{:S(2)}) collective-permute-start(f32[384,128]{1,0:T(8,128)S(1)} %get-tuple-element.11), channel_id=1, source_target_pairs={{0,36},{1,37},{2,38},{3,39},{4,0},{5,1},{6,2},{7,3},{8,44},{9,45},... | collective-permute-start | bytes 589832 | tf_op jit(solution)/shard_map/ppermute | solution.py:57
  100.5 0.5 shard_map.50.refs_4_
  101.0 0.8 shard_map.51.refs_2_
  101.8 1.3 %shard_map.52 = f32[192,768]{1,0:T(8,128)} custom-call(bf16[4,4,192,128]{3,2,1,0:T(8,128)(2,1)S(1)} %pad_maximum_fusion.own, bf16[4,4,192,128]{3,2,1,0:T(8,128)(2,1)S(1)} %collective-permute-done.7.other, bf16[512,768]{1,0:T(8,128)(2,1)S(1)} %collective-permute-done.11.refs_0_, bf16[512,768]{1,0:T(8,128)(2,1)S(1)} %collective-permute-done.15.refs_1_, ...), custom_call_target="tpu_custom_call" | custom-call | flops 301989888 | bytes 3145728 | tf_op jit(solution)/shard_map/pallas_call | solution.py:156
  103.1 1.5 %collective-permute-done.21.two_before = f32[384,128]{1,0:T(8,128)S(1)} collective-permute-done((f32[384,128]{1,0:T(8,128)S(1)}, f32[384,128]{1,0:T(8,128)S(1)}, u32[]{:S(2)}, u32[]{:S(2)}) %collective-permute-start.21) | collective-permute-done | bytes 196640 | tf_op jit(solution)/shard_map/ppermute | solution.py:57
  104.6 6.0 %collective-permute-done.22.two_after = f32[384,128]{1,0:T(8,128)S(1)} collective-permute-done((f32[384,128]{1,0:T(8,128)S(1)}, f32[384,128]{1,0:T(8,128)S(1)}, u32[]{:S(2)}, u32[]{:S(2)}) %collective-permute-start.22) | collective-permute-done | bytes 196640 | tf_op jit(solution)/shard_map/ppermute | solution.py:57
  110.5 0.8 shard_map.56
  (20 shorter events, 0.2 us)
Async XLA Ops:
  0.6 12.2 %collective-permute-start.8 = (bf16[128,768]{1,0:T(8,128)(2,1)}, bf16[128,768]{1,0:T(8,128)(2,1)S(1)}, u32[]{:S(2)}, u32[]{:S(2)}) collective-permute-start(bf16[128,768]{1,0:T(8,128)(2,1)} %near.3), channel_id=1, source_target_pairs={{0,32},{1,33},{2,34},{3,35},{4,36},{5,37},{6,38},{7,39},{8,40},{9,... | collective-permute-start | bytes 589832 | tf_op jit(solution)/shard_map/ppermute | solution.py:57
  12.8 36.2 %collective-permute-start.12 = (bf16[256,768]{1,0:T(8,128)(2,1)S(1)}, bf16[256,768]{1,0:T(8,128)(2,1)S(1)}, u32[]{:S(2)}, u32[]{:S(2)}) collective-permute-start(bf16[256,768]{1,0:T(8,128)(2,1)S(1)} %get-tuple-element.12.refs_0_), channel_id=1, source_target_pairs={{0,192},{1,25},{2,194},{3,27},{4,196},{5,29},{6,198},{7,31},{8,200... | collective-permute-start | bytes 1179656 | tf_op jit(solution)/shard_map/ppermute | solution.py:57
  17.2 3.7 %copy-start = (bf16[6144,768]{1,0:T(8,128)(2,1)S(1)}, bf16[6144,768]{1,0:T(8,128)(2,1)}, u32[]{:S(2)}) copy-start(bf16[6144,768]{1,0:T(8,128)(2,1)} %weight.5) | copy-start | bytes 28311556
  20.9 0.9 copy-start.2
  20.9 28.2 %collective-permute-start.13 = (bf16[256,768]{1,0:T(8,128)(2,1)S(1)}, bf16[256,768]{1,0:T(8,128)(2,1)S(1)}, u32[]{:S(2)}, u32[]{:S(2)}) collective-permute-start(bf16[256,768]{1,0:T(8,128)(2,1)S(1)} %get-tuple-element.12.refs_0_), channel_id=1, source_target_pairs={{0,128},{1,17},{2,130},{3,19},{4,132},{5,21},{6,134},{7,23},{8,136... | collective-permute-start | bytes 1179656 | tf_op jit(solution)/shard_map/ppermute | solution.py:57
  21.8 3.7 %copy-start.1 = (bf16[6144,768]{1,0:T(8,128)(2,1)S(1)}, bf16[6144,768]{1,0:T(8,128)(2,1)}, u32[]{:S(2)}) copy-start(bf16[6144,768]{1,0:T(8,128)(2,1)} %weight.5) | copy-start | bytes 28311556
  27.0 53.9 %collective-permute-start.18 = (f32[4,768,128]{2,1,0:T(8,128)S(1)}, f32[4,768,128]{2,1,0:T(8,128)S(1)}, u32[]{:S(2)}, u32[]{:S(2)}) collective-permute-start(f32[4,768,128]{2,1,0:T(8,128)S(1)} %shard_map.54), channel_id=1, source_target_pairs={{0,1},{1,0},{2,3},{3,2},{4,5},{5,4},{6,7},{7,6},{8,9},{9,8},{10,11... | collective-permute-start | bytes 4718600 | tf_op jit(solution)/shard_map/ppermute | solution.py:57
  28.5 4.0 %collective-permute-start = (bf16[192,128]{1,0:T(8,128)(2,1)S(1)}, bf16[192,128]{1,0:T(8,128)(2,1)S(1)}, u32[]{:S(2)}, u32[]{:S(2)}) collective-permute-start(bf16[192,128]{1,0:T(8,128)(2,1)S(1)} %get-tuple-element.19), channel_id=1, source_target_pairs={{0,8},{1,9},{2,10},{3,11},{4,12},{5,13},{6,14},{7,15},{8,0},{9,1},... | collective-permute-start | bytes 147464 | tf_op jit(solution)/shard_map/ppermute | solution.py:57
  29.9 5.5 %collective-permute-start.1 = (bf16[192,128]{1,0:T(8,128)(2,1)S(1)}, bf16[192,128]{1,0:T(8,128)(2,1)S(1)}, u32[]{:S(2)}, u32[]{:S(2)}) collective-permute-start(bf16[192,128]{1,0:T(8,128)(2,1)S(1)} %get-tuple-element.18), channel_id=1, source_target_pairs={{0,16},{1,17},{2,18},{3,19},{4,20},{5,21},{6,22},{7,23},{8,24},{9,... | collective-permute-start | bytes 147464 | tf_op jit(solution)/shard_map/ppermute | solution.py:57
  32.5 4.2 %collective-permute-start.2 = (bf16[192,128]{1,0:T(8,128)(2,1)S(1)}, bf16[192,128]{1,0:T(8,128)(2,1)S(1)}, u32[]{:S(2)}, u32[]{:S(2)}) collective-permute-start(bf16[192,128]{1,0:T(8,128)(2,1)S(1)} %get-tuple-element.17), channel_id=1, source_target_pairs={{0,24},{1,25},{2,26},{3,27},{4,28},{5,29},{6,30},{7,31},{8,16},{9,... | collective-permute-start | bytes 147464 | tf_op jit(solution)/shard_map/ppermute | solution.py:57
  35.4 15.3 %collective-permute-start.9 = (bf16[256,768]{1,0:T(8,128)(2,1)S(1)}, bf16[256,768]{1,0:T(8,128)(2,1)S(1)}, u32[]{:S(2)}, u32[]{:S(2)}) collective-permute-start(bf16[256,768]{1,0:T(8,128)(2,1)S(1)} %get-tuple-element.12.refs_0_), channel_id=1, source_target_pairs={{0,64},{1,9},{2,66},{3,11},{4,68},{5,13},{6,70},{7,15},{8,72},{9,1... | collective-permute-start | bytes 1179656 | tf_op jit(solution)/shard_map/ppermute | solution.py:57
  36.7 15.8 %collective-permute-start.3 = (bf16[4,192,128]{2,1,0:T(8,128)(2,1)S(1)}, bf16[4,192,128]{2,1,0:T(8,128)(2,1)S(1)}, u32[]{:S(2)}, u32[]{:S(2)}) collective-permute-start(bf16[4,192,128]{2,1,0:T(8,128)(2,1)S(1)} %pad_maximum_fusion.1), channel_id=1, source_target_pairs={{0,0},{1,32},{2,66},{3,98},{4,132},{5,164},{6,198},{7,230},{8,8},{... | collective-permute-start | bytes 589832 | tf_op jit(solution)/shard_map/ppermute | solution.py:57
  49.1 29.5 %collective-permute-start.14 = (bf16[512,768]{1,0:T(8,128)(2,1)S(1)}, bf16[512,768]{1,0:T(8,128)(2,1)S(1)}, u32[]{:S(2)}, u32[]{:S(2)}) collective-permute-start(bf16[512,768]{1,0:T(8,128)(2,1)S(1)} %constant_dynamic-update-slice_fusion.5), channel_id=1, source_target_pairs={{0,8},{1,65},{2,10},{3,67},{4,12},{5,69},{6,14},{7,71},{8,0},{9,73... | collective-permute-start | bytes 2359304 | tf_op jit(solution)/shard_map/ppermute | solution.py:57
  50.7 28.0 %collective-permute-start.10 = (bf16[512,768]{1,0:T(8,128)(2,1)S(1)}, bf16[512,768]{1,0:T(8,128)(2,1)S(1)}, u32[]{:S(2)}, u32[]{:S(2)}) collective-permute-start(bf16[512,768]{1,0:T(8,128)(2,1)S(1)} %constant_dynamic-update-slice_fusion.2), channel_id=1, source_target_pairs={{0,24},{1,193},{2,26},{3,195},{4,28},{5,197},{6,30},{7,199},{8,16}... | collective-permute-start | bytes 2359304 | tf_op jit(solution)/shard_map/ppermute | solution.py:57
  52.5 18.2 %collective-permute-start.5 = (bf16[4,192,128]{2,1,0:T(8,128)(2,1)S(1)}, bf16[4,192,128]{2,1,0:T(8,128)(2,1)S(1)}, u32[]{:S(2)}, u32[]{:S(2)}) collective-permute-start(bf16[4,192,128]{2,1,0:T(8,128)(2,1)S(1)} %collective-permute-done.3), channel_id=1, source_target_pairs={{0,4},{1,5},{2,6},{3,7},{4,0},{5,1},{6,2},{7,3},{8,12},{9,13},{10,... | collective-permute-start | bytes 589832 | tf_op jit(solution)/shard_map/ppermute | solution.py:57
  56.8 13.8 %collective-permute-start.6 = (bf16[4,192,128]{2,1,0:T(8,128)(2,1)S(1)}, bf16[4,192,128]{2,1,0:T(8,128)(2,1)S(1)}, u32[]{:S(2)}, u32[]{:S(2)}) collective-permute-start(bf16[4,192,128]{2,1,0:T(8,128)(2,1)S(1)} %collective-permute-done.3), channel_id=1, source_target_pairs={{0,6},{1,7},{2,4},{3,5},{4,2},{5,3},{6,0},{7,1},{8,14},{9,15},{10,... | collective-permute-start | bytes 589832 | tf_op jit(solution)/shard_map/ppermute | solution.py:57
  70.6 6.0 %collective-permute-start.4 = (bf16[4,192,128]{2,1,0:T(8,128)(2,1)S(1)}, bf16[4,192,128]{2,1,0:T(8,128)(2,1)S(1)}, u32[]{:S(2)}, u32[]{:S(2)}) collective-permute-start(bf16[4,192,128]{2,1,0:T(8,128)(2,1)S(1)} %collective-permute-done.3), channel_id=1, source_target_pairs={{0,2},{1,3},{2,0},{3,1},{4,6},{5,7},{6,4},{7,5},{8,10},{9,11},{10,... | collective-permute-start | bytes 589832 | tf_op jit(solution)/shard_map/ppermute | solution.py:57
  76.7 6.5 %collective-permute-start.7 = (bf16[4,4,192,128]{3,2,1,0:T(8,128)(2,1)S(1)}, bf16[4,4,192,128]{3,2,1,0:T(8,128)(2,1)S(1)}, u32[]{:S(2)}, u32[]{:S(2)}) collective-permute-start(bf16[4,4,192,128]{3,2,1,0:T(8,128)(2,1)S(1)} %pad_maximum_fusion.own), channel_id=1, source_target_pairs={{0,1},{1,0},{2,3},{3,2},{4,5},{5,4},{6,7},{7,6},{8,9},{9,8},{10,11... | collective-permute-start | bytes 2359304 | tf_op jit(solution)/shard_map/ppermute | solution.py:57
  78.2 12.3 %collective-permute-start.17 = (bf16[512,768]{1,0:T(8,128)(2,1)S(1)}, bf16[512,768]{1,0:T(8,128)(2,1)S(1)}, u32[]{:S(2)}, u32[]{:S(2)}) collective-permute-start(bf16[512,768]{1,0:T(8,128)(2,1)S(1)} %constant_dynamic-update-slice_fusion.5), channel_id=1, source_target_pairs={{0,24},{1,193},{2,26},{3,195},{4,28},{5,197},{6,30},{7,199},{8,16}... | collective-permute-start | bytes 2359304 | tf_op jit(solution)/shard_map/ppermute | solution.py:57
  78.6 13.7 %collective-permute-start.16 = (bf16[512,768]{1,0:T(8,128)(2,1)S(1)}, bf16[512,768]{1,0:T(8,128)(2,1)S(1)}, u32[]{:S(2)}, u32[]{:S(2)}) collective-permute-start(bf16[512,768]{1,0:T(8,128)(2,1)S(1)} %constant_dynamic-update-slice_fusion.2), channel_id=1, source_target_pairs={{0,8},{1,65},{2,10},{3,67},{4,12},{5,69},{6,14},{7,71},{8,0},{9,73... | collective-permute-start | bytes 2359304 | tf_op jit(solution)/shard_map/ppermute | solution.py:57
  78.7 20.3 %collective-permute-start.15 = (bf16[512,768]{1,0:T(8,128)(2,1)S(1)}, bf16[512,768]{1,0:T(8,128)(2,1)S(1)}, u32[]{:S(2)}, u32[]{:S(2)}) collective-permute-start(bf16[512,768]{1,0:T(8,128)(2,1)S(1)} %collective-permute-done.14.refs_1_), channel_id=1, source_target_pairs={{0,24},{1,193},{2,26},{3,195},{4,28},{5,197},{6,30},{7,199},{8,16}... | collective-permute-start | bytes 2359304 | tf_op jit(solution)/shard_map/ppermute | solution.py:57
  80.9 20.9 %collective-permute-start.11 = (bf16[512,768]{1,0:T(8,128)(2,1)S(1)}, bf16[512,768]{1,0:T(8,128)(2,1)S(1)}, u32[]{:S(2)}, u32[]{:S(2)}) collective-permute-start(bf16[512,768]{1,0:T(8,128)(2,1)S(1)} %collective-permute-done.10.refs_2_), channel_id=1, source_target_pairs={{0,8},{1,65},{2,10},{3,67},{4,12},{5,69},{6,14},{7,71},{8,0},{9,73... | collective-permute-start | bytes 2359304 | tf_op jit(solution)/shard_map/ppermute | solution.py:57
  83.3 27.3 %collective-permute-start.19 = (f32[768,128]{1,0:T(8,128)S(1)}, f32[768,128]{1,0:T(8,128)S(1)}, u32[]{:S(2)}, u32[]{:S(2)}) collective-permute-start(f32[768,128]{1,0:T(8,128)S(1)} %get-tuple-element.8), channel_id=1, source_target_pairs={{0,2},{1,3},{2,4},{3,5},{4,6},{5,7},{6,32},{7,33},{8,10},{9,11},{1... | collective-permute-start | bytes 1179656 | tf_op jit(solution)/shard_map/ppermute | solution.py:57
  90.5 20.0 %collective-permute-start.20 = (f32[768,128]{1,0:T(8,128)S(1)}, f32[768,128]{1,0:T(8,128)S(1)}, u32[]{:S(2)}, u32[]{:S(2)}) collective-permute-start(f32[768,128]{1,0:T(8,128)S(1)} %get-tuple-element.9), channel_id=1, source_target_pairs={{0,38},{1,39},{2,0},{3,1},{4,2},{5,3},{6,4},{7,5},{8,46},{9,47},{1... | collective-permute-start | bytes 1179656 | tf_op jit(solution)/shard_map/ppermute | solution.py:57
  92.4 12.2 %collective-permute-start.21 = (f32[384,128]{1,0:T(8,128)S(1)}, f32[384,128]{1,0:T(8,128)S(1)}, u32[]{:S(2)}, u32[]{:S(2)}) collective-permute-start(f32[384,128]{1,0:T(8,128)S(1)} %get-tuple-element.10), channel_id=1, source_target_pairs={{0,4},{1,5},{2,6},{3,7},{4,32},{5,33},{6,34},{7,35},{8,12},{9,13},... | collective-permute-start | bytes 589832 | tf_op jit(solution)/shard_map/ppermute | solution.py:57
  98.9 11.6 %collective-permute-start.22 = (f32[384,128]{1,0:T(8,128)S(1)}, f32[384,128]{1,0:T(8,128)S(1)}, u32[]{:S(2)}, u32[]{:S(2)}) collective-permute-start(f32[384,128]{1,0:T(8,128)S(1)} %get-tuple-element.11), channel_id=1, source_target_pairs={{0,36},{1,37},{2,38},{3,39},{4,0},{5,1},{6,2},{7,3},{8,44},{9,45},... | collective-permute-start | bytes 589832 | tf_op jit(solution)/shard_map/ppermute | solution.py:57
